TPU v7x, 32 devices: a whole 2x2x4 slice. The times are simulated.
32 devices in a mesh: section: 2 (over core), seq: 4 (over y, x), head: 4 (over z).
Axes of the slice: x: 2, y: 2, z: 4, core: 2. Of those that a mesh axis runs over, the one named last changes fastest.
Arguments:
- tokens: bfloat16 [2, 2048, 1792], P(None, 'seq'), may hold values from -6 to 6
- lengths: int32 [2, 4], replicated, may hold values from 1 to 1024, 2048 in all within a row
- gain_attn: bfloat16 [2, 1792], P('section'), may hold values from 0.5 to 1.5
- w_query: bfloat16 [2, 1792, 256], P('section', 'seq', 'head'), may hold values from -0.125 to 0.125
- w_key: bfloat16 [2, 1792, 256], P('section', 'seq', 'head'), may hold values from -0.125 to 0.125
- w_value: bfloat16 [2, 1792, 1792], P('section', 'seq', 'head'), may hold values from -0.125 to 0.125
- w_gate_conv: bfloat16 [2, 1792, 1792], P('section', 'seq', 'head'), may hold values from -0.125 to 0.125
- conv_taps: bfloat16 [2, 3, 1792], P('section'), may hold values from -3 to 3
- w_out: bfloat16 [2, 1792, 1792], P('section', 'head', 'seq'), may hold values from -1 to 1
- gain_ffn: bfloat16 [2, 1792], P('section'), may hold values from 0.5 to 1.5
- w_gate: bfloat16 [2, 1792, 4864], P('section', 'seq', 'head'), may hold values from -0.125 to 0.125
- w_up: bfloat16 [2, 1792, 4864], P('section', 'seq', 'head'), may hold values from -0.125 to 0.125
- w_down: bfloat16 [2, 4864, 1792], P('section', 'head', 'seq'), may hold values from -0.078125 to 0.078125
- cotangent: bfloat16 [2, 2048, 1792], P(None, 'seq'), may hold values from -6 to 6
Outputs:
- activations: bfloat16 [2, 2, 2048, 1792], P('section', None, 'seq')
- input_grads: bfloat16 [2, 2, 2048, 1792], P('section', None, 'seq')
- grad_gain_attn: float32 [2, 1792], P('section')
- grad_w_query: float32 [2, 1792, 256], P('section', 'seq', 'head')
- grad_w_key: float32 [2, 1792, 256], P('section', 'seq', 'head')
- grad_w_value: float32 [2, 1792, 1792], P('section', 'seq', 'head')
- grad_w_gate_conv: float32 [2, 1792, 1792], P('section', 'seq', 'head')
- grad_conv_taps: float32 [2, 3, 1792], P('section')
- grad_w_out: float32 [2, 1792, 1792], P('section', 'head', 'seq')
- grad_gain_ffn: float32 [2, 1792], P('section')
- grad_w_gate: float32 [2, 1792, 4864], P('section', 'seq', 'head')
- grad_w_up: float32 [2, 1792, 4864], P('section', 'seq', 'head')
- grad_w_down: float32 [2, 4864, 1792], P('section', 'head', 'seq')
Inputs may be any that keep to these rules, and one draw needn't show every extreme that they name: Each row holds the lengths of 4 sequences that fill the 2048 tokens of one micro-batch; in every row the longest is exactly 1024.
All inputs are finite; a program needn't handle non-finite values.
Results may differ from a plain program's by a relative error of at most 0.035.
Values may be sent and summed in bfloat16 or wider, within the bound.
A program may use at most 256 MiB of HBM per device.

v0:
```python
import math

import jax
import jax.numpy as jnp
from jax import lax
from jax.sharding import PartitionSpec as P

FK = 16
KW = 3


precise = lax.Precision.HIGHEST
epsilon = 1e-05


def carried_in_2(x, axis, join, neutral):
    place = lax.axis_index(axis)
    gathered = jax.tree.map(
        lambda a, kind: lax.all_gather(a.astype(kind), axis),
        x,
        (jnp.bfloat16, jnp.bfloat16, jnp.bfloat16),
    )
    state = jax.tree.map(lambda a, e: jnp.zeros_like(a) + jnp.asarray(e, a.dtype), x, neutral)

    def one(turn, state):
        return join(
            state,
            jax.tree.map(
                lambda a, own: lax.dynamic_index_in_dim(a, turn, 0, False).astype(own.dtype),
                gathered,
                x,
            ),
        )

    return lax.fori_loop(0, place, one, state)


def carried_in_3(x, axis, combine, identity):
    devices, mine = (lax.axis_size(axis), lax.axis_index(axis))
    everything = jax.tree.map(
        lambda part, kind: lax.all_gather(part.astype(kind), axis),
        x,
        jax.tree.map(lambda a: jnp.bfloat16 if a.dtype == jnp.float32 else a.dtype, x),
    )
    start = jax.tree.map(
        lambda part, zero: jnp.broadcast_to(jnp.asarray(zero, part.dtype), part.shape), x, identity
    )

    def turn(k, before):
        at = devices - 1 - k
        reached = at > mine
        new = combine(
            before, jax.tree.map(lambda part, own: part[at].astype(own.dtype), everything, x)
        )
        return jax.tree.map(lambda a, b: jnp.where(reached, a, b), new, before)

    return lax.fori_loop(0, devices, turn, start)


def from_behind(x, axis, by):
    devices = lax.axis_size(axis)
    pairs = [(i, i + by) for i in range(devices) if 0 <= i + by < devices]
    return lax.ppermute(x, axis, pairs)


def rms_norm(vector, scale_gain):
    return (
        vector * lax.rsqrt(jnp.mean(vector * vector, axis=-1, keepdims=True) + epsilon) * scale_gain
    )


def features(vector):
    second = vector[..., :, None] * vector[..., None, :] / (4.0 * math.sqrt(2.0))
    constant = jnp.ones(vector.shape[:-1] + (1,), jnp.float32)
    squares = second.reshape(vector.shape[:-1] + (vector.shape[-1] * vector.shape[-1],))
    return jnp.concatenate([constant, vector * 0.5, squares], axis=-1)


def seq_begin(lengths_row, positions):
    seq_starts = jnp.cumsum(lengths_row) - lengths_row
    chosen = jnp.where(seq_starts[None, :] <= positions[:, None], seq_starts[None, :], 0)
    return jnp.max(chosen, axis=1)


def chain_combine(earlier_part, later_part):
    carried = 1.0 - later_part[2][0]
    return (
        later_part[0] + carried * earlier_part[0],
        later_part[1] + carried * earlier_part[1],
        jnp.maximum(earlier_part[2], later_part[2]),
    )


def carry_forward(local_state, local_norm, restart):
    identity = (
        jnp.zeros_like(local_state),
        jnp.zeros_like(local_norm),
        jnp.zeros((1,), jnp.float32),
    )
    prefix = carried_in_2((local_state, local_norm, restart[None]), "seq", chain_combine, identity)
    state_in, norm_in = (prefix[0], prefix[1])
    return (state_in, norm_in)


def carry_backward(state_grad, norm_grad, restart):
    identity = (jnp.zeros_like(state_grad), jnp.zeros_like(norm_grad), jnp.zeros((1,), jnp.float32))
    suffix = carried_in_3((state_grad, norm_grad, restart[None]), "seq", chain_combine, identity)
    state_out, norm_out = (suffix[0], suffix[1])
    return (state_out, norm_out)


def head_total(part_sum):
    return lax.psum(part_sum.astype(jnp.bfloat16), "head").astype(jnp.float32)


def head_back(part_sum):
    return lax.psum(part_sum.astype(jnp.bfloat16), "head").astype(jnp.float32)


def own_scores(query_heads, key_heads, starts_at):
    row_count = starts_at.shape[0]
    scores = (
        jnp.einsum("thf,shf->hts", query_heads, key_heads, preferred_element_type=jnp.float32)
        * 0.25
    )
    places = jnp.arange(row_count, dtype=jnp.int32)
    visible = (starts_at[:, None] == starts_at[None, :]) & (places[None, :] <= places[:, None])
    return (scores, visible)


def forward_layer(inputs, begin_ext, setting):
    weights_all, gain_one, gain_two, taps_local, block_start = setting
    (
        query_weight,
        key_weight,
        value_weight,
        gconv_weight,
        out_weight,
        gate_weight,
        up_weight,
        down_weight,
    ) = weights_all
    row_count = inputs.shape[0]
    starts_at = begin_ext[:row_count]
    positions = block_start + jnp.arange(row_count, dtype=jnp.int32)
    normed = rms_norm(inputs, gain_one).astype(jnp.bfloat16)
    queries = jnp.dot(normed, query_weight, preferred_element_type=jnp.float32).astype(jnp.bfloat16)
    keys_low = jnp.dot(normed, key_weight, preferred_element_type=jnp.float32).astype(jnp.bfloat16)
    values_low = jnp.dot(normed, value_weight, preferred_element_type=jnp.float32).astype(
        jnp.bfloat16
    )
    gate_conv = jnp.dot(normed, gconv_weight, preferred_element_type=jnp.float32)
    local_heads = queries.shape[1] // FK
    query_heads = queries.reshape(row_count, local_heads, FK)
    key_heads = keys_low.reshape(row_count, local_heads, FK)
    value_heads = values_low.reshape(row_count, local_heads, -1)
    scores, visible = own_scores(query_heads, key_heads, starts_at)
    attn_weights = jnp.where(visible[None], 1.0 + scores + 0.5 * scores * scores, 0.0).astype(
        jnp.bfloat16
    )
    phi_query = features(query_heads.astype(jnp.float32))
    phi_key = features(key_heads.astype(jnp.float32))
    last_rows = (starts_at == starts_at[row_count - 1]).astype(jnp.float32)
    restart = (starts_at[row_count - 1] >= block_start).astype(jnp.float32)
    phi_last = phi_key * last_rows[:, None, None]
    local_state = jnp.einsum(
        "shp,she->hpe", phi_last, value_heads.astype(jnp.float32), precision=precise
    )
    local_norm = jnp.sum(phi_last, axis=0)
    state_in, norm_in = carry_forward(local_state, local_norm, restart)
    carried_in = (starts_at < block_start).astype(jnp.float32)
    numerator = jnp.einsum(
        "hts,she->the", attn_weights, value_heads, preferred_element_type=jnp.float32
    ) + carried_in[:, None, None] * jnp.einsum(
        "thp,hpe->the", phi_query, state_in, precision=precise
    )
    denominator = jnp.transpose(jnp.sum(attn_weights, axis=2, dtype=jnp.float32)) + carried_in[
        :, None
    ] * jnp.einsum("thp,hp->th", phi_query, norm_in, precision=precise)
    attended = (numerator / denominator[:, :, None]).reshape(row_count, -1)
    edge_rows = from_behind(attended[row_count - 2 :], "seq", 1)
    extended = jnp.concatenate([edge_rows, attended], axis=0)
    conv_out = taps_local[0] * extended[2:]
    for offset in range(1, KW):
        allowed = (positions - offset >= starts_at).astype(jnp.float32)
        conv_out = (
            conv_out
            + taps_local[offset] * extended[2 - offset : 2 - offset + row_count] * allowed[:, None]
        )
    gated_out = (conv_out * gate_conv).astype(jnp.bfloat16)
    branch_part = jnp.dot(gated_out, out_weight, preferred_element_type=jnp.float32)
    middle = inputs + head_total(branch_part)
    normed_two = rms_norm(middle, gain_two).astype(jnp.bfloat16)
    gate_pre = jnp.dot(normed_two, gate_weight, preferred_element_type=jnp.float32)
    upward = jnp.dot(normed_two, up_weight, preferred_element_type=jnp.float32)
    hidden = (jax.nn.silu(gate_pre) * upward).astype(jnp.bfloat16)
    ffn_part = jnp.dot(hidden, down_weight, preferred_element_type=jnp.float32)
    output = middle + head_total(ffn_part)
    stored = (
        inputs,
        begin_ext,
        normed,
        queries,
        keys_low,
        values_low,
        gate_conv,
        state_in,
        norm_in,
        numerator,
        denominator,
        extended,
        conv_out,
        gated_out,
        middle,
        normed_two,
        gate_pre,
        upward,
        hidden,
    )
    return (output, stored)


def backward_layer(grad_out, stored, setting):
    weights_all, gain_one, gain_two, taps_local, block_start = setting
    (
        query_weight,
        key_weight,
        value_weight,
        gconv_weight,
        out_weight,
        gate_weight,
        up_weight,
        down_weight,
    ) = weights_all
    (
        inputs,
        begin_ext,
        normed,
        queries,
        keys_low,
        values_low,
        gate_conv,
        state_in,
        norm_in,
        numerator,
        denominator,
        extended,
        conv_out,
        gated_out,
        middle,
        normed_two,
        gate_pre,
        upward,
        hidden,
    ) = stored
    row_count = inputs.shape[0]
    starts_at = begin_ext[:row_count]
    positions_ext = block_start + jnp.arange(row_count + 2, dtype=jnp.int32)
    grad_low = grad_out.astype(jnp.bfloat16)
    grad_down = jnp.einsum("tf,td->fd", hidden, grad_low, preferred_element_type=jnp.float32)
    back_hidden = jnp.einsum("td,fd->tf", grad_low, down_weight, preferred_element_type=jnp.float32)
    silu_value, silu_back = jax.vjp(jax.nn.silu, gate_pre)
    back_gate = silu_back(back_hidden * upward)[0].astype(jnp.bfloat16)
    back_up = (back_hidden * silu_value).astype(jnp.bfloat16)
    grad_gate = jnp.einsum("tc,tf->cf", normed_two, back_gate, preferred_element_type=jnp.float32)
    grad_up = jnp.einsum("tc,tf->cf", normed_two, back_up, preferred_element_type=jnp.float32)
    part_two = jnp.einsum(
        "tf,cf->tc", back_gate, gate_weight, preferred_element_type=jnp.float32
    ) + jnp.einsum("tf,cf->tc", back_up, up_weight, preferred_element_type=jnp.float32)
    back_norm_two = head_back(part_two)
    unused_two, norm_back_two = jax.vjp(rms_norm, middle, gain_two)
    back_middle, grad_gain_two = norm_back_two(back_norm_two)
    back_middle = grad_out + back_middle
    back_branch = back_middle.astype(jnp.bfloat16)
    grad_out_weight = jnp.einsum(
        "tc,td->cd", gated_out, back_branch, preferred_element_type=jnp.float32
    )
    back_gated = jnp.einsum(
        "td,cd->tc", back_branch, out_weight, preferred_element_type=jnp.float32
    )
    back_conv = back_gated * gate_conv
    back_gconv = (back_gated * conv_out).astype(jnp.bfloat16)
    grad_gconv = jnp.einsum("tc,tf->cf", normed, back_gconv, preferred_element_type=jnp.float32)
    edge_back = from_behind(back_conv[:2], "seq", -1)
    conv_ext = jnp.concatenate([back_conv, edge_back], axis=0)
    back_attended = taps_local[0] * back_conv
    taps_rows = [jnp.sum(back_conv * extended[2:], axis=0)]
    for offset in range(1, KW):
        allowed_ext = (positions_ext - offset >= begin_ext).astype(jnp.float32)
        back_attended = (
            back_attended
            + taps_local[offset]
            * conv_ext[offset : offset + row_count]
            * allowed_ext[offset : offset + row_count, None]
        )
        allowed = allowed_ext[:row_count]
        taps_rows.append(
            jnp.sum(
                back_conv * extended[2 - offset : 2 - offset + row_count] * allowed[:, None], axis=0
            )
        )
    local_heads = queries.shape[1] // FK
    query_heads = queries.reshape(row_count, local_heads, FK)
    key_heads = keys_low.reshape(row_count, local_heads, FK)
    value_heads = values_low.reshape(row_count, local_heads, -1)
    back_out = back_attended.reshape(row_count, local_heads, -1)
    back_numer = (back_out / denominator[:, :, None]).astype(jnp.bfloat16)
    back_numer_wide = back_numer.astype(jnp.float32)
    back_denom = -jnp.sum(back_out * numerator, axis=2) / (denominator * denominator)
    scores, visible = own_scores(query_heads, key_heads, starts_at)
    attn_weights = jnp.where(visible[None], 1.0 + scores + 0.5 * scores * scores, 0.0).astype(
        jnp.bfloat16
    )
    back_weights = (
        jnp.einsum("the,she->hts", back_numer, value_heads, preferred_element_type=jnp.float32)
        + jnp.transpose(back_denom)[:, :, None]
    )
    back_scores = jnp.where(visible[None], back_weights * (1.0 + scores), 0.0).astype(jnp.bfloat16)
    back_query = (
        jnp.einsum("hts,shf->thf", back_scores, key_heads, preferred_element_type=jnp.float32)
        * 0.25
    )
    back_key = (
        jnp.einsum("hts,thf->shf", back_scores, query_heads, preferred_element_type=jnp.float32)
        * 0.25
    )
    back_value = jnp.einsum(
        "hts,the->she", attn_weights, back_numer, preferred_element_type=jnp.float32
    )
    phi_query, phi_back_query = jax.vjp(features, query_heads.astype(jnp.float32))
    phi_key, phi_back_key = jax.vjp(features, key_heads.astype(jnp.float32))
    carried_in = (starts_at < block_start).astype(jnp.float32)
    back_phi_query = carried_in[:, None, None] * (
        jnp.einsum("the,hpe->thp", back_numer_wide, state_in, precision=precise)
        + back_denom[:, :, None] * norm_in[None]
    )
    phi_used = phi_query * carried_in[:, None, None]
    state_grad = jnp.einsum("thp,the->hpe", phi_used, back_numer_wide, precision=precise)
    norm_grad = jnp.einsum("thp,th->hp", phi_used, back_denom, precision=precise)
    last_rows = (starts_at == starts_at[row_count - 1]).astype(jnp.float32)
    restart = (starts_at[row_count - 1] >= block_start).astype(jnp.float32)
    state_out, norm_out = carry_backward(state_grad, norm_grad, restart)
    back_phi_key = last_rows[:, None, None] * (
        jnp.einsum("she,hpe->shp", value_heads.astype(jnp.float32), state_out, precision=precise)
        + norm_out[None]
    )
    back_value = back_value + last_rows[:, None, None] * jnp.einsum(
        "shp,hpe->she", phi_key, state_out, precision=precise
    )
    back_query = back_query + phi_back_query(back_phi_query)[0]
    back_key = back_key + phi_back_key(back_phi_key)[0]
    query_low = back_query.reshape(row_count, -1).astype(jnp.bfloat16)
    key_low = back_key.reshape(row_count, -1).astype(jnp.bfloat16)
    value_low = back_value.reshape(row_count, -1).astype(jnp.bfloat16)
    grad_query = jnp.einsum("tc,tf->cf", normed, query_low, preferred_element_type=jnp.float32)
    grad_key = jnp.einsum("tc,tf->cf", normed, key_low, preferred_element_type=jnp.float32)
    grad_value = jnp.einsum("tc,tf->cf", normed, value_low, preferred_element_type=jnp.float32)
    part_one = (
        jnp.einsum("tf,cf->tc", query_low, query_weight, preferred_element_type=jnp.float32)
        + jnp.einsum("tf,cf->tc", key_low, key_weight, preferred_element_type=jnp.float32)
        + jnp.einsum("tf,cf->tc", value_low, value_weight, preferred_element_type=jnp.float32)
        + jnp.einsum("tf,cf->tc", back_gconv, gconv_weight, preferred_element_type=jnp.float32)
    )
    back_normed = head_back(part_one)
    unused_one, norm_back_one = jax.vjp(rms_norm, inputs, gain_one)
    back_inputs, grad_gain_one = norm_back_one(back_normed)
    back_inputs = back_middle + back_inputs
    weight_grads = (
        grad_query,
        grad_key,
        grad_value,
        grad_gconv,
        grad_out_weight,
        grad_gate,
        grad_up,
        grad_down,
    )
    small_grads = (grad_gain_one, grad_gain_two, jnp.stack(taps_rows))
    return (back_inputs, weight_grads, small_grads)


def choose_tree(section_index, early_tree, late_tree):
    return jax.tree.map(
        lambda early_part, late_part: jnp.where(section_index == 0, early_part, late_part),
        early_tree,
        late_tree,
    )


def on_device(
    tokens,
    lengths,
    gain_attn,
    w_query,
    w_key,
    w_value,
    w_gate_conv,
    conv_taps,
    w_out,
    gain_ffn,
    w_gate,
    w_up,
    w_down,
    cotangent,
):
    head_count = lax.axis_size("head")
    head_index = lax.axis_index("head")
    section_index = lax.axis_index("section")
    micro_count, row_count, model_width = tokens.shape
    channels = model_width // head_count
    gathered = (
        lax.all_gather(w_query[0], "seq", axis=0, tiled=True),
        lax.all_gather(w_key[0], "seq", axis=0, tiled=True),
        lax.all_gather(w_value[0], "seq", axis=0, tiled=True),
        lax.all_gather(w_gate_conv[0], "seq", axis=0, tiled=True),
        lax.all_gather(w_out[0], "seq", axis=1, tiled=True),
        lax.all_gather(w_gate[0], "seq", axis=0, tiled=True),
        lax.all_gather(w_up[0], "seq", axis=0, tiled=True),
        lax.all_gather(w_down[0], "seq", axis=1, tiled=True),
    )
    taps_local = lax.dynamic_slice_in_dim(
        conv_taps[0].astype(jnp.float32), head_index * channels, channels, 1
    )
    block_start = lax.axis_index("seq") * row_count
    positions_ext = block_start + jnp.arange(row_count + 2, dtype=jnp.int32)
    begin_list = [
        seq_begin(lengths[micro_index], positions_ext) for micro_index in range(micro_count)
    ]
    setting = (
        gathered,
        gain_attn[0].astype(jnp.float32),
        gain_ffn[0].astype(jnp.float32),
        taps_local,
        block_start,
    )
    received = jnp.zeros((row_count, model_width), jnp.bfloat16)
    outputs_list = []
    stored_list = []
    for moment in range(micro_count + 1):
        early = min(moment, micro_count - 1)
        late = max(moment - 1, 0)
        layer_in = jnp.where(section_index == 0, tokens[early], received)
        starts_at = jnp.where(section_index == 0, begin_list[early], begin_list[late])
        layer_out, stored = forward_layer(layer_in.astype(jnp.float32), starts_at, setting)
        layer_low = layer_out.astype(jnp.bfloat16)
        outputs_list.append(layer_low)
        stored_list.append(stored)
        if moment < micro_count:
            received = from_behind(layer_low, "section", 1)
    arriving = jnp.zeros((row_count, model_width), jnp.bfloat16)
    back_list = []
    grad_totals = None
    small_totals = None
    for moment in range(micro_count + 1):
        stored = choose_tree(
            section_index,
            stored_list[max(moment - 1, 0)],
            stored_list[min(moment + 1, micro_count)],
        )
        if moment < micro_count:
            from_top = cotangent[moment]
        else:
            from_top = jnp.zeros((row_count, model_width), jnp.bfloat16)
        grad_in = jnp.where(section_index == 1, from_top, arriving)
        back_inputs, weight_grads, small_grads = backward_layer(
            grad_in.astype(jnp.float32), stored, setting
        )
        back_rows = back_inputs.astype(jnp.bfloat16)
        back_list.append(back_rows)
        if moment < micro_count:
            arriving = from_behind(back_rows, "section", -1)
        small_totals = (
            small_grads
            if small_totals is None
            else jax.tree.map(jnp.add, small_totals, small_grads)
        )
        grad_totals = (
            weight_grads
            if grad_totals is None
            else jax.tree.map(jnp.add, grad_totals, weight_grads)
        )
    grad_query, grad_key, grad_value, grad_gconv, grad_out_weight, grad_gate, grad_up, grad_down = (
        grad_totals
    )
    grad_shards = (
        lax.psum_scatter(
            grad_query.astype(jnp.bfloat16), "seq", scatter_dimension=0, tiled=True
        ).astype(jnp.float32),
        lax.psum_scatter(
            grad_key.astype(jnp.bfloat16), "seq", scatter_dimension=0, tiled=True
        ).astype(jnp.float32),
        lax.psum_scatter(
            grad_value.astype(jnp.bfloat16), "seq", scatter_dimension=0, tiled=True
        ).astype(jnp.float32),
        lax.psum_scatter(
            grad_gconv.astype(jnp.bfloat16), "seq", scatter_dimension=0, tiled=True
        ).astype(jnp.float32),
        lax.psum_scatter(
            grad_out_weight.astype(jnp.bfloat16), "seq", scatter_dimension=1, tiled=True
        ).astype(jnp.float32),
        lax.psum_scatter(
            grad_gate.astype(jnp.bfloat16), "seq", scatter_dimension=0, tiled=True
        ).astype(jnp.float32),
        lax.psum_scatter(
            grad_up.astype(jnp.bfloat16), "seq", scatter_dimension=0, tiled=True
        ).astype(jnp.float32),
        lax.psum_scatter(
            grad_down.astype(jnp.bfloat16), "seq", scatter_dimension=1, tiled=True
        ).astype(jnp.float32),
    )
    column_mask = (jnp.arange(model_width, dtype=jnp.int32) // channels == head_index).astype(
        jnp.float32
    )
    gain_one_sum, gain_two_sum, taps_sum = small_totals
    taps_full = lax.dynamic_update_slice_in_dim(
        jnp.zeros((taps_sum.shape[0], model_width), jnp.float32), taps_sum, head_index * channels, 1
    )
    total_gain_one, total_gain_two, total_taps = lax.psum(
        (gain_one_sum * column_mask, gain_two_sum * column_mask, taps_full), ("seq", "head")
    )
    activations = jnp.stack(
        [
            jnp.where(section_index == 0, outputs_list[micro_index], outputs_list[micro_index + 1])
            for micro_index in range(micro_count)
        ]
    )[None]
    input_grads = jnp.stack(
        [
            jnp.where(section_index == 0, back_list[micro_index + 1], back_list[micro_index])
            for micro_index in range(micro_count)
        ]
    )[None]
    return (
        activations,
        input_grads,
        total_gain_one[None],
        grad_shards[0][None],
        grad_shards[1][None],
        grad_shards[2][None],
        grad_shards[3][None],
        total_taps[None],
        grad_shards[4][None],
        total_gain_two[None],
        grad_shards[5][None],
        grad_shards[6][None],
        grad_shards[7][None],
    )


def solution(mesh):
    placed = (
        P(None, "seq", None),
        P(),
        P("section", None),
        P("section", "seq", "head"),
        P("section", "seq", "head"),
        P("section", "seq", "head"),
        P("section", "seq", "head"),
        P("section", None, None),
        P("section", "head", "seq"),
        P("section", None),
        P("section", "seq", "head"),
        P("section", "seq", "head"),
        P("section", "head", "seq"),
        P(None, "seq", None),
    )
    return jax.shard_map(
        on_device,
        mesh=mesh,
        in_specs=placed,
        out_specs=(
            P("section", None, "seq", None),
            P("section", None, "seq", None),
            P("section", None),
            P("section", "seq", "head"),
            P("section", "seq", "head"),
            P("section", "seq", "head"),
            P("section", "seq", "head"),
            P("section", None, None),
            P("section", "head", "seq"),
            P("section", None),
            P("section", "seq", "head"),
            P("section", "seq", "head"),
            P("section", "head", "seq"),
        ),
        check_vma=False,
    )
```

profile of v0, /device:TPU:0, one launch (start us, length us, event | category | flops | bytes accessed | tf_op | source)
XLA Modules:
  0.0 2109.5 jit_solution(13312513631223001929)
XLA Ops:
  13.5 18.8 all-gather.1
  38.0 19.0 all-gather.2
  71.2 8.3 all-gather.20
  88.3 10.0 all-reduce.10
  103.0 14.1 all-gather.3
  131.3 8.7 copy.105
  140.0 7.9 all-gather.35.cloned.1.call-done
  147.9 5.6 multiply_convert_fusion.14
  159.0 77.1 %all-reduce.21.cloned.1.call-done = bf16[512,1792]{1,0:T(8,128)(2,1)} async-done(((bf16[512,1792]{1,0:T(8,128)(2,1)}), bf16[512,1792]{1,0:T(8,128)(2,1)}) %all-reduce.21.cloned.1.call-update) | async-done | bytes 1835024 | tf_op jit(solution)/shard_map/psum | solution.py:113
  241.6 51.0 %all-gather.39.cloned.1.call-done = bf16[1,1792,1216]{2,1,0:T(8,128)(2,1)} async-done(((bf16[1,448,1216]{2,1,0:T(8,128)(2,1)}), bf16[1,1792,1216]{2,1,0:T(8,128)(2,1)}) %all-gather.39.cloned.1.call-update) | async-done | bytes 4358160 | tf_op jit(solution)/shard_map/all_gather | solution.py:417
  292.6 6.3 fusion.40
  298.9 51.3 %all-gather.41.cloned.1.call-done = bf16[1,1792,1216]{2,1,0:T(8,128)(2,1)} async-done(((bf16[1,448,1216]{2,1,0:T(8,128)(2,1)}), bf16[1,1792,1216]{2,1,0:T(8,128)(2,1)}) %all-gather.41.cloned.1.call-update) | async-done | bytes 4358160 | tf_op jit(solution)/shard_map/all_gather | solution.py:418
  350.2 7.7 multiply_convert_fusion.8
  357.9 50.0 %all-gather.43.cloned.1.call-done = bf16[1,1216,1792]{1,2,0:T(8,128)(2,1)} async-done(((bf16[1,1216,448]{1,2,0:T(8,128)(2,1)}), bf16[1,1216,1792]{1,2,0:T(8,128)(2,1)}) %all-gather.43.cloned.1.call-update) | async-done | bytes 4358160 | tf_op jit(solution)/shard_map/all_gather | solution.py:419
  407.9 6.5 fusion.90
  414.5 77.7 %all-reduce.23.cloned.1.call-done = bf16[512,1792]{1,0:T(8,128)(2,1)} async-done(((bf16[512,1792]{1,0:T(8,128)(2,1)}), bf16[512,1792]{1,0:T(8,128)(2,1)}) %all-reduce.23.cloned.1.call-update) | async-done | bytes 1835024 | tf_op jit(solution)/shard_map/psum | solution.py:113
  511.7 17.2 all-gather.10
  528.9 7.9 all-gather.21
  546.1 6.7 collective-permute-start.2
  562.0 85.5 %all-reduce.25.cloned.1.call-done = bf16[512,1792]{1,0:T(8,128)(2,1)} async-done(((bf16[512,1792]{1,0:T(8,128)(2,1)}), bf16[512,1792]{1,0:T(8,128)(2,1)}) %all-reduce.25.cloned.1.call-update) | async-done | bytes 1835024 | tf_op jit(solution)/shard_map/psum | solution.py:113
  647.6 5.8 multiply_reduce_fusion.5
  654.1 7.2 fusion.26
  665.3 7.8 fusion.104
  690.8 132.2 %all-reduce.37.cloned.1.call-done = (bf16[512,1792]{1,0:T(8,128)(2,1)}, bf16[512,1792]{1,0:T(8,128)(2,1)}) async-done(((bf16[512,1792]{1,0:T(8,128)(2,1)}, bf16[512,1792]{1,0:T(8,128)(2,1)}), (bf16[512,1792]{1,0:T(8,128)(2,1)}, bf16[512,1792]{1,0:T(8,128)(2,1)})) %all-reduce.37.cloned.1.call-update) | async-done | bytes 3670032 | tf_op jit(solution)/shard_map/psum | solution.py:113
  851.9 13.8 all-gather.12
  865.7 8.3 all-gather.22
  884.0 7.8 collective-permute-start.4
  904.1 10.2 collective-permute-done.5
  923.3 18.1 all-gather.14
  943.8 8.0 all-gather.23
  951.8 22.5 %while.99 = (s32[]{:T(128)}, f32[4,273,112]{2,1,0:T(8,128)}, f32[4,273]{1,0:T(4,128)}, s32[]{:T(128)}, bf16[4,4,273,112]{3,2,1,0:T(8,128)(2,1)}, /*index=5*/bf16...) while((s32[]{:T(128)}, f32[4,273,112]{2,1,0:T(8,128)}, ...), condition=%wide.region_35.36_spmd.clone, body=%wide.region_34.35_spmd.clone.sunk | while | flops 616989 | bytes 1234171 | solution.py:57
  999.3 134.3 %all-reduce.35.cloned.1.call-done = (bf16[512,1792]{1,0:T(8,128)(2,1)}, bf16[512,1792]{1,0:T(8,128)(2,1)}) async-done(((bf16[512,1792]{1,0:T(8,128)(2,1)}, bf16[512,1792]{1,0:T(8,128)(2,1)}), (bf16[512,1792]{1,0:T(8,128)(2,1)}, bf16[512,1792]{1,0:T(8,128)(2,1)})) %all-reduce.35.cloned.1.call-update) | async-done | bytes 3670032 | tf_op jit(solution)/shard_map/psum | solution.py:113
  1133.6 9.9 multiply_reduce_fusion.3
  1147.7 7.3 fusion.24
  1159.2 6.8 fusion.107
  1187.3 63.3 %all-reduce.27.cloned.1.call-done = bf16[512,1792]{1,0:T(8,128)(2,1)} async-done(((bf16[512,1792]{1,0:T(8,128)(2,1)}), bf16[512,1792]{1,0:T(8,128)(2,1)}) %all-reduce.27.cloned.1.call-update) | async-done | bytes 1835024 | tf_op jit(solution)/shard_map/psum | solution.py:117
  1263.8 6.1 collective-permute-done.7
  1273.9 15.1 all-gather.16
  1291.5 7.8 all-gather.24
  1299.3 20.5 while.100
  1342.4 76.6 %all-reduce.29.cloned.1.call-done = bf16[512,1792]{1,0:T(8,128)(2,1)} async-done(((bf16[512,1792]{1,0:T(8,128)(2,1)}), bf16[512,1792]{1,0:T(8,128)(2,1)}) %all-reduce.29.cloned.1.call-update) | async-done | bytes 1835024 | tf_op jit(solution)/shard_map/psum | solution.py:117
  1424.1 7.2 select_bitcast_fusion
  1440.1 9.7 fusion.110
  1467.3 66.9 %all-reduce.31.cloned.1.call-done = bf16[512,1792]{1,0:T(8,128)(2,1)} async-done(((bf16[512,1792]{1,0:T(8,128)(2,1)}), bf16[512,1792]{1,0:T(8,128)(2,1)}) %all-reduce.31.cloned.1.call-update) | async-done | bytes 1835024 | tf_op jit(solution)/shard_map/psum | solution.py:117
  1547.8 6.4 collective-permute-done.9
  1558.2 14.0 all-gather.18
  1574.7 8.7 all-gather.25
  1583.4 20.4 while.101
  1628.8 6.2 add_convert_fusion.14
  1657.4 6.3 fusion.96
  1672.0 6.3 fusion.379
  1678.3 6.3 fusion.381
  1684.5 11.6 add_convert_fusion.2
  1697.4 6.3 fusion.378
  1703.8 6.3 fusion.380
  1710.0 11.2 add_convert_fusion.1
  1726.9 6.2 fusion.240
  1733.1 8.8 add_convert_fusion
  1750.7 31.4 %reduce-scatter.15.cloned.1.call-done = bf16[448,448]{1,0:T(8,128)(2,1)} async-done(((bf16[1792,448]{1,0:T(8,128)(2,1)}), bf16[448,448]{1,0:T(8,128)(2,1)}) %reduce-scatter.15.cloned.1.call-update) | async-done | bytes 401424 | tf_op jit(solution)/shard_map/reduce_scatter | solution.py:492
  1784.1 138.8 %all-reduce.33.cloned.1.call-done = (bf16[512,1792]{1,0:T(8,128)(2,1)}, bf16[512,1792]{1,0:T(8,128)(2,1)}) async-done(((bf16[512,1792]{1,0:T(8,128)(2,1)}, bf16[512,1792]{1,0:T(8,128)(2,1)}), (bf16[512,1792]{1,0:T(8,128)(2,1)}, bf16[512,1792]{1,0:T(8,128)(2,1)})) %all-reduce.33.cloned.1.call-update) | async-done | bytes 3670032 | tf_op jit(solution)/shard_map/psum | solution.py:113
  1926.6 77.3 %all-reduce.6 = (f32[1,1792]{1,0:T(1,128)}, f32[1,3,1792]{2,0,1:T(1,128)}, f32[1,1792]{1,0:T(1,128)}) all-reduce(f32[1,1792]{1,0:T(1,128)S(1)} %broadcast_in_dim.148, f32[1,3,1792]{2,0,1:T(1,128)S(1)} %dynamic_update_slice.4, f32[1,1792]{1,0:T(1,128)S(1)} %broadcast_in_dim.161), channel_id=1, replica_groups=mesh['section'=2,'seq'=4,'head'=4] {'seq','head'}, use_global_device_ids=true, to_apply=%region_70.71 | all-reduce | flops 8960 | bytes 71680 | tf_op jit(solution)/shard_map/psum | solution.py:518
  2003.9 6.7 fusion.142
  2017.7 23.2 %reduce-scatter.21.cloned.1.call-done = bf16[448,1216]{1,0:T(8,128)(2,1)} async-done(((bf16[1792,1216]{1,0:T(8,128)(2,1)}), bf16[448,1216]{1,0:T(8,128)(2,1)}) %reduce-scatter.21.cloned.1.call-update) | async-done | bytes 1089552 | tf_op jit(solution)/shard_map/reduce_scatter | solution.py:504
  2043.6 56.2 %reduce-scatter.23.cloned.1.call-done = bf16[1216,448]{0,1:T(8,128)(2,1)} async-done(((bf16[1216,1792]{0,1:T(8,128)(2,1)}), bf16[1216,448]{0,1:T(8,128)(2,1)}) %reduce-scatter.23.cloned.1.call-update) | async-done | bytes 1089552 | tf_op jit(solution)/shard_map/reduce_scatter | solution.py:507
  (1147 shorter events, 480.9 us)
Async XLA Ops:
  7.2 91.1 %all-gather.33.cloned.1.call-start = ((), (), s32[]{:S(2)}) async-start(), calls=%async_computation.19 | async-start | bytes 2293760 | tf_op jit(solution)/shard_map/all_gather | solution.py:414
  7.9 123.4 %all-gather.37.cloned.1.call-start = ((), (), s32[]{:S(2)}) async-start(), calls=%async_computation.21 | async-start | bytes 4587520 | tf_op jit(solution)/shard_map/all_gather | solution.py:416
  11.5 21.8 %copy-start.334 = (bf16[1,1792]{1,0:T(2,128)(2,1)S(1)}, bf16[1,1792]{1,0:T(2,128)(2,1)}, u32[]{:S(2)}) copy-start(bf16[1,1792]{1,0:T(2,128)(2,1)} %param.28) | copy-start | bytes 10756
  11.5 136.4 %all-gather.35.cloned.1.call-start = ((), (), s32[]{:S(2)}) async-start(), calls=%async_computation.20 | async-start | bytes 2293760 | tf_op jit(solution)/shard_map/all_gather | solution.py:415
  12.2 223.8 %all-reduce.21.cloned.1.call-start = ((), (), s32[]{:S(2)}) async-start(), calls=%async_computation.8 | async-start | bytes 3670016 | tf_op jit(solution)/shard_map/psum | solution.py:113
  33.3 803.1 %copy-start.118 = (bf16[1,1792,64]{1,2,0:T(8,128)(2,1)}, bf16[1,1792,64]{1,2,0:T(8,128)(2,1)S(1)}, u32[]{:S(2)}) copy-start(bf16[1,1792,64]{1,2,0:T(8,128)(2,1)S(1)} %copy.100) | copy-start | bytes 688132
  33.3 814.0 %copy-start.211 = (f32[1792]{0:T(1024)}, f32[1792]{0:T(1024)S(1)}, u32[]{:S(2)}) copy-start(f32[1792]{0:T(1024)S(1)} %convert_reduce_fusion.4) | copy-start | bytes 21508
  35.4 112.5 %copy-start.306 = (f32[512]{0:T(512)}, f32[512]{0:T(512)S(1)}, u32[]{:S(2)}) copy-start(f32[512]{0:T(512)S(1)} %add_rsqrt_fusion.5) | copy-start | bytes 6148
  57.9 779.9 %copy-start.122 = (bf16[1,1792,64]{1,2,0:T(8,128)(2,1)}, bf16[1,1792,64]{1,2,0:T(8,128)(2,1)S(1)}, u32[]{:S(2)}) copy-start(bf16[1,1792,64]{1,2,0:T(8,128)(2,1)S(1)} %copy.102) | copy-start | bytes 688132
  60.3 25.2 %copy-start.221 = (bf16[512,64]{0,1:T(8,128)(2,1)}, bf16[512,64]{0,1:T(8,128)(2,1)S(1)}, u32[]{:S(2)}) copy-start(bf16[512,64]{0,1:T(8,128)(2,1)S(1)} %convolution_convert_fusion.7) | copy-start | bytes 196612
  70.6 779.8 %copy-start.240 = (f32[273]{0:T(512)}, f32[273]{0:T(512)S(1)}, u32[]{:S(2)}) copy-start(f32[273]{0:T(512)S(1)} %pad.58.clone) | copy-start | bytes 3280
  126.6 21.3 %collective-permute-start = (f32[2,448]{0,1:T(8,128)S(1)}, f32[2,448]{0,1:T(8,128)S(1)}, u32[]{:S(2)}, u32[]{:S(2)}) collective-permute-start(f32[2,448]{0,1:T(8,128)S(1)} %bitcast.795), channel_id=1, source_target_pairs={{0,4},{4,8},{8,12},{1,5},{5,9},{9,13},{2,6},{6,10},{10,14},{3,7},{... | collective-permute-start | bytes 10760 | tf_op jit(solution)/shard_map/ppermute | solution.py:63
  131.2 16.7 copy-start.278
  131.2 16.7 copy-start.283
  156.7 135.9 %all-gather.39.cloned.1.call-start = ((), (), s32[]{:S(2)}) async-start(), calls=%async_computation.22 | async-start | bytes 5734400 | tf_op jit(solution)/shard_map/all_gather | solution.py:417
  157.3 192.9 %all-gather.41.cloned.1.call-start = ((), (), s32[]{:S(2)}) async-start(), calls=%async_computation.23 | async-start | bytes 5734400 | tf_op jit(solution)/shard_map/all_gather | solution.py:418
  157.9 250.0 %all-gather.43.cloned.1.call-start = ((), (), s32[]{:S(2)}) async-start(), calls=%async_computation.24 | async-start | bytes 5734400 | tf_op jit(solution)/shard_map/all_gather | solution.py:419
  158.7 333.6 %all-reduce.23.cloned.1.call-start = ((), (), s32[]{:S(2)}) async-start(), calls=%async_computation.9 | async-start | bytes 3670016 | tf_op jit(solution)/shard_map/psum | solution.py:113
  159.0 673.2 %copy-start.181 = (f32[1792]{0:T(1024)}, f32[1792]{0:T(1024)S(1)}, u32[]{:S(2)}) copy-start(f32[1792]{0:T(1024)S(1)} %convert_reduce_fusion.3) | copy-start | bytes 21508
  241.6 108.6 %copy-start.19 = (bf16[512,1792]{1,0:T(8,128)(2,1)}, bf16[512,1792]{1,0:T(8,128)(2,1)S(1)}, u32[]{:S(2)}) copy-start(bf16[512,1792]{1,0:T(8,128)(2,1)S(1)} %multiply_convert_fusion.2) | copy-start | bytes 5505028
  414.4 77.8 %copy-start.27 = (bf16[512,1792]{1,0:T(8,128)(2,1)S(1)}, bf16[512,1792]{1,0:T(8,128)(2,1)}, u32[]{:S(2)}) copy-start(bf16[512,1792]{1,0:T(8,128)(2,1)} %all-reduce.21.cloned.1.call-done) | copy-start | bytes 5505028
  414.5 233.1 %all-reduce.25.cloned.1.call-start = ((), (), s32[]{:S(2)}) async-start(), calls=%async_computation.10 | async-start | bytes 3670016 | tf_op jit(solution)/shard_map/psum | solution.py:113
  496.3 5.1 collective-permute-start.1
  503.6 920.4 %copy-start = (bf16[512,1792]{1,0:T(8,128)(2,1)}, bf16[512,1792]{1,0:T(8,128)(2,1)S(1)}, u32[]{:S(2)}) copy-start(bf16[512,1792]{1,0:T(8,128)(2,1)S(1)} %get-tuple-element.976) | copy-start | bytes 5505028
  510.2 18.7 copy-start.206
  536.8 437.4 %copy-start.32 = (f32[4,273,112]{2,1,0:T(8,128)}, f32[4,273,112]{2,1,0:T(8,128)S(1)}, u32[]{:S(2)}) copy-start(f32[4,273,112]{2,1,0:T(8,128)S(1)} %get-tuple-element.723) | copy-start | bytes 1467652
  546.1 10.0 collective-permute-start.2
  562.0 261.0 %all-reduce.37.cloned.1.call-start = ((), (), s32[]{:S(2)}) async-start(), calls=%async_computation.30 | async-start | bytes 7340032 | tf_op jit(solution)/shard_map/psum | solution.py:113
  685.7 447.8 %all-reduce.35.cloned.1.call-start = ((), (), s32[]{:S(2)}) async-start(), calls=%async_computation.29 | async-start | bytes 7340032 | tf_op jit(solution)/shard_map/psum | solution.py:113
  828.0 7.5 collective-permute-start.3
  884.0 11.3 collective-permute-start.4
  901.9 12.3 collective-permute-start.5
  918.6 22.8 %copy-start.273 = (f32[512,4]{0,1:T(4,128)}, f32[512,4]{0,1:T(4,128)S(1)}, u32[]{:S(2)}) copy-start(f32[512,4]{0,1:T(4,128)S(1)} %get-tuple-element.963) | copy-start | bytes 24580
  921.7 19.7 copy-start.141
  996.8 136.8 %copy-start.213 = (f32[1792]{0:T(1024)S(1)}, f32[1792]{0:T(1024)}, u32[]{:S(2)}) copy-start(f32[1792]{0:T(1024)} %copy-done.211) | copy-start | bytes 21508
  996.8 253.8 %all-reduce.27.cloned.1.call-start = ((), (), s32[]{:S(2)}) async-start(), calls=%async_computation.11 | async-start | bytes 3670016 | tf_op jit(solution)/shard_map/psum | solution.py:117
  1145.4 13.5 collective-permute-start.6
  1173.0 246.1 %all-reduce.29.cloned.1.call-start = ((), (), s32[]{:S(2)}) async-start(), calls=%async_computation.12 | async-start | bytes 3670016 | tf_op jit(solution)/shard_map/psum | solution.py:117
  1261.6 8.3 collective-permute-start.7
  1271.3 17.8 copy-start.272
  1272.0 17.0 copy-start.139
  1339.6 79.4 %copy-start.214 = (f32[1792]{0:T(1024)S(1)}, f32[1792]{0:T(1024)}, u32[]{:S(2)}) copy-start(f32[1792]{0:T(1024)} %copy-done.211) | copy-start | bytes 21508
  1342.1 192.2 %all-reduce.31.cloned.1.call-start = ((), (), s32[]{:S(2)}) async-start(), calls=%async_computation.13 | async-start | bytes 3670016 | tf_op jit(solution)/shard_map/psum | solution.py:117
  1342.4 81.6 %copy-start.307 = (f32[512]{0:T(512)S(1)}, f32[512]{0:T(512)}, u32[]{:S(2)}) copy-start(f32[512]{0:T(512)} %copy-done.306) | copy-start | bytes 6148
  1342.4 81.6 %copy-start.310 = (f32[512]{0:T(512)S(1)}, f32[512]{0:T(512)}, u32[]{:S(2)}) copy-start(f32[512]{0:T(512)} %copy-done.308) | copy-start | bytes 6148
  1342.4 81.6 %copy-start.313 = (f32[512]{0:T(512)S(1)}, f32[512]{0:T(512)}, u32[]{:S(2)}) copy-start(f32[512]{0:T(512)} %copy-done.311) | copy-start | bytes 6148
  1431.3 8.8 collective-permute-start.8
  1433.8 138.5 %copy-start.305 = (f32[512]{0:T(512)}, f32[512]{0:T(512)S(1)}, u32[]{:S(2)}) copy-start(f32[512]{0:T(512)S(1)} %get-tuple-element.1040) | copy-start | bytes 6148
  1434.8 17.7 slice-start.8
  1456.4 286.5 %reduce-scatter.25.cloned.1.call-start = ((), (), s32[]{:S(2)}) async-start(), calls=%async_computation.25 | async-start | bytes 573440
  1466.1 68.1 %copy-start.184 = (f32[1792]{0:T(1024)S(1)}, f32[1792]{0:T(1024)}, u32[]{:S(2)}) copy-start(f32[1792]{0:T(1024)} %copy-done.181) | copy-start | bytes 21508
  1545.1 9.1 collective-permute-start.9
  1555.6 16.7 copy-start.271
  1583.3 20.4 copy-start.33
  1619.1 124.9 %reduce-scatter.27.cloned.1.call-start = ((), (), s32[]{:S(2)}) async-start(), calls=%async_computation.26 | async-start | bytes 573440
  1628.8 117.6 %reduce-scatter.29.cloned.1.call-start = ((), (), s32[]{:S(2)}) async-start(), calls=%async_computation.27 | async-start | bytes 2293760
  1638.9 109.7 %reduce-scatter.17.cloned.1.call-start = ((), (), s32[]{:S(2)}) async-start(), calls=%async_computation.15 | async-start | bytes 2293760 | tf_op jit(solution)/shard_map/reduce_scatter | solution.py:495
  1645.9 136.2 %reduce-scatter.15.cloned.1.call-start = ((), (), s32[]{:S(2)}) async-start(), calls=%async_computation.14 | async-start | bytes 2293760 | tf_op jit(solution)/shard_map/reduce_scatter | solution.py:492
  1657.1 265.9 %all-reduce.33.cloned.1.call-start = ((), (), s32[]{:S(2)}) async-start(), calls=%async_computation.28 | async-start | bytes 7340032 | tf_op jit(solution)/shard_map/psum | solution.py:113
  1670.2 344.7 %reduce-scatter.19.cloned.1.call-start = ((), (), s32[]{:S(2)}) async-start(), calls=%async_computation.16 | async-start | bytes 5734400 | tf_op jit(solution)/shard_map/reduce_scatter | solution.py:501
  1696.2 344.7 %reduce-scatter.21.cloned.1.call-start = ((), (), s32[]{:S(2)}) async-start(), calls=%async_computation.17 | async-start | bytes 5734400 | tf_op jit(solution)/shard_map/reduce_scatter | solution.py:504
  1721.3 378.5 %reduce-scatter.23.cloned.1.call-start = ((), (), s32[]{:S(2)}) async-start(), calls=%async_computation.18 | async-start | bytes 5734400 | tf_op jit(solution)/shard_map/reduce_scatter | solution.py:507
  1747.6 175.4 %copy-start.1 = (bf16[512,1792]{1,0:T(8,128)(2,1)S(1)}, bf16[512,1792]{1,0:T(8,128)(2,1)}, u32[]{:S(2)}) copy-start(bf16[512,1792]{1,0:T(8,128)(2,1)} %copy-done) | copy-start | bytes 5505028
  1747.6 175.4 %copy-start.215 = (f32[1792]{0:T(1024)S(1)}, f32[1792]{0:T(1024)}, u32[]{:S(2)}) copy-start(f32[1792]{0:T(1024)} %copy-done.211) | copy-start | bytes 21508
  (329 other events, 1514.4 us)
Sparse Core Ops, SparseCore 0:
  9.8 46.1 all-gather.32
  58.5 51.0 all-gather.36
  111.4 36.4 all-gather.34
  156.9 79.1 all-reduce.20
  237.8 54.8 all-gather.38
  294.3 55.8 all-gather.40
  352.0 55.8 all-gather.42
  414.6 77.5 all-reduce.22
  562.1 85.4 all-reduce.24
  685.9 137.0 all-reduce.36
  997.0 136.5 all-reduce.34
  1173.1 77.4 all-reduce.26
  1342.2 76.7 all-reduce.28
  1456.6 77.6 all-reduce.30
  1619.3 26.0 reduce-scatter.24
  1648.0 24.8 reduce-scatter.26
  1675.8 32.9 reduce-scatter.28
  1712.3 33.0 reduce-scatter.16
  1749.0 33.0 reduce-scatter.14
  1784.9 138.0 all-reduce.32
  1926.0 55.6 reduce-scatter.18
  1984.8 55.9 reduce-scatter.20
  2043.9 55.8 reduce-scatter.22
where the time goes:
time: 2120 us; the launch traced here: 2110 us
  waiting for transfers between devices  1150 us (54%)
  matrix products  334 us (16%)
  blocking collectives  267 us (13%)
  other arithmetic  220 us (10%)
  local copies, waits for them, and re-layouts  78 us (4%)
  starting transfers between devices  34 us (2%)
  between operations  22.7 us (1%)
    psum x6, waiting for transfers between devices, head_total(): return lax.psum(part_sum.astype(jnp.bfloat16), 'head').astype(jnp.float32)  646 us
    psum x3, waiting for transfers between devices, head_back(): return lax.psum(part_sum.astype(jnp.bfloat16), 'head').astype(jnp.float32)  207 us
    psum x1, blocking collectives, on_device(): lax.psum((gain_one_sum * column_mask, gain_two_sum * column_mask, taps_fu...  77.3 us
    all_gather x6, blocking collectives, carried_in_3(): lax.all_gather(part.astype(kind), axis)  71.7 us
    all_gather x6, blocking collectives, carried_in_2(): lax.all_gather(a.astype(kind), axis)  69.6 us
    reduce_scatter x1, waiting for transfers between devices, on_device(): lax.psum_scatter(grad_down.astype(jnp.bfloat16), 'seq', scatter_dimension...  56.2 us
    unnamed x742, local copies, waits for them, and re-layouts  55.3 us
    all_gather x1, waiting for transfers between devices, on_device(): lax.all_gather(w_up[0], 'seq', axis=0, tiled=True)  51.3 us
  transfers between devices with their start and end apart: 33, of which 21 were waited for; matrix products, arithmetic and copies ran while one was open for 13% of the time, Pallas kernels for 0%

commit v1 on v0

--- a/solution.py
+++ b/solution.py
@@ -9,7 +9,6 @@
 KW = 3
 
 
-precise = lax.Precision.HIGHEST
 epsilon = 1e-05
 
 
@@ -164,7 +163,7 @@
     restart = (starts_at[row_count - 1] >= block_start).astype(jnp.float32)
     phi_last = phi_key * last_rows[:, None, None]
     local_state = jnp.einsum(
-        "shp,she->hpe", phi_last, value_heads.astype(jnp.float32), precision=precise
+        "shp,she->hpe", phi_last, value_heads.astype(jnp.float32)
     )
     local_norm = jnp.sum(phi_last, axis=0)
     state_in, norm_in = carry_forward(local_state, local_norm, restart)
@@ -172,11 +171,11 @@
     numerator = jnp.einsum(
         "hts,she->the", attn_weights, value_heads, preferred_element_type=jnp.float32
     ) + carried_in[:, None, None] * jnp.einsum(
-        "thp,hpe->the", phi_query, state_in, precision=precise
+        "thp,hpe->the", phi_query, state_in
     )
     denominator = jnp.transpose(jnp.sum(attn_weights, axis=2, dtype=jnp.float32)) + carried_in[
         :, None
-    ] * jnp.einsum("thp,hp->th", phi_query, norm_in, precision=precise)
+    ] * jnp.einsum("thp,hp->th", phi_query, norm_in)
     attended = (numerator / denominator[:, :, None]).reshape(row_count, -1)
     edge_rows = from_behind(attended[row_count - 2 :], "seq", 1)
     extended = jnp.concatenate([edge_rows, attended], axis=0)
@@ -188,13 +187,17 @@
             + taps_local[offset] * extended[2 - offset : 2 - offset + row_count] * allowed[:, None]
         )
     gated_out = (conv_out * gate_conv).astype(jnp.bfloat16)
-    branch_part = jnp.dot(gated_out, out_weight, preferred_element_type=jnp.float32)
+    branch_part = jnp.einsum(
+        "tc,dc->td", gated_out, out_weight, preferred_element_type=jnp.float32
+    )
     middle = inputs + head_total(branch_part)
     normed_two = rms_norm(middle, gain_two).astype(jnp.bfloat16)
     gate_pre = jnp.dot(normed_two, gate_weight, preferred_element_type=jnp.float32)
     upward = jnp.dot(normed_two, up_weight, preferred_element_type=jnp.float32)
     hidden = (jax.nn.silu(gate_pre) * upward).astype(jnp.bfloat16)
-    ffn_part = jnp.dot(hidden, down_weight, preferred_element_type=jnp.float32)
+    ffn_part = jnp.einsum(
+        "tf,df->td", hidden, down_weight, preferred_element_type=jnp.float32
+    )
     output = middle + head_total(ffn_part)
     stored = (
         inputs,
@@ -257,8 +260,8 @@
     starts_at = begin_ext[:row_count]
     positions_ext = block_start + jnp.arange(row_count + 2, dtype=jnp.int32)
     grad_low = grad_out.astype(jnp.bfloat16)
-    grad_down = jnp.einsum("tf,td->fd", hidden, grad_low, preferred_element_type=jnp.float32)
-    back_hidden = jnp.einsum("td,fd->tf", grad_low, down_weight, preferred_element_type=jnp.float32)
+    grad_down = jnp.einsum("tf,td->df", hidden, grad_low, preferred_element_type=jnp.float32)
+    back_hidden = jnp.einsum("td,df->tf", grad_low, down_weight, preferred_element_type=jnp.float32)
     silu_value, silu_back = jax.vjp(jax.nn.silu, gate_pre)
     back_gate = silu_back(back_hidden * upward)[0].astype(jnp.bfloat16)
     back_up = (back_hidden * silu_value).astype(jnp.bfloat16)
@@ -273,10 +276,10 @@
     back_middle = grad_out + back_middle
     back_branch = back_middle.astype(jnp.bfloat16)
     grad_out_weight = jnp.einsum(
-        "tc,td->cd", gated_out, back_branch, preferred_element_type=jnp.float32
+        "tc,td->dc", gated_out, back_branch, preferred_element_type=jnp.float32
     )
     back_gated = jnp.einsum(
-        "td,cd->tc", back_branch, out_weight, preferred_element_type=jnp.float32
+        "td,dc->tc", back_branch, out_weight, preferred_element_type=jnp.float32
     )
     back_conv = back_gated * gate_conv
     back_gconv = (back_gated * conv_out).astype(jnp.bfloat16)
@@ -331,21 +334,21 @@
     phi_key, phi_back_key = jax.vjp(features, key_heads.astype(jnp.float32))
     carried_in = (starts_at < block_start).astype(jnp.float32)
     back_phi_query = carried_in[:, None, None] * (
-        jnp.einsum("the,hpe->thp", back_numer_wide, state_in, precision=precise)
+        jnp.einsum("the,hpe->thp", back_numer_wide, state_in)
         + back_denom[:, :, None] * norm_in[None]
     )
     phi_used = phi_query * carried_in[:, None, None]
-    state_grad = jnp.einsum("thp,the->hpe", phi_used, back_numer_wide, precision=precise)
-    norm_grad = jnp.einsum("thp,th->hp", phi_used, back_denom, precision=precise)
+    state_grad = jnp.einsum("thp,the->hpe", phi_used, back_numer_wide)
+    norm_grad = jnp.einsum("thp,th->hp", phi_used, back_denom)
     last_rows = (starts_at == starts_at[row_count - 1]).astype(jnp.float32)
     restart = (starts_at[row_count - 1] >= block_start).astype(jnp.float32)
     state_out, norm_out = carry_backward(state_grad, norm_grad, restart)
     back_phi_key = last_rows[:, None, None] * (
-        jnp.einsum("she,hpe->shp", value_heads.astype(jnp.float32), state_out, precision=precise)
+        jnp.einsum("she,hpe->shp", value_heads.astype(jnp.float32), state_out)
         + norm_out[None]
     )
     back_value = back_value + last_rows[:, None, None] * jnp.einsum(
-        "shp,hpe->she", phi_key, state_out, precision=precise
+        "shp,hpe->she", phi_key, state_out
     )
     back_query = back_query + phi_back_query(back_phi_query)[0]
     back_key = back_key + phi_back_key(back_phi_key)[0]
@@ -379,11 +382,16 @@
     return (back_inputs, weight_grads, small_grads)
 
 
-def choose_tree(section_index, early_tree, late_tree):
-    return jax.tree.map(
-        lambda early_part, late_part: jnp.where(section_index == 0, early_part, late_part),
-        early_tree,
-        late_tree,
+def both_layers(weight):
+    gathered = lax.all_gather(weight, ("section", "seq"), axis=0, tiled=True)
+    rows = gathered.shape[0] // 2
+    return (gathered[:rows], gathered[rows:])
+
+
+def scatter_layers(first_grad, second_grad):
+    both = jnp.concatenate([first_grad, second_grad], axis=0).astype(jnp.bfloat16)
+    return lax.psum_scatter(both, ("section", "seq"), scatter_dimension=0, tiled=True).astype(
+        jnp.float32
     )
 
 
@@ -405,145 +413,116 @@
 ):
     head_count = lax.axis_size("head")
     head_index = lax.axis_index("head")
-    section_index = lax.axis_index("section")
+    micro = lax.axis_index("section")
     micro_count, row_count, model_width = tokens.shape
     channels = model_width // head_count
-    gathered = (
-        lax.all_gather(w_query[0], "seq", axis=0, tiled=True),
-        lax.all_gather(w_key[0], "seq", axis=0, tiled=True),
-        lax.all_gather(w_value[0], "seq", axis=0, tiled=True),
-        lax.all_gather(w_gate_conv[0], "seq", axis=0, tiled=True),
-        lax.all_gather(w_out[0], "seq", axis=1, tiled=True),
-        lax.all_gather(w_gate[0], "seq", axis=0, tiled=True),
-        lax.all_gather(w_up[0], "seq", axis=0, tiled=True),
-        lax.all_gather(w_down[0], "seq", axis=1, tiled=True),
-    )
-    taps_local = lax.dynamic_slice_in_dim(
-        conv_taps[0].astype(jnp.float32), head_index * channels, channels, 1
+    query_both = both_layers(w_query[0])
+    key_both = both_layers(w_key[0])
+    value_both = both_layers(w_value[0])
+    gconv_both = both_layers(w_gate_conv[0])
+    out_both = both_layers(w_out[0].T)
+    gate_both = both_layers(w_gate[0])
+    up_both = both_layers(w_up[0])
+    down_both = both_layers(w_down[0].T)
+    gains_one = lax.all_gather(gain_attn[0], "section").astype(jnp.float32)
+    gains_two = lax.all_gather(gain_ffn[0], "section").astype(jnp.float32)
+    taps_both = lax.dynamic_slice_in_dim(
+        lax.all_gather(conv_taps[0], "section").astype(jnp.float32),
+        head_index * channels,
+        channels,
+        2,
     )
     block_start = lax.axis_index("seq") * row_count
     positions_ext = block_start + jnp.arange(row_count + 2, dtype=jnp.int32)
-    begin_list = [
-        seq_begin(lengths[micro_index], positions_ext) for micro_index in range(micro_count)
+    starts_at = seq_begin(lax.dynamic_index_in_dim(lengths, micro, 0, False), positions_ext)
+    settings = [
+        (
+            (
+                query_both[layer],
+                key_both[layer],
+                value_both[layer],
+                gconv_both[layer],
+                out_both[layer],
+                gate_both[layer],
+                up_both[layer],
+                down_both[layer],
+            ),
+            gains_one[layer],
+            gains_two[layer],
+            taps_both[layer],
+            block_start,
+        )
+        for layer in range(2)
     ]
-    setting = (
-        gathered,
-        gain_attn[0].astype(jnp.float32),
-        gain_ffn[0].astype(jnp.float32),
-        taps_local,
-        block_start,
-    )
-    received = jnp.zeros((row_count, model_width), jnp.bfloat16)
-    outputs_list = []
-    stored_list = []
-    for moment in range(micro_count + 1):
-        early = min(moment, micro_count - 1)
-        late = max(moment - 1, 0)
-        layer_in = jnp.where(section_index == 0, tokens[early], received)
-        starts_at = jnp.where(section_index == 0, begin_list[early], begin_list[late])
-        layer_out, stored = forward_layer(layer_in.astype(jnp.float32), starts_at, setting)
-        layer_low = layer_out.astype(jnp.bfloat16)
-        outputs_list.append(layer_low)
-        stored_list.append(stored)
-        if moment < micro_count:
-            received = from_behind(layer_low, "section", 1)
-    arriving = jnp.zeros((row_count, model_width), jnp.bfloat16)
-    back_list = []
-    grad_totals = None
-    small_totals = None
-    for moment in range(micro_count + 1):
-        stored = choose_tree(
-            section_index,
-            stored_list[max(moment - 1, 0)],
-            stored_list[min(moment + 1, micro_count)],
-        )
-        if moment < micro_count:
-            from_top = cotangent[moment]
-        else:
-            from_top = jnp.zeros((row_count, model_width), jnp.bfloat16)
-        grad_in = jnp.where(section_index == 1, from_top, arriving)
-        back_inputs, weight_grads, small_grads = backward_layer(
-            grad_in.astype(jnp.float32), stored, setting
-        )
-        back_rows = back_inputs.astype(jnp.bfloat16)
-        back_list.append(back_rows)
-        if moment < micro_count:
-            arriving = from_behind(back_rows, "section", -1)
-        small_totals = (
-            small_grads
-            if small_totals is None
-            else jax.tree.map(jnp.add, small_totals, small_grads)
-        )
-        grad_totals = (
-            weight_grads
-            if grad_totals is None
-            else jax.tree.map(jnp.add, grad_totals, weight_grads)
-        )
-    grad_query, grad_key, grad_value, grad_gconv, grad_out_weight, grad_gate, grad_up, grad_down = (
-        grad_totals
-    )
-    grad_shards = (
-        lax.psum_scatter(
-            grad_query.astype(jnp.bfloat16), "seq", scatter_dimension=0, tiled=True
-        ).astype(jnp.float32),
-        lax.psum_scatter(
-            grad_key.astype(jnp.bfloat16), "seq", scatter_dimension=0, tiled=True
-        ).astype(jnp.float32),
-        lax.psum_scatter(
-            grad_value.astype(jnp.bfloat16), "seq", scatter_dimension=0, tiled=True
-        ).astype(jnp.float32),
-        lax.psum_scatter(
-            grad_gconv.astype(jnp.bfloat16), "seq", scatter_dimension=0, tiled=True
-        ).astype(jnp.float32),
-        lax.psum_scatter(
-            grad_out_weight.astype(jnp.bfloat16), "seq", scatter_dimension=1, tiled=True
-        ).astype(jnp.float32),
-        lax.psum_scatter(
-            grad_gate.astype(jnp.bfloat16), "seq", scatter_dimension=0, tiled=True
-        ).astype(jnp.float32),
-        lax.psum_scatter(
-            grad_up.astype(jnp.bfloat16), "seq", scatter_dimension=0, tiled=True
-        ).astype(jnp.float32),
-        lax.psum_scatter(
-            grad_down.astype(jnp.bfloat16), "seq", scatter_dimension=1, tiled=True
-        ).astype(jnp.float32),
-    )
+    current = lax.dynamic_index_in_dim(tokens, micro, 0, False)
+    outputs = []
+    stored = []
+    for layer in range(2):
+        layer_out, kept = forward_layer(current.astype(jnp.float32), starts_at, settings[layer])
+        current = layer_out.astype(jnp.bfloat16)
+        outputs.append(current)
+        stored.append(kept)
+    grad_in = lax.dynamic_index_in_dim(cotangent, micro, 0, False)
+    back = [None, None]
+    grads = [None, None]
+    smalls = [None, None]
+    for layer in (1, 0):
+        back_inputs, grads[layer], smalls[layer] = backward_layer(
+            grad_in.astype(jnp.float32), stored[layer], settings[layer]
+        )
+        grad_in = back_inputs.astype(jnp.bfloat16)
+        back[layer] = grad_in
+    shards = [scatter_layers(a, b) for a, b in zip(grads[0], grads[1])]
+    shards[4] = shards[4].T
+    shards[7] = shards[7].T
     column_mask = (jnp.arange(model_width, dtype=jnp.int32) // channels == head_index).astype(
         jnp.float32
     )
-    gain_one_sum, gain_two_sum, taps_sum = small_totals
-    taps_full = lax.dynamic_update_slice_in_dim(
-        jnp.zeros((taps_sum.shape[0], model_width), jnp.float32), taps_sum, head_index * channels, 1
-    )
-    total_gain_one, total_gain_two, total_taps = lax.psum(
-        (gain_one_sum * column_mask, gain_two_sum * column_mask, taps_full), ("seq", "head")
-    )
-    activations = jnp.stack(
-        [
-            jnp.where(section_index == 0, outputs_list[micro_index], outputs_list[micro_index + 1])
-            for micro_index in range(micro_count)
-        ]
-    )[None]
-    input_grads = jnp.stack(
-        [
-            jnp.where(section_index == 0, back_list[micro_index + 1], back_list[micro_index])
-            for micro_index in range(micro_count)
-        ]
-    )[None]
+    packed = []
+    for layer in range(2):
+        gain_one_sum, gain_two_sum, taps_sum = smalls[layer]
+        taps_full = lax.dynamic_update_slice_in_dim(
+            jnp.zeros((taps_sum.shape[0], model_width), jnp.float32),
+            taps_sum,
+            head_index * channels,
+            1,
+        )
+        packed.append(
+            jnp.concatenate(
+                [
+                    (gain_one_sum * column_mask)[None],
+                    (gain_two_sum * column_mask)[None],
+                    taps_full,
+                ],
+                axis=0,
+            )
+        )
+    totals = lax.dynamic_index_in_dim(
+        lax.psum(jnp.stack(packed), ("section", "seq", "head")), micro, 0, False
+    )
+
+    def to_layers(pair):
+        mine = lax.dynamic_index_in_dim(jnp.stack(pair), micro, 0, False)
+        theirs = lax.dynamic_index_in_dim(jnp.stack(pair), 1 - micro, 0, False)
+        swapped = lax.ppermute(theirs, "section", [(0, 1), (1, 0)])
+        first = jnp.where(micro == 0, mine, swapped)
+        second = jnp.where(micro == 0, swapped, mine)
+        return jnp.stack([first, second])[None]
+
     return (
-        activations,
-        input_grads,
-        total_gain_one[None],
-        grad_shards[0][None],
-        grad_shards[1][None],
-        grad_shards[2][None],
-        grad_shards[3][None],
-        total_taps[None],
-        grad_shards[4][None],
-        total_gain_two[None],
-        grad_shards[5][None],
-        grad_shards[6][None],
-        grad_shards[7][None],
+        to_layers(outputs),
+        to_layers(back),
+        totals[0][None],
+        shards[0][None],
+        shards[1][None],
+        shards[2][None],
+        shards[3][None],
+        totals[2:][None],
+        shards[4][None],
+        totals[1][None],
+        shards[5][None],
+        shards[6][None],
+        shards[7][None],
     )
 
 

time: 2120 us -> 1920 us (0.906)
  matrix products: 334 us -> 198 us
  other arithmetic: 220 us -> 148 us
  local copies, waits for them, and re-layouts: 78 us -> 137 us
  blocking collectives: 267 us -> 212 us
  waiting for transfers between devices: 1150 us -> 1180 us
    unnamed x26 -> x30, waiting for transfers between devices: 3.45 us -> 364 us
    psum x6 -> x4, waiting for transfers between devices: 646 us -> 359 us  [head_total(): return lax.psum(part_sum.astype(jnp.bfloat16), 'head').astype(jnp.float32)]
    reduce_scatter x5 -> x0, waiting for transfers between devices: 111 us -> none  [the longest x1 56.2 us: on_device(): lax.psum_scatter(grad_down.astype(jnp.bfloat16), 'seq', scatter_dimension...]
    psum x1 -> x0, blocking collectives: 77.3 us -> none  [on_device(): lax.psum((gain_one_sum * column_mask, gain_two_sum * column_mask, taps_fu...]
    all_gather x2 -> x5, blocking collectives: 37.9 us -> 113 us  [the longest x2 107 us: both_layers(): gathered = lax.all_gather(weight, ('section', 'seq'), axis=0, tiled=True)]
    unnamed x742 -> x503, local copies, waits for them, and re-layouts: 55.3 us -> 122 us
    dot_general x42 -> x28, matrix products: 139 us -> 72.8 us  [the longest x2 15.1 us: backward_layer(): jnp.einsum('td,df->tf', grad_low, down_weight, preferred_element_type=jnp...]
    psum x0 -> x1, waiting for transfers between devices: none -> 53 us  [on_device(): lax.psum(jnp.stack(packed), ('section', 'seq', 'head'))]
  transfers between devices with their start and end apart: 33 -> 28, of which waited for: 21 -> 21; matrix products, arithmetic and copies ran while one was open for 13% -> 14% of each run, Pallas kernels for 0% -> 0%
where the time goes in v1:
time: 1920 us; the launch traced here: 1910 us
  waiting for transfers between devices  1180 us (61%)
  blocking collectives  212 us (11%)
  matrix products  198 us (10%)
  other arithmetic  148 us (8%)
  local copies, waits for them, and re-layouts  137 us (7%)
    unnamed x30, waiting for transfers between devices  364 us
    psum x4, waiting for transfers between devices, head_total(): return lax.psum(part_sum.astype(jnp.bfloat16), 'head').astype(jnp.float32)  359 us
    psum x3, waiting for transfers between devices, head_back(): return lax.psum(part_sum.astype(jnp.bfloat16), 'head').astype(jnp.float32)  229 us
    all_gather x6, waiting for transfers between devices, both_layers(): gathered = lax.all_gather(weight, ('section', 'seq'), axis=0, tiled=True)  157 us
    unnamed x503, local copies, waits for them, and re-layouts  122 us
    all_gather x2, blocking collectives, both_layers(): gathered = lax.all_gather(weight, ('section', 'seq'), axis=0, tiled=True)  107 us
    psum x1, waiting for transfers between devices, on_device(): lax.psum(jnp.stack(packed), ('section', 'seq', 'head'))  53 us
    all_gather x4, blocking collectives, carried_in_3(): lax.all_gather(part.astype(kind), axis)  46.8 us
  transfers between devices with their start and end apart: 28, of which 21 were waited for; matrix products, arithmetic and copies ran while one was open for 14% of the time, Pallas kernels for 0%

profile of v1, /device:TPU:0, one launch (start us, length us, event | category | flops | bytes accessed | tf_op | source)
XLA Modules:
  0.0 1906.4 jit_solution(14574387112890826813)
XLA Ops:
  16.1 54.8 %all-gather.2 = bf16[1,3584,64]{2,0,1:T(2,128)(2,1)S(1)} all-gather(bf16[1,448,64]{2,0,1:T(2,128)(2,1)S(1)} %copy.87), channel_id=4, replica_groups=mesh['section'=2,'seq'=4,'head'=4] {'section','seq'}, dimensions={1}, use_global_device_ids=true | all-gather | bytes 516096 | tf_op jit(solution)/shard_map/all_gather | solution.py:386
  83.6 52.1 %all-gather.1 = bf16[1,3584,64]{2,0,1:T(2,128)(2,1)S(1)} all-gather(bf16[1,448,64]{2,0,1:T(2,128)(2,1)S(1)} %copy.85), channel_id=3, replica_groups=mesh['section'=2,'seq'=4,'head'=4] {'section','seq'}, dimensions={1}, use_global_device_ids=true | all-gather | bytes 516096 | tf_op jit(solution)/shard_map/all_gather | solution.py:386
  149.4 8.7 all-reduce
  158.2 8.1 all-gather.15
  176.9 13.1 all-gather.3
  196.3 4.9 collective-permute-start
  204.7 4.8 multiply_convert_fusion.9
  218.1 79.2 %all-reduce.11.cloned.1.call-done = bf16[512,1792]{1,0:T(8,128)(2,1)} async-done(((bf16[512,1792]{1,0:T(8,128)(2,1)}), bf16[512,1792]{1,0:T(8,128)(2,1)}) %all-reduce.11.cloned.1.call-update) | async-done | bytes 1835024 | tf_op jit(solution)/shard_map/psum | solution.py:112
  303.6 52.1 %all-gather.35.cloned.1.call-done = bf16[1,3584,1216]{2,1,0:T(8,128)(2,1)} async-done(((bf16[1,448,1216]{2,1,0:T(8,128)(2,1)}), bf16[1,3584,1216]{2,1,0:T(8,128)(2,1)}) %all-gather.35.cloned.1.call-update) | async-done | bytes 8716304 | tf_op jit(solution)/shard_map/all_gather | solution.py:386
  355.7 6.2 fusion.18
  361.9 53.1 %all-gather.37.cloned.1.call-done = bf16[1,3584,1216]{2,1,0:T(8,128)(2,1)} async-done(((bf16[1,448,1216]{2,1,0:T(8,128)(2,1)}), bf16[1,3584,1216]{2,1,0:T(8,128)(2,1)}) %all-gather.37.cloned.1.call-update) | async-done | bytes 8716304 | tf_op jit(solution)/shard_map/all_gather | solution.py:386
  415.0 7.7 multiply_convert_fusion.5
  422.7 51.8 %all-gather.29.cloned.1.call-done = bf16[3584,1216]{1,0:T(8,128)(2,1)} async-done(((bf16[448,1216]{1,0:T(8,128)(2,1)}), bf16[3584,1216]{1,0:T(8,128)(2,1)}) %all-gather.29.cloned.1.call-update) | async-done | bytes 8716304 | tf_op jit(solution)/shard_map/all_gather | solution.py:386
  474.5 6.5 fusion.53
  483.2 75.7 %all-reduce.13.cloned.1.call-done = bf16[512,1792]{1,0:T(8,128)(2,1)} async-done(((bf16[512,1792]{1,0:T(8,128)(2,1)}), bf16[512,1792]{1,0:T(8,128)(2,1)}) %all-reduce.13.cloned.1.call-update) | async-done | bytes 1835024 | tf_op jit(solution)/shard_map/psum | solution.py:112
  575.8 8.1 all-gather.17
  583.9 14.7 all-gather.8
  601.7 5.9 collective-permute-start.1
  617.1 83.2 %all-reduce.15.cloned.1.call-done = bf16[512,1792]{1,0:T(8,128)(2,1)} async-done(((bf16[512,1792]{1,0:T(8,128)(2,1)}), bf16[512,1792]{1,0:T(8,128)(2,1)}) %all-reduce.15.cloned.1.call-update) | async-done | bytes 1835024 | tf_op jit(solution)/shard_map/psum | solution.py:112
  703.5 7.0 fusion.24
  710.5 6.3 fusion.22
  716.9 7.0 multiply_convert_fusion.3
  727.9 6.2 add_convert_fusion.3
  734.8 76.1 %all-reduce.17.cloned.1.call-done = bf16[512,1792]{1,0:T(8,128)(2,1)} async-done(((bf16[512,1792]{1,0:T(8,128)(2,1)}), bf16[512,1792]{1,0:T(8,128)(2,1)}) %all-reduce.17.cloned.1.call-update) | async-done | bytes 1835024 | tf_op jit(solution)/shard_map/psum | solution.py:116
  810.8 4.3 fusion.37
  815.2 4.2 fusion.100
  823.4 6.3 collective-permute-done.3
  840.0 9.0 all-gather.18
  849.0 13.9 all-gather.10
  862.9 12.9 while.66
  894.5 76.5 %all-reduce.19.cloned.1.call-done = bf16[512,1792]{1,0:T(8,128)(2,1)} async-done(((bf16[512,1792]{1,0:T(8,128)(2,1)}), bf16[512,1792]{1,0:T(8,128)(2,1)}) %all-reduce.19.cloned.1.call-update) | async-done | bytes 1835024 | tf_op jit(solution)/shard_map/psum | solution.py:116
  974.3 4.7 fusion.47
  979.1 8.2 multiply_convert_fusion.2
  994.1 76.5 %all-reduce.21.cloned.1.call-done = bf16[512,1792]{1,0:T(8,128)(2,1)} async-done(((bf16[512,1792]{1,0:T(8,128)(2,1)}), bf16[512,1792]{1,0:T(8,128)(2,1)}) %all-reduce.21.cloned.1.call-update) | async-done | bytes 1835024 | tf_op jit(solution)/shard_map/psum | solution.py:116
  1070.6 4.3 fusion.39
  1086.8 6.2 fusion.56
  1101.1 9.7 all-gather.19
  1110.9 14.1 all-gather.12
  1125.0 12.9 while.67
  1173.1 120.5 %all-reduce.25.cloned.1.call-done = (bf16[512,1792]{1,0:T(8,128)(2,1)}, bf16[512,1792]{1,0:T(8,128)(2,1)}) async-done(((bf16[512,1792]{1,0:T(8,128)(2,1)}, bf16[512,1792]{1,0:T(8,128)(2,1)}), (bf16[512,1792]{1,0:T(8,128)(2,1)}, bf16[512,1792]{1,0:T(8,128)(2,1)})) %all-reduce.25.cloned.1.call-update) | async-done | bytes 3670032 | tf_op jit(solution)/shard_map/psum | solution.py:112
  1301.4 5.9 copy.132
  1308.3 4.5 convolution_convert_fusion.8
  1315.8 5.7 copy.134
  1328.3 5.7 copy.130
  1335.4 6.1 convolution_convert_fusion.2
  1341.5 4.5 convolution_convert_fusion.3
  1346.0 7.5 pad_maximum_fusion.1
  1353.5 12.7 copy.138
  1366.5 6.4 convolution_convert_fusion
  1373.0 4.4 convolution_convert_fusion.1
  1377.4 7.6 pad_maximum_fusion.2
  1385.0 12.6 copy.140
  1398.9 6.1 convolution_convert_fusion.4
  1405.1 4.5 convolution_convert_fusion.5
  1409.6 7.6 pad_maximum_fusion
  1417.2 12.9 copy.136
  1433.5 4.4 fusion.82
  1444.0 53.0 %all-reduce.23.cloned.1.call-done = f32[2,5,1792]{2,0,1:T(2,128)} async-done(((f32[2,5,1792]{2,0,1:T(2,128)}), f32[2,5,1792]{2,0,1:T(2,128)}) %all-reduce.23.cloned.1.call-update) | async-done | bytes 71696 | tf_op jit(solution)/shard_map/psum | solution.py:501
  1499.7 51.2 %reduce-scatter.31.cloned.1.call-done = bf16[448,448]{1,0:T(8,128)(2,1)} async-done(((bf16[3584,448]{1,0:T(8,128)(2,1)}), bf16[448,448]{1,0:T(8,128)(2,1)}) %reduce-scatter.31.cloned.1.call-update) | async-done | bytes 401424
  1553.5 49.3 %reduce-scatter.33.cloned.1.call-done = bf16[448,448]{1,0:T(8,128)(2,1)} async-done(((bf16[3584,448]{1,0:T(8,128)(2,1)}), bf16[448,448]{1,0:T(8,128)(2,1)}) %reduce-scatter.33.cloned.1.call-update) | async-done | bytes 401424
  1605.1 50.4 %reduce-scatter.29.cloned.1.call-done = bf16[448,448]{1,0:T(8,128)(2,1)} async-done(((bf16[3584,448]{1,0:T(8,128)(2,1)}), bf16[448,448]{1,0:T(8,128)(2,1)}) %reduce-scatter.29.cloned.1.call-update) | async-done | bytes 401424
  1669.1 65.2 %reduce-scatter.37.cloned.1.call-done = bf16[448,1216]{1,0:T(8,128)(2,1)} async-done(((bf16[3584,1216]{1,0:T(8,128)(2,1)}), bf16[448,1216]{1,0:T(8,128)(2,1)}) %reduce-scatter.37.cloned.1.call-update) | async-done | bytes 1089552
  1741.0 72.3 %reduce-scatter.39.cloned.1.call-done = bf16[448,1216]{1,0:T(8,128)(2,1)} async-done(((bf16[3584,1216]{1,0:T(8,128)(2,1)}), bf16[448,1216]{1,0:T(8,128)(2,1)}) %reduce-scatter.39.cloned.1.call-update) | async-done | bytes 1089552
  1820.1 72.3 %reduce-scatter.35.cloned.1.call-done = bf16[448,1216]{1,0:T(8,128)(2,1)} async-done(((bf16[3584,1216]{1,0:T(8,128)(2,1)}), bf16[448,1216]{1,0:T(8,128)(2,1)}) %reduce-scatter.35.cloned.1.call-update) | async-done | bytes 1089552
  (768 shorter events, 303.0 us)
Async XLA Ops:
  7.2 165.7 %all-gather.31.cloned.1.call-start = ((), (), s32[]{:S(2)}) async-start(), calls=%async_computation.17 | async-start | bytes 4128768 | tf_op jit(solution)/shard_map/all_gather | solution.py:386
  7.9 193.9 %all-gather.33.cloned.1.call-start = ((), (), s32[]{:S(2)}) async-start(), calls=%async_computation.18 | async-start | bytes 4128768 | tf_op jit(solution)/shard_map/all_gather | solution.py:386
  8.7 200.9 %all-gather.27.cloned.1.call-start = ((), (), s32[]{:S(2)}) async-start(), calls=%async_computation.8 | async-start | bytes 4128768 | tf_op jit(solution)/shard_map/all_gather | solution.py:386
  10.7 286.6 %all-reduce.11.cloned.1.call-start = ((), (), s32[]{:S(2)}) async-start(), calls=%async_computation.9 | async-start | bytes 3670016 | tf_op jit(solution)/shard_map/psum | solution.py:112
  12.7 192.0 %copy-start.169 = (f32[512]{0:T(512)}, f32[512]{0:T(512)S(1)}, u32[]{:S(2)}) copy-start(f32[512]{0:T(512)S(1)} %fusion.210) | copy-start | bytes 6148
  15.9 188.8 %copy-start.137 = (f32[1792]{0:T(1024)}, f32[1792]{0:T(1024)S(1)}, u32[]{:S(2)}) copy-start(f32[1792]{0:T(1024)S(1)} %get-tuple-element.618) | copy-start | bytes 21508
  78.9 90.0 %copy-start.102 = (bf16[512,64]{0,1:T(8,128)(2,1)}, bf16[512,64]{0,1:T(8,128)(2,1)S(1)}, u32[]{:S(2)}) copy-start(bf16[512,64]{0,1:T(8,128)(2,1)S(1)} %convolution_convert_fusion.20) | copy-start | bytes 196612
  79.6 96.8 %copy-start.74 = (f32[512,4,16]{0,2,1:T(8,128)}, f32[512,4,16]{0,2,1:T(8,128)S(1)}, u32[]{:S(2)}) copy-start(f32[512,4,16]{0,2,1:T(8,128)S(1)} %get-tuple-element.714) | copy-start | bytes 393220
  79.9 78.3 %copy-start.150 = (s32[514]{0:T(1024)}, s32[514]{0:T(1024)S(1)}, u32[]{:S(2)}) copy-start(s32[514]{0:T(1024)S(1)} %select_reduce_fusion) | copy-start | bytes 6172
  81.1 95.2 %copy-start.129 = (f32[512]{0:T(512)}, f32[512]{0:T(512)S(1)}, u32[]{:S(2)}) copy-start(f32[512]{0:T(512)S(1)} %get-tuple-element.734) | copy-start | bytes 6148
  81.2 112.4 %copy-start.133 = (f32[512]{0:T(512)}, f32[512]{0:T(512)S(1)}, u32[]{:S(2)}) copy-start(f32[512]{0:T(512)S(1)} %get-tuple-element.736) | copy-start | bytes 6148
  81.2 123.6 %copy-start.198 = (f32[512]{0:T(512)}, f32[512]{0:T(512)S(1)}, u32[]{:S(2)}) copy-start(f32[512]{0:T(512)S(1)} %get-tuple-element.733) | copy-start | bytes 6148
  81.2 123.6 %copy-start.200 = (f32[512]{0:T(512)}, f32[512]{0:T(512)S(1)}, u32[]{:S(2)}) copy-start(f32[512]{0:T(512)S(1)} %get-tuple-element.735) | copy-start | bytes 6148
  143.9 25.0 %copy-start.104 = (bf16[512,64]{0,1:T(8,128)(2,1)}, bf16[512,64]{0,1:T(8,128)(2,1)S(1)}, u32[]{:S(2)}) copy-start(bf16[512,64]{0,1:T(8,128)(2,1)S(1)} %convolution_convert_fusion.21) | copy-start | bytes 196612
  145.8 47.7 %copy-start.145 = (f32[273]{0:T(512)}, f32[273]{0:T(512)S(1)}, u32[]{:S(2)}) copy-start(f32[273]{0:T(512)S(1)} %pad.55.clone) | copy-start | bytes 3280
  167.2 26.3 %copy-start.123 = (f32[512,4,16]{0,2,1:T(8,128)}, f32[512,4,16]{0,2,1:T(8,128)S(1)}, u32[]{:S(2)}) copy-start(f32[512,4,16]{0,2,1:T(8,128)S(1)} %get-tuple-element.716) | copy-start | bytes 393220
  196.3 8.4 collective-permute-start
  213.7 142.0 %all-gather.35.cloned.1.call-start = ((), (), s32[]{:S(2)}) async-start(), calls=%async_computation.19 | async-start | bytes 10321920 | tf_op jit(solution)/shard_map/all_gather | solution.py:386
  214.3 200.7 %all-gather.37.cloned.1.call-start = ((), (), s32[]{:S(2)}) async-start(), calls=%async_computation.20 | async-start | bytes 10321920 | tf_op jit(solution)/shard_map/all_gather | solution.py:386
  214.9 259.7 %all-gather.29.cloned.1.call-start = ((), (), s32[]{:S(2)}) async-start(), calls=%async_computation.10 | async-start | bytes 10321920 | tf_op jit(solution)/shard_map/all_gather | solution.py:386
  215.6 343.2 %all-reduce.13.cloned.1.call-start = ((), (), s32[]{:S(2)}) async-start(), calls=%async_computation.11 | async-start | bytes 3670016 | tf_op jit(solution)/shard_map/psum | solution.py:112
  218.1 85.4 %copy-start.127 = (f32[1792]{0:T(1024)}, f32[1792]{0:T(1024)S(1)}, u32[]{:S(2)}) copy-start(f32[1792]{0:T(1024)S(1)} %get-tuple-element.616) | copy-start | bytes 21508
  303.6 111.5 %copy-start.62 = (bf16[512,1792]{1,0:T(8,128)(2,1)}, bf16[512,1792]{1,0:T(8,128)(2,1)S(1)}, u32[]{:S(2)}) copy-start(bf16[512,1792]{1,0:T(8,128)(2,1)S(1)} %multiply_convert_fusion.1) | copy-start | bytes 5505028
  481.1 219.3 %all-reduce.15.cloned.1.call-start = ((), (), s32[]{:S(2)}) async-start(), calls=%async_computation.12 | async-start | bytes 3670016 | tf_op jit(solution)/shard_map/psum | solution.py:112
  482.2 80.8 %copy-start.53 = (bf16[1,1792,64]{1,2,0:T(8,128)(2,1)}, bf16[1,1792,64]{1,2,0:T(8,128)(2,1)S(1)}, u32[]{:S(2)}) copy-start(bf16[1,1792,64]{1,2,0:T(8,128)(2,1)S(1)} %copy.145) | copy-start | bytes 688132
  483.1 81.3 %copy-start.51 = (bf16[1,1792,64]{1,2,0:T(8,128)(2,1)}, bf16[1,1792,64]{1,2,0:T(8,128)(2,1)S(1)}, u32[]{:S(2)}) copy-start(bf16[1,1792,64]{1,2,0:T(8,128)(2,1)S(1)} %copy.144) | copy-start | bytes 688132
  483.1 79.3 %copy-start.121 = (f32[1792]{0:T(1024)S(1)}, f32[1792]{0:T(1024)}, u32[]{:S(2)}) copy-start(f32[1792]{0:T(1024)} %get-tuple-element.617) | copy-start | bytes 21508
  565.8 33.7 %copy-start.125 = (f32[512,4,16]{0,2,1:T(8,128)}, f32[512,4,16]{0,2,1:T(8,128)S(1)}, u32[]{:S(2)}) copy-start(f32[512,4,16]{0,2,1:T(8,128)S(1)} %get-tuple-element.720) | copy-start | bytes 393220
  574.2 24.4 %copy-start.29 = (bf16[4,512,512]{1,2,0:T(8,128)(2,1)}, bf16[4,512,512]{1,2,0:T(8,128)(2,1)S(1)}, u32[]{:S(2)}) copy-start(bf16[4,512,512]{1,2,0:T(8,128)(2,1)S(1)} %get-tuple-element.684) | copy-start | bytes 6291460
  574.2 25.3 %copy-start.163 = (f32[4,512]{1,0:T(4,128)}, f32[4,512]{1,0:T(4,128)S(1)}, u32[]{:S(2)}) copy-start(f32[4,512]{1,0:T(4,128)S(1)} %get-tuple-element.683) | copy-start | bytes 24580
  574.2 24.4 %copy-start.204 = (bf16[4,1]{0,1:T(2,128)(2,1)S(1)}, bf16[4,1]{0,1:T(2,128)(2,1)}, u32[]{:S(2)}) copy-start(bf16[4,1]{0,1:T(2,128)(2,1)} %copy-done.203) | copy-start | bytes 28
  601.7 9.4 collective-permute-start.1
  616.7 86.0 %copy-start.119 = (f32[1792]{0:T(1024)S(1)}, f32[1792]{0:T(1024)}, u32[]{:S(2)}) copy-start(f32[1792]{0:T(1024)} %get-tuple-element.615) | copy-start | bytes 21508
  616.7 194.1 %all-reduce.17.cloned.1.call-start = ((), (), s32[]{:S(2)}) async-start(), calls=%async_computation.13 | async-start | bytes 3670016 | tf_op jit(solution)/shard_map/psum | solution.py:116
  702.7 112.4 %copy-start.152 = (f32[512]{0:T(512)}, f32[512]{0:T(512)S(1)}, u32[]{:S(2)}) copy-start(f32[512]{0:T(512)S(1)} %fusion.213) | copy-start | bytes 6148
  734.1 237.0 %all-reduce.19.cloned.1.call-start = ((), (), s32[]{:S(2)}) async-start(), calls=%async_computation.14 | async-start | bytes 3670016 | tf_op jit(solution)/shard_map/psum | solution.py:116
  821.3 8.5 collective-permute-start.3
  839.4 23.5 %copy-start.118 = (f32[4,273]{1,0:T(4,128)S(1)}, f32[4,273]{1,0:T(4,128)}, u32[]{:S(2)}) copy-start(f32[4,273]{1,0:T(4,128)} %custom-call.1) | copy-start | bytes 13108
  839.4 23.5 %copy-start.205 = (bf16[4,1]{0,1:T(2,128)(2,1)S(1)}, bf16[4,1]{0,1:T(2,128)(2,1)}, u32[]{:S(2)}) copy-start(bf16[4,1]{0,1:T(2,128)(2,1)} %copy-done.203) | copy-start | bytes 28
  891.5 79.5 %copy-start.122 = (f32[1792]{0:T(1024)S(1)}, f32[1792]{0:T(1024)}, u32[]{:S(2)}) copy-start(f32[1792]{0:T(1024)} %get-tuple-element.617) | copy-start | bytes 21508
  891.5 79.5 %copy-start.157 = (f32[512]{0:T(512)S(1)}, f32[512]{0:T(512)}, u32[]{:S(2)}) copy-start(f32[512]{0:T(512)} %copy-done.156) | copy-start | bytes 6148
  894.0 80.2 %copy-start.176 = (f32[512]{0:T(512)S(1)}, f32[512]{0:T(512)}, u32[]{:S(2)}) copy-start(f32[512]{0:T(512)} %copy-done.175) | copy-start | bytes 6148
  894.0 80.2 %copy-start.120 = (f32[1792]{0:T(1024)S(1)}, f32[1792]{0:T(1024)}, u32[]{:S(2)}) copy-start(f32[1792]{0:T(1024)} %get-tuple-element.615) | copy-start | bytes 21508
  894.0 80.2 %copy-start.153 = (f32[512]{0:T(512)S(1)}, f32[512]{0:T(512)}, u32[]{:S(2)}) copy-start(f32[512]{0:T(512)} %copy-done.152) | copy-start | bytes 6148
  894.1 80.2 %copy-start.179 = (f32[512]{0:T(512)S(1)}, f32[512]{0:T(512)}, u32[]{:S(2)}) copy-start(f32[512]{0:T(512)} %copy-done.178) | copy-start | bytes 6148
  894.1 176.6 %all-reduce.21.cloned.1.call-start = ((), (), s32[]{:S(2)}) async-start(), calls=%async_computation.15 | async-start | bytes 3670016 | tf_op jit(solution)/shard_map/psum | solution.py:116
  990.0 80.7 %copy-start.128 = (f32[1792]{0:T(1024)S(1)}, f32[1792]{0:T(1024)}, u32[]{:S(2)}) copy-start(f32[1792]{0:T(1024)} %copy-done.127) | copy-start | bytes 21508
  990.0 80.7 %copy-start.155 = (f32[512]{0:T(512)S(1)}, f32[512]{0:T(512)}, u32[]{:S(2)}) copy-start(f32[512]{0:T(512)} %copy-done.154) | copy-start | bytes 6148
  993.9 299.7 %all-reduce.25.cloned.1.call-start = ((), (), s32[]{:S(2)}) async-start(), calls=%async_computation.29 | async-start | bytes 7340032 | tf_op jit(solution)/shard_map/psum | solution.py:112
  994.1 80.8 %copy-start.168 = (f32[512]{0:T(512)S(1)}, f32[512]{0:T(512)}, u32[]{:S(2)}) copy-start(f32[512]{0:T(512)} %copy-done.167) | copy-start | bytes 6148
  1085.4 8.2 collective-permute-start.4
  1100.6 24.4 %copy-start.207 = (bf16[4,1]{0,1:T(2,128)(2,1)S(1)}, bf16[4,1]{0,1:T(2,128)(2,1)}, u32[]{:S(2)}) copy-start(bf16[4,1]{0,1:T(2,128)(2,1)} %copy-done.206) | copy-start | bytes 28
  1157.0 273.1 %reduce-scatter.27.cloned.1.call-start = ((), (), s32[]{:S(2)}) async-start(), calls=%async_computation.22 | async-start | bytes 1032192
  1169.5 261.7 %reduce-scatter.25.cloned.1.call-start = ((), (), s32[]{:S(2)}) async-start(), calls=%async_computation.21 | async-start | bytes 1032192
  1173.1 125.0 %copy-start.68 = (bf16[1792,448]{0,1:T(8,128)(2,1)S(1)}, bf16[1792,448]{0,1:T(8,128)(2,1)}, u32[]{:S(2)}) copy-start(bf16[1792,448]{0,1:T(8,128)(2,1)} %convolution_convert_fusion.10) | copy-start | bytes 4816900
  1173.1 323.9 %all-reduce.23.cloned.1.call-start = ((), (), s32[]{:S(2)}) async-start(), calls=%async_computation.16 | async-start | bytes 143360 | tf_op jit(solution)/shard_map/psum | solution.py:501
  1298.0 252.9 %reduce-scatter.31.cloned.1.call-start = ((), (), s32[]{:S(2)}) async-start(), calls=%async_computation.24 | async-start | bytes 4128768
  1307.3 295.5 %reduce-scatter.33.cloned.1.call-start = ((), (), s32[]{:S(2)}) async-start(), calls=%async_computation.25 | async-start | bytes 4128768
  1321.6 333.9 %reduce-scatter.29.cloned.1.call-start = ((), (), s32[]{:S(2)}) async-start(), calls=%async_computation.23 | async-start | bytes 4128768
  1334.1 400.2 %reduce-scatter.37.cloned.1.call-start = ((), (), s32[]{:S(2)}) async-start(), calls=%async_computation.27 | async-start | bytes 10321920
  1366.3 447.0 %reduce-scatter.39.cloned.1.call-start = ((), (), s32[]{:S(2)}) async-start(), calls=%async_computation.28 | async-start | bytes 10321920
  1397.6 494.7 %reduce-scatter.35.cloned.1.call-start = ((), (), s32[]{:S(2)}) async-start(), calls=%async_computation.26 | async-start | bytes 10321920
  1439.8 218.2 %collective-permute-start.5 = (bf16[512,1792]{1,0:T(8,128)(2,1)}, bf16[512,1792]{1,0:T(8,128)(2,1)}, u32[]{:S(2)}, u32[]{:S(2)}) collective-permute-start(bf16[512,1792]{1,0:T(8,128)(2,1)} %fusion.85), channel_id=1, source_target_pairs={{0,16},{16,0},{1,17},{17,1},{2,18},{18,2},{3,19},{19,3},{4,20},{20... | collective-permute-start | bytes 5505032 | tf_op jit(solution)/shard_map/ppermute | solution.py:507
  1444.0 220.3 %collective-permute-start.2 = (bf16[512,1792]{1,0:T(8,128)(2,1)}, bf16[512,1792]{1,0:T(8,128)(2,1)}, u32[]{:S(2)}, u32[]{:S(2)}) collective-permute-start(bf16[512,1792]{1,0:T(8,128)(2,1)} %fusion.89), channel_id=1, source_target_pairs={{0,16},{16,0},{1,17},{17,1},{2,18},{18,2},{3,19},{19,3},{4,20},{20... | collective-permute-start | bytes 5505032 | tf_op jit(solution)/shard_map/ppermute | solution.py:507
  (200 other events, 913.1 us)
Sparse Core Ops, SparseCore 0:
  9.9 51.7 all-gather.30
  63.5 43.5 all-gather.32
  109.6 38.8 all-gather.26
  213.8 83.4 all-reduce.10
  299.1 56.5 all-gather.34
  357.4 57.5 all-gather.36
  416.9 57.5 all-gather.28
  481.2 77.5 all-reduce.12
  616.8 83.5 all-reduce.14
  734.2 76.5 all-reduce.16
  894.1 76.8 all-reduce.18
  994.0 76.5 all-reduce.20
  1157.1 136.4 all-reduce.24
  1297.2 34.3 reduce-scatter.26
  1335.3 35.3 reduce-scatter.24
  1376.7 120.2 all-reduce.22
  1500.3 50.6 reduce-scatter.30
  1554.2 48.5 reduce-scatter.32
  1606.8 48.5 reduce-scatter.28
  1658.9 75.3 reduce-scatter.36
  1737.9 75.3 reduce-scatter.38
  1816.9 75.3 reduce-scatter.34

commit v2 on v1

v2 whole, which is shorter than its diff:
```python
import functools
import math

import jax
import jax.numpy as jnp
from jax import lax
from jax.experimental import pallas as pl
from jax.experimental.pallas import tpu as pltpu
from jax.sharding import PartitionSpec as P

FK = 16
KW = 3
MESH = pl.DeviceIdType.MESH
epsilon = 1e-05


def remote(src, dst, send, recv, **where):
    return pltpu.make_async_remote_copy(
        src_ref=src,
        dst_ref=dst,
        send_sem=send,
        recv_sem=recv,
        device_id=where,
        device_id_type=MESH,
    )


def greet(line, spread):
    core, z, q = lax.axis_index("section"), lax.axis_index("head"), lax.axis_index("seq")
    depth, count = lax.axis_size("head"), lax.axis_size("seq")
    barrier = pltpu.get_barrier_semaphore()

    def hello(**where):
        pl.semaphore_signal(barrier, inc=1, device_id=where, device_id_type=MESH)

    hello(section=1 - core)
    expected = 1
    if spread:
        for j in range(1, count):
            for h in range(2):
                hello(section=h, seq=lax.rem(q + j, count))
        expected += 2 * (count - 1)
    if line:

        @pl.when(z > 0)
        def _():
            hello(head=z - 1)

        @pl.when(z < depth - 1)
        def _():
            hello(head=z + 1)

        expected = expected + jnp.where(z > 0, 1, 0) + jnp.where(z < depth - 1, 1, 0)
    pl.semaphore_wait(barrier, expected)


class LineSum:
    def __init__(self, p_ref, o_ref, scratch, chunks, lag):
        self.p_ref, self.o_ref, self.chunks, self.lag = p_ref, o_ref, chunks, lag
        self.pin, self.low, self.high, self.out = scratch[:4]
        self.ps, self.pr, self.rs, self.rl, self.rh, self.bs, self.br, self.ts, self.tr = scratch[4:]
        self.z, self.n = lax.axis_index("head"), lax.axis_size("head")
        self.core = lax.axis_index("section")
        self.half = p_ref.shape[1] // 2
        self.step = self.half // chunks
        self.depth = max((self.n - 1) // 2, self.n - 1 - (self.n - 1) // 2)
        self.turns = chunks + 2 * self.depth * lag

    @staticmethod
    def scratch(rows, width, chunks):
        sem = pltpu.SemaphoreType.DMA((2, chunks))
        bank = pltpu.SemaphoreType.DMA((2, 2, chunks))
        return [pltpu.VMEM((rows, width), jnp.bfloat16)] * 4 + [
            sem, sem, sem, sem, sem, bank, sem, sem, sem
        ]

    def root(self, d):
        return (self.n - 1) // 2 if d == 0 else self.n - 1 - (self.n - 1) // 2

    def rng(self, d, k):
        return pl.ds(pl.multiple_of(d * self.half + k * self.step, self.step), self.step)

    def part(self, d, k):
        r = self.rng(d, k)
        other = 1 - self.core
        return remote(
            self.p_ref.at[other, r], self.pin.at[r], self.ps.at[d, k], self.pr.at[d, k], section=other
        )

    def up(self, d, k):
        r = self.rng(d, k)
        return remote(
            self.out.at[r], self.low.at[r], self.rs.at[d, k], self.rl.at[d, k], head=self.z + 1
        )

    def down(self, d, k):
        r = self.rng(d, k)
        return remote(
            self.out.at[r], self.high.at[r], self.rs.at[d, k], self.rh.at[d, k], head=self.z - 1
        )

    def share(self, d, k, side):
        r = self.rng(d, k)
        at = self.o_ref.at[self.core, r]
        return remote(
            at, at, self.bs.at[side, d, k], self.br.at[d, k], head=self.z + (1 if side else -1)
        )

    def give(self, d, k):
        r = self.rng(d, k)
        at = self.o_ref.at[self.core, r]
        return remote(at, at, self.ts.at[d, k], self.tr.at[d, k], section=1 - self.core)

    def start(self):
        for k in range(self.chunks):
            for d in range(2):
                self.part(d, k).start()

    def gathered(self, d, k):
        r = self.rng(d, k)
        z, n, root = self.z, self.n, self.root(d)
        self.part(d, k).wait_recv()
        mine = self.p_ref[self.core, r, :].astype(jnp.float32) + self.pin[r, :].astype(jnp.float32)

        @pl.when((z == 0) & (root > 0))
        def _():
            self.out[r, :] = mine.astype(jnp.bfloat16)
            self.up(d, k).start()

        @pl.when((z == n - 1) & (root < n - 1))
        def _():
            self.out[r, :] = mine.astype(jnp.bfloat16)
            self.down(d, k).start()

        @pl.when((z > 0) & (z < root))
        def _():
            self.up(d, k).wait_recv()
            self.out[r, :] = (mine + self.low[r, :].astype(jnp.float32)).astype(jnp.bfloat16)
            self.up(d, k).start()

        @pl.when((z < n - 1) & (z > root))
        def _():
            self.down(d, k).wait_recv()
            self.out[r, :] = (mine + self.high[r, :].astype(jnp.float32)).astype(jnp.bfloat16)
            self.down(d, k).start()

        @pl.when(z == root)
        def _():
            total = mine
            if root > 0:
                self.up(d, k).wait_recv()
                total = total + self.low[r, :].astype(jnp.float32)
            if root < n - 1:
                self.down(d, k).wait_recv()
                total = total + self.high[r, :].astype(jnp.float32)
            self.o_ref[self.core, r, :] = total.astype(jnp.bfloat16)
            if root > 0:
                self.share(d, k, 0).start()
            if root < n - 1:
                self.share(d, k, 1).start()
            self.give(d, k).start()

    def passed(self, d, k):
        z, n, root = self.z, self.n, self.root(d)
        self.share(d, k, 0).wait_recv()

        @pl.when((z < root) & (z > 0))
        def _():
            self.share(d, k, 0).start()

        @pl.when((z > root) & (z < n - 1))
        def _():
            self.share(d, k, 1).start()

        self.give(d, k).start()

    def turn(self, t):
        z, n = self.z, self.n
        for d in range(2):
            root = self.root(d)
            deep = max(root, n - 1 - root)
            below = jnp.where(z < root, z, jnp.where(z > root, n - 1 - z, deep))
            k = t - below * self.lag
            far = jnp.abs(z - root)

            @pl.when((k >= 0) & (k < self.chunks))
            def _():
                self.gathered(d, k)

            b = t - (deep + far) * self.lag

            @pl.when((b >= 0) & (b < self.chunks) & (far > 0))
            def _():
                self.passed(d, b)

    def finish(self):
        z, n = self.z, self.n
        for d in range(2):
            root = self.root(d)
            for k in range(self.chunks):
                self.part(d, k).wait_send()
                self.give(d, k).wait_recv()
                self.give(d, k).wait_send()

                @pl.when(z < root)
                def _():
                    self.up(d, k).wait_send()

                @pl.when(z > root)
                def _():
                    self.down(d, k).wait_send()

                if root > 0:

                    @pl.when((z <= root) & (z > 0))
                    def _():
                        self.share(d, k, 0).wait_send()

                if root < n - 1:

                    @pl.when((z >= root) & (z < n - 1))
                    def _():
                        self.share(d, k, 1).wait_send()


class Gather:
    def __init__(self, layer, srcs, dsts, sems):
        self.layer, self.srcs, self.dsts = layer, srcs, dsts
        self.ss, self.rr, self.ls = sems
        self.core, self.q = lax.axis_index("section"), lax.axis_index("seq")
        self.n = lax.axis_size("seq")

    @staticmethod
    def scratch(count, n):
        return [
            pltpu.SemaphoreType.DMA((count, n, 2)),
            pltpu.SemaphoreType.DMA((count, n)),
            pltpu.SemaphoreType.DMA((count,)),
        ]

    def copies(self, a):
        for j in range(1, self.n):
            for h in range(2):
                yield remote(
                    self.srcs[a].at[h], self.dsts[a].at[self.q], self.ss.at[a, j, h],
                    self.rr.at[a, self.q], section=h, seq=lax.rem(self.q + j, self.n),
                )
        yield remote(
            self.srcs[a].at[1 - self.layer], self.dsts[a].at[self.q], self.ss.at[a, 0, 0],
            self.rr.at[a, self.q], section=1 - self.layer,
        )

    def local(self, a):
        return pltpu.make_async_copy(
            self.srcs[a].at[self.layer], self.dsts[a].at[self.q], self.ls.at[a]
        )

    def arrival(self, a, s):
        return remote(
            self.srcs[a].at[0], self.dsts[a].at[s], self.ss.at[a, 0, 0], self.rr.at[a, s],
            section=1 - self.core,
        )

    def start(self):
        @pl.when(self.core == self.layer)
        def _():
            for a in range(len(self.srcs)):
                for copy in self.copies(a):
                    copy.start()
                self.local(a).start()

    def finish(self):
        for a in range(len(self.srcs)):
            for j in range(1, self.n):
                self.arrival(a, lax.rem(self.q + j, self.n)).wait_recv()

            @pl.when(self.core == self.layer)
            def _():
                self.local(a).wait()
                for copy in self.copies(a):
                    copy.wait_send()

            @pl.when(self.core != self.layer)
            def _():
                self.arrival(a, self.q).wait_recv()


class Scatter:
    def __init__(self, layer, srcs, dsts, sems):
        self.layer, self.srcs, self.dsts = layer, srcs, dsts
        self.ss, self.rr, self.ls = sems
        self.core, self.q = lax.axis_index("section"), lax.axis_index("seq")
        self.n = lax.axis_size("seq")

    @staticmethod
    def scratch(count, n):
        return [
            pltpu.SemaphoreType.DMA((count, n)),
            pltpu.SemaphoreType.DMA((count, 2, n)),
            pltpu.SemaphoreType.DMA((count,)),
        ]

    def copies(self, a):
        for j in range(1, self.n):
            t = lax.rem(self.q + j, self.n)
            yield remote(
                self.srcs[a].at[t], self.dsts[a].at[self.core, self.q], self.ss.at[a, j],
                self.rr.at[a, self.core, self.q], section=self.layer, seq=t,
            )

    def near(self, a):
        return remote(
            self.srcs[a].at[self.q], self.dsts[a].at[self.core, self.q], self.ss.at[a, 0],
            self.rr.at[a, self.core, self.q], section=self.layer,
        )

    def local(self, a):
        return pltpu.make_async_copy(
            self.srcs[a].at[self.q], self.dsts[a].at[self.core, self.q], self.ls.at[a]
        )

    def arrival(self, a, h, s):
        return remote(
            self.srcs[a].at[self.q], self.dsts[a].at[h, s], self.ss.at[a, 0], self.rr.at[a, h, s],
            section=1 - self.core,
        )

    def start(self):
        for a in range(len(self.srcs)):
            for copy in self.copies(a):
                copy.start()

            @pl.when(self.core == self.layer)
            def _():
                self.local(a).start()

            @pl.when(self.core != self.layer)
            def _():
                self.near(a).start()

    def finish(self):
        for a in range(len(self.srcs)):

            @pl.when(self.core == self.layer)
            def _():
                for j in range(1, self.n):
                    for h in range(2):
                        self.arrival(a, h, lax.rem(self.q + j, self.n)).wait_recv()
                self.arrival(a, 1 - self.layer, self.q).wait_recv()
                self.local(a).wait()

            @pl.when(self.core != self.layer)
            def _():
                self.near(a).wait_send()

            for copy in self.copies(a):
                copy.wait_send()


def comm_kernel(plan, *refs):
    has_sum, layer_in, count_in, layer_out, count_out, chunks, lag = plan
    refs = list(refs)

    def take(count):
        taken = refs[:count]
        del refs[:count]
        return taken

    p_in, w_in, g_in = take(has_sum), take(count_in), take(count_out)
    p_out, w_out, g_out = take(has_sum), take(count_in), take(count_out)
    greet(has_sum, count_in + count_out > 0)
    jobs = []
    if has_sum:
        line = LineSum(p_in[0], p_out[0], take(13), chunks, lag)
        line.start()
    if count_in:
        jobs.append(Gather(layer_in, w_in, w_out, take(3)))
    if count_out:
        jobs.append(Scatter(layer_out, g_in, g_out, take(3)))
    for job in jobs:
        job.start()
    if has_sum:

        def turn(t, carry):
            line.turn(t)
            return carry

        lax.fori_loop(0, line.turns, turn, 0)
        line.finish()
    for job in jobs:
        job.finish()


def communicate(cid, partial=None, gather=None, scatter=None, chunks=16, lag=3):
    n = lax.axis_size("seq")
    layer_in, w_in = gather if gather else (0, [])
    layer_out, g_in = scatter if scatter else (0, [])
    p_in = [] if partial is None else [partial]
    vmem, anywhere = pl.BlockSpec(memory_space=pltpu.VMEM), pl.BlockSpec(memory_space=pl.ANY)
    scratch = []
    if p_in:
        scratch += LineSum.scratch(partial.shape[1], partial.shape[2], chunks)
    if w_in:
        scratch += Gather.scratch(len(w_in), n)
    if g_in:
        scratch += Scatter.scratch(len(g_in), n)
    shapes = (
        [jax.ShapeDtypeStruct(p.shape, jnp.bfloat16) for p in p_in]
        + [jax.ShapeDtypeStruct((n,) + w.shape[1:], jnp.bfloat16) for w in w_in]
        + [jax.ShapeDtypeStruct((2,) + g.shape, jnp.bfloat16) for g in g_in]
    )
    plan = (len(p_in), layer_in, len(w_in), layer_out, len(g_in), chunks, lag)
    outs = pl.pallas_call(
        functools.partial(comm_kernel, plan),
        out_shape=shapes,
        in_specs=[vmem] * (len(p_in) + len(w_in)) + [anywhere] * len(g_in),
        out_specs=[vmem] * len(p_in) + [anywhere] * (len(w_in) + len(g_in)),
        scratch_shapes=scratch,
        name=f"comm{cid}",
        compiler_params=pltpu.CompilerParams(
            collective_id=cid, has_side_effects=True, vmem_limit_bytes=48 << 20
        ),
    )(*p_in, *w_in, *g_in)
    p, w = outs[: len(p_in)], outs[len(p_in) : len(p_in) + len(w_in)]
    return (
        p[0] if p else None,
        [a.reshape((-1,) + a.shape[2:]) for a in w],
        outs[len(p_in) + len(w_in) :],
    )


def exchange_kernel(x_ref, o_ref, ss, rr):
    q, n = lax.axis_index("seq"), lax.axis_size("seq")
    barrier = pltpu.get_barrier_semaphore()
    for j in range(1, n):
        pl.semaphore_signal(
            barrier, inc=1, device_id={"seq": lax.rem(q + j, n)}, device_id_type=MESH
        )
    pl.semaphore_wait(barrier, n - 1)

    def copy(j):
        return remote(x_ref, o_ref.at[q], ss.at[j], rr.at[q], seq=lax.rem(q + j, n))

    for j in range(1, n):
        copy(j).start()
    o_ref[q] = x_ref[...]
    for j in range(1, n):
        s = lax.rem(q + j, n)
        remote(x_ref, o_ref.at[s], ss.at[j], rr.at[s], seq=s).wait_recv()
    for j in range(1, n):
        copy(j).wait_send()


def exchange(x, cid):
    n = lax.axis_size("seq")
    vmem = pl.BlockSpec(memory_space=pltpu.VMEM)
    return pl.pallas_call(
        exchange_kernel,
        out_shape=jax.ShapeDtypeStruct((n,) + x.shape, x.dtype),
        in_specs=[vmem],
        out_specs=vmem,
        scratch_shapes=[pltpu.SemaphoreType.DMA((n,)), pltpu.SemaphoreType.DMA((n,))],
        name=f"exchange{cid}",
        compiler_params=pltpu.CompilerParams(collective_id=cid, has_side_effects=True),
    )(x)


def rms_norm(vector, scale_gain):
    return (
        vector * lax.rsqrt(jnp.mean(vector * vector, axis=-1, keepdims=True) + epsilon) * scale_gain
    )


def features(vector):
    second = vector[..., :, None] * vector[..., None, :] / (4.0 * math.sqrt(2.0))
    constant = jnp.ones(vector.shape[:-1] + (1,), jnp.float32)
    squares = second.reshape(vector.shape[:-1] + (vector.shape[-1] * vector.shape[-1],))
    return jnp.concatenate([constant, vector * 0.5, squares], axis=-1)


def seq_begin(lengths_row, positions):
    seq_starts = jnp.cumsum(lengths_row) - lengths_row
    chosen = jnp.where(seq_starts[None, :] <= positions[:, None], seq_starts[None, :], 0)
    return jnp.max(chosen, axis=1)


def own_scores(query_heads, key_heads, starts_at):
    row_count = starts_at.shape[0]
    scores = (
        jnp.einsum("thf,shf->hts", query_heads, key_heads, preferred_element_type=jnp.float32)
        * 0.25
    )
    places = jnp.arange(row_count, dtype=jnp.int32)
    visible = (starts_at[:, None] == starts_at[None, :]) & (places[None, :] <= places[:, None])
    return (scores, visible)


def split_heads(proj, rows):
    query = proj[:, :32].astype(jnp.bfloat16).reshape(2, rows, 2, FK)
    key = proj[:, 32:64].astype(jnp.bfloat16).reshape(2, rows, 2, FK)
    value = proj[:, 64:288].astype(jnp.bfloat16).reshape(2, rows, 2, -1)
    return query, key, value


def mb_state(key, value, last_rows):
    phi_last = features(key.astype(jnp.float32)) * last_rows[:, None, None]
    wide = jnp.concatenate(
        [value.astype(jnp.float32), jnp.ones(value.shape[:2] + (1,), jnp.float32)], axis=-1
    )
    return jnp.einsum("shp,she->hpe", phi_last, wide)


def mb_attend(query, key, value, state_in, starts_at, carried_in):
    scores, visible = own_scores(query, key, starts_at)
    weights = jnp.where(visible[None], 1.0 + scores + 0.5 * scores * scores, 0.0).astype(
        jnp.bfloat16
    )
    wide = jnp.concatenate([value, jnp.ones(value.shape[:2] + (1,), jnp.bfloat16)], axis=-1)
    both = jnp.einsum("hts,she->the", weights, wide, preferred_element_type=jnp.float32)
    both = both + carried_in[:, None, None] * jnp.einsum(
        "thp,hpe->the", features(query.astype(jnp.float32)), state_in
    )
    return both[..., :-1], both[..., -1]


def mb_back_before(back_attended, numerator, denominator, query, carried_in):
    back_out = back_attended.reshape(numerator.shape)
    back_numer = (back_out / denominator[:, :, None]).astype(jnp.bfloat16)
    back_denom = -jnp.sum(back_out * numerator, axis=2) / (denominator * denominator)
    wide = jnp.concatenate([back_numer.astype(jnp.float32), back_denom[:, :, None]], axis=-1)
    phi_used = features(query.astype(jnp.float32)) * carried_in[:, None, None]
    return wide, jnp.einsum("thp,the->hpe", phi_used, wide)


def mb_back_after(wide, query, key, value, state_in, state_out, starts_at, carried_in, last_rows):
    back_numer = wide[..., :-1].astype(jnp.bfloat16)
    back_denom = wide[..., -1]
    scores, visible = own_scores(query, key, starts_at)
    weights = jnp.where(visible[None], 1.0 + scores + 0.5 * scores * scores, 0.0).astype(
        jnp.bfloat16
    )
    back_weights = (
        jnp.einsum("the,she->hts", back_numer, value, preferred_element_type=jnp.float32)
        + jnp.transpose(back_denom)[:, :, None]
    )
    back_scores = jnp.where(visible[None], back_weights * (1.0 + scores), 0.0).astype(jnp.bfloat16)
    back_query = 0.25 * jnp.einsum(
        "hts,shf->thf", back_scores, key, preferred_element_type=jnp.float32
    )
    back_key = 0.25 * jnp.einsum(
        "hts,thf->shf", back_scores, query, preferred_element_type=jnp.float32
    )
    back_value = jnp.einsum("hts,the->she", weights, back_numer, preferred_element_type=jnp.float32)
    phi_query, phi_back_query = jax.vjp(features, query.astype(jnp.float32))
    phi_key, phi_back_key = jax.vjp(features, key.astype(jnp.float32))
    back_phi_query = carried_in[:, None, None] * jnp.einsum("the,hpe->thp", wide, state_in)
    value_wide = jnp.concatenate(
        [value.astype(jnp.float32), jnp.ones(value.shape[:2] + (1,), jnp.float32)], axis=-1
    )
    back_phi_key = last_rows[:, None, None] * jnp.einsum("she,hpe->shp", value_wide, state_out)
    back_value = back_value + last_rows[:, None, None] * jnp.einsum(
        "shp,hpe->she", phi_key, state_out[..., :-1]
    )
    return (
        back_query + phi_back_query(back_phi_query)[0],
        back_key + phi_back_key(back_phi_key)[0],
        back_value,
    )


def attention_forward(proj, taps, marks, cids):
    rows = proj.shape[0] // 2
    mine = lax.axis_index("seq")
    query, key, value = split_heads(proj, rows)
    gate_conv = proj[:, 288:].reshape(2, rows, -1)
    state = jax.vmap(mb_state)(key, value, marks["last"])
    states = exchange(state.reshape(2, -1, state.shape[-1]).astype(jnp.bfloat16), cids[0])
    state_in = jnp.einsum("nm,nmpe->mpe", marks["before"], states.astype(jnp.float32)).reshape(
        state.shape
    )
    numerator, denominator = jax.vmap(mb_attend)(
        query, key, value, state_in, marks["begin"], marks["carried"]
    )
    attended = (numerator / denominator[..., None]).reshape(2, rows, -1)
    edges = exchange(attended[:, rows - 2 :], cids[1])
    edge = lax.dynamic_index_in_dim(edges, jnp.maximum(mine - 1, 0), 0, False)
    edge = jnp.where(mine > 0, edge, 0.0)
    extended = jnp.concatenate([edge, attended], axis=1)
    conv_out = taps[0] * attended
    for offset in range(1, KW):
        conv_out = (
            conv_out
            + taps[offset]
            * extended[:, 2 - offset : 2 - offset + rows]
            * marks["allowed"][offset][:, :rows, None]
        )
    gated = (conv_out * gate_conv).astype(jnp.bfloat16)
    return gated.reshape(2 * rows, -1), (state_in, numerator, denominator, extended, conv_out)


def attention_backward(back_gated, proj, kept, taps, marks, cids):
    state_in, numerator, denominator, extended, conv_out = kept
    rows = proj.shape[0] // 2
    count, mine = lax.axis_size("seq"), lax.axis_index("seq")
    query, key, value = split_heads(proj, rows)
    gate_conv = proj[:, 288:].reshape(2, rows, -1)
    back_gated = back_gated.reshape(2, rows, -1)
    back_conv = back_gated * gate_conv
    back_gconv = (back_gated * conv_out).astype(jnp.bfloat16)
    edges = exchange(back_conv[:, :2], cids[0])
    edge = lax.dynamic_index_in_dim(edges, jnp.minimum(mine + 1, count - 1), 0, False)
    edge = jnp.where(mine < count - 1, edge, 0.0)
    conv_ext = jnp.concatenate([back_conv, edge], axis=1)
    back_attended = taps[0] * back_conv
    taps_rows = [jnp.sum(back_conv * extended[:, 2:], axis=(0, 1))]
    for offset in range(1, KW):
        allowed = marks["allowed"][offset]
        back_attended = (
            back_attended
            + taps[offset]
            * conv_ext[:, offset : offset + rows]
            * allowed[:, offset : offset + rows, None]
        )
        taps_rows.append(
            jnp.sum(
                back_conv
                * extended[:, 2 - offset : 2 - offset + rows]
                * allowed[:, :rows, None],
                axis=(0, 1),
            )
        )
    wide, state_grad = jax.vmap(mb_back_before)(
        back_attended, numerator, denominator, query, marks["carried"]
    )
    states = exchange(
        state_grad.reshape(2, -1, state_grad.shape[-1]).astype(jnp.bfloat16), cids[1]
    )
    state_out = jnp.einsum("nm,nmpe->mpe", marks["after"], states.astype(jnp.float32)).reshape(
        state_grad.shape
    )
    back_query, back_key, back_value = jax.vmap(mb_back_after)(
        wide, query, key, value, state_in, state_out, marks["begin"], marks["carried"],
        marks["last"],
    )
    flat = [a.astype(jnp.bfloat16).reshape(2 * rows, -1) for a in (back_query, back_key, back_value)]
    back_proj = jnp.concatenate(flat + [back_gconv.reshape(2 * rows, -1)], axis=1)
    return back_proj, jnp.stack(taps_rows)


def sequence_marks(lengths, rows):
    count, mine = lax.axis_size("seq"), lax.axis_index("seq")
    start = mine * rows
    positions = start + jnp.arange(rows + 2, dtype=jnp.int32)
    begin_ext = jax.vmap(lambda row: seq_begin(row, positions))(lengths)
    begin = begin_ext[:, :rows]
    ends = (jnp.arange(count, dtype=jnp.int32) + 1) * rows - 1
    stays = jax.vmap(lambda row: seq_begin(row, ends))(lengths) < (ends - rows + 1)[None, :]
    stays = stays.astype(jnp.float32)
    before = []
    after = []
    for b in range(count):
        through = jnp.where(mine > b, 1.0, 0.0) * jnp.ones_like(stays[:, 0])
        for j in range(b + 1, count):
            through = through * jnp.where(j < mine, stays[:, j], 1.0)
        before.append(through)
        through = jnp.where(mine < b, 1.0, 0.0) * jnp.ones_like(stays[:, 0])
        for j in range(b):
            through = through * jnp.where(j > mine, stays[:, j], 1.0)
        after.append(through)
    return {
        "begin": begin,
        "carried": (begin < start).astype(jnp.float32),
        "last": (begin == begin[:, rows - 1 :]).astype(jnp.float32),
        "before": jnp.stack(before),
        "after": jnp.stack(after),
        "allowed": [(positions - j >= begin_ext).astype(jnp.float32) for j in range(KW)],
    }


def by_seq(grad):
    n = lax.axis_size("seq")
    return grad.reshape((n, grad.shape[0] // n) + grad.shape[1:])


def dot_t(a, b):
    return jnp.einsum("tc,dc->td", a, b, preferred_element_type=jnp.float32)


def dot_n(a, b):
    return jnp.dot(a, b, preferred_element_type=jnp.float32)


def outer(a, b):
    return jnp.einsum("tc,tf->cf", a, b, preferred_element_type=jnp.float32).astype(jnp.bfloat16)


def on_device(
    tokens,
    lengths,
    gain_attn,
    w_query,
    w_key,
    w_value,
    w_gate_conv,
    conv_taps,
    w_out,
    gain_ffn,
    w_gate,
    w_up,
    w_down,
    cotangent,
):
    head_index = lax.axis_index("head")
    core = lax.axis_index("section")
    micro_count, rows, width = tokens.shape
    total = micro_count * rows

    def halves(weight):
        cols = weight.shape[1] // 2
        return jnp.stack([weight[:, :cols], weight[:, cols:]])

    own_mix = jnp.concatenate(
        [halves(w[0]) for w in (w_query, w_key, w_value, w_gate_conv)], axis=2
    )
    own_out = halves(w_out[0].T)
    own_ffn = jnp.concatenate([halves(w_gate[0]), halves(w_up[0])], axis=2)
    own_down = halves(w_down[0].T)
    gains_one = lax.all_gather(gain_attn[0], "section").astype(jnp.float32)
    gains_two = lax.all_gather(gain_ffn[0], "section").astype(jnp.float32)
    taps_all = lax.all_gather(conv_taps[0], "section").astype(jnp.float32)
    channels = own_out.shape[2]
    taps_both = lax.dynamic_slice_in_dim(
        taps_all, (head_index * 2 + core) * channels, channels, 2
    )
    marks = sequence_marks(lengths, rows)
    hidden_cols = own_down.shape[2]

    def as_parts(flat):
        return flat.astype(jnp.bfloat16).reshape(micro_count, rows, width)

    def wide(summed):
        return summed.astype(jnp.float32).reshape(total, width)

    mix = [None, None]
    ffn = [None, None]
    _, mix[0], _ = communicate(1, gather=(0, [own_mix, own_out]))
    x = tokens.reshape(total, width).astype(jnp.float32)
    kept = [None, None]
    outputs = []
    for layer in range(2):
        w_mix, w_o = mix[layer]
        normed = rms_norm(x, gains_one[layer]).astype(jnp.bfloat16)
        proj = dot_n(normed, w_mix)
        gated, attn = attention_forward(proj, taps_both[layer], marks, (10, 11))
        summed, ffn[layer], _ = communicate(
            2 + layer, partial=as_parts(dot_t(gated, w_o)), gather=(layer, [own_ffn, own_down])
        )
        w_gu, w_d = ffn[layer]
        middle = x + wide(summed)
        normed_two = rms_norm(middle, gains_two[layer]).astype(jnp.bfloat16)
        both = dot_n(normed_two, w_gu)
        hidden = (jax.nn.silu(both[:, :hidden_cols]) * both[:, hidden_cols:]).astype(jnp.bfloat16)
        partial = as_parts(dot_t(hidden, w_d))
        if layer == 0:
            summed, mix[1], _ = communicate(4, partial=partial, gather=(1, [own_mix, own_out]))
        else:
            summed, _, _ = communicate(5, partial=partial)
        out = (middle + wide(summed)).astype(jnp.bfloat16)
        outputs.append(out)
        kept[layer] = (x, normed, proj, gated, attn, middle, normed_two, both, hidden)
        x = out.astype(jnp.float32)

    grad = cotangent.reshape(total, width)
    back = [None, None]
    smalls = [None, None]
    received = [[None] * 4, [None] * 4]
    late = None
    for layer in (1, 0):
        x, normed, proj, gated, attn, middle, normed_two, both, hidden = kept[layer]
        w_mix, w_o = mix[layer]
        w_gu, w_d = ffn[layer]
        grad_wide = grad.astype(jnp.float32)
        back_hidden = dot_n(grad, w_d)
        gate_pre, upward = both[:, :hidden_cols], both[:, hidden_cols:]
        silu_value, silu_back = jax.vjp(jax.nn.silu, gate_pre)
        back_both = jnp.concatenate(
            [
                silu_back(back_hidden * upward)[0].astype(jnp.bfloat16),
                (back_hidden * silu_value).astype(jnp.bfloat16),
            ],
            axis=1,
        )
        partial = as_parts(dot_t(back_both, w_gu))
        if layer == 1:
            summed, _, _ = communicate(5, partial=partial)
        else:
            summed, _, received[1][:2] = communicate(6, partial=partial, scatter=(1, late))
        grad_gu = outer(normed_two, back_both)
        grad_d = outer(grad, hidden)
        _, norm_back_two = jax.vjp(rms_norm, middle, gains_two[layer])
        back_middle, gain_two = norm_back_two(wide(summed))
        back_middle = grad_wide + back_middle
        back_branch = back_middle.astype(jnp.bfloat16)
        grad_o = outer(back_branch, gated)
        back_gated = dot_n(back_branch, w_o)
        back_proj, taps_grad = attention_backward(
            back_gated, proj, attn, taps_both[layer], marks, (12, 13)
        )
        grad_mix = outer(normed, back_proj)
        partial = as_parts(dot_t(back_proj, w_mix))
        summed, _, received[layer][2:] = communicate(
            7 + layer, partial=partial, scatter=(layer, [by_seq(grad_gu), by_seq(grad_d)])
        )
        late = [by_seq(grad_mix), by_seq(grad_o)]
        _, norm_back_one = jax.vjp(rms_norm, x, gains_one[layer])
        back_x, gain_one = norm_back_one(wide(summed))
        grad = (back_middle + back_x).astype(jnp.bfloat16)
        back[layer] = grad
        smalls[layer] = (gain_one, gain_two, taps_grad)
    _, _, received[0][:2] = communicate(9, scatter=(0, late))

    def collect(index):
        picked = jnp.where(core == 0, received[0][index], received[1][index])
        return jnp.sum(picked.astype(jnp.float32), axis=1)

    grad_mix, grad_o, grad_gu, grad_d = [collect(i) for i in range(4)]

    def joined(pair):
        return jnp.concatenate([pair[0], pair[1]], axis=1)

    qk = w_query.shape[2] // 2
    vg = w_value.shape[2] // 2
    grad_query = joined(grad_mix[:, :, :qk])
    grad_key = joined(grad_mix[:, :, qk : 2 * qk])
    grad_value = joined(grad_mix[:, :, 2 * qk : 2 * qk + vg])
    grad_gconv = joined(grad_mix[:, :, 2 * qk + vg :])
    grad_out = joined(grad_o).T
    grad_gate = joined(grad_gu[:, :, :hidden_cols])
    grad_up = joined(grad_gu[:, :, hidden_cols:])
    grad_down = joined(grad_d).T

    block = width // (2 * lax.axis_size("head"))
    column_mask = (
        jnp.arange(width, dtype=jnp.int32) // block == head_index * 2 + core
    ).astype(jnp.float32)
    packed = []
    for gain_one, gain_two, taps_grad in smalls:
        taps_full = lax.dynamic_update_slice_in_dim(
            jnp.zeros((KW, width), jnp.float32), taps_grad, (head_index * 2 + core) * channels, 1
        )
        packed.append(
            jnp.concatenate(
                [(gain_one * column_mask)[None], (gain_two * column_mask)[None], taps_full], axis=0
            )
        )
    totals = lax.psum(jnp.stack(packed), ("section", "seq", "head"))
    totals = lax.dynamic_index_in_dim(totals, core, 0, False)

    def chosen(pair):
        return jnp.where(core == 0, pair[0], pair[1]).reshape(1, micro_count, rows, width)

    return (
        chosen(outputs),
        chosen(back),
        totals[0][None],
        grad_query[None],
        grad_key[None],
        grad_value[None],
        grad_gconv[None],
        totals[2:][None],
        grad_out[None],
        totals[1][None],
        grad_gate[None],
        grad_up[None],
        grad_down[None],
    )


def solution(mesh):
    placed = (
        P(None, "seq", None),
        P(),
        P("section", None),
        P("section", "seq", "head"),
        P("section", "seq", "head"),
        P("section", "seq", "head"),
        P("section", "seq", "head"),
        P("section", None, None),
        P("section", "head", "seq"),
        P("section", None),
        P("section", "seq", "head"),
        P("section", "seq", "head"),
        P("section", "head", "seq"),
        P(None, "seq", None),
    )
    return jax.shard_map(
        on_device,
        mesh=mesh,
        in_specs=placed,
        out_specs=(
            P("section", None, "seq", None),
            P("section", None, "seq", None),
            P("section", None),
            P("section", "seq", "head"),
            P("section", "seq", "head"),
            P("section", "seq", "head"),
            P("section", "seq", "head"),
            P("section", None, None),
            P("section", "head", "seq"),
            P("section", None),
            P("section", "seq", "head"),
            P("section", "seq", "head"),
            P("section", "head", "seq"),
        ),
        check_vma=False,
    )
```

time: 1920 us -> 1200 us (0.62)
  waiting for transfers between devices: 1180 us -> 0.02 us
  Pallas kernels: 0 us -> 755 us
  blocking collectives: 212 us -> 6.31 us
  local copies, waits for them, and re-layouts: 137 us -> 102 us
  matrix products: 198 us -> 168 us
    pallas_call x0 -> x18, Pallas kernels: none -> 755 us  [the longest x10 663 us: communicate(): pl.pallas_call(functools.partial(comm_kernel, plan), out_shape=shapes, in...]
    psum x8 -> x1, waiting for transfers between devices: 641 us -> 0.01 us  [on_device(): totals = lax.psum(jnp.stack(packed), ('section', 'seq', 'head'))]
    unnamed x30 -> x1, waiting for transfers between devices: 364 us -> 0.02 us
    all_gather x11 -> x1, blocking collectives: 200 us -> 1.99 us  [on_device(): taps_all = lax.all_gather(conv_taps[0], 'section').astype(jnp.float32)]
    all_gather x6 -> x0, waiting for transfers between devices: 157 us -> none  [both_layers(): gathered = lax.all_gather(weight, ('section', 'seq'), axis=0, tiled=True)]
    unnamed x503 -> x462, local copies, waits for them, and re-layouts: 122 us -> 17.5 us
    convert_element_type x12 -> x20, other arithmetic: 9.99 us -> 41.7 us  [the longest x2 14.5 us: on_device(): grad = (back_middle + back_x).astype(jnp.bfloat16)]
    convert_element_type x0 -> x16, local copies, waits for them, and re-layouts: none -> 29.8 us  [the longest x6 23.4 us: outer(): jnp.einsum('tc,tf->cf', a, b, preferred_element_type=jnp.float32)]
  transfers between devices with their start and end apart: 28 -> 1, of which waited for: 21 -> 0; matrix products, arithmetic and copies ran while one was open for 14% -> 4% of each run, Pallas kernels for 0% -> 8%
where the time goes in v2:
time: 1200 us; the launch traced here: 1190 us
  Pallas kernels  755 us (63%)
  matrix products  168 us (14%)
  other arithmetic  143 us (12%)
  local copies, waits for them, and re-layouts  102 us (8%)
  between operations  17.8 us (1%)
    pallas_call x10, Pallas kernels, communicate(): pl.pallas_call(functools.partial(comm_kernel, plan), out_shape=shapes, in...  663 us
    pallas_call x8, Pallas kernels, exchange(): pl.pallas_call(exchange_kernel, out_shape=jax.ShapeDtypeStruct((n,) + x.s...  92.3 us
    dot_general x8, matrix products, dot_t(): return jnp.einsum('tc,dc->td', a, b, preferred_element_type=jnp.float32)  43 us
    dot_general x8, matrix products, dot_n(): return jnp.dot(a, b, preferred_element_type=jnp.float32)  38.8 us
    dot_general x8, matrix products, outer(): jnp.einsum('tc,tf->cf', a, b, preferred_element_type=jnp.float32)  34.4 us
  transfers between devices with their start and end apart: 1, of which 0 were waited for; matrix products, arithmetic and copies ran while one was open for 4% of the time, Pallas kernels for 8%

profile of v2, /device:TPU:0, one launch (start us, length us, event | category | flops | bytes accessed | tf_op | source)
XLA Modules:
  0.0 1192.8 jit_solution(14233120471301557182)
XLA Ops:
  17.9 34.7 %comm1.1 = (bf16[4,448,512]{2,1,0:T(8,128)(2,1)S(1)}, bf16[4,448,224]{2,1,0:T(8,128)(2,1)S(1)}) custom-call(bf16[2,448,512]{2,1,0:T(8,128)(2,1)S(1)} %maximum_maximum_fusion.1.refs_0_.refs_1_, bf16[2,448,224]{2,1,0:T(8,128)(2,1)S(1)} %pad_maximum_fusion.59.refs_1_.refs_2_), custom_call_target="tpu_custom_call" | custom-call | tf_op jit(solution)/shard_map/comm1/pallas_call | solution.py:413
  53.9 3.4 fusion.221
  82.5 18.0 %exchange10.2 = bf16[4,2,546,113]{3,2,1,0:T(8,128)(2,1)} custom-call(bf16[2,546,113]{2,1,0:T(8,128)(2,1)} %convert_element_type.452.x_ref), custom_call_target="tpu_custom_call" | custom-call | tf_op jit(solution)/shard_map/exchange10/pallas_call | solution.py:457
  105.8 3.8 fusion.151
  112.5 5.9 exchange11.2
  125.5 3.0 convolution_convert_fusion.9
  129.2 84.4 %comm2.1 = (bf16[2,512,1792]{2,1,0:T(8,128)(2,1)}, bf16[4,448,1216]{2,1,0:T(8,128)(2,1)}, bf16[4,448,608]{2,1,0:T(8,128)(2,1)S(1)}) custom-call(bf16[2,512,1792]{2,1,0:T(8,128)(2,1)} %bitcast.460, bf16[2,448,1216]{2,1,0:T(8,128)(2,1)S(1)} %maximum_maximum_fusion.refs_1_, bf16[2,448,608]{2,1,0:T(8,128)(2,1)S(1)} %pad_maximum_fusion.46.refs_2_), custom_call_target="tpu_custom_call" | custom-call | tf_op jit(solution)/shard_map/comm2/pallas_call | solution.py:413
  213.7 4.2 multiply_reduce_fusion.3
  219.8 7.0 fusion.223
  227.6 4.6 convolution_convert_fusion.7
  232.3 67.1 %comm4.1 = (bf16[2,512,1792]{2,1,0:T(8,128)(2,1)}, bf16[4,448,512]{2,1,0:T(8,128)(2,1)S(1)}, bf16[4,448,224]{2,1,0:T(8,128)(2,1)S(1)}) custom-call(bf16[2,512,1792]{2,1,0:T(8,128)(2,1)} %bitcast.487, bf16[2,448,512]{2,1,0:T(8,128)(2,1)S(1)} %copy-done.8, bf16[2,448,224]{2,1,0:T(8,128)(2,1)S(1)} %copy-done.10), custom_call_target="tpu_custom_call" | custom-call | tf_op jit(solution)/shard_map/comm4/pallas_call | solution.py:413
  299.4 5.0 fusion.25
  306.3 3.4 fusion.222
  318.0 3.5 fusion.162
  337.9 17.5 %exchange10.3 = bf16[4,2,546,113]{3,2,1,0:T(8,128)(2,1)} custom-call(bf16[2,546,113]{2,1,0:T(8,128)(2,1)} %convert_element_type.472.x_ref), custom_call_target="tpu_custom_call" | custom-call | tf_op jit(solution)/shard_map/exchange10/pallas_call | solution.py:457
  359.8 3.9 fusion.147
  370.3 5.9 exchange11.3
  377.0 3.0 multiply_convert_fusion.9
  380.1 3.0 convolution_convert_fusion.8
  383.1 78.7 %comm3.1 = (bf16[2,512,1792]{2,1,0:T(8,128)(2,1)}, bf16[4,448,1216]{2,1,0:T(8,128)(2,1)}, bf16[4,448,608]{2,1,0:T(8,128)(2,1)S(1)}) custom-call(bf16[2,512,1792]{2,1,0:T(8,128)(2,1)} %bitcast.461, bf16[2,448,1216]{2,1,0:T(8,128)(2,1)S(1)} %maximum_maximum_fusion.refs_1_, bf16[2,448,608]{2,1,0:T(8,128)(2,1)S(1)} %pad_maximum_fusion.46.refs_2_), custom_call_target="tpu_custom_call" | custom-call | tf_op jit(solution)/shard_map/comm3/pallas_call | solution.py:413
  461.8 4.2 multiply_reduce_fusion.2
  467.3 8.9 fusion.224
  476.2 7.3 fusion.49
  483.5 6.5 convolution_convert_fusion.5
  490.0 68.3 %comm5.3 = bf16[2,512,1792]{2,1,0:T(8,128)(2,1)S(1)} custom-call(bf16[2,512,1792]{2,1,0:T(8,128)(2,1)} %bitcast.488), custom_call_target="tpu_custom_call" | custom-call | tf_op jit(solution)/shard_map/comm5/pallas_call | solution.py:413
  558.4 3.7 multiply_reduce_fusion
  569.6 6.0 exchange12.2
  580.2 4.7 fusion.213
  590.3 6.2 fusion.44
  596.4 3.3 copy.302
  603.2 16.9 %exchange13.2 = bf16[4,2,546,113]{3,2,1,0:T(8,128)(2,1)} custom-call(bf16[2,546,113]{2,1,0:T(8,128)(2,1)} %convert_element_type.494.x_ref), custom_call_target="tpu_custom_call" | custom-call | tf_op jit(solution)/shard_map/exchange13/pallas_call | solution.py:457
  637.4 8.1 multiply_convert_fusion.1
  645.5 7.3 convolution_convert_fusion.1
  652.7 7.6 copy.301
  660.3 5.8 convolution_convert_fusion.4
  666.1 82.1 %comm8.1 = (bf16[2,512,1792]{2,1,0:T(8,128)(2,1)S(1)}, bf16[2,4,448,1216]{3,2,1,0:T(8,128)(2,1)}, bf16[2,4,448,608]{3,2,1,0:T(8,128)(2,1)}) custom-call(bf16[2,512,1792]{2,1,0:T(8,128)(2,1)} %bitcast.483, bf16[4,448,1216]{2,1,0:T(8,128)(2,1)} %bitcast.463, bf16[4,448,608]{2,1,0:T(8,128)(2,1)S(1)} %bitcast.440), custom_call_target="tpu_custom_call" | custom-call | tf_op jit(solution)/shard_map/comm8/pallas_call | solution.py:413
  748.2 3.5 fusion.7
  752.7 8.1 fusion.18
  760.8 3.5 fusion.52
  764.4 9.9 convolution_convert_fusion.3
  777.5 67.4 %comm6.1 = (bf16[2,512,1792]{2,1,0:T(8,128)(2,1)}, bf16[2,4,448,512]{3,2,1,0:T(8,128)(2,1)}, bf16[2,4,448,224]{3,2,1,0:T(8,128)(2,1)S(1)}) custom-call(bf16[2,512,1792]{2,1,0:T(8,128)(2,1)} %bitcast.486, bf16[4,448,512]{2,1,0:T(8,128)(2,1)S(1)} %bitcast.445, bf16[4,448,224]{2,1,0:T(8,128)(2,1)S(1)} %bitcast.441), custom_call_target="tpu_custom_call" | custom-call | tf_op jit(solution)/shard_map/comm6/pallas_call | solution.py:413
  844.9 5.9 fusion.10
  851.0 2.9 fusion.38
  854.0 3.3 multiply_reduce_fusion.13
  857.9 5.9 exchange12.3
  866.9 4.7 fusion.212
  875.7 7.3 convolution_convert_fusion
  883.1 6.4 fusion.22
  889.6 3.8 convolution_convert_fusion.10
  893.3 3.3 copy.317
  896.6 7.2 copy.316
  909.0 16.2 %exchange13.3 = bf16[4,2,546,113]{3,2,1,0:T(8,128)(2,1)} custom-call(bf16[2,546,113]{2,1,0:T(8,128)(2,1)} %convert_element_type.525.x_ref), custom_call_target="tpu_custom_call" | custom-call | tf_op jit(solution)/shard_map/exchange13/pallas_call | solution.py:457
  929.0 3.2 select_convert_fusion
  938.5 4.0 convolution_convert_fusion.2
  942.5 83.3 %comm7.1 = (bf16[2,512,1792]{2,1,0:T(8,128)(2,1)S(1)}, bf16[2,4,448,1216]{3,2,1,0:T(8,128)(2,1)}, bf16[2,4,448,608]{3,2,1,0:T(8,128)(2,1)}) custom-call(bf16[2,512,1792]{2,1,0:T(8,128)(2,1)} %bitcast.484, bf16[4,448,1216]{2,1,0:T(8,128)(2,1)} %bitcast.462, bf16[4,448,608]{2,1,0:T(8,128)(2,1)S(1)} %bitcast.439), custom_call_target="tpu_custom_call" | custom-call | tf_op jit(solution)/shard_map/comm7/pallas_call | solution.py:413
  1029.9 6.3 convolution_convert_fusion.6
  1037.9 4.3 convolution_convert_fusion.12
  1042.2 33.9 %comm9.1 = (bf16[2,4,448,512]{3,2,1,0:T(8,128)(2,1)}, bf16[2,4,448,224]{3,2,1,0:T(8,128)(2,1)S(1)}) custom-call(bf16[4,448,512]{2,1,0:T(8,128)(2,1)S(1)} %bitcast.446, bf16[4,448,224]{2,1,0:T(8,128)(2,1)S(1)} %bitcast.442), custom_call_target="tpu_custom_call" | custom-call | tf_op jit(solution)/shard_map/comm9/pallas_call | solution.py:413
  1076.1 3.3 convert_reduce_fusion.2
  1081.8 63.3 %comm5.2 = bf16[2,512,1792]{2,1,0:T(8,128)(2,1)S(1)} custom-call(bf16[2,512,1792]{2,1,0:T(8,128)(2,1)} %bitcast.485), custom_call_target="tpu_custom_call" | custom-call | tf_op jit(solution)/shard_map/comm5/pallas_call | solution.py:413
  1145.1 3.4 fusion.33
  1150.1 6.0 convert_reduce_fusion
  1156.8 4.3 convert_reduce_fusion.1
  1164.0 7.2 fusion.35
  (676 shorter events, 186.5 us)
Async XLA Ops:
  7.2 9.3 copy-start.127
  7.2 1175.8 %all-reduce.6.cloned.1.call-start = ((), (), s32[]{:S(2)}) async-start(), calls=%async_computation | async-start | bytes 143360 | tf_op jit(solution)/shard_map/psum | solution.py:856
  9.0 55.6 %copy-start.144 = (s32[2,514]{1,0:T(2,128)}, s32[2,514]{1,0:T(2,128)S(1)}, u32[]{:S(2)}) copy-start(s32[2,514]{1,0:T(2,128)S(1)} %select_reduce_fusion) | copy-start | bytes 12340
  13.5 39.1 %copy-start.145 = (f32[2,512]{1,0:T(2,128)}, f32[2,512]{1,0:T(2,128)S(1)}, u32[]{:S(2)}) copy-start(f32[2,512]{1,0:T(2,128)S(1)} %get-tuple-element.231) | copy-start | bytes 12292
  16.1 36.5 %copy-start.132 = (f32[1792]{0:T(1024)}, f32[1792]{0:T(1024)S(1)}, u32[]{:S(2)}) copy-start(f32[1792]{0:T(1024)S(1)} %get-tuple-element.134) | copy-start | bytes 21508
  16.7 35.9 %copy-start.24 = (bf16[2,512,1792]{2,1,0:T(8,128)(2,1)S(1)}, bf16[2,512,1792]{2,1,0:T(8,128)(2,1)}, u32[]{:S(2)}) copy-start(bf16[2,512,1792]{2,1,0:T(8,128)(2,1)} %param.14) | copy-start | bytes 11010052
  17.0 36.6 %copy-start.9 = (bf16[2,448,224]{2,1,0:T(8,128)(2,1)}, bf16[2,448,224]{2,1,0:T(8,128)(2,1)S(1)}, u32[]{:S(2)}) copy-start(bf16[2,448,224]{2,1,0:T(8,128)(2,1)S(1)} %pad_maximum_fusion.59.refs_1_.refs_2_) | copy-start | bytes 1204228
  17.9 35.7 %copy-start.7 = (bf16[2,448,512]{2,1,0:T(8,128)(2,1)}, bf16[2,448,512]{2,1,0:T(8,128)(2,1)S(1)}, u32[]{:S(2)}) copy-start(bf16[2,448,512]{2,1,0:T(8,128)(2,1)S(1)} %maximum_maximum_fusion.1.refs_0_.refs_1_) | copy-start | bytes 2752516
  52.7 72.8 %copy-start.15 = (bf16[4,448,224]{2,1,0:T(8,128)(2,1)}, bf16[4,448,224]{2,1,0:T(8,128)(2,1)S(1)}, u32[]{:S(2)}) copy-start(bf16[4,448,224]{2,1,0:T(8,128)(2,1)S(1)} %get-tuple-element.36) | copy-start | bytes 2408452
  57.3 11.1 copy-start.189
  57.4 16.2 %copy-start.97 = (bf16[2,512,2,16]{1,0,3,2:T(2,128)(2,1)}, bf16[2,512,2,16]{1,0,3,2:T(2,128)(2,1)S(1)}, u32[]{:S(2)}) copy-start(bf16[2,512,2,16]{1,0,3,2:T(2,128)(2,1)S(1)} %reshape.1104) | copy-start | bytes 196612
  58.1 19.8 %copy-start.116 = (f32[2,512,2,16]{1,3,2,0:T(8,128)}, f32[2,512,2,16]{1,3,2,0:T(8,128)S(1)}, u32[]{:S(2)}) copy-start(f32[2,512,2,16]{1,3,2,0:T(8,128)S(1)} %get-tuple-element.203) | copy-start | bytes 393220
  58.1 15.4 %copy-start.99 = (bf16[2,512,2,16]{1,0,3,2:T(2,128)(2,1)}, bf16[2,512,2,16]{1,0,3,2:T(2,128)(2,1)S(1)}, u32[]{:S(2)}) copy-start(bf16[2,512,2,16]{1,0,3,2:T(2,128)(2,1)S(1)} %reshape.1103) | copy-start | bytes 196612
  58.9 50.8 %copy-start.118 = (f32[2,512,2,16]{1,3,2,0:T(8,128)}, f32[2,512,2,16]{1,3,2,0:T(8,128)S(1)}, u32[]{:S(2)}) copy-start(f32[2,512,2,16]{1,3,2,0:T(8,128)S(1)} %get-tuple-element.201) | copy-start | bytes 393220
  77.6 32.1 %copy-start.56 = (f32[2,512,2,16,16]{1,4,3,2,0:T(8,128)}, f32[2,512,2,16,16]{1,4,3,2,0:T(8,128)S(1)}, u32[]{:S(2)}) copy-start(f32[2,512,2,16,16]{1,4,3,2,0:T(8,128)S(1)} %multiply_multiply_fusion.2) | copy-start | bytes 6291460
  77.6 22.9 %copy-start.209 = (bf16[4,2,1,1]{0,2,3,1:T(2,128)(2,1)S(1)}, bf16[4,2,1,1]{0,2,3,1:T(2,128)(2,1)}, u32[]{:S(2)}) copy-start(bf16[4,2,1,1]{0,2,3,1:T(2,128)(2,1)} %copy.326) | copy-start | bytes 52
  80.7 23.6 %slice-start.2 = ((s32[2,514]{1,0:T(2,128)}), s32[2,512]{1,0:T(2,128)S(1)}, s32[]{:S(2)}) async-start(s32[2,514]{1,0:T(2,128)} %copy-done.144), calls=%async_computation.3 | async-start | bytes 8192 | tf_op jit(solution)/shard_map/slice | solution.py:655
  111.8 13.7 %copy-start.68 = (f32[2,512,224]{2,1,0:T(8,128)}, f32[2,512,224]{2,1,0:T(8,128)S(1)}, u32[]{:S(2)}) copy-start(f32[2,512,224]{2,1,0:T(8,128)S(1)} %copy.277) | copy-start | bytes 2752516
  111.8 10.9 copy-start.155
  111.8 10.9 copy-start.157
  111.8 10.9 copy-start.190
  111.8 10.9 copy-start.192
  111.8 10.9 copy-start.194
  129.2 84.5 %copy-start.25 = (bf16[2,512,1792]{2,1,0:T(8,128)(2,1)S(1)}, bf16[2,512,1792]{2,1,0:T(8,128)(2,1)}, u32[]{:S(2)}) copy-start(bf16[2,512,1792]{2,1,0:T(8,128)(2,1)} %param.14) | copy-start | bytes 11010052
  213.7 13.9 %copy-start.19 = (bf16[4,448,608]{2,1,0:T(8,128)(2,1)}, bf16[4,448,608]{2,1,0:T(8,128)(2,1)S(1)}, u32[]{:S(2)}) copy-start(bf16[4,448,608]{2,1,0:T(8,128)(2,1)S(1)} %get-tuple-element.39) | copy-start | bytes 6537220
  312.0 11.7 copy-start.101
  332.2 23.1 %copy-start.210 = (bf16[4,2,1,1]{0,2,3,1:T(2,128)(2,1)S(1)}, bf16[4,2,1,1]{0,2,3,1:T(2,128)(2,1)}, u32[]{:S(2)}) copy-start(bf16[4,2,1,1]{0,2,3,1:T(2,128)(2,1)} %copy.326) | copy-start | bytes 52
  363.8 13.2 %copy-start.158 = (f32[2,512]{1,0:T(2,128)S(1)}, f32[2,512]{1,0:T(2,128)}, u32[]{:S(2)}) copy-start(f32[2,512]{1,0:T(2,128)} %get-tuple-element.225) | copy-start | bytes 12292
  363.8 13.2 %copy-start.196 = (f32[1,1,224]{2,1,0:T(1,128)S(1)}, f32[1,1,224]{2,1,0:T(1,128)}, u32[]{:S(2)}) copy-start(f32[1,1,224]{2,1,0:T(1,128)} %get-tuple-element.216) | copy-start | bytes 2692
  363.8 13.2 %copy-start.197 = (f32[1,1,224]{2,1,0:T(1,128)S(1)}, f32[1,1,224]{2,1,0:T(1,128)}, u32[]{:S(2)}) copy-start(f32[1,1,224]{2,1,0:T(1,128)} %get-tuple-element.217) | copy-start | bytes 2692
  363.8 13.2 %copy-start.198 = (f32[1,1,224]{2,1,0:T(1,128)S(1)}, f32[1,1,224]{2,1,0:T(1,128)}, u32[]{:S(2)}) copy-start(f32[1,1,224]{2,1,0:T(1,128)} %get-tuple-element.221) | copy-start | bytes 2692
  383.1 78.7 %copy-start.31 = (bf16[2,512,1792]{2,1,0:T(8,128)(2,1)S(1)}, bf16[2,512,1792]{2,1,0:T(8,128)(2,1)}, u32[]{:S(2)}) copy-start(bf16[2,512,1792]{2,1,0:T(8,128)(2,1)} %copy-done.30) | copy-start | bytes 11010052
  461.8 14.4 %copy-start.17 = (bf16[4,448,608]{2,1,0:T(8,128)(2,1)}, bf16[4,448,608]{2,1,0:T(8,128)(2,1)S(1)}, u32[]{:S(2)}) copy-start(bf16[4,448,608]{2,1,0:T(8,128)(2,1)S(1)} %get-tuple-element.45) | copy-start | bytes 6537220
  467.3 16.2 %slice-start.3 = ((s8[4587520]{0:T(1024)(128)(4,1)}), s8[393216]{0:T(1024)(128)(4,1)S(1)}, s32[]{:S(2)}) async-start(s8[4587520]{0:T(1024)(128)(4,1)} %bitcast.572), calls=%async_computation.4 | async-start | bytes 786432
  567.0 9.3 copy-start.151
  567.0 9.3 copy-start.153
  569.0 15.9 %copy-start.71 = (f32[2,512,224]{2,1,0:T(8,128)}, f32[2,512,224]{2,1,0:T(8,128)S(1)}, u32[]{:S(2)}) copy-start(f32[2,512,224]{2,1,0:T(8,128)S(1)} %get-tuple-element.180) | copy-start | bytes 2752516
  569.0 9.0 copy-start.66
  596.4 23.6 %copy-start.208 = (bf16[4,2,1,1]{0,2,3,1:T(2,128)(2,1)S(1)}, bf16[4,2,1,1]{0,2,3,1:T(2,128)(2,1)}, u32[]{:S(2)}) copy-start(bf16[4,2,1,1]{0,2,3,1:T(2,128)(2,1)} %copy.333) | copy-start | bytes 52
  636.1 9.4 copy-start.166
  666.1 82.1 %copy-start.32 = (bf16[2,512,1792]{2,1,0:T(8,128)(2,1)S(1)}, bf16[2,512,1792]{2,1,0:T(8,128)(2,1)}, u32[]{:S(2)}) copy-start(bf16[2,512,1792]{2,1,0:T(8,128)(2,1)} %copy-done.30) | copy-start | bytes 11010052
  666.1 82.2 %copy-start.150 = (f32[2,512]{1,0:T(2,128)S(1)}, f32[2,512]{1,0:T(2,128)}, u32[]{:S(2)}) copy-start(f32[2,512]{1,0:T(2,128)} %copy-done.149) | copy-start | bytes 12292
  666.1 85.6 %copy-start.169 = (f32[2,512]{1,0:T(2,128)S(1)}, f32[2,512]{1,0:T(2,128)}, u32[]{:S(2)}) copy-start(f32[2,512]{1,0:T(2,128)} %copy-done.168) | copy-start | bytes 12292
  666.1 85.7 %copy-start.171 = (f32[2,512]{1,0:T(2,128)S(1)}, f32[2,512]{1,0:T(2,128)}, u32[]{:S(2)}) copy-start(f32[2,512]{1,0:T(2,128)} %copy-done.170) | copy-start | bytes 12292
  748.2 12.5 %slice-start = ((s8[4980736]{0:T(1024)(128)(4,1)}), s8[4194304]{0:T(1024)(128)(4,1)S(1)}, s32[]{:S(2)}) async-start(s8[4980736]{0:T(1024)(128)(4,1)} %bitcast.478), calls=%async_computation.1 | async-start | bytes 8388608
  764.4 9.9 copy-start.215
  764.4 9.9 copy-start.217
  764.4 10.5 copy-start.53
  764.4 10.5 copy-start.128
  764.4 10.5 copy-start.129
  774.9 69.9 %copy-start.41 = (bf16[2,512,1792]{2,1,0:T(8,128)(2,1)S(1)}, bf16[2,512,1792]{2,1,0:T(8,128)(2,1)}, u32[]{:S(2)}) copy-start(bf16[2,512,1792]{2,1,0:T(8,128)(2,1)} %get-tuple-element.37) | copy-start | bytes 11010052
  777.5 67.4 %copy-start.27 = (bf16[2,512,1792]{2,1,0:T(8,128)(2,1)S(1)}, bf16[2,512,1792]{2,1,0:T(8,128)(2,1)}, u32[]{:S(2)}) copy-start(bf16[2,512,1792]{2,1,0:T(8,128)(2,1)} %param.14) | copy-start | bytes 11010052
  777.5 67.4 %copy-start.140 = (f32[2,512]{1,0:T(2,128)S(1)}, f32[2,512]{1,0:T(2,128)}, u32[]{:S(2)}) copy-start(f32[2,512]{1,0:T(2,128)} %copy-done.139) | copy-start | bytes 12292
  854.0 10.5 copy-start.152
  854.0 10.5 copy-start.154
  854.0 10.5 copy-start.191
  854.0 10.5 copy-start.193
  854.0 10.5 copy-start.195
  903.8 25.2 %copy-start.90 = (bf16[2,512,2,112]{1,0,3,2:T(2,128)(2,1)S(1)}, bf16[2,512,2,112]{1,0,3,2:T(2,128)(2,1)}, u32[]{:S(2)}) copy-start(bf16[2,512,2,112]{1,0,3,2:T(2,128)(2,1)} %copy-done.89) | copy-start | bytes 1376260
  942.5 83.3 %copy-start.28 = (bf16[2,512,1792]{2,1,0:T(8,128)(2,1)S(1)}, bf16[2,512,1792]{2,1,0:T(8,128)(2,1)}, u32[]{:S(2)}) copy-start(bf16[2,512,1792]{2,1,0:T(8,128)(2,1)} %param.14) | copy-start | bytes 11010052
  942.5 83.4 %copy-start.146 = (f32[2,512]{1,0:T(2,128)S(1)}, f32[2,512]{1,0:T(2,128)}, u32[]{:S(2)}) copy-start(f32[2,512]{1,0:T(2,128)} %copy-done.145) | copy-start | bytes 12292
  1037.8 38.3 %copy-start.78 = (bf16[2,4,448,512]{3,2,1,0:T(8,128)(2,1)S(1)}, bf16[2,4,448,512]{3,2,1,0:T(8,128)(2,1)}, u32[]{:S(2)}) copy-start(bf16[2,4,448,512]{3,2,1,0:T(8,128)(2,1)} %get-tuple-element.50) | copy-start | bytes 11010052
  1081.8 63.3 %copy-start.33 = (bf16[2,512,1792]{2,1,0:T(8,128)(2,1)S(1)}, bf16[2,512,1792]{2,1,0:T(8,128)(2,1)}, u32[]{:S(2)}) copy-start(bf16[2,512,1792]{2,1,0:T(8,128)(2,1)} %copy-done.30) | copy-start | bytes 11010052
  1081.8 63.3 %copy-start.38 = (bf16[2,512,1792]{2,1,0:T(8,128)(2,1)S(1)}, bf16[2,512,1792]{2,1,0:T(8,128)(2,1)}, u32[]{:S(2)}) copy-start(bf16[2,512,1792]{2,1,0:T(8,128)(2,1)} %get-tuple-element.43) | copy-start | bytes 11010052
  (161 other events, 704.2 us)
Sparse Core Ops, SparseCore 0:
  1030.0 128.8 all-reduce.5

commit v3 on v2

--- a/solution.py
+++ b/solution.py
@@ -6,6 +6,7 @@
 from jax import lax
 from jax.experimental import pallas as pl
 from jax.experimental.pallas import tpu as pltpu
+import numpy as np
 from jax.sharding import PartitionSpec as P
 
 FK = 16
@@ -429,222 +430,490 @@
     )
 
 
-def exchange_kernel(x_ref, o_ref, ss, rr):
-    q, n = lax.axis_index("seq"), lax.axis_size("seq")
-    barrier = pltpu.get_barrier_semaphore()
-    for j in range(1, n):
-        pl.semaphore_signal(
-            barrier, inc=1, device_id={"seq": lax.rem(q + j, n)}, device_id_type=MESH
-        )
-    pl.semaphore_wait(barrier, n - 1)
-
-    def copy(j):
-        return remote(x_ref, o_ref.at[q], ss.at[j], rr.at[q], seq=lax.rem(q + j, n))
-
-    for j in range(1, n):
-        copy(j).start()
-    o_ref[q] = x_ref[...]
-    for j in range(1, n):
-        s = lax.rem(q + j, n)
-        remote(x_ref, o_ref.at[s], ss.at[j], rr.at[s], seq=s).wait_recv()
-    for j in range(1, n):
-        copy(j).wait_send()
-
-
-def exchange(x, cid):
-    n = lax.axis_size("seq")
-    vmem = pl.BlockSpec(memory_space=pltpu.VMEM)
-    return pl.pallas_call(
-        exchange_kernel,
-        out_shape=jax.ShapeDtypeStruct((n,) + x.shape, x.dtype),
-        in_specs=[vmem],
-        out_specs=vmem,
-        scratch_shapes=[pltpu.SemaphoreType.DMA((n,)), pltpu.SemaphoreType.DMA((n,))],
-        name=f"exchange{cid}",
-        compiler_params=pltpu.CompilerParams(collective_id=cid, has_side_effects=True),
-    )(x)
-
-
 def rms_norm(vector, scale_gain):
     return (
         vector * lax.rsqrt(jnp.mean(vector * vector, axis=-1, keepdims=True) + epsilon) * scale_gain
     )
 
 
-def features(vector):
-    second = vector[..., :, None] * vector[..., None, :] / (4.0 * math.sqrt(2.0))
-    constant = jnp.ones(vector.shape[:-1] + (1,), jnp.float32)
-    squares = second.reshape(vector.shape[:-1] + (vector.shape[-1] * vector.shape[-1],))
-    return jnp.concatenate([constant, vector * 0.5, squares], axis=-1)
-
-
 def seq_begin(lengths_row, positions):
     seq_starts = jnp.cumsum(lengths_row) - lengths_row
     chosen = jnp.where(seq_starts[None, :] <= positions[:, None], seq_starts[None, :], 0)
     return jnp.max(chosen, axis=1)
 
 
-def own_scores(query_heads, key_heads, starts_at):
-    row_count = starts_at.shape[0]
-    scores = (
-        jnp.einsum("thf,shf->hts", query_heads, key_heads, preferred_element_type=jnp.float32)
-        * 0.25
+HEADS = 2
+PAIRS = FK * (FK + 1) // 2
+STATE = 160
+BLOCK = 128
+
+
+def feature_tables(values):
+    wide = values + HEADS * FK
+    first = np.zeros((HEADS, wide, wide), np.float32)
+    second = np.zeros((HEADS, wide, wide), np.float32)
+    rest = np.zeros((8, wide), np.float32)
+    for h in range(HEADS):
+        at = values + h * FK
+        lane = 0
+        for a in range(FK):
+            for b in range(a, FK):
+                first[h, at + a, lane] = 1
+                second[h, at + b, lane] = 1
+                rest[2, lane] = 0.25 if a < b else 1 / (4.0 * math.sqrt(2.0))
+                lane += 1
+        for a in range(FK):
+            first[h, at + a, lane] = 1
+            rest[1, lane] = 1
+            rest[2, lane] = 0.5
+            lane += 1
+        rest[0, lane] = rest[1, lane] = rest[2, lane] = 1
+    return np.stack([first, second], axis=1), rest
+
+
+def mm(a, b):
+    return lax.dot_general(a, b, (((1,), (0,)), ((), ())), preferred_element_type=jnp.float32)
+
+
+def mm_nt(a, b):
+    return lax.dot_general(a, b, (((1,), (1,)), ((), ())), preferred_element_type=jnp.float32)
+
+
+def mm_tn(a, b):
+    return lax.dot_general(a, b, (((0,), (0,)), ((), ())), preferred_element_type=jnp.float32)
+
+
+class Lanes:
+    def __init__(self, wide, values):
+        self.values = values
+        self.lane = lax.broadcasted_iota(jnp.int32, (1, wide), 1)
+        lane, dim = self.lane, values // HEADS
+        self.is_value = lane < values
+        self.is_one = (lane >= values) & (lane < values + 2 * HEADS)
+        self.head = jnp.where(
+            self.is_value, jnp.where(lane < dim, 0, 1), jnp.where(self.is_one, (lane - values) % 2, 9)
+        )
+
+    def of(self, h, x):
+        return jnp.where(self.head == h, x, jnp.zeros_like(x))
+
+    def key(self, h, x):
+        at = self.values + h * FK
+        return jnp.where((self.lane >= at) & (self.lane < at + FK), x, jnp.zeros_like(x))
+
+    def extended(self, a):
+        return jnp.where(
+            self.is_value, a, jnp.where(self.is_one, jnp.ones_like(a), jnp.zeros_like(a))
+        )
+
+    def column(self, x, index):
+        return jnp.sum(
+            jnp.where(self.lane == self.values + index, x, 0.0), axis=1, keepdims=True
+        )
+
+    def denominator(self, x):
+        return jnp.where(
+            self.lane < self.values // HEADS, self.column(x, 0), self.column(x, 1)
+        )
+
+
+def meet(direction, reach):
+    q, n = lax.axis_index("seq"), lax.axis_size("seq")
+    barrier = pltpu.get_barrier_semaphore()
+    count = 0
+    for d in range(1, reach + 1):
+        source = q - direction * d
+        target = q + direction * d
+
+        @pl.when((source >= 0) & (source < n))
+        def _():
+            pl.semaphore_signal(barrier, inc=1, device_id={"seq": source}, device_id_type=MESH)
+
+        count = count + jnp.where((target >= 0) & (target < n), 1, 0)
+
+    @pl.when(count > 0)
+    def _():
+        pl.semaphore_wait(barrier, count)
+
+
+class Pass:
+    def __init__(self, direction, reach, src, dst, send, recv):
+        self.direction, self.reach = direction, reach
+        self.src, self.dst, self.send, self.recv = src, dst, send, recv
+        self.q, self.n = lax.axis_index("seq"), lax.axis_size("seq")
+
+    def has_source(self, d):
+        at = self.q - self.direction * d
+        return (at >= 0) & (at < self.n)
+
+    def has_target(self, d):
+        at = self.q + self.direction * d
+        return (at >= 0) & (at < self.n)
+
+    def copy(self, d):
+        return remote(
+            self.src, self.dst.at[d - 1], self.send.at[d - 1], self.recv.at[d - 1],
+            seq=self.q + self.direction * d,
+        )
+
+    def start(self):
+        for d in range(1, self.reach + 1):
+
+            @pl.when(self.has_target(d))
+            def _():
+                self.copy(d).start()
+
+    def arrived(self):
+        for d in range(1, self.reach + 1):
+
+            @pl.when(self.has_source(d))
+            def _():
+                self.copy(d).wait_recv()
+
+    def sent(self):
+        for d in range(1, self.reach + 1):
+
+            @pl.when(self.has_target(d))
+            def _():
+                self.copy(d).wait_send()
+
+
+def sum_states(states, coef, total):
+    for m in range(2):
+        total[m] = jnp.zeros(total.shape[1:], total.dtype)
+        for d in range(1, states.reach + 1):
+
+            @pl.when(states.has_source(d))
+            def _():
+                total[m, :STATE, :] += coef[d - 1, m] * states.dst[d - 1, m].astype(jnp.float32)
+
+
+def shifted(a, tail, fresh, by):
+    row = lax.broadcasted_iota(jnp.int32, (a.shape[0], 1), 0)
+    moved = pltpu.roll(a, by, 0)
+    rows = tail.shape[0]
+    for r in range(by):
+        edge = jnp.where(fresh, tail[rows - by + r : rows - by + r + 1, :], 0.0)
+        moved = jnp.where(row == r, edge, moved)
+    return moved
+
+
+def attn_forward_kernel(
+    reach, proj, col, row, coef, e, c, taps, gated, att, conv, sin, edge, acc, phi, s_acc, s_src,
+    s_all, s_sum, e_src, ss, sr, es, er,
+):
+    q = lax.axis_index("seq")
+    rows, wide = proj.shape[1], proj.shape[2] // 2
+    values = wide - HEADS * FK
+    lanes = Lanes(wide, values)
+    meet(1, reach)
+    states = Pass(1, reach, s_src, s_all, ss, sr)
+    edges = Pass(1, 1, e_src, edge, es, er)
+
+    def sides(m):
+        return proj[m, :, :wide].astype(jnp.bfloat16), proj[m, :, wide:].astype(jnp.bfloat16)
+
+    def phi_of(a, h):
+        return (mm(a, e[h, 0]) + c[0:1, :]) * (mm(a, e[h, 1]) + c[1:2, :]) * c[2:3, :]
+
+    def make_state(i, carry):
+        m, h = i // HEADS, i % HEADS
+        a, b = sides(m)
+        phi[m, h] = (phi_of(a, h) * col[m, :, 1:2]).astype(jnp.bfloat16)
+        keyed = (phi_of(b, h) * col[m, :, 2:3]).astype(jnp.bfloat16)
+        part = mm_tn(keyed, lanes.of(h, lanes.extended(a)))
+
+        @pl.when(h == 0)
+        def _():
+            s_acc[m] = part
+
+        @pl.when(h > 0)
+        def _():
+            s_acc[m] += part
+
+        return carry
+
+    lax.fori_loop(0, 2 * HEADS, make_state, 0)
+    for m in range(2):
+        s_src[m] = s_acc[m, :STATE, :].astype(jnp.bfloat16)
+    states.start()
+
+    def make_block(i, carry):
+        m, h = i // HEADS, i % HEADS
+        a, b = sides(m)
+        asked = lanes.key(h, a)
+        valued = lanes.of(h, lanes.extended(a))
+        for r in range(rows // BLOCK):
+            lo, hi = r * BLOCK, (r + 1) * BLOCK
+            x = mm_nt(asked[lo:hi], b[:hi]) * 0.25
+            seen = (col[m, lo:hi, 0:1] == row[m, 0:1, :hi]) & (
+                lax.broadcasted_iota(jnp.int32, (BLOCK, hi), 1)
+                <= lo + lax.broadcasted_iota(jnp.int32, (BLOCK, hi), 0)
+            )
+            w = jnp.where(seen, 1.0 + x + 0.5 * x * x, 0.0).astype(jnp.bfloat16)
+            part = mm(w, valued[:hi])
+
+            @pl.when(h == 0)
+            def _():
+                acc[m, lo:hi, :] = part
+
+            @pl.when(h > 0)
+            def _():
+                acc[m, lo:hi, :] += part
+
+        return carry
+
+    lax.fori_loop(0, 2 * HEADS, make_block, 0)
+    states.arrived()
+    sum_states(states, coef, s_sum)
+
+    def attend(m, lo):
+        s = s_sum[m].astype(jnp.bfloat16)
+        both = acc[m, lo:, :]
+        for h in range(HEADS):
+            both = both + mm(phi[m, h, lo:, :], lanes.of(h, s))
+        return jnp.where(lanes.is_value, both / lanes.denominator(both), both)
+
+    for m in range(2):
+        sin[m] = s_sum[m, :STATE, :].astype(jnp.bfloat16)
+        e_src[m] = attend(m, rows - 16)
+    edges.start()
+    for m in range(2):
+        att[m] = attend(m, 0)
+    edges.arrived()
+    for m in range(2):
+        a = att[m]
+        tail = edge[0, m]
+        out = taps[0:1, :] * a
+        for by in (1, 2):
+            out = out + taps[by : by + 1, :] * shifted(a, tail, q > 0, by) * col[m, :, 2 + by : 3 + by]
+        conv[m] = out
+        gated[m] = (out * proj[m, :, wide:]).astype(jnp.bfloat16)
+    states.sent()
+    edges.sent()
+
+
+def attn_backward_kernel(
+    reach, bg, proj, att, conv, sin, edge, col, row, coef, late, e, c, taps, out, grad_taps,
+    phi_q, phi_k, near, acc_a, acc_b, s_acc, s_src, s_all, s_sum, e_src, e_dst, ss, sr, es, er,
+):
+    q, n = lax.axis_index("seq"), lax.axis_size("seq")
+    rows, wide = proj.shape[1], proj.shape[2] // 2
+    values = wide - HEADS * FK
+    lanes = Lanes(wide, values)
+    meet(-1, reach)
+    states = Pass(-1, reach, s_src, s_all, ss, sr)
+    edges = Pass(-1, 1, e_src, e_dst, es, er)
+    for m in range(2):
+        e_src[m] = bg[m, :16, :] * proj[m, :16, wide:]
+    edges.start()
+
+    def sides(m):
+        return proj[m, :, :wide].astype(jnp.bfloat16), proj[m, :, wide:].astype(jnp.bfloat16)
+
+    def factors(a, h):
+        return mm(a, e[h, 0]) + c[0:1, :], mm(a, e[h, 1]) + c[1:2, :]
+
+    def make_phi(i, carry):
+        m, h = i // HEADS, i % HEADS
+        a, b = sides(m)
+        u, w = factors(a, h)
+        phi_q[m, h] = (u * w * c[2:3, :] * col[m, :, 1:2]).astype(jnp.bfloat16)
+        u, w = factors(b, h)
+        phi_k[m, h] = (u * w * c[2:3, :] * col[m, :, 2:3]).astype(jnp.bfloat16)
+        return carry
+
+    lax.fori_loop(0, 2 * HEADS, make_phi, 0)
+    edges.arrived()
+    sums = [jnp.zeros((1, wide), jnp.float32)] * KW
+    place = lax.broadcasted_iota(jnp.int32, (rows, 1), 0)
+    for m in range(2):
+        back = bg[m]
+        back_conv = back * proj[m, :, wide:]
+        a = jnp.where(lanes.is_value, att[m], 0.0)
+        tail = edge[0, m]
+        nxt = e_dst[0, m]
+        total = taps[0:1, :] * back_conv
+        sums[0] = sums[0] + jnp.sum(back_conv * a, axis=0, keepdims=True)
+        for by in (1, 2):
+            kept = back_conv * col[m, :, 2 + by : 3 + by]
+            sums[by] = sums[by] + jnp.sum(
+                kept * shifted(a, tail, q > 0, by), axis=0, keepdims=True
+            )
+            moved = pltpu.roll(kept, rows - by, 0)
+            for r in range(by):
+                fresh = jnp.where(q < n - 1, nxt[r : r + 1, :] * late[by - 1 + r, m], 0.0)
+                moved = jnp.where(place == rows - by + r, fresh, moved)
+            total = total + taps[by : by + 1, :] * moved
+        out[m, :, wide:] = jnp.where(lanes.is_value, back * conv[m], 0.0).astype(jnp.bfloat16)
+        back_numer = total / lanes.denominator(att[m])
+        spent = back_numer * a
+        found = jnp.where(lanes.is_value, back_numer, 0.0)
+        for h in range(HEADS):
+            denom = -jnp.sum(lanes.of(h, spent), axis=1, keepdims=True)
+            high = denom.astype(jnp.bfloat16).astype(jnp.float32)
+            found = jnp.where(lanes.lane == values + h, high, found)
+            found = jnp.where(lanes.lane == values + 2 + h, denom - high, found)
+        near[m] = found.astype(jnp.bfloat16)
+        part = jnp.zeros((wide, wide), jnp.float32)
+        for h in range(HEADS):
+            part = part + mm_tn(phi_q[m, h], lanes.of(h, near[m]))
+        s_src[m] = part[:STATE].astype(jnp.bfloat16)
+    states.start()
+    grad_taps[...] = jnp.zeros(grad_taps.shape, jnp.float32)
+    for by in range(KW):
+        grad_taps[by : by + 1, :] = sums[by]
+    acc_a[...] = jnp.zeros(acc_a.shape, jnp.float32)
+    acc_b[...] = jnp.zeros(acc_b.shape, jnp.float32)
+    for m in range(2):
+        s_sum[m] = jnp.zeros(s_sum.shape[1:], jnp.float32)
+        s_sum[m, :STATE, :] = sin[m].astype(jnp.float32)
+
+    def through_phi(scaled, factors_of, h):
+        u, w = factors_of
+        return mm_nt((scaled * w).astype(jnp.bfloat16), e[h, 0]) + mm_nt(
+            (scaled * u).astype(jnp.bfloat16), e[h, 1]
+        )
+
+    def make_block(i, carry):
+        m, h = i // HEADS, i % HEADS
+        a, b = sides(m)
+        asked, keyed = lanes.key(h, a), lanes.key(h, b)
+        valued = lanes.extended(a)
+        given = lanes.of(h, near[m])
+        given_v = jnp.where(lanes.is_value, given, jnp.zeros_like(given))
+        for r in range(rows // BLOCK):
+            lo, hi = r * BLOCK, (r + 1) * BLOCK
+            x = mm_nt(asked[lo:hi], b[:hi]) * 0.25
+            seen = (col[m, lo:hi, 0:1] == row[m, 0:1, :hi]) & (
+                lax.broadcasted_iota(jnp.int32, (BLOCK, hi), 1)
+                <= lo + lax.broadcasted_iota(jnp.int32, (BLOCK, hi), 0)
+            )
+            w = jnp.where(seen, 1.0 + x + 0.5 * x * x, 0.0).astype(jnp.bfloat16)
+            back_w = mm_nt(given[lo:hi], valued[:hi])
+            back_s = jnp.where(seen, back_w * (1.0 + x), 0.0).astype(jnp.bfloat16)
+            acc_a[m, lo:hi, :] += 0.25 * mm(back_s, keyed[:hi])
+            acc_b[m, :hi, :] += 0.25 * mm_tn(back_s, asked[lo:hi])
+            acc_a[m, :hi, :] += mm_tn(w, given_v[lo:hi])
+        s = s_sum[m].astype(jnp.bfloat16)
+        scaled = mm_nt(given, s) * col[m, :, 1:2] * c[2:3, :]
+        acc_a[m] += through_phi(scaled, factors(a, h), h)
+        return carry
+
+    lax.fori_loop(0, 2 * HEADS, make_block, 0)
+    states.arrived()
+    sum_states(states, coef, s_sum)
+
+    def make_late(i, carry):
+        m, h = i // HEADS, i % HEADS
+        a, b = sides(m)
+        s = s_sum[m].astype(jnp.bfloat16)
+        scaled = mm_nt(lanes.of(h, lanes.extended(a)), s) * col[m, :, 2:3] * c[2:3, :]
+        acc_b[m] += through_phi(scaled, factors(b, h), h)
+        s_v = lanes.of(h, jnp.where(lanes.is_value, s, jnp.zeros_like(s)))
+        acc_a[m] += mm(phi_k[m, h], s_v)
+        return carry
+
+    lax.fori_loop(0, 2 * HEADS, make_late, 0)
+    for m in range(2):
+        out[m, :, :wide] = acc_a[m].astype(jnp.bfloat16)
+        out[m, :, wide:] = jnp.where(
+            lanes.is_value, out[m, :, wide:].astype(jnp.float32), acc_b[m]
+        ).astype(jnp.bfloat16)
+    states.sent()
+    edges.sent()
+
+
+def seq_reach():
+    n = lax.axis_size("seq")
+    return n // 2 if n % 2 == 0 else n - 1
+
+
+def attention_call(kernel, cid, inputs, scalars, shapes, scratch):
+    vmem, smem = pl.BlockSpec(memory_space=pltpu.VMEM), pl.BlockSpec(memory_space=pltpu.SMEM)
+    return pl.pallas_call(
+        functools.partial(kernel, seq_reach()),
+        out_shape=shapes,
+        in_specs=[smem if i in scalars else vmem for i in range(len(inputs))],
+        out_specs=[vmem] * len(shapes),
+        scratch_shapes=scratch,
+        name=f"attention{cid}",
+        compiler_params=pltpu.CompilerParams(
+            collective_id=cid, has_side_effects=True, vmem_limit_bytes=48 << 20
+        ),
+    )(*inputs)
+
+
+def passing(reach, wide):
+    dma = pltpu.SemaphoreType.DMA
+    return (
+        [
+            pltpu.VMEM((2, STATE, wide), jnp.bfloat16),
+            pltpu.VMEM((reach, 2, STATE, wide), jnp.bfloat16),
+            pltpu.VMEM((2, wide, wide), jnp.float32),
+        ],
+        [dma((reach,)), dma((reach,)), dma((1,)), dma((1,))],
     )
-    places = jnp.arange(row_count, dtype=jnp.int32)
-    visible = (starts_at[:, None] == starts_at[None, :]) & (places[None, :] <= places[:, None])
-    return (scores, visible)
-
-
-def split_heads(proj, rows):
-    query = proj[:, :32].astype(jnp.bfloat16).reshape(2, rows, 2, FK)
-    key = proj[:, 32:64].astype(jnp.bfloat16).reshape(2, rows, 2, FK)
-    value = proj[:, 64:288].astype(jnp.bfloat16).reshape(2, rows, 2, -1)
-    return query, key, value
-
-
-def mb_state(key, value, last_rows):
-    phi_last = features(key.astype(jnp.float32)) * last_rows[:, None, None]
-    wide = jnp.concatenate(
-        [value.astype(jnp.float32), jnp.ones(value.shape[:2] + (1,), jnp.float32)], axis=-1
+
+
+def attention_forward(proj, taps, marks, tables):
+    m, rows, double = proj.shape
+    wide = double // 2
+    f32, bf16 = jnp.float32, jnp.bfloat16
+    buffers, sems = passing(seq_reach(), wide)
+    shape = jax.ShapeDtypeStruct
+    return attention_call(
+        attn_forward_kernel,
+        10,
+        [proj, marks["col"], marks["row"], marks["before"], *tables, taps],
+        (3,),
+        [
+            shape((m, rows, wide), bf16),
+            shape((m, rows, wide), f32),
+            shape((m, rows, wide), f32),
+            shape((m, STATE, wide), bf16),
+            shape((1, m, 16, wide), f32),
+        ],
+        [
+            pltpu.VMEM((m, rows, wide), f32),
+            pltpu.VMEM((m, HEADS, rows, wide), bf16),
+            pltpu.VMEM((m, wide, wide), f32),
+            *buffers,
+            pltpu.VMEM((m, 16, wide), f32),
+            *sems,
+        ],
     )
-    return jnp.einsum("shp,she->hpe", phi_last, wide)
-
-
-def mb_attend(query, key, value, state_in, starts_at, carried_in):
-    scores, visible = own_scores(query, key, starts_at)
-    weights = jnp.where(visible[None], 1.0 + scores + 0.5 * scores * scores, 0.0).astype(
-        jnp.bfloat16
+
+
+def attention_backward(back_gated, proj, kept, taps, marks, tables):
+    att, conv, sin, edge = kept
+    m, rows, double = proj.shape
+    wide = double // 2
+    f32, bf16 = jnp.float32, jnp.bfloat16
+    buffers, sems = passing(seq_reach(), wide)
+    shape = jax.ShapeDtypeStruct
+    return attention_call(
+        attn_backward_kernel,
+        11,
+        [
+            back_gated, proj, att, conv, sin, edge, marks["col"], marks["row"], marks["after"],
+            marks["late"], *tables, taps,
+        ],
+        (8, 9),
+        [shape((m, rows, double), bf16), shape((8, wide), f32)],
+        [
+            pltpu.VMEM((m, HEADS, rows, wide), bf16),
+            pltpu.VMEM((m, HEADS, rows, wide), bf16),
+            pltpu.VMEM((m, rows, wide), bf16),
+            pltpu.VMEM((m, rows, wide), f32),
+            pltpu.VMEM((m, rows, wide), f32),
+            pltpu.VMEM((m, wide, wide), f32),
+            *buffers,
+            pltpu.VMEM((m, 16, wide), f32),
+            pltpu.VMEM((1, m, 16, wide), f32),
+            *sems,
+        ],
     )
-    wide = jnp.concatenate([value, jnp.ones(value.shape[:2] + (1,), jnp.bfloat16)], axis=-1)
-    both = jnp.einsum("hts,she->the", weights, wide, preferred_element_type=jnp.float32)
-    both = both + carried_in[:, None, None] * jnp.einsum(
-        "thp,hpe->the", features(query.astype(jnp.float32)), state_in
-    )
-    return both[..., :-1], both[..., -1]
-
-
-def mb_back_before(back_attended, numerator, denominator, query, carried_in):
-    back_out = back_attended.reshape(numerator.shape)
-    back_numer = (back_out / denominator[:, :, None]).astype(jnp.bfloat16)
-    back_denom = -jnp.sum(back_out * numerator, axis=2) / (denominator * denominator)
-    wide = jnp.concatenate([back_numer.astype(jnp.float32), back_denom[:, :, None]], axis=-1)
-    phi_used = features(query.astype(jnp.float32)) * carried_in[:, None, None]
-    return wide, jnp.einsum("thp,the->hpe", phi_used, wide)
-
-
-def mb_back_after(wide, query, key, value, state_in, state_out, starts_at, carried_in, last_rows):
-    back_numer = wide[..., :-1].astype(jnp.bfloat16)
-    back_denom = wide[..., -1]
-    scores, visible = own_scores(query, key, starts_at)
-    weights = jnp.where(visible[None], 1.0 + scores + 0.5 * scores * scores, 0.0).astype(
-        jnp.bfloat16
-    )
-    back_weights = (
-        jnp.einsum("the,she->hts", back_numer, value, preferred_element_type=jnp.float32)
-        + jnp.transpose(back_denom)[:, :, None]
-    )
-    back_scores = jnp.where(visible[None], back_weights * (1.0 + scores), 0.0).astype(jnp.bfloat16)
-    back_query = 0.25 * jnp.einsum(
-        "hts,shf->thf", back_scores, key, preferred_element_type=jnp.float32
-    )
-    back_key = 0.25 * jnp.einsum(
-        "hts,thf->shf", back_scores, query, preferred_element_type=jnp.float32
-    )
-    back_value = jnp.einsum("hts,the->she", weights, back_numer, preferred_element_type=jnp.float32)
-    phi_query, phi_back_query = jax.vjp(features, query.astype(jnp.float32))
-    phi_key, phi_back_key = jax.vjp(features, key.astype(jnp.float32))
-    back_phi_query = carried_in[:, None, None] * jnp.einsum("the,hpe->thp", wide, state_in)
-    value_wide = jnp.concatenate(
-        [value.astype(jnp.float32), jnp.ones(value.shape[:2] + (1,), jnp.float32)], axis=-1
-    )
-    back_phi_key = last_rows[:, None, None] * jnp.einsum("she,hpe->shp", value_wide, state_out)
-    back_value = back_value + last_rows[:, None, None] * jnp.einsum(
-        "shp,hpe->she", phi_key, state_out[..., :-1]
-    )
-    return (
-        back_query + phi_back_query(back_phi_query)[0],
-        back_key + phi_back_key(back_phi_key)[0],
-        back_value,
-    )
-
-
-def attention_forward(proj, taps, marks, cids):
-    rows = proj.shape[0] // 2
-    mine = lax.axis_index("seq")
-    query, key, value = split_heads(proj, rows)
-    gate_conv = proj[:, 288:].reshape(2, rows, -1)
-    state = jax.vmap(mb_state)(key, value, marks["last"])
-    states = exchange(state.reshape(2, -1, state.shape[-1]).astype(jnp.bfloat16), cids[0])
-    state_in = jnp.einsum("nm,nmpe->mpe", marks["before"], states.astype(jnp.float32)).reshape(
-        state.shape
-    )
-    numerator, denominator = jax.vmap(mb_attend)(
-        query, key, value, state_in, marks["begin"], marks["carried"]
-    )
-    attended = (numerator / denominator[..., None]).reshape(2, rows, -1)
-    edges = exchange(attended[:, rows - 2 :], cids[1])
-    edge = lax.dynamic_index_in_dim(edges, jnp.maximum(mine - 1, 0), 0, False)
-    edge = jnp.where(mine > 0, edge, 0.0)
-    extended = jnp.concatenate([edge, attended], axis=1)
-    conv_out = taps[0] * attended
-    for offset in range(1, KW):
-        conv_out = (
-            conv_out
-            + taps[offset]
-            * extended[:, 2 - offset : 2 - offset + rows]
-            * marks["allowed"][offset][:, :rows, None]
-        )
-    gated = (conv_out * gate_conv).astype(jnp.bfloat16)
-    return gated.reshape(2 * rows, -1), (state_in, numerator, denominator, extended, conv_out)
-
-
-def attention_backward(back_gated, proj, kept, taps, marks, cids):
-    state_in, numerator, denominator, extended, conv_out = kept
-    rows = proj.shape[0] // 2
-    count, mine = lax.axis_size("seq"), lax.axis_index("seq")
-    query, key, value = split_heads(proj, rows)
-    gate_conv = proj[:, 288:].reshape(2, rows, -1)
-    back_gated = back_gated.reshape(2, rows, -1)
-    back_conv = back_gated * gate_conv
-    back_gconv = (back_gated * conv_out).astype(jnp.bfloat16)
-    edges = exchange(back_conv[:, :2], cids[0])
-    edge = lax.dynamic_index_in_dim(edges, jnp.minimum(mine + 1, count - 1), 0, False)
-    edge = jnp.where(mine < count - 1, edge, 0.0)
-    conv_ext = jnp.concatenate([back_conv, edge], axis=1)
-    back_attended = taps[0] * back_conv
-    taps_rows = [jnp.sum(back_conv * extended[:, 2:], axis=(0, 1))]
-    for offset in range(1, KW):
-        allowed = marks["allowed"][offset]
-        back_attended = (
-            back_attended
-            + taps[offset]
-            * conv_ext[:, offset : offset + rows]
-            * allowed[:, offset : offset + rows, None]
-        )
-        taps_rows.append(
-            jnp.sum(
-                back_conv
-                * extended[:, 2 - offset : 2 - offset + rows]
-                * allowed[:, :rows, None],
-                axis=(0, 1),
-            )
-        )
-    wide, state_grad = jax.vmap(mb_back_before)(
-        back_attended, numerator, denominator, query, marks["carried"]
-    )
-    states = exchange(
-        state_grad.reshape(2, -1, state_grad.shape[-1]).astype(jnp.bfloat16), cids[1]
-    )
-    state_out = jnp.einsum("nm,nmpe->mpe", marks["after"], states.astype(jnp.float32)).reshape(
-        state_grad.shape
-    )
-    back_query, back_key, back_value = jax.vmap(mb_back_after)(
-        wide, query, key, value, state_in, state_out, marks["begin"], marks["carried"],
-        marks["last"],
-    )
-    flat = [a.astype(jnp.bfloat16).reshape(2 * rows, -1) for a in (back_query, back_key, back_value)]
-    back_proj = jnp.concatenate(flat + [back_gconv.reshape(2 * rows, -1)], axis=1)
-    return back_proj, jnp.stack(taps_rows)
 
 
 def sequence_marks(lengths, rows):
@@ -656,24 +925,30 @@
     ends = (jnp.arange(count, dtype=jnp.int32) + 1) * rows - 1
     stays = jax.vmap(lambda row: seq_begin(row, ends))(lengths) < (ends - rows + 1)[None, :]
     stays = stays.astype(jnp.float32)
-    before = []
-    after = []
-    for b in range(count):
-        through = jnp.where(mine > b, 1.0, 0.0) * jnp.ones_like(stays[:, 0])
-        for j in range(b + 1, count):
-            through = through * jnp.where(j < mine, stays[:, j], 1.0)
-        before.append(through)
-        through = jnp.where(mine < b, 1.0, 0.0) * jnp.ones_like(stays[:, 0])
-        for j in range(b):
-            through = through * jnp.where(j > mine, stays[:, j], 1.0)
-        after.append(through)
+    blocks = jnp.arange(count, dtype=jnp.int32)
+
+    def through(first, last):
+        inside = (blocks >= first) & (blocks <= last)
+        return jnp.min(jnp.where(inside[None, :], stays, 1.0), axis=1)
+
+    reach = seq_reach()
+    before = [through(mine - d + 1, mine - 1) for d in range(1, reach + 1)]
+    after = [through(mine + 1, mine + d - 1) for d in range(1, reach + 1)]
+    allowed = [(positions - j >= begin_ext).astype(jnp.float32) for j in range(KW)]
+    columns = [
+        begin.astype(jnp.float32),
+        (begin < start).astype(jnp.float32),
+        (begin == begin[:, rows - 1 :]).astype(jnp.float32),
+        allowed[1][:, :rows],
+        allowed[2][:, :rows],
+    ]
+    col = jnp.stack(columns + [jnp.zeros_like(columns[0])] * 3, axis=2)
     return {
-        "begin": begin,
-        "carried": (begin < start).astype(jnp.float32),
-        "last": (begin == begin[:, rows - 1 :]).astype(jnp.float32),
+        "col": col,
+        "row": jnp.broadcast_to(columns[0][:, None, :], (2, 8, rows)),
         "before": jnp.stack(before),
         "after": jnp.stack(after),
-        "allowed": [(positions - j >= begin_ext).astype(jnp.float32) for j in range(KW)],
+        "late": jnp.stack([allowed[1][:, rows], allowed[2][:, rows], allowed[2][:, rows + 1]]),
     }
 
 
@@ -720,25 +995,28 @@
         return jnp.stack([weight[:, :cols], weight[:, cols:]])
 
     own_mix = jnp.concatenate(
-        [halves(w[0]) for w in (w_query, w_key, w_value, w_gate_conv)], axis=2
+        [halves(w[0]) for w in (w_value, w_query, w_gate_conv, w_key)], axis=2
     )
-    own_out = halves(w_out[0].T)
+    values = w_value.shape[2] // 2
+    keys = w_query.shape[2] // 2
+    wide = values + keys
+    own_out = jnp.pad(halves(w_out[0].T), ((0, 0), (0, 0), (0, keys)))
     own_ffn = jnp.concatenate([halves(w_gate[0]), halves(w_up[0])], axis=2)
     own_down = halves(w_down[0].T)
     gains_one = lax.all_gather(gain_attn[0], "section").astype(jnp.float32)
     gains_two = lax.all_gather(gain_ffn[0], "section").astype(jnp.float32)
     taps_all = lax.all_gather(conv_taps[0], "section").astype(jnp.float32)
-    channels = own_out.shape[2]
-    taps_both = lax.dynamic_slice_in_dim(
-        taps_all, (head_index * 2 + core) * channels, channels, 2
-    )
+    taps_both = lax.dynamic_slice_in_dim(taps_all, (head_index * 2 + core) * values, values, 2)
+    taps_both = jnp.pad(taps_both, ((0, 0), (0, 8 - KW), (0, keys)))
+    first, rest = feature_tables(values)
+    tables = (jnp.asarray(first, jnp.bfloat16), jnp.asarray(rest))
     marks = sequence_marks(lengths, rows)
     hidden_cols = own_down.shape[2]
 
     def as_parts(flat):
         return flat.astype(jnp.bfloat16).reshape(micro_count, rows, width)
 
-    def wide(summed):
+    def spread(summed):
         return summed.astype(jnp.float32).reshape(total, width)
 
     mix = [None, None]
@@ -750,13 +1028,14 @@
     for layer in range(2):
         w_mix, w_o = mix[layer]
         normed = rms_norm(x, gains_one[layer]).astype(jnp.bfloat16)
-        proj = dot_n(normed, w_mix)
-        gated, attn = attention_forward(proj, taps_both[layer], marks, (10, 11))
+        proj = dot_n(normed, w_mix).reshape(micro_count, rows, 2 * wide)
+        gated, *attn = attention_forward(proj, taps_both[layer], marks, tables)
+        gated = gated.reshape(total, wide)
         summed, ffn[layer], _ = communicate(
             2 + layer, partial=as_parts(dot_t(gated, w_o)), gather=(layer, [own_ffn, own_down])
         )
         w_gu, w_d = ffn[layer]
-        middle = x + wide(summed)
+        middle = x + spread(summed)
         normed_two = rms_norm(middle, gains_two[layer]).astype(jnp.bfloat16)
         both = dot_n(normed_two, w_gu)
         hidden = (jax.nn.silu(both[:, :hidden_cols]) * both[:, hidden_cols:]).astype(jnp.bfloat16)
@@ -765,7 +1044,7 @@
             summed, mix[1], _ = communicate(4, partial=partial, gather=(1, [own_mix, own_out]))
         else:
             summed, _, _ = communicate(5, partial=partial)
-        out = (middle + wide(summed)).astype(jnp.bfloat16)
+        out = (middle + spread(summed)).astype(jnp.bfloat16)
         outputs.append(out)
         kept[layer] = (x, normed, proj, gated, attn, middle, normed_two, both, hidden)
         x = out.astype(jnp.float32)
@@ -798,14 +1077,15 @@
         grad_gu = outer(normed_two, back_both)
         grad_d = outer(grad, hidden)
         _, norm_back_two = jax.vjp(rms_norm, middle, gains_two[layer])
-        back_middle, gain_two = norm_back_two(wide(summed))
+        back_middle, gain_two = norm_back_two(spread(summed))
         back_middle = grad_wide + back_middle
         back_branch = back_middle.astype(jnp.bfloat16)
         grad_o = outer(back_branch, gated)
         back_gated = dot_n(back_branch, w_o)
         back_proj, taps_grad = attention_backward(
-            back_gated, proj, attn, taps_both[layer], marks, (12, 13)
-        )
+            back_gated.reshape(micro_count, rows, wide), proj, attn, taps_both[layer], marks, tables
+        )
+        back_proj = back_proj.reshape(total, 2 * wide)
         grad_mix = outer(normed, back_proj)
         partial = as_parts(dot_t(back_proj, w_mix))
         summed, _, received[layer][2:] = communicate(
@@ -813,7 +1093,7 @@
         )
         late = [by_seq(grad_mix), by_seq(grad_o)]
         _, norm_back_one = jax.vjp(rms_norm, x, gains_one[layer])
-        back_x, gain_one = norm_back_one(wide(summed))
+        back_x, gain_one = norm_back_one(spread(summed))
         grad = (back_middle + back_x).astype(jnp.bfloat16)
         back[layer] = grad
         smalls[layer] = (gain_one, gain_two, taps_grad)
@@ -828,13 +1108,11 @@
     def joined(pair):
         return jnp.concatenate([pair[0], pair[1]], axis=1)
 
-    qk = w_query.shape[2] // 2
-    vg = w_value.shape[2] // 2
-    grad_query = joined(grad_mix[:, :, :qk])
-    grad_key = joined(grad_mix[:, :, qk : 2 * qk])
-    grad_value = joined(grad_mix[:, :, 2 * qk : 2 * qk + vg])
-    grad_gconv = joined(grad_mix[:, :, 2 * qk + vg :])
-    grad_out = joined(grad_o).T
+    grad_value = joined(grad_mix[:, :, :values])
+    grad_query = joined(grad_mix[:, :, values:wide])
+    grad_gconv = joined(grad_mix[:, :, wide : wide + values])
+    grad_key = joined(grad_mix[:, :, wide + values :])
+    grad_out = joined(grad_o[:, :, :values]).T
     grad_gate = joined(grad_gu[:, :, :hidden_cols])
     grad_up = joined(grad_gu[:, :, hidden_cols:])
     grad_down = joined(grad_d).T
@@ -846,7 +1124,10 @@
     packed = []
     for gain_one, gain_two, taps_grad in smalls:
         taps_full = lax.dynamic_update_slice_in_dim(
-            jnp.zeros((KW, width), jnp.float32), taps_grad, (head_index * 2 + core) * channels, 1
+            jnp.zeros((KW, width), jnp.float32),
+            taps_grad[:KW, :values],
+            (head_index * 2 + core) * values,
+            1,
         )
         packed.append(
             jnp.concatenate(

time: 1200 us -> 1050 us (0.88)
  matrix products: 168 us -> 109 us
  local copies, waits for them, and re-layouts: 102 us -> 63.1 us
  other arithmetic: 143 us -> 112 us
  Pallas kernels: 755 us -> 734 us
    dot_general x28 -> x0, matrix products: 52.1 us -> none  [the longest x2 9.4 us: mb_back_after(): jnp.einsum('hts,the->she', weights, back_numer, preferred_element_type=jn...]
    pallas_call x8 -> x4, Pallas kernels: 92.3 us -> 62 us  [attention_call(): pl.pallas_call(functools.partial(kernel, seq_reach()), out_shape=shapes,...]
    reshape x16 -> x0, local copies, waits for them, and re-layouts: 16.7 us -> none  [the longest x4 3.6 us: split_heads(): value = proj[:, 64:288].astype(jnp.bfloat16).reshape(2, rows, 2, -1)]
  transfers between devices with their start and end apart: 1 -> 1, of which waited for: 0 -> 0; matrix products, arithmetic and copies ran while one was open for 4% -> 5% of each run, Pallas kernels for 8% -> 9%
where the time goes in v3:
time: 1050 us; the launch traced here: 1040 us
  Pallas kernels  734 us (70%)
  other arithmetic  112 us (11%)
  matrix products  109 us (10%)
  local copies, waits for them, and re-layouts  63.1 us (6%)
  between operations  16.6 us (2%)
    pallas_call x10, Pallas kernels, communicate(): pl.pallas_call(functools.partial(comm_kernel, plan), out_shape=shapes, in...  672 us
    pallas_call x4, Pallas kernels, attention_call(): pl.pallas_call(functools.partial(kernel, seq_reach()), out_shape=shapes,...  62 us
    dot_general x8, matrix products, dot_t(): return jnp.einsum('tc,dc->td', a, b, preferred_element_type=jnp.float32)  43.2 us
    dot_general x8, matrix products, outer(): jnp.einsum('tc,tf->cf', a, b, preferred_element_type=jnp.float32)  33.6 us
    dot_general x8, matrix products, dot_n(): return jnp.dot(a, b, preferred_element_type=jnp.float32)  31.9 us
    convert_element_type x4, local copies, waits for them, and re-layouts, outer(): jnp.einsum('tc,tf->cf', a, b, preferred_element_type=jnp.float32)  21.3 us
  transfers between devices with their start and end apart: 1, of which 0 were waited for; matrix products, arithmetic and copies ran while one was open for 5% of the time, Pallas kernels for 9%

profile of v3, /device:TPU:0, one launch (start us, length us, event | category | flops | bytes accessed | tf_op | source)
XLA Modules:
  0.0 1040.4 jit_solution(7420927073972062688)
XLA Ops:
  10.7 2.8 fusion.21
  14.2 2.0 all-gather
  16.2 1.8 all-gather.1
  18.1 1.8 all_gather.10
  28.9 1.9 slice_bitcast_fusion.9
  31.2 34.7 %comm1.1 = (bf16[4,448,512]{2,1,0:T(8,128)(2,1)S(1)}, bf16[4,448,256]{2,1,0:T(8,128)(2,1)S(1)}) custom-call(bf16[2,448,512]{2,1,0:T(8,128)(2,1)S(1)} %pad_maximum_fusion.7.refs_0_.refs_1_, bf16[2,448,256]{2,1,0:T(8,128)(2,1)S(1)} %fusion.56.refs_1_.refs_2_), custom_call_target="tpu_custom_call" | custom-call | tf_op jit(solution)/shard_map/comm1/pallas_call | solution.py:414
  65.9 3.5 fusion.37.proj
  71.1 2.5 stack.152.col
  75.2 12.4 %attention10.2 = (bf16[2,512,256]{2,1,0:T(8,128)(2,1)S(1)}, f32[2,512,256]{2,1,0:T(8,128)S(1)}, f32[2,512,256]{2,1,0:T(8,128)S(1)}, bf16[2,160,256]{2,1,0:T(8,128)(2,1)S(1)}, f32[1,2,16,256]{3,2,1,0:T(8,128)S(1)}) custom-call(f32[2,512,512]{2,1,0:T(8,128)S(1)} %copy-done.7, f32[2,512,8]{2,1,0:T(8,128)S(1)} %stack.152.col, ...), custom_call_target="tpu_custom_call" | custom-call | tf_op jit(solution)/shard_map/attention10/pallas_call | solution.py:834
  87.7 3.0 convolution_convert_fusion.9
  91.8 88.6 %comm2.1 = (bf16[2,512,1792]{2,1,0:T(8,128)(2,1)}, bf16[4,448,1216]{2,1,0:T(8,128)(2,1)}, bf16[4,448,608]{2,1,0:T(8,128)(2,1)S(1)}) custom-call(bf16[2,512,1792]{2,1,0:T(8,128)(2,1)} %bitcast.306, bf16[2,448,1216]{2,1,0:T(8,128)(2,1)S(1)} %maximum_maximum_fusion.refs_1_, bf16[2,448,608]{2,1,0:T(8,128)(2,1)S(1)} %pad_maximum_fusion.6.refs_2_), custom_call_target="tpu_custom_call" | custom-call | tf_op jit(solution)/shard_map/comm2/pallas_call | solution.py:414
  180.4 4.2 multiply_reduce_fusion.3
  186.0 7.0 fusion.79
  193.8 4.6 convolution_convert_fusion.7
  198.4 67.1 %comm4.1 = (bf16[2,512,1792]{2,1,0:T(8,128)(2,1)}, bf16[4,448,512]{2,1,0:T(8,128)(2,1)S(1)}, bf16[4,448,256]{2,1,0:T(8,128)(2,1)S(1)}) custom-call(bf16[2,512,1792]{2,1,0:T(8,128)(2,1)} %bitcast.316, bf16[2,448,512]{2,1,0:T(8,128)(2,1)S(1)} %pad_maximum_fusion.7.refs_0_.refs_1_, bf16[2,448,256]{2,1,0:T(8,128)(2,1)S(1)} %copy-done.11), custom_call_target="tpu_custom_call" | custom-call | tf_op jit(solution)/shard_map/comm4/pallas_call | solution.py:414
  265.6 7.3 fusion.23
  272.9 2.1 fusion.40.proj
  275.1 12.4 %attention10.3 = (bf16[2,512,256]{2,1,0:T(8,128)(2,1)S(1)}, f32[2,512,256]{2,1,0:T(8,128)S(1)}, f32[2,512,256]{2,1,0:T(8,128)S(1)}, bf16[2,160,256]{2,1,0:T(8,128)(2,1)S(1)}, f32[1,2,16,256]{3,2,1,0:T(8,128)S(1)}) custom-call(f32[2,512,512]{2,1,0:T(8,128)S(1)} %fusion.40.proj, f32[2,512,8]{2,1,0:T(8,128)S(1)} %stack.152.col, ...), custom_call_target="tpu_custom_call" | custom-call | tf_op jit(solution)/shard_map/attention10/pallas_call | solution.py:834
  287.6 3.0 convolution_convert_fusion.8
  290.6 82.8 %comm3.1 = (bf16[2,512,1792]{2,1,0:T(8,128)(2,1)}, bf16[4,448,1216]{2,1,0:T(8,128)(2,1)}, bf16[4,448,608]{2,1,0:T(8,128)(2,1)S(1)}) custom-call(bf16[2,512,1792]{2,1,0:T(8,128)(2,1)} %bitcast.307, bf16[2,448,1216]{2,1,0:T(8,128)(2,1)S(1)} %maximum_maximum_fusion.refs_1_, bf16[2,448,608]{2,1,0:T(8,128)(2,1)S(1)} %pad_maximum_fusion.6.refs_2_), custom_call_target="tpu_custom_call" | custom-call | tf_op jit(solution)/shard_map/comm3/pallas_call | solution.py:414
  373.5 4.2 multiply_reduce_fusion.2
  379.1 6.5 fusion.80
  385.5 6.0 fusion.46
  391.6 6.7 convolution_convert_fusion.5
  398.3 68.3 %comm5.3 = bf16[2,512,1792]{2,1,0:T(8,128)(2,1)S(1)} custom-call(bf16[2,512,1792]{2,1,0:T(8,128)(2,1)} %bitcast.317), custom_call_target="tpu_custom_call" | custom-call | tf_op jit(solution)/shard_map/comm5/pallas_call | solution.py:414
  466.6 3.2 multiply_reduce_fusion
  472.2 3.8 fusion.35
  476.0 3.3 copy.181
  479.3 6.8 fusion.53
  486.1 2.1 fusion.42
  489.8 18.7 %attention11.2 = (bf16[2,512,512]{2,1,0:T(8,128)(2,1)S(1)}, f32[8,256]{1,0:T(8,128)S(1)}) custom-call(f32[2,512,256]{2,1,0:T(8,128)S(1)} %fusion.81.bg, f32[2,512,512]{2,1,0:T(8,128)} %copy-done.8, f32[2,512,256]{2,1,0:T(8,128)S(1)} %copy-done.24, f32[2,512,256]{2,1,0:T(8,128)S(1)} %copy-done.26, bf16[2,160,256]{2,1,0:T(8,128)(2,1)S(1)} %copy-done.34, ...), custom_call_target="tpu_custom_call" | custom-call | tf_op jit(solution)/shard_map/attention11/pallas_call | solution.py:834
  509.2 3.5 bitcast_convert_fusion.1
  515.1 3.1 multiply_convert_fusion
  518.2 7.3 convolution_convert_fusion.1
  525.5 7.2 copy.180
  532.7 5.8 convolution_convert_fusion.4
  538.6 82.2 %comm8.1 = (bf16[2,512,1792]{2,1,0:T(8,128)(2,1)S(1)}, bf16[2,4,448,1216]{3,2,1,0:T(8,128)(2,1)}, bf16[2,4,448,608]{3,2,1,0:T(8,128)(2,1)}) custom-call(bf16[2,512,1792]{2,1,0:T(8,128)(2,1)} %bitcast.312, bf16[4,448,1216]{2,1,0:T(8,128)(2,1)} %bitcast.309, bf16[4,448,608]{2,1,0:T(8,128)(2,1)S(1)} %bitcast.279), custom_call_target="tpu_custom_call" | custom-call | tf_op jit(solution)/shard_map/comm8/pallas_call | solution.py:414
  620.9 2.8 fusion.7
  625.3 7.6 fusion.14
  633.0 4.6 fusion.49
  638.6 9.9 convolution_convert_fusion.3
  648.5 67.4 %comm6.1 = (bf16[2,512,1792]{2,1,0:T(8,128)(2,1)}, bf16[2,4,448,512]{3,2,1,0:T(8,128)(2,1)}, bf16[2,4,448,256]{3,2,1,0:T(8,128)(2,1)S(1)}) custom-call(bf16[2,512,1792]{2,1,0:T(8,128)(2,1)} %bitcast.315, bf16[4,448,512]{2,1,0:T(8,128)(2,1)S(1)} %bitcast.281, bf16[4,448,256]{2,1,0:T(8,128)(2,1)S(1)} %bitcast.285), custom_call_target="tpu_custom_call" | custom-call | tf_op jit(solution)/shard_map/comm6/pallas_call | solution.py:414
  717.3 5.4 fusion.10
  724.0 10.9 %fusion.18 = (bf16[1024,1792]{1,0:T(8,128)(2,1)S(1)}, bf16[1024,1792]{1,0:T(8,128)(2,1)}) fusion(bf16[2,512,1792]{2,1,0:T(8,128)(2,1)S(1)} %copy-done.4, bf16[2,512,1792]{2,1,0:T(8,128)(2,1)S(1)} %copy-done.2, bf16[2,512,1792]{2,1,0:T(8,128)(2,1)} %get-tuple-element.59, f32[1024]{0:T(1024)S(1)} %get-tuple-element.249, f32[1024]{0:T(1024)S(1)} %get-tuple-element.248, ...), kind=kLoop, calls=%fused_computation.44 | loop fusion | flops 45875200 | bytes 33072128 | tf_op jit(solution)/shard_map/convert_element_type | solution.py:1097
  734.9 3.8 convolution_convert_fusion.10
  738.7 3.3 copy.185
  741.9 9.5 convolution_convert_fusion
  751.5 7.6 copy.184
  759.0 6.8 fusion.34
  768.7 18.5 %attention11.3 = (bf16[2,512,512]{2,1,0:T(8,128)(2,1)S(1)}, f32[8,256]{1,0:T(8,128)S(1)}) custom-call(f32[2,512,256]{2,1,0:T(8,128)S(1)} %fusion.82.bg, f32[2,512,512]{2,1,0:T(8,128)} %fusion.37.proj, f32[2,512,256]{2,1,0:T(8,128)S(1)} %copy-done.20, f32[2,512,256]{2,1,0:T(8,128)S(1)} %copy-done.22, bf16[2,160,256]{2,1,0:T(8,128)(2,1)S(1)} %get-tuple-element.71.sin, ...), custom_call_target="tpu_custom_call" | custom-call | tf_op jit(solution)/shard_map/attention11/pallas_call | solution.py:834
  787.9 3.9 convolution_convert_fusion.2
  791.9 83.4 %comm7.1 = (bf16[2,512,1792]{2,1,0:T(8,128)(2,1)S(1)}, bf16[2,4,448,1216]{3,2,1,0:T(8,128)(2,1)}, bf16[2,4,448,608]{3,2,1,0:T(8,128)(2,1)}) custom-call(bf16[2,512,1792]{2,1,0:T(8,128)(2,1)} %bitcast.313, bf16[4,448,1216]{2,1,0:T(8,128)(2,1)} %bitcast.308, bf16[4,448,608]{2,1,0:T(8,128)(2,1)S(1)} %bitcast.280), custom_call_target="tpu_custom_call" | custom-call | tf_op jit(solution)/shard_map/comm7/pallas_call | solution.py:414
  875.4 2.8 fusion.11
  879.4 6.3 convolution_convert_fusion.6
  888.1 2.4 bitcast_convert_fusion
  890.5 34.0 %comm9.1 = (bf16[2,4,448,512]{3,2,1,0:T(8,128)(2,1)}, bf16[2,4,448,256]{3,2,1,0:T(8,128)(2,1)S(1)}) custom-call(bf16[4,448,512]{2,1,0:T(8,128)(2,1)S(1)} %bitcast.282, bf16[4,448,256]{2,1,0:T(8,128)(2,1)S(1)} %bitcast.290), custom_call_target="tpu_custom_call" | custom-call | tf_op jit(solution)/shard_map/comm9/pallas_call | solution.py:414
  924.5 3.3 convert_reduce_fusion.2
  930.3 63.4 %comm5.2 = bf16[2,512,1792]{2,1,0:T(8,128)(2,1)S(1)} custom-call(bf16[2,512,1792]{2,1,0:T(8,128)(2,1)} %bitcast.314), custom_call_target="tpu_custom_call" | custom-call | tf_op jit(solution)/shard_map/comm5/pallas_call | solution.py:414
  993.7 3.4 fusion.31
  998.5 6.0 convert_reduce_fusion
  1005.2 4.0 convert_reduce_fusion.1
  1012.1 7.3 fusion.33
  1022.2 1.8 maximum_bitcast_fusion.1
  1024.0 1.8 maximum_bitcast_fusion.2
  (441 shorter events, 57.6 us)
Async XLA Ops:
  7.2 7.0 copy-start.147
  7.2 9.0 copy-start.148
  7.2 10.9 %copy-start.146 = (bf16[1,3,1792]{2,1,0:T(4,128)(2,1)S(1)}, bf16[1,3,1792]{2,1,0:T(4,128)(2,1)}, u32[]{:S(2)}) copy-start(bf16[1,3,1792]{2,1,0:T(4,128)(2,1)} %param.23) | copy-start | bytes 32260
  7.2 12.8 %copy-start.121 = (bf16[1,448,64]{1,2,0:T(8,128)(2,1)S(1)}, bf16[1,448,64]{1,2,0:T(8,128)(2,1)}, u32[]{:S(2)}) copy-start(bf16[1,448,64]{1,2,0:T(8,128)(2,1)} %param.19) | copy-start | bytes 172036
  7.2 12.9 %copy-start.122 = (bf16[1,448,64]{1,2,0:T(8,128)(2,1)S(1)}, bf16[1,448,64]{1,2,0:T(8,128)(2,1)}, u32[]{:S(2)}) copy-start(bf16[1,448,64]{1,2,0:T(8,128)(2,1)} %param.20) | copy-start | bytes 172036
  7.2 14.5 %copy-start.103 = (bf16[1,448,448]{2,1,0:T(8,128)(2,1)S(1)}, bf16[1,448,448]{2,1,0:T(8,128)(2,1)}, u32[]{:S(2)}) copy-start(bf16[1,448,448]{2,1,0:T(8,128)(2,1)} %param.24) | copy-start | bytes 1204228
  7.2 1023.3 %all-reduce.4.cloned.1.call-start = ((), (), s32[]{:S(2)}) async-start(), calls=%async_computation | async-start | bytes 143360 | tf_op jit(solution)/shard_map/psum | solution.py:1137
  13.6 13.7 %copy-start.94 = (bf16[1,1216,448]{1,2,0:T(8,128)(2,1)S(1)}, bf16[1,1216,448]{1,2,0:T(8,128)(2,1)}, u32[]{:S(2)}) copy-start(bf16[1,1216,448]{1,2,0:T(8,128)(2,1)} %param.28) | copy-start | bytes 3268612
  13.6 52.3 %copy-start.123 = (f32[2,512]{1,0:T(2,128)}, f32[2,512]{1,0:T(2,128)S(1)}, u32[]{:S(2)}) copy-start(f32[2,512]{1,0:T(2,128)S(1)} %fusion.64) | copy-start | bytes 12292
  16.2 49.7 %copy-start.118 = (f32[1792]{0:T(1024)}, f32[1792]{0:T(1024)S(1)}, u32[]{:S(2)}) copy-start(f32[1792]{0:T(1024)S(1)} %get-tuple-element.187) | copy-start | bytes 21508
  16.2 256.7 %copy-start.109 = (f32[1792]{0:T(1024)}, f32[1792]{0:T(1024)S(1)}, u32[]{:S(2)}) copy-start(f32[1792]{0:T(1024)S(1)} %get-tuple-element.186) | copy-start | bytes 21508
  18.1 166.5 %copy-start.106 = (f32[1792]{0:T(1024)}, f32[1792]{0:T(1024)S(1)}, u32[]{:S(2)}) copy-start(f32[1792]{0:T(1024)S(1)} %get-tuple-element.185) | copy-start | bytes 21508
  18.1 448.5 %copy-start.104 = (f32[1792]{0:T(1024)}, f32[1792]{0:T(1024)S(1)}, u32[]{:S(2)}) copy-start(f32[1792]{0:T(1024)S(1)} %get-tuple-element.184) | copy-start | bytes 21508
  20.1 53.6 %copy-start.36 = (f32[8,256]{1,0:T(8,128)}, f32[8,256]{1,0:T(8,128)S(1)}, u32[]{:S(2)}) copy-start(f32[8,256]{1,0:T(8,128)S(1)} %get-tuple-element.239.taps) | copy-start | bytes 24580
  28.9 37.0 %copy-start.56 = (bf16[2,512,1792]{2,1,0:T(8,128)(2,1)S(1)}, bf16[2,512,1792]{2,1,0:T(8,128)(2,1)}, u32[]{:S(2)}) copy-start(bf16[2,512,1792]{2,1,0:T(8,128)(2,1)} %param.16) | copy-start | bytes 11010052
  75.2 12.5 %copy-start.29 = (bf16[4,448,256]{2,1,0:T(8,128)(2,1)S(1)}, bf16[4,448,256]{2,1,0:T(8,128)(2,1)}, u32[]{:S(2)}) copy-start(bf16[4,448,256]{2,1,0:T(8,128)(2,1)} %copy-done.28) | copy-start | bytes 2752516
  91.8 88.7 %copy-start.57 = (bf16[2,512,1792]{2,1,0:T(8,128)(2,1)S(1)}, bf16[2,512,1792]{2,1,0:T(8,128)(2,1)}, u32[]{:S(2)}) copy-start(bf16[2,512,1792]{2,1,0:T(8,128)(2,1)} %param.16) | copy-start | bytes 11010052
  180.4 13.4 %copy-start.48 = (bf16[4,448,608]{2,1,0:T(8,128)(2,1)}, bf16[4,448,608]{2,1,0:T(8,128)(2,1)S(1)}, u32[]{:S(2)}) copy-start(bf16[4,448,608]{2,1,0:T(8,128)(2,1)S(1)} %get-tuple-element.54) | copy-start | bytes 6537220
  265.6 7.4 copy-start.52
  265.6 22.0 %copy-start.31 = (bf16[4,448,256]{2,1,0:T(8,128)(2,1)}, bf16[4,448,256]{2,1,0:T(8,128)(2,1)S(1)}, u32[]{:S(2)}) copy-start(bf16[4,448,256]{2,1,0:T(8,128)(2,1)S(1)} %get-tuple-element.58) | copy-start | bytes 2752516
  272.9 193.7 %copy-start.61 = (bf16[2,512,1792]{2,1,0:T(8,128)(2,1)}, bf16[2,512,1792]{2,1,0:T(8,128)(2,1)S(1)}, u32[]{:S(2)}) copy-start(bf16[2,512,1792]{2,1,0:T(8,128)(2,1)S(1)} %get-tuple-element.195) | copy-start | bytes 11010052
  275.1 15.5 %copy-start.8 = (f32[2,512,512]{2,1,0:T(8,128)}, f32[2,512,512]{2,1,0:T(8,128)S(1)}, u32[]{:S(2)}) copy-start(f32[2,512,512]{2,1,0:T(8,128)S(1)} %fusion.40.proj) | copy-start | bytes 6291460
  373.4 12.1 %copy-start.46 = (bf16[4,448,608]{2,1,0:T(8,128)(2,1)}, bf16[4,448,608]{2,1,0:T(8,128)(2,1)S(1)}, u32[]{:S(2)}) copy-start(bf16[4,448,608]{2,1,0:T(8,128)(2,1)S(1)} %get-tuple-element.61) | copy-start | bytes 6537220
  377.6 89.0 %copy-start.116 = (f32[2,512]{1,0:T(2,128)}, f32[2,512]{1,0:T(2,128)S(1)}, u32[]{:S(2)}) copy-start(f32[2,512]{1,0:T(2,128)S(1)} %fusion.71) | copy-start | bytes 12292
  391.5 6.7 copy-start.155
  391.6 80.7 %copy-start.154 = (bf16[1024,608]{0,1:T(8,128)(2,1)}, bf16[1024,608]{0,1:T(8,128)(2,1)S(1)}, u32[]{:S(2)}) copy-start(bf16[1024,608]{0,1:T(8,128)(2,1)S(1)} %get-tuple-element.203) | copy-start | bytes 3735556
  479.3 6.8 copy-start.18
  489.4 19.7 %copy-start.62 = (bf16[2,512,1792]{2,1,0:T(8,128)(2,1)S(1)}, bf16[2,512,1792]{2,1,0:T(8,128)(2,1)}, u32[]{:S(2)}) copy-start(bf16[2,512,1792]{2,1,0:T(8,128)(2,1)} %copy-done.61) | copy-start | bytes 11010052
  489.4 19.7 %copy-start.110 = (f32[1792]{0:T(1024)S(1)}, f32[1792]{0:T(1024)}, u32[]{:S(2)}) copy-start(f32[1792]{0:T(1024)} %copy-done.109) | copy-start | bytes 21508
  489.4 19.7 %copy-start.135 = (f32[2,512]{1,0:T(2,128)S(1)}, f32[2,512]{1,0:T(2,128)}, u32[]{:S(2)}) copy-start(f32[2,512]{1,0:T(2,128)} %copy-done.134) | copy-start | bytes 12292
  489.5 23.3 %copy-start.44 = (f32[2,2]{1,0:T(2,128)}, f32[2,2]{1,0:T(2,128)S(1)}, u32[]{:S(2)}) copy-start(f32[2,2]{1,0:T(2,128)S(1)} %pad_maximum_fusion.16.coef) | copy-start | bytes 52
  489.5 23.2 %copy-start.42 = (f32[3,2]{1,0:T(4,128)}, f32[3,2]{1,0:T(4,128)S(1)}, u32[]{:S(2)}) copy-start(f32[3,2]{1,0:T(4,128)S(1)} %pad_maximum_fusion.14.late) | copy-start | bytes 76
  538.5 82.3 %copy-start.63 = (bf16[2,512,1792]{2,1,0:T(8,128)(2,1)S(1)}, bf16[2,512,1792]{2,1,0:T(8,128)(2,1)}, u32[]{:S(2)}) copy-start(bf16[2,512,1792]{2,1,0:T(8,128)(2,1)} %copy-done.61) | copy-start | bytes 11010052
  538.5 82.3 %copy-start.111 = (f32[1792]{0:T(1024)S(1)}, f32[1792]{0:T(1024)}, u32[]{:S(2)}) copy-start(f32[1792]{0:T(1024)} %copy-done.109) | copy-start | bytes 21508
  538.5 82.3 %copy-start.136 = (f32[2,512]{1,0:T(2,128)S(1)}, f32[2,512]{1,0:T(2,128)}, u32[]{:S(2)}) copy-start(f32[2,512]{1,0:T(2,128)} %copy-done.134) | copy-start | bytes 12292
  538.5 85.2 %copy-start.131 = (f32[2,512]{1,0:T(2,128)S(1)}, f32[2,512]{1,0:T(2,128)}, u32[]{:S(2)}) copy-start(f32[2,512]{1,0:T(2,128)} %copy-done.130) | copy-start | bytes 12292
  538.5 85.2 %copy-start.117 = (f32[2,512]{1,0:T(2,128)S(1)}, f32[2,512]{1,0:T(2,128)}, u32[]{:S(2)}) copy-start(f32[2,512]{1,0:T(2,128)} %copy-done.116) | copy-start | bytes 12292
  538.5 85.2 %copy-start.138 = (f32[2,512]{1,0:T(2,128)S(1)}, f32[2,512]{1,0:T(2,128)}, u32[]{:S(2)}) copy-start(f32[2,512]{1,0:T(2,128)} %get-tuple-element.255) | copy-start | bytes 12292
  620.9 12.1 %slice-start.2 = ((s8[4980736]{0:T(1024)(128)(4,1)}), s8[4194304]{0:T(1024)(128)(4,1)S(1)}, s32[]{:S(2)}) async-start(s8[4980736]{0:T(1024)(128)(4,1)} %bitcast.310), calls=%async_computation.3 | async-start | bytes 8388608
  625.3 7.7 copy-start.49
  625.3 7.7 slice-start.3
  637.6 10.9 %copy-start.159 = (bf16[1024,608]{0,1:T(8,128)(2,1)}, bf16[1024,608]{0,1:T(8,128)(2,1)S(1)}, u32[]{:S(2)}) copy-start(bf16[1024,608]{0,1:T(8,128)(2,1)S(1)} %get-tuple-element.196) | copy-start | bytes 3735556
  638.6 9.9 copy-start.14
  638.6 9.9 copy-start.27
  648.5 68.7 %copy-start.58 = (bf16[2,512,1792]{2,1,0:T(8,128)(2,1)S(1)}, bf16[2,512,1792]{2,1,0:T(8,128)(2,1)}, u32[]{:S(2)}) copy-start(bf16[2,512,1792]{2,1,0:T(8,128)(2,1)} %param.16) | copy-start | bytes 11010052
  648.5 68.7 %copy-start.107 = (f32[1792]{0:T(1024)S(1)}, f32[1792]{0:T(1024)}, u32[]{:S(2)}) copy-start(f32[1792]{0:T(1024)} %copy-done.106) | copy-start | bytes 21508
  648.5 68.7 %copy-start.114 = (f32[2,512]{1,0:T(2,128)S(1)}, f32[2,512]{1,0:T(2,128)}, u32[]{:S(2)}) copy-start(f32[2,512]{1,0:T(2,128)} %copy-done.113) | copy-start | bytes 12292
  717.2 6.7 copy-start.2
  717.2 6.7 copy-start.4
  724.0 10.9 %copy-start.91 = (bf16[1024,608]{0,1:T(8,128)(2,1)S(1)}, bf16[1024,608]{0,1:T(8,128)(2,1)}, u32[]{:S(2)}) copy-start(bf16[1024,608]{0,1:T(8,128)(2,1)} %copy-done.90) | copy-start | bytes 3735556
  759.0 6.9 copy-start.30
  765.8 21.4 %copy-start.79 = (bf16[2,512,1792]{2,1,0:T(8,128)(2,1)}, bf16[2,512,1792]{2,1,0:T(8,128)(2,1)S(1)}, u32[]{:S(2)}) copy-start(bf16[2,512,1792]{2,1,0:T(8,128)(2,1)S(1)} %fusion.34) | copy-start | bytes 11010052
  767.1 20.9 %copy-start.51 = (bf16[4,448,512]{2,1,0:T(8,128)(2,1)S(1)}, bf16[4,448,512]{2,1,0:T(8,128)(2,1)}, u32[]{:S(2)}) copy-start(bf16[4,448,512]{2,1,0:T(8,128)(2,1)} %copy-done.50) | copy-start | bytes 5505028
  791.9 83.5 %copy-start.59 = (bf16[2,512,1792]{2,1,0:T(8,128)(2,1)S(1)}, bf16[2,512,1792]{2,1,0:T(8,128)(2,1)}, u32[]{:S(2)}) copy-start(bf16[2,512,1792]{2,1,0:T(8,128)(2,1)} %param.16) | copy-start | bytes 11010052
  791.9 83.5 %copy-start.119 = (f32[1792]{0:T(1024)S(1)}, f32[1792]{0:T(1024)}, u32[]{:S(2)}) copy-start(f32[1792]{0:T(1024)} %copy-done.118) | copy-start | bytes 21508
  791.9 83.5 %copy-start.124 = (f32[2,512]{1,0:T(2,128)S(1)}, f32[2,512]{1,0:T(2,128)}, u32[]{:S(2)}) copy-start(f32[2,512]{1,0:T(2,128)} %copy-done.123) | copy-start | bytes 12292
  888.1 36.4 %copy-start.78 = (bf16[2,4,448,512]{3,2,1,0:T(8,128)(2,1)S(1)}, bf16[2,4,448,512]{3,2,1,0:T(8,128)(2,1)}, u32[]{:S(2)}) copy-start(bf16[2,4,448,512]{3,2,1,0:T(8,128)(2,1)} %get-tuple-element.78) | copy-start | bytes 11010052
  930.3 63.4 %copy-start.65 = (bf16[2,512,1792]{2,1,0:T(8,128)(2,1)S(1)}, bf16[2,512,1792]{2,1,0:T(8,128)(2,1)}, u32[]{:S(2)}) copy-start(bf16[2,512,1792]{2,1,0:T(8,128)(2,1)} %copy-done.61) | copy-start | bytes 11010052
  930.3 63.4 %copy-start.68 = (bf16[2,512,1792]{2,1,0:T(8,128)(2,1)S(1)}, bf16[2,512,1792]{2,1,0:T(8,128)(2,1)}, u32[]{:S(2)}) copy-start(bf16[2,512,1792]{2,1,0:T(8,128)(2,1)} %get-tuple-element.59) | copy-start | bytes 11010052
  1012.1 7.3 copy-start.89
  1012.1 7.6 copy-start.99
  1012.1 7.6 copy-start.100
  1012.1 7.7 copy-start.87
  1012.1 7.7 copy-start.88
  (103 other events, 352.3 us)
Sparse Core Ops, SparseCore 0:
  879.5 126.7 all-reduce.3

commit v4 on v3

--- a/solution.py
+++ b/solution.py
@@ -358,8 +358,63 @@
                 copy.wait_send()
 
 
+TILE = 256
+
+
+class Product:
+    def __init__(self, lhs, rhs, out, scratch):
+        self.lhs, self.rhs, self.out = lhs, rhs, out
+        self.left, self.right, self.stage, self.loads, self.stores = scratch
+        self.tiles = lhs.shape[1] // TILE
+
+    @staticmethod
+    def scratch(lhs, rhs):
+        return [
+            pltpu.VMEM(lhs.shape, jnp.bfloat16),
+            pltpu.VMEM(rhs.shape, jnp.bfloat16),
+            pltpu.VMEM((2, TILE, rhs.shape[1]), jnp.bfloat16),
+            pltpu.SemaphoreType.DMA((2,)),
+            pltpu.SemaphoreType.DMA((2,)),
+        ]
+
+    def load(self, side):
+        src, dst = ((self.lhs, self.left), (self.rhs, self.right))[side]
+        return pltpu.make_async_copy(src, dst, self.loads.at[side])
+
+    def store(self, i):
+        at = pl.ds(pl.multiple_of(i * TILE, TILE), TILE)
+        return pltpu.make_async_copy(self.stage.at[i % 2], self.out.at[at], self.stores.at[i % 2])
+
+    def start(self):
+        self.load(0).start()
+        self.load(1).start()
+
+    def step(self, i):
+        @pl.when(i == 0)
+        def _():
+            self.load(0).wait()
+            self.load(1).wait()
+
+        @pl.when(i >= 2)
+        def _():
+            self.store(i - 2).wait()
+
+        at = pl.ds(pl.multiple_of(i * TILE, TILE), TILE)
+        self.stage[i % 2] = lax.dot_general(
+            self.left[:, at],
+            self.right[...],
+            (((0,), (0,)), ((), ())),
+            preferred_element_type=jnp.float32,
+        ).astype(jnp.bfloat16)
+        self.store(i).start()
+
+    def finish(self):
+        for i in range(max(self.tiles - 2, 0), self.tiles):
+            self.store(i).wait()
+
+
 def comm_kernel(plan, *refs):
-    has_sum, layer_in, count_in, layer_out, count_out, chunks, lag = plan
+    has_sum, layer_in, count_in, layer_out, count_out, kept, count_made, chunks, lag = plan
     refs = list(refs)
 
     def take(count):
@@ -367,8 +422,12 @@
         del refs[:count]
         return taken
 
-    p_in, w_in, g_in = take(has_sum), take(count_in), take(count_out)
-    p_out, w_out, g_out = take(has_sum), take(count_in), take(count_out)
+    p_in, w_in, g_in, _, m_in = (
+        take(has_sum), take(count_in), take(count_out), take(kept), take(2 * count_made)
+    )
+    p_out, w_out, g_out, m_out = (
+        take(has_sum), take(count_in), take(count_out), take(count_made)
+    )
     greet(has_sum, count_in + count_out > 0)
     jobs = []
     if has_sum:
@@ -378,25 +437,40 @@
         jobs.append(Gather(layer_in, w_in, w_out, take(3)))
     if count_out:
         jobs.append(Scatter(layer_out, g_in, g_out, take(3)))
-    for job in jobs:
+    made = [
+        Product(m_in[2 * i], m_in[2 * i + 1], m_out[i], take(5)) for i in range(count_made)
+    ]
+    for job in made + jobs:
         job.start()
     if has_sum:
+        tiles = sum(product.tiles for product in made)
 
         def turn(t, carry):
             line.turn(t)
+            i = t - 2
+            for product in made:
+
+                @pl.when((i >= 0) & (i < product.tiles))
+                def _(product=product, i=i):
+                    product.step(i)
+
+                i = i - product.tiles
             return carry
 
-        lax.fori_loop(0, line.turns, turn, 0)
+        lax.fori_loop(0, max(line.turns, tiles + 2), turn, 0)
         line.finish()
-    for job in jobs:
+    for job in made + jobs:
         job.finish()
 
 
-def communicate(cid, partial=None, gather=None, scatter=None, chunks=16, lag=3):
+def communicate(
+    cid, partial=None, gather=None, scatter=None, into=(), products=(), chunks=16, lag=2
+):
     n = lax.axis_size("seq")
     layer_in, w_in = gather if gather else (0, [])
     layer_out, g_in = scatter if scatter else (0, [])
     p_in = [] if partial is None else [partial]
+    m_in = [a for pair in products for a in pair]
     vmem, anywhere = pl.BlockSpec(memory_space=pltpu.VMEM), pl.BlockSpec(memory_space=pl.ANY)
     scratch = []
     if p_in:
@@ -405,28 +479,35 @@
         scratch += Gather.scratch(len(w_in), n)
     if g_in:
         scratch += Scatter.scratch(len(g_in), n)
+    for pair in products:
+        scratch += Product.scratch(*pair)
     shapes = (
         [jax.ShapeDtypeStruct(p.shape, jnp.bfloat16) for p in p_in]
         + [jax.ShapeDtypeStruct((n,) + w.shape[1:], jnp.bfloat16) for w in w_in]
         + [jax.ShapeDtypeStruct((2,) + g.shape, jnp.bfloat16) for g in g_in]
-    )
-    plan = (len(p_in), layer_in, len(w_in), layer_out, len(g_in), chunks, lag)
+        + [jax.ShapeDtypeStruct((a.shape[1], b.shape[1]), jnp.bfloat16) for a, b in products]
+    )
+    plan = (
+        len(p_in), layer_in, len(w_in), layer_out, len(g_in), len(into), len(products), chunks, lag
+    )
+    first = len(p_in) + len(w_in)
     outs = pl.pallas_call(
         functools.partial(comm_kernel, plan),
         out_shape=shapes,
-        in_specs=[vmem] * (len(p_in) + len(w_in)) + [anywhere] * len(g_in),
-        out_specs=[vmem] * len(p_in) + [anywhere] * (len(w_in) + len(g_in)),
+        in_specs=[vmem] * first + [anywhere] * (len(g_in) + len(into) + len(m_in)),
+        out_specs=[vmem] * len(p_in) + [anywhere] * (len(w_in) + len(g_in) + len(products)),
         scratch_shapes=scratch,
+        input_output_aliases={first + len(g_in) + i: first + i for i in range(len(into))},
         name=f"comm{cid}",
         compiler_params=pltpu.CompilerParams(
-            collective_id=cid, has_side_effects=True, vmem_limit_bytes=48 << 20
+            collective_id=cid, has_side_effects=True, vmem_limit_bytes=52 << 20
         ),
-    )(*p_in, *w_in, *g_in)
-    p, w = outs[: len(p_in)], outs[len(p_in) : len(p_in) + len(w_in)]
+    )(*p_in, *w_in, *g_in, *into, *m_in)
     return (
-        p[0] if p else None,
-        [a.reshape((-1,) + a.shape[2:]) for a in w],
-        outs[len(p_in) + len(w_in) :],
+        outs[0] if p_in else None,
+        [a.reshape((-1,) + a.shape[2:]) for a in outs[len(p_in) : first]],
+        outs[first : first + len(g_in)],
+        outs[first + len(g_in) :],
     )
 
 
@@ -965,10 +1046,6 @@
     return jnp.dot(a, b, preferred_element_type=jnp.float32)
 
 
-def outer(a, b):
-    return jnp.einsum("tc,tf->cf", a, b, preferred_element_type=jnp.float32).astype(jnp.bfloat16)
-
-
 def on_device(
     tokens,
     lengths,
@@ -1019,47 +1096,48 @@
     def spread(summed):
         return summed.astype(jnp.float32).reshape(total, width)
 
-    mix = [None, None]
-    ffn = [None, None]
-    _, mix[0], _ = communicate(1, gather=(0, [own_mix, own_out]))
+    _, (mix_0, out_0), _, _ = communicate(1, gather=(0, [own_mix, own_out]))
+    w_mix, w_o, w_gu, w_d = [mix_0, None], [out_0, None], [None, None], [None, None]
     x = tokens.reshape(total, width).astype(jnp.float32)
     kept = [None, None]
     outputs = []
+    last_partial = None
     for layer in range(2):
-        w_mix, w_o = mix[layer]
         normed = rms_norm(x, gains_one[layer]).astype(jnp.bfloat16)
-        proj = dot_n(normed, w_mix).reshape(micro_count, rows, 2 * wide)
+        proj = dot_n(normed, w_mix[layer]).reshape(micro_count, rows, 2 * wide)
         gated, *attn = attention_forward(proj, taps_both[layer], marks, tables)
         gated = gated.reshape(total, wide)
-        summed, ffn[layer], _ = communicate(
-            2 + layer, partial=as_parts(dot_t(gated, w_o)), gather=(layer, [own_ffn, own_down])
-        )
-        w_gu, w_d = ffn[layer]
+        partial = as_parts(dot_t(gated, w_o[layer]))
+        if layer == 0:
+            summed, (w_gu[0], w_d[0]), _, _ = communicate(
+                2, partial=partial, gather=(0, [own_ffn, own_down])
+            )
+        else:
+            summed, (w_gu[1],), _, _ = communicate(3, partial=partial, gather=(1, [own_ffn]))
         middle = x + spread(summed)
         normed_two = rms_norm(middle, gains_two[layer]).astype(jnp.bfloat16)
-        both = dot_n(normed_two, w_gu)
+        both = dot_n(normed_two, w_gu[layer])
         hidden = (jax.nn.silu(both[:, :hidden_cols]) * both[:, hidden_cols:]).astype(jnp.bfloat16)
-        partial = as_parts(dot_t(hidden, w_d))
+        partial = as_parts(dot_t(hidden, w_d[layer]))
+        kept[layer] = (x, normed, proj, gated, attn, middle, normed_two, both, hidden)
         if layer == 0:
-            summed, mix[1], _ = communicate(4, partial=partial, gather=(1, [own_mix, own_out]))
+            summed, (w_mix[1], w_o[1], w_d[1]), _, _ = communicate(
+                4, partial=partial, gather=(1, [own_mix, own_out, own_down])
+            )
+            outputs.append((middle + spread(summed)).astype(jnp.bfloat16))
+            x = outputs[0].astype(jnp.float32)
         else:
-            summed, _, _ = communicate(5, partial=partial)
-        out = (middle + spread(summed)).astype(jnp.bfloat16)
-        outputs.append(out)
-        kept[layer] = (x, normed, proj, gated, attn, middle, normed_two, both, hidden)
-        x = out.astype(jnp.float32)
+            last_partial = partial
 
     grad = cotangent.reshape(total, width)
     back = [None, None]
     smalls = [None, None]
-    received = [[None] * 4, [None] * 4]
-    late = None
+    made = []
+    into = [None] * 4
     for layer in (1, 0):
         x, normed, proj, gated, attn, middle, normed_two, both, hidden = kept[layer]
-        w_mix, w_o = mix[layer]
-        w_gu, w_d = ffn[layer]
         grad_wide = grad.astype(jnp.float32)
-        back_hidden = dot_n(grad, w_d)
+        back_hidden = dot_n(grad, w_d[layer])
         gate_pre, upward = both[:, :hidden_cols], both[:, hidden_cols:]
         silu_value, silu_back = jax.vjp(jax.nn.silu, gate_pre)
         back_both = jnp.concatenate(
@@ -1069,41 +1147,45 @@
             ],
             axis=1,
         )
-        partial = as_parts(dot_t(back_both, w_gu))
+        partial = as_parts(dot_t(back_both, w_gu[layer]))
+        products = ((normed_two, back_both), (grad, hidden))
         if layer == 1:
-            summed, _, _ = communicate(5, partial=partial)
+            summed, _, _, (grad_gu, grad_d) = communicate(5, partial=partial, products=products)
         else:
-            summed, _, received[1][:2] = communicate(6, partial=partial, scatter=(1, late))
-        grad_gu = outer(normed_two, back_both)
-        grad_d = outer(grad, hidden)
+            summed, _, into[1:], (grad_gu, grad_d) = communicate(
+                6, partial=partial, scatter=(1, made), products=products
+            )
         _, norm_back_two = jax.vjp(rms_norm, middle, gains_two[layer])
         back_middle, gain_two = norm_back_two(spread(summed))
         back_middle = grad_wide + back_middle
         back_branch = back_middle.astype(jnp.bfloat16)
-        grad_o = outer(back_branch, gated)
-        back_gated = dot_n(back_branch, w_o)
+        back_gated = dot_n(back_branch, w_o[layer])
         back_proj, taps_grad = attention_backward(
             back_gated.reshape(micro_count, rows, wide), proj, attn, taps_both[layer], marks, tables
         )
         back_proj = back_proj.reshape(total, 2 * wide)
-        grad_mix = outer(normed, back_proj)
-        partial = as_parts(dot_t(back_proj, w_mix))
-        summed, _, received[layer][2:] = communicate(
-            7 + layer, partial=partial, scatter=(layer, [by_seq(grad_gu), by_seq(grad_d)])
-        )
-        late = [by_seq(grad_mix), by_seq(grad_o)]
+        partial = as_parts(dot_t(back_proj, w_mix[layer]))
+        summed, _, into[:1], (grad_mix, grad_o) = communicate(
+            7 + layer,
+            partial=partial,
+            scatter=(layer, [by_seq(grad_gu)]),
+            into=into[:1] if layer == 0 else (),
+            products=((normed, back_proj), (back_branch, gated)),
+        )
+        made = [by_seq(grad_d), by_seq(grad_mix), by_seq(grad_o)]
         _, norm_back_one = jax.vjp(rms_norm, x, gains_one[layer])
         back_x, gain_one = norm_back_one(spread(summed))
         grad = (back_middle + back_x).astype(jnp.bfloat16)
         back[layer] = grad
         smalls[layer] = (gain_one, gain_two, taps_grad)
-    _, _, received[0][:2] = communicate(9, scatter=(0, late))
-
-    def collect(index):
-        picked = jnp.where(core == 0, received[0][index], received[1][index])
-        return jnp.sum(picked.astype(jnp.float32), axis=1)
-
-    grad_mix, grad_o, grad_gu, grad_d = [collect(i) for i in range(4)]
+    summed, _, into[1:], _ = communicate(
+        9, partial=last_partial, scatter=(0, made), into=into[1:]
+    )
+    outputs.append((kept[1][5] + spread(summed)).astype(jnp.bfloat16))
+    grad_gu, grad_d, grad_mix, grad_o = [
+        jnp.sum(received.astype(jnp.float32), axis=1).reshape((2, -1) + received.shape[3:])
+        for received in into
+    ]
 
     def joined(pair):
         return jnp.concatenate([pair[0], pair[1]], axis=1)

time: 1050 us -> 925 us (0.88)
  Pallas kernels: 734 us -> 636 us
  matrix products: 109 us -> 75.5 us
  local copies, waits for them, and re-layouts: 63.1 us -> 37.2 us
  other arithmetic: 112 us -> 130 us
  waiting for transfers between devices: 0.02 us -> 13.3 us
    pallas_call x10 -> x9, Pallas kernels: 672 us -> 574 us  [communicate(): pl.pallas_call(functools.partial(comm_kernel, plan), out_shape=shapes, in...]
    dot_general x8 -> x0, matrix products: 33.6 us -> none  [outer(): jnp.einsum('tc,tf->cf', a, b, preferred_element_type=jnp.float32)]
    convert_element_type x4 -> x0, local copies, waits for them, and re-layouts: 21.3 us -> none  [outer(): jnp.einsum('tc,tf->cf', a, b, preferred_element_type=jnp.float32)]
    psum x1, waiting for transfers between devices: 0.01 us -> 13.3 us  [on_device(): totals = lax.psum(jnp.stack(packed), ('section', 'seq', 'head'))]
  transfers between devices with their start and end apart: 1 -> 1, of which waited for: 0 -> 1; matrix products, arithmetic and copies ran while one was open for 5% -> 6% of each run, Pallas kernels for 9% -> 7%
where the time goes in v4:
time: 925 us; the launch traced here: 915 us
  Pallas kernels  636 us (69%)
  other arithmetic  130 us (14%)
  matrix products  75.5 us (8%)
  local copies, waits for them, and re-layouts  37.2 us (4%)
  between operations  16 us (2%)
  waiting for transfers between devices  13.3 us (1%)
    pallas_call x9, Pallas kernels, communicate(): pl.pallas_call(functools.partial(comm_kernel, plan), out_shape=shapes, in...  574 us
    pallas_call x4, Pallas kernels, attention_call(): pl.pallas_call(functools.partial(kernel, seq_reach()), out_shape=shapes,...  62.1 us
    dot_general x8, matrix products, dot_t(): return jnp.einsum('tc,dc->td', a, b, preferred_element_type=jnp.float32)  42.8 us
    dot_general x8, matrix products, dot_n(): return jnp.dot(a, b, preferred_element_type=jnp.float32)  32.7 us
    reduce_sum x4, other arithmetic, rms_norm(): vector * lax.rsqrt(jnp.mean(vector * vector, axis=-1, keepdims=True) + ep...  21.1 us
  transfers between devices with their start and end apart: 1, of which 1 were waited for; matrix products, arithmetic and copies ran while one was open for 6% of the time, Pallas kernels for 7%

profile of v4, /device:TPU:0, one launch (start us, length us, event | category | flops | bytes accessed | tf_op | source)
XLA Modules:
  0.0 914.5 jit_solution(15536201160327513203)
XLA Ops:
  14.6 2.2 all_gather.10
  19.2 2.0 all-gather
  21.2 2.8 fusion.8
  27.8 35.8 %comm1.1 = (bf16[4,448,512]{2,1,0:T(8,128)(2,1)}, bf16[4,448,256]{2,1,0:T(8,128)(2,1)S(1)}) custom-call(bf16[2,448,512]{2,1,0:T(8,128)(2,1)} %pad_maximum_fusion.3.refs_0_.refs_1_, bf16[2,448,256]{2,1,0:T(8,128)(2,1)S(1)} %fusion.60.refs_1_.refs_2_), custom_call_target="tpu_custom_call" | custom-call | tf_op jit(solution)/shard_map/comm1/pallas_call | solution.py:494
  63.6 3.9 fusion.35.proj
  69.3 2.5 stack.152.col
  71.9 12.3 %attention10.2 = (bf16[2,512,256]{2,1,0:T(8,128)(2,1)S(1)}, f32[2,512,256]{2,1,0:T(8,128)S(1)}, f32[2,512,256]{2,1,0:T(8,128)S(1)}, bf16[2,160,256]{2,1,0:T(8,128)(2,1)S(1)}, f32[1,2,16,256]{3,2,1,0:T(8,128)S(1)}) custom-call(f32[2,512,512]{2,1,0:T(8,128)S(1)} %fusion.35.proj, f32[2,512,8]{2,1,0:T(8,128)S(1)} %stack.152.col, ...), custom_call_target="tpu_custom_call" | custom-call | tf_op jit(solution)/shard_map/attention10/pallas_call | solution.py:915
  84.2 3.0 convolution_convert_fusion.7
  88.6 2.2 maximum_maximum_fusion.refs_1_
  90.8 89.5 %comm2.1 = (bf16[2,512,1792]{2,1,0:T(8,128)(2,1)}, bf16[4,448,1216]{2,1,0:T(8,128)(2,1)}, bf16[4,448,608]{2,1,0:T(8,128)(2,1)}) custom-call(bf16[2,512,1792]{2,1,0:T(8,128)(2,1)} %bitcast.299, bf16[2,448,1216]{2,1,0:T(8,128)(2,1)} %maximum_maximum_fusion.refs_1_, bf16[2,448,608]{2,1,0:T(8,128)(2,1)S(1)} %pad_maximum_fusion.2.refs_2_.refs_3_), custom_call_target="tpu_custom_call" | custom-call | tf_op jit(solution)/shard_map/comm2/pallas_call | solution.py:494
  180.3 3.5 multiply_reduce_fusion.5
  184.4 2.4 all-gather.1
  188.3 4.9 fusion.81
  194.0 1.8 copy-done.46
  196.6 4.5 convolution_convert_fusion.5
  201.1 64.3 %comm4.1 = (bf16[2,512,1792]{2,1,0:T(8,128)(2,1)}, bf16[4,448,512]{2,1,0:T(8,128)(2,1)}, bf16[4,448,256]{2,1,0:T(8,128)(2,1)S(1)}, bf16[4,448,608]{2,1,0:T(8,128)(2,1)}) custom-call(bf16[2,512,1792]{2,1,0:T(8,128)(2,1)} %bitcast.310, bf16[2,448,512]{2,1,0:T(8,128)(2,1)} %pad_maximum_fusion.3.refs_0_.refs_1_, bf16[2,448,256]{2,1,0:T(8,128)(2,1)S(1)} %copy-done.5, ...), custom_call_target="tpu_custom_call" | custom-call | tf_op jit(solution)/shard_map/comm4/pallas_call | solution.py:494
  265.4 6.3 fusion.23
  271.8 2.1 fusion.37.proj
  273.9 12.2 %attention10.3 = (bf16[2,512,256]{2,1,0:T(8,128)(2,1)S(1)}, f32[2,512,256]{2,1,0:T(8,128)S(1)}, f32[2,512,256]{2,1,0:T(8,128)S(1)}, bf16[2,160,256]{2,1,0:T(8,128)(2,1)S(1)}, f32[1,2,16,256]{3,2,1,0:T(8,128)S(1)}) custom-call(f32[2,512,512]{2,1,0:T(8,128)S(1)} %fusion.37.proj, f32[2,512,8]{2,1,0:T(8,128)S(1)} %stack.152.col, ...), custom_call_target="tpu_custom_call" | custom-call | tf_op jit(solution)/shard_map/attention10/pallas_call | solution.py:915
  286.1 3.0 convolution_convert_fusion.6
  289.1 67.9 %comm3.1 = (bf16[2,512,1792]{2,1,0:T(8,128)(2,1)}, bf16[4,448,1216]{2,1,0:T(8,128)(2,1)}) custom-call(bf16[2,512,1792]{2,1,0:T(8,128)(2,1)} %bitcast.300, bf16[2,448,1216]{2,1,0:T(8,128)(2,1)} %maximum_maximum_fusion.refs_1_), custom_call_target="tpu_custom_call" | custom-call | tf_op jit(solution)/shard_map/comm3/pallas_call | solution.py:494
  357.1 4.6 multiply_reduce_fusion.4
  362.4 3.2 multiply_convert_fusion.2
  365.6 8.5 fusion.82
  374.0 3.6 fusion.50
  377.6 2.4 pad_maximum_fusion.refs_2_
  380.0 9.1 convolution_convert_fusion.3
  389.5 6.7 fusion.11
  396.2 3.1 multiply_convert_fusion.1.refs_1_
  399.3 61.2 %comm5.1 = (bf16[2,512,1792]{2,1,0:T(8,128)(2,1)}, bf16[1792,1216]{1,0:T(8,128)(2,1)}, bf16[1792,608]{1,0:T(8,128)(2,1)}) custom-call(bf16[2,512,1792]{2,1,0:T(8,128)(2,1)} %bitcast.306, bf16[1024,1792]{1,0:T(8,128)(2,1)} %multiply_convert_fusion.1.refs_1_, bf16[1024,1216]{1,0:T(8,128)(2,1)} %pad_maximum_fusion.refs_2_, bf16[1024,1792]{1,0:T(8,128)(2,1)} %bitcast.297, ...), custom_call_target="tpu_custom_call" | custom-call | tf_op jit(solution)/shard_map/comm5/pallas_call | solution.py:494
  460.5 5.9 multiply_reduce_fusion
  467.9 5.8 fusion.79.refs_4_
  473.7 2.9 fusion.41.bg
  476.7 18.8 %attention11.2 = (bf16[2,512,512]{2,1,0:T(8,128)(2,1)S(1)}, f32[8,256]{1,0:T(8,128)S(1)}) custom-call(f32[2,512,256]{2,1,0:T(8,128)S(1)} %fusion.41.bg, f32[2,512,512]{2,1,0:T(8,128)} %copy-done.2, f32[2,512,256]{2,1,0:T(8,128)S(1)} %get-tuple-element.73.att, f32[2,512,256]{2,1,0:T(8,128)S(1)} %get-tuple-element.74.conv, ...), custom_call_target="tpu_custom_call" | custom-call | tf_op jit(solution)/shard_map/attention11/pallas_call | solution.py:915
  495.6 3.9 convolution_convert_fusion.2
  499.5 62.1 %comm8.1 = (bf16[2,512,1792]{2,1,0:T(8,128)(2,1)}, bf16[2,4,448,1216]{3,2,1,0:T(8,128)(2,1)}, bf16[1792,512]{1,0:T(8,128)(2,1)}, bf16[1792,256]{1,0:T(8,128)(2,1)S(1)}) custom-call(bf16[2,512,1792]{2,1,0:T(8,128)(2,1)} %bitcast.313, bf16[4,448,1216]{2,1,0:T(8,128)(2,1)} %bitcast.305, bf16[1024,1792]{1,0:T(8,128)(2,1)} %get-tuple-element.214.refs_2_, ...), custom_call_target="tpu_custom_call" | custom-call | tf_op jit(solution)/shard_map/comm8/pallas_call | solution.py:494
  561.6 5.0 fusion.5
  566.9 8.2 fusion.15
  575.2 3.6 fusion.53
  578.8 2.4 pad_maximum_fusion.1.refs_5_
  581.2 9.1 convolution_convert_fusion.1
  590.4 8.6 fusion.17.refs_6_
  599.0 63.7 %comm6.1 = (bf16[2,512,1792]{2,1,0:T(8,128)(2,1)}, bf16[2,4,448,608]{3,2,1,0:T(8,128)(2,1)}, bf16[2,4,448,512]{3,2,1,0:T(8,128)(2,1)}, bf16[2,4,448,256]{3,2,1,0...) custom-call(bf16[2,512,1792]{2,1,0:T(8,128)(2,1)} %bitcast.307, bf16[4,448,608]{2,1,0:T(8,128)(2,1)} %bitcast.315, ...), custom_call_target="tpu_custom_call" | custom-call | tf_op jit(solution)/shard_map/comm6/pallas_call | solution.py:494
  662.7 5.3 multiply_reduce_fusion.1
  669.1 5.7 fusion.20
  674.8 3.1 fusion.39.bg
  678.0 18.8 %attention11.3 = (bf16[2,512,512]{2,1,0:T(8,128)(2,1)S(1)}, f32[8,256]{1,0:T(8,128)S(1)}) custom-call(f32[2,512,256]{2,1,0:T(8,128)S(1)} %fusion.39.bg, f32[2,512,512]{2,1,0:T(8,128)} %copy-done.1, f32[2,512,256]{2,1,0:T(8,128)S(1)} %get-tuple-element.85.att, f32[2,512,256]{2,1,0:T(8,128)S(1)} %get-tuple-element.86.conv, ...), custom_call_target="tpu_custom_call" | custom-call | tf_op jit(solution)/shard_map/attention11/pallas_call | solution.py:915
  696.8 3.9 convolution_convert_fusion
  700.8 63.5 %comm7.1 = (bf16[2,512,1792]{2,1,0:T(8,128)(2,1)}, bf16[2,4,448,1216]{3,2,1,0:T(8,128)(2,1)}, bf16[1792,512]{1,0:T(8,128)(2,1)}, bf16[1792,256]{1,0:T(8,128)(2,1)S(1)}) custom-call(bf16[2,512,1792]{2,1,0:T(8,128)(2,1)} %bitcast.308, bf16[4,448,1216]{2,1,0:T(8,128)(2,1)} %bitcast.304, ...), custom_call_target="tpu_custom_call", output_to_operand_aliasing={{1}: (2, {})} | custom-call | tf_op jit(solution)/shard_map/comm7/pallas_call | solution.py:494
  764.3 4.9 fusion.7
  770.7 6.2 convolution_convert_fusion.4
  776.9 66.1 %comm9.1 = (bf16[2,512,1792]{2,1,0:T(8,128)(2,1)}, bf16[2,4,448,608]{3,2,1,0:T(8,128)(2,1)}, bf16[2,4,448,512]{3,2,1,0:T(8,128)(2,1)}, bf16[2,4,448,256]{3,2,1,0:T(8,128)(2,1)}) custom-call(bf16[2,512,1792]{2,1,0:T(8,128)(2,1)} %bitcast.309, bf16[4,448,608]{2,1,0:T(8,128)(2,1)} %bitcast.314, ...), custom_call_target="tpu_custom_call", output_to_operand_aliasing={{1}: (4, {}), {2}: (5, {}), {3}: (6, {})} | custom-call | tf_op jit(solution)/shard_map/comm9/pallas_call | solution.py:494
  843.0 2.8 convert_reduce_fusion.2
  848.1 3.3 convert_reduce_fusion.1
  851.4 1.5 slice_bitcast_fusion.1
  852.9 5.9 convert_reduce_fusion
  858.8 2.1 slice_bitcast_fusion.3
  864.6 9.4 %fusion.34 = bf16[1,2,512,1792]{3,2,1,0:T(8,128)(2,1)} fusion(bf16[2,512,1792]{2,1,0:T(8,128)(2,1)} %copy-done.42, bf16[2,512,1792]{2,1,0:T(8,128)(2,1)S(1)} %copy-done.18, bf16[2,512,1792]{2,1,0:T(8,128)(2,1)S(1)} %copy-done.41, f32[2,512]{1,0:T(2,128)S(1)} %multiply_multiply_fusion, f32[1792]{0:T(1024)S(1)} %copy-done.67, f32[2,512]{1,0:T(2,128)S(1)} %copy-done.72, ...), kind=kLoop, calls=%fused_computation.87 | loop fusion | flops 36700160 | bytes 22050816 | tf_op jit(solution)/shard_map/jit(_where)/select_n | solution.py:1223
  874.1 5.6 fusion.32
  879.7 1.8 maximum_bitcast_fusion.2
  881.9 1.8 maximum_bitcast_fusion.1
  883.7 1.8 maximum_bitcast_fusion
  891.2 13.3 %all-reduce.4.cloned.1.call-done = f32[2,5,1792]{2,0,1:T(2,128)} async-done(((f32[2,5,1792]{2,0,1:T(2,128)}), f32[2,5,1792]{2,0,1:T(2,128)}) %all-reduce.4.cloned.1.call-update) | async-done | bytes 71696 | tf_op jit(solution)/shard_map/psum | solution.py:1219
  904.5 1.4 constant_dynamic-slice_fusion
  (290 shorter events, 38.7 us)
Async XLA Ops:
  7.2 11.7 %copy-start.64 = (bf16[1,448,448]{2,1,0:T(8,128)(2,1)S(1)}, bf16[1,448,448]{2,1,0:T(8,128)(2,1)}, u32[]{:S(2)}) copy-start(bf16[1,448,448]{2,1,0:T(8,128)(2,1)} %param.24) | copy-start | bytes 1204228
  7.2 12.0 %copy-start.81 = (bf16[1,1792]{1,0:T(2,128)(2,1)S(1)}, bf16[1,1792]{1,0:T(2,128)(2,1)}, u32[]{:S(2)}) copy-start(bf16[1,1792]{1,0:T(2,128)(2,1)} %param.18) | copy-start | bytes 10756
  7.2 897.3 %all-reduce.4.cloned.1.call-start = ((), (), s32[]{:S(2)}) async-start(), calls=%async_computation | async-start | bytes 143360 | tf_op jit(solution)/shard_map/psum | solution.py:1219
  13.4 11.3 %copy-start.57 = (bf16[1,1216,448]{1,2,0:T(8,128)(2,1)S(1)}, bf16[1,1216,448]{1,2,0:T(8,128)(2,1)}, u32[]{:S(2)}) copy-start(bf16[1,1216,448]{1,2,0:T(8,128)(2,1)} %param.28) | copy-start | bytes 3268612
  19.0 7.1 copy-start.62
  19.0 7.1 copy-start.63
  21.2 42.4 %copy-start.65 = (f32[1792]{0:T(1024)}, f32[1792]{0:T(1024)S(1)}, u32[]{:S(2)}) copy-start(f32[1792]{0:T(1024)S(1)} %get-tuple-element.207) | copy-start | bytes 21508
  24.7 38.9 %copy-start.70 = (f32[2,512]{1,0:T(2,128)}, f32[2,512]{1,0:T(2,128)S(1)}, u32[]{:S(2)}) copy-start(f32[2,512]{1,0:T(2,128)S(1)} %get-tuple-element.269) | copy-start | bytes 12292
  26.0 37.7 %copy-start.14 = (bf16[2,512,1792]{2,1,0:T(8,128)(2,1)S(1)}, bf16[2,512,1792]{2,1,0:T(8,128)(2,1)}, u32[]{:S(2)}) copy-start(bf16[2,512,1792]{2,1,0:T(8,128)(2,1)} %param.16) | copy-start | bytes 11010052
  26.5 41.1 %copy-start.4 = (bf16[2,448,256]{2,1,0:T(8,128)(2,1)}, bf16[2,448,256]{2,1,0:T(8,128)(2,1)S(1)}, u32[]{:S(2)}) copy-start(bf16[2,448,256]{2,1,0:T(8,128)(2,1)S(1)} %fusion.60.refs_1_.refs_2_) | copy-start | bytes 1376260
  63.6 4.0 copy-start.10
  67.6 16.6 %copy-start.1 = (f32[2,512,512]{2,1,0:T(8,128)}, f32[2,512,512]{2,1,0:T(8,128)S(1)}, u32[]{:S(2)}) copy-start(f32[2,512,512]{2,1,0:T(8,128)S(1)} %fusion.35.proj) | copy-start | bytes 6291460
  67.6 4.2 copy-start.3
  67.6 4.2 copy-start.13
  71.8 12.4 %copy-start.11 = (bf16[4,448,256]{2,1,0:T(8,128)(2,1)S(1)}, bf16[4,448,256]{2,1,0:T(8,128)(2,1)}, u32[]{:S(2)}) copy-start(bf16[4,448,256]{2,1,0:T(8,128)(2,1)} %copy-done.10) | copy-start | bytes 2752516
  88.6 91.6 %copy-start = (bf16[2,448,608]{2,1,0:T(8,128)(2,1)}, bf16[2,448,608]{2,1,0:T(8,128)(2,1)S(1)}, u32[]{:S(2)}) copy-start(bf16[2,448,608]{2,1,0:T(8,128)(2,1)S(1)} %pad_maximum_fusion.2.refs_2_.refs_3_) | copy-start | bytes 3268612
  90.8 89.5 %copy-start.15 = (bf16[2,512,1792]{2,1,0:T(8,128)(2,1)S(1)}, bf16[2,512,1792]{2,1,0:T(8,128)(2,1)}, u32[]{:S(2)}) copy-start(bf16[2,512,1792]{2,1,0:T(8,128)(2,1)} %param.16) | copy-start | bytes 11010052
  180.3 4.2 copy-start.82
  180.3 6.7 copy-start.23
  180.3 8.0 slice-start.2
  183.8 4.4 copy-start.68
  194.0 7.1 copy-start.45
  196.6 4.5 copy-start.5
  265.4 6.4 copy-start.87
  273.9 15.2 %copy-start.2 = (f32[2,512,512]{2,1,0:T(8,128)}, f32[2,512,512]{2,1,0:T(8,128)S(1)}, u32[]{:S(2)}) copy-start(f32[2,512,512]{2,1,0:T(8,128)S(1)} %fusion.37.proj) | copy-start | bytes 6291460
  357.0 4.6 copy-start.19
  357.1 5.3 copy-start.27
  365.6 8.5 copy-start.31
  365.6 8.5 copy-start.83
  380.0 9.5 %copy-start.16 = (bf16[2,512,1792]{2,1,0:T(8,128)(2,1)S(1)}, bf16[2,512,1792]{2,1,0:T(8,128)(2,1)}, u32[]{:S(2)}) copy-start(bf16[2,512,1792]{2,1,0:T(8,128)(2,1)} %param.16) | copy-start | bytes 11010052
  460.5 6.0 copy-start.20
  460.5 6.4 copy-start.32
  460.5 7.4 copy-start.35
  467.9 5.8 copy-start.28
  467.9 5.8 copy-start.37
  476.7 18.9 %copy-start.88 = (bf16[4,448,512]{2,1,0:T(8,128)(2,1)S(1)}, bf16[4,448,512]{2,1,0:T(8,128)(2,1)}, u32[]{:S(2)}) copy-start(bf16[4,448,512]{2,1,0:T(8,128)(2,1)} %get-tuple-element.66) | copy-start | bytes 5505028
  495.6 4.0 copy-start.9
  561.6 5.1 copy-start.21
  561.6 5.3 copy-start.29
  561.6 13.5 %slice-start = ((s8[5242880]{0:T(1024)(128)(4,1)}), s8[4194304]{0:T(1024)(128)(4,1)S(1)}, s32[]{:S(2)}) async-start(s8[5242880]{0:T(1024)(128)(4,1)} %bitcast.302), calls=%async_computation.1 | async-start | bytes 8388608
  566.9 8.2 slice-start.1
  566.9 8.3 copy-start.85
  581.2 9.1 copy-start.33
  581.2 9.1 %copy-start.36 = (bf16[1024,1792]{1,0:T(8,128)(2,1)S(1)}, bf16[1024,1792]{1,0:T(8,128)(2,1)}, u32[]{:S(2)}) copy-start(bf16[1024,1792]{1,0:T(8,128)(2,1)} %copy-done.34) | copy-start | bytes 11010052
  598.9 63.7 %copy-start.17 = (bf16[2,512,1792]{2,1,0:T(8,128)(2,1)S(1)}, bf16[2,512,1792]{2,1,0:T(8,128)(2,1)}, u32[]{:S(2)}) copy-start(bf16[2,512,1792]{2,1,0:T(8,128)(2,1)} %param.16) | copy-start | bytes 11010052
  599.0 63.7 %copy-start.69 = (f32[2,512]{1,0:T(2,128)S(1)}, f32[2,512]{1,0:T(2,128)}, u32[]{:S(2)}) copy-start(f32[2,512]{1,0:T(2,128)} %copy-done.68) | copy-start | bytes 12292
  662.7 5.4 copy-start.74
  662.7 5.5 copy-start.80
  662.7 5.5 copy-start.24
  662.7 5.5 copy-start.38
  662.7 6.4 copy-start.40
  662.7 6.4 copy-start.66
  668.1 6.7 copy-start.77
  669.1 5.7 copy-start.12
  669.1 5.7 copy-start.43
  677.9 18.9 %copy-start.86 = (bf16[4,448,512]{2,1,0:T(8,128)(2,1)S(1)}, bf16[4,448,512]{2,1,0:T(8,128)(2,1)}, u32[]{:S(2)}) copy-start(bf16[4,448,512]{2,1,0:T(8,128)(2,1)} %get-tuple-element.59) | copy-start | bytes 5505028
  696.8 4.0 copy-start.8
  700.8 63.5 %copy-start.71 = (f32[2,512]{1,0:T(2,128)S(1)}, f32[2,512]{1,0:T(2,128)}, u32[]{:S(2)}) copy-start(f32[2,512]{1,0:T(2,128)} %copy-done.70) | copy-start | bytes 12292
  852.9 9.5 %copy-start.41 = (bf16[2,512,1792]{2,1,0:T(8,128)(2,1)S(1)}, bf16[2,512,1792]{2,1,0:T(8,128)(2,1)}, u32[]{:S(2)}) copy-start(bf16[2,512,1792]{2,1,0:T(8,128)(2,1)} %get-tuple-element.98) | copy-start | bytes 11010052
  858.8 4.5 copy-start.39
  864.6 9.5 %copy-start.22 = (bf16[2,512,1792]{2,1,0:T(8,128)(2,1)S(1)}, bf16[2,512,1792]{2,1,0:T(8,128)(2,1)}, u32[]{:S(2)}) copy-start(bf16[2,512,1792]{2,1,0:T(8,128)(2,1)} %get-tuple-element.69) | copy-start | bytes 11010052
  864.6 9.5 %copy-start.30 = (bf16[2,512,1792]{2,1,0:T(8,128)(2,1)S(1)}, bf16[2,512,1792]{2,1,0:T(8,128)(2,1)}, u32[]{:S(2)}) copy-start(bf16[2,512,1792]{2,1,0:T(8,128)(2,1)} %copy-done.26) | copy-start | bytes 11010052
  874.1 5.6 copy-start.49
  874.1 5.6 copy-start.50
  (30 other events, 78.2 us)
Sparse Core Ops, SparseCore 0:
  770.8 133.6 all-reduce.3

commit v5 on v4

--- a/solution.py
+++ b/solution.py
@@ -26,7 +26,7 @@
     )
 
 
-def greet(line, spread):
+def greet(line, spread, everyone):
     core, z, q = lax.axis_index("section"), lax.axis_index("head"), lax.axis_index("seq")
     depth, count = lax.axis_size("head"), lax.axis_size("seq")
     barrier = pltpu.get_barrier_semaphore()
@@ -41,7 +41,12 @@
             for h in range(2):
                 hello(section=h, seq=lax.rem(q + j, count))
         expected += 2 * (count - 1)
-    if line:
+    if everyone:
+        for j in range(1, depth):
+            for h in range(2):
+                hello(section=h, head=lax.rem(z + j, depth))
+        expected += 2 * (depth - 1)
+    elif line:
 
         @pl.when(z > 0)
         def _():
@@ -53,6 +58,9 @@
 
         expected = expected + jnp.where(z > 0, 1, 0) + jnp.where(z < depth - 1, 1, 0)
     pl.semaphore_wait(barrier, expected)
+
+
+PIECES = 4
 
 
 class LineSum:
@@ -69,10 +77,10 @@
 
     @staticmethod
     def scratch(rows, width, chunks):
-        sem = pltpu.SemaphoreType.DMA((2, chunks))
-        bank = pltpu.SemaphoreType.DMA((2, 2, chunks))
+        dma = pltpu.SemaphoreType.DMA
+        each = dma((2, chunks))
         return [pltpu.VMEM((rows, width), jnp.bfloat16)] * 4 + [
-            sem, sem, sem, sem, sem, bank, sem, sem, sem
+            dma((1,)), dma((2, PIECES)), dma((2,)), each, each, dma((2, 2)), each, dma((1,)), dma((1,))
         ]
 
     def root(self, d):
@@ -82,45 +90,51 @@
         return pl.ds(pl.multiple_of(d * self.half + k * self.step, self.step), self.step)
 
     def part(self, d, k):
-        r = self.rng(d, k)
+        size = self.half // PIECES
+        r = pl.ds(pl.multiple_of(d * self.half + k * size, size), size)
         other = 1 - self.core
         return remote(
-            self.p_ref.at[other, r], self.pin.at[r], self.ps.at[d, k], self.pr.at[d, k], section=other
+            self.p_ref.at[other, r], self.pin.at[r], self.ps.at[0], self.pr.at[d, k], section=other
         )
 
     def up(self, d, k):
         r = self.rng(d, k)
         return remote(
-            self.out.at[r], self.low.at[r], self.rs.at[d, k], self.rl.at[d, k], head=self.z + 1
+            self.out.at[r], self.low.at[r], self.rs.at[d], self.rl.at[d, k], head=self.z + 1
         )
 
     def down(self, d, k):
         r = self.rng(d, k)
         return remote(
-            self.out.at[r], self.high.at[r], self.rs.at[d, k], self.rh.at[d, k], head=self.z - 1
+            self.out.at[r], self.high.at[r], self.rs.at[d], self.rh.at[d, k], head=self.z - 1
         )
 
     def share(self, d, k, side):
         r = self.rng(d, k)
         at = self.o_ref.at[self.core, r]
         return remote(
-            at, at, self.bs.at[side, d, k], self.br.at[d, k], head=self.z + (1 if side else -1)
+            at, at, self.bs.at[side, d], self.br.at[d, k], head=self.z + (1 if side else -1)
         )
 
     def give(self, d, k):
         r = self.rng(d, k)
         at = self.o_ref.at[self.core, r]
-        return remote(at, at, self.ts.at[d, k], self.tr.at[d, k], section=1 - self.core)
+        return remote(at, at, self.ts.at[0], self.tr.at[0], section=1 - self.core)
 
     def start(self):
-        for k in range(self.chunks):
+        for k in range(PIECES):
             for d in range(2):
                 self.part(d, k).start()
 
     def gathered(self, d, k):
         r = self.rng(d, k)
         z, n, root = self.z, self.n, self.root(d)
-        self.part(d, k).wait_recv()
+        group = self.chunks // PIECES
+
+        @pl.when(k % group == 0)
+        def _():
+            self.part(d, k // group).wait_recv()
+
         mine = self.p_ref[self.core, r, :].astype(jnp.float32) + self.pin[r, :].astype(jnp.float32)
 
         @pl.when((z == 0) & (root > 0))
@@ -195,56 +209,79 @@
                 self.passed(d, b)
 
     def finish(self):
-        z, n = self.z, self.n
+        z, n, other = self.z, self.n, 1 - self.core
+        remote(
+            self.p_ref.at[other], self.pin, self.ps.at[0], self.pr.at[0, 0], section=other
+        ).wait_send()
+        mine = self.o_ref.at[self.core]
+        given = remote(mine, mine, self.ts.at[0], self.tr.at[0], section=other)
+        given.wait_recv()
+        given.wait_send()
         for d in range(2):
             root = self.root(d)
-            for k in range(self.chunks):
-                self.part(d, k).wait_send()
-                self.give(d, k).wait_recv()
-                self.give(d, k).wait_send()
-
-                @pl.when(z < root)
+            r = pl.ds(d * self.half, self.half)
+            at = self.o_ref.at[self.core, r]
+
+            def summed(head):
+                return remote(
+                    self.out.at[r], self.low.at[r], self.rs.at[d], self.rl.at[d, 0], head=head
+                )
+
+            def shared(side):
+                return remote(
+                    at, at, self.bs.at[side, d], self.br.at[d, 0], head=z + (1 if side else -1)
+                )
+
+            @pl.when(z < root)
+            def _():
+                summed(z + 1).wait_send()
+
+            @pl.when(z > root)
+            def _():
+                summed(z - 1).wait_send()
+
+            if root > 0:
+
+                @pl.when((z <= root) & (z > 0))
                 def _():
-                    self.up(d, k).wait_send()
-
-                @pl.when(z > root)
+                    shared(0).wait_send()
+
+            if root < n - 1:
+
+                @pl.when((z >= root) & (z < n - 1))
                 def _():
-                    self.down(d, k).wait_send()
-
-                if root > 0:
-
-                    @pl.when((z <= root) & (z > 0))
-                    def _():
-                        self.share(d, k, 0).wait_send()
-
-                if root < n - 1:
-
-                    @pl.when((z >= root) & (z < n - 1))
-                    def _():
-                        self.share(d, k, 1).wait_send()
+                    shared(1).wait_send()
 
 
 class Gather:
     def __init__(self, layer, srcs, dsts, sems):
         self.layer, self.srcs, self.dsts = layer, srcs, dsts
-        self.ss, self.rr, self.ls = sems
+        self.ss, self.rr, self.ls, self.fs, self.fr = sems
         self.core, self.q = lax.axis_index("section"), lax.axis_index("seq")
         self.n = lax.axis_size("seq")
+        self.square = self.n == 4
 
     @staticmethod
     def scratch(count, n):
-        return [
-            pltpu.SemaphoreType.DMA((count, n, 2)),
-            pltpu.SemaphoreType.DMA((count, n)),
-            pltpu.SemaphoreType.DMA((count,)),
-        ]
+        dma = pltpu.SemaphoreType.DMA
+        return [dma((count, n, 2)), dma((count, n)), dma((count,)), dma((count, 2)), dma((count, 2))]
+
+    def peer(self, j):
+        if not self.square:
+            return lax.rem(self.q + j, self.n)
+        x, y = self.q % 2, self.q // 2
+        x, y = (1 - x if j % 2 else x), (1 - y if j // 2 else y)
+        return y * 2 + x
+
+    def direct(self):
+        return range(1, 3 if self.square else self.n)
 
     def copies(self, a):
-        for j in range(1, self.n):
+        for j in self.direct():
             for h in range(2):
                 yield remote(
                     self.srcs[a].at[h], self.dsts[a].at[self.q], self.ss.at[a, j, h],
-                    self.rr.at[a, self.q], section=h, seq=lax.rem(self.q + j, self.n),
+                    self.rr.at[a, self.q], section=h, seq=self.peer(j),
                 )
         yield remote(
             self.srcs[a].at[1 - self.layer], self.dsts[a].at[self.q], self.ss.at[a, 0, 0],
@@ -262,6 +299,16 @@
             section=1 - self.core,
         )
 
+    def relay(self, a, i):
+        size = self.srcs[a].shape[1] // 2
+        at = self.dsts[a].at[self.peer(1 + i), pl.ds(i * size, size)]
+        return remote(at, at, self.fs.at[a, i], self.fr.at[a, i], seq=self.peer(2 - i))
+
+    def corner(self, a, i):
+        size = self.srcs[a].shape[1] // 2
+        at = self.dsts[a].at[self.peer(3), pl.ds(i * size, size)]
+        return remote(at, at, self.fs.at[a, i], self.fr.at[a, i], seq=self.peer(2 - i))
+
     def start(self):
         @pl.when(self.core == self.layer)
         def _():
@@ -270,10 +317,25 @@
                     copy.start()
                 self.local(a).start()
 
+    def due(self):
+        sent, turns = 0, []
+        for src in self.srcs:
+            sent += 2 * src.shape[1] * src.shape[2] * 2
+            turns.append(3 + sent // 200_000)
+        return turns
+
+    def middle(self, a):
+        for j in self.direct():
+            self.arrival(a, self.peer(j)).wait_recv()
+            if self.square:
+                self.relay(a, j - 1).start()
+
     def finish(self):
         for a in range(len(self.srcs)):
-            for j in range(1, self.n):
-                self.arrival(a, lax.rem(self.q + j, self.n)).wait_recv()
+            if self.square:
+                for i in range(2):
+                    self.corner(a, i).wait_recv()
+                    self.relay(a, i).wait_send()
 
             @pl.when(self.core == self.layer)
             def _():
@@ -284,6 +346,76 @@
             @pl.when(self.core != self.layer)
             def _():
                 self.arrival(a, self.q).wait_recv()
+
+
+class SmallSum:
+    def __init__(self, g_ref, total, spread, scratch):
+        self.g_ref, self.total, self.spread = g_ref, total, spread
+        self.got, self.src, self.ss, self.sr, self.ts, self.tr = scratch
+        self.core, self.q, self.z = (lax.axis_index(a) for a in ("section", "seq", "head"))
+        self.n, self.depth = lax.axis_size("seq"), lax.axis_size("head")
+
+    @staticmethod
+    def scratch(shape, narrow, n, depth):
+        dma = pltpu.SemaphoreType.DMA
+        return [
+            pltpu.VMEM((n,) + shape, jnp.float32),
+            pltpu.VMEM((8, narrow), jnp.float32),
+            dma((n,)),
+            dma((n,)),
+            dma((2 * depth,)),
+            dma((2 * depth,)),
+        ]
+
+    def first(self, j):
+        return remote(
+            self.g_ref, self.got.at[self.q], self.ss.at[j], self.sr.at[self.q],
+            seq=lax.rem(self.q + j, self.n),
+        )
+
+    def others(self):
+        for j in range(self.depth):
+            for flip in range(2):
+                if j or flip:
+                    core = 1 - self.core if flip else self.core
+                    yield 2 * j + flip, lax.rem(self.z + j, self.depth), core
+
+    def second(self, i, z, core):
+        slot = self.z * 2 + self.core
+        return remote(
+            self.src, self.spread.at[slot], self.ts.at[i], self.tr.at[slot], head=z, section=core
+        )
+
+    def start(self):
+        for j in range(1, self.n):
+            self.first(j).start()
+        self.got[self.q] = self.g_ref[...]
+
+    def middle(self):
+        for j in range(1, self.n):
+            s = lax.rem(self.q + j, self.n)
+            remote(
+                self.g_ref, self.got.at[s], self.ss.at[j], self.sr.at[s], seq=s
+            ).wait_recv()
+        summed = self.got[0]
+        for s in range(1, self.n):
+            summed = summed + self.got[s]
+        self.total[...] = summed[:8]
+        own = summed[8:, : self.src.shape[1]]
+        self.src[...] = own
+        self.spread[self.z * 2 + self.core] = own
+        for i, z, core in self.others():
+            self.second(i, z, core).start()
+
+    def finish(self):
+        for i, z, core in self.others():
+            slot = z * 2 + core
+            remote(
+                self.src, self.spread.at[slot], self.ts.at[i], self.tr.at[slot], head=z, section=core
+            ).wait_recv()
+            self.second(i, z, core).wait_send()
+        for j in range(1, self.n):
+            self.first(j).wait_send()
 
 
 class Scatter:
@@ -414,7 +546,7 @@
 
 
 def comm_kernel(plan, *refs):
-    has_sum, layer_in, count_in, layer_out, count_out, kept, count_made, chunks, lag = plan
+    has_sum, layer_in, count_in, layer_out, count_out, kept, count_made, small_in, chunks, lag = plan
     refs = list(refs)
 
     def take(count):
@@ -422,24 +554,33 @@
         del refs[:count]
         return taken
 
-    p_in, w_in, g_in, _, m_in = (
-        take(has_sum), take(count_in), take(count_out), take(kept), take(2 * count_made)
-    )
-    p_out, w_out, g_out, m_out = (
-        take(has_sum), take(count_in), take(count_out), take(count_made)
-    )
-    greet(has_sum, count_in + count_out > 0)
+    p_in, w_in, g_in, _, m_in, s_in = (
+        take(has_sum), take(count_in), take(count_out), take(kept), take(2 * count_made),
+        take(small_in),
+    )
+    p_out, w_out, g_out, m_out, s_out = (
+        take(has_sum), take(count_in), take(count_out), take(count_made), take(2 * small_in)
+    )
+    greet(has_sum, count_in + count_out > 0, small_in)
     jobs = []
+    later = []
     if has_sum:
         line = LineSum(p_in[0], p_out[0], take(13), chunks, lag)
         line.start()
     if count_in:
-        jobs.append(Gather(layer_in, w_in, w_out, take(3)))
+        weights = Gather(layer_in, w_in, w_out, take(5))
+        jobs.append(weights)
+        for a, turn in enumerate(weights.due()):
+            later.append((turn, functools.partial(weights.middle, a)))
     if count_out:
         jobs.append(Scatter(layer_out, g_in, g_out, take(3)))
     made = [
         Product(m_in[2 * i], m_in[2 * i + 1], m_out[i], take(5)) for i in range(count_made)
     ]
+    if small_in:
+        small = SmallSum(s_in[0], s_out[0], s_out[1], take(6))
+        jobs.insert(0, small)
+        later.append((12, small.middle))
     for job in made + jobs:
         job.start()
     if has_sum:
@@ -455,16 +596,26 @@
                     product.step(i)
 
                 i = i - product.tiles
+            for when, act in later:
+
+                @pl.when(t == when)
+                def _(act=act):
+                    act()
+
             return carry
 
-        lax.fori_loop(0, max(line.turns, tiles + 2), turn, 0)
+        last = max([line.turns, tiles + 2] + [when + 1 for when, _ in later])
+        lax.fori_loop(0, last, turn, 0)
         line.finish()
+    else:
+        for _, act in later:
+            act()
     for job in made + jobs:
         job.finish()
 
 
 def communicate(
-    cid, partial=None, gather=None, scatter=None, into=(), products=(), chunks=16, lag=2
+    cid, partial=None, gather=None, scatter=None, into=(), products=(), small=None, chunks=16, lag=2
 ):
     n = lax.axis_size("seq")
     layer_in, w_in = gather if gather else (0, [])
@@ -481,28 +632,42 @@
         scratch += Scatter.scratch(len(g_in), n)
     for pair in products:
         scratch += Product.scratch(*pair)
+    s_in, s_shapes = [], []
+    if small is not None:
+        s_in, narrow, depth = [small[0]], small[1], lax.axis_size("head")
+        scratch += SmallSum.scratch(small[0].shape, narrow, n, depth)
+        s_shapes = [
+            jax.ShapeDtypeStruct((8, small[0].shape[1]), jnp.float32),
+            jax.ShapeDtypeStruct((2 * depth, 8, narrow), jnp.float32),
+        ]
     shapes = (
         [jax.ShapeDtypeStruct(p.shape, jnp.bfloat16) for p in p_in]
         + [jax.ShapeDtypeStruct((n,) + w.shape[1:], jnp.bfloat16) for w in w_in]
         + [jax.ShapeDtypeStruct((2,) + g.shape, jnp.bfloat16) for g in g_in]
         + [jax.ShapeDtypeStruct((a.shape[1], b.shape[1]), jnp.bfloat16) for a, b in products]
+        + s_shapes
     )
     plan = (
-        len(p_in), layer_in, len(w_in), layer_out, len(g_in), len(into), len(products), chunks, lag
+        len(p_in), layer_in, len(w_in), layer_out, len(g_in), len(into), len(products), len(s_in),
+        chunks, lag,
     )
     first = len(p_in) + len(w_in)
     outs = pl.pallas_call(
         functools.partial(comm_kernel, plan),
         out_shape=shapes,
-        in_specs=[vmem] * first + [anywhere] * (len(g_in) + len(into) + len(m_in)),
-        out_specs=[vmem] * len(p_in) + [anywhere] * (len(w_in) + len(g_in) + len(products)),
+        in_specs=[vmem] * first
+        + [anywhere] * (len(g_in) + len(into) + len(m_in))
+        + [vmem] * len(s_in),
+        out_specs=[vmem] * len(p_in)
+        + [anywhere] * (len(w_in) + len(g_in) + len(products))
+        + [vmem] * len(s_shapes),
         scratch_shapes=scratch,
         input_output_aliases={first + len(g_in) + i: first + i for i in range(len(into))},
         name=f"comm{cid}",
         compiler_params=pltpu.CompilerParams(
             collective_id=cid, has_side_effects=True, vmem_limit_bytes=52 << 20
         ),
-    )(*p_in, *w_in, *g_in, *into, *m_in)
+    )(*p_in, *w_in, *g_in, *into, *m_in, *s_in)
     return (
         outs[0] if p_in else None,
         [a.reshape((-1,) + a.shape[2:]) for a in outs[len(p_in) : first]],
@@ -1178,8 +1343,16 @@
         grad = (back_middle + back_x).astype(jnp.bfloat16)
         back[layer] = grad
         smalls[layer] = (gain_one, gain_two, taps_grad)
-    summed, _, into[1:], _ = communicate(
-        9, partial=last_partial, scatter=(0, made), into=into[1:]
+    gains = jnp.stack([smalls[0][0], smalls[1][0], smalls[0][1], smalls[1][1]])
+    taps_rows = jnp.concatenate([smalls[0][2][:KW], smalls[1][2][:KW]])
+    packed = jnp.concatenate(
+        [
+            jnp.pad(gains, ((0, 4), (0, 0))),
+            jnp.pad(taps_rows, ((0, 8 - 2 * KW), (0, width - wide))),
+        ]
+    )
+    summed, _, into[1:], (gains, taps_rows) = communicate(
+        9, partial=last_partial, scatter=(0, made), into=into[1:], small=(packed, wide)
     )
     outputs.append((kept[1][5] + spread(summed)).astype(jnp.bfloat16))
     grad_gu, grad_d, grad_mix, grad_o = [
@@ -1199,25 +1372,11 @@
     grad_up = joined(grad_gu[:, :, hidden_cols:])
     grad_down = joined(grad_d).T
 
-    block = width // (2 * lax.axis_size("head"))
-    column_mask = (
-        jnp.arange(width, dtype=jnp.int32) // block == head_index * 2 + core
-    ).astype(jnp.float32)
-    packed = []
-    for gain_one, gain_two, taps_grad in smalls:
-        taps_full = lax.dynamic_update_slice_in_dim(
-            jnp.zeros((KW, width), jnp.float32),
-            taps_grad[:KW, :values],
-            (head_index * 2 + core) * values,
-            1,
-        )
-        packed.append(
-            jnp.concatenate(
-                [(gain_one * column_mask)[None], (gain_two * column_mask)[None], taps_full], axis=0
-            )
-        )
-    totals = lax.psum(jnp.stack(packed), ("section", "seq", "head"))
-    totals = lax.dynamic_index_in_dim(totals, core, 0, False)
+    gains = lax.dynamic_index_in_dim(gains[:4].reshape(2, 2, width), core, 1, False)
+    taps_rows = lax.dynamic_index_in_dim(
+        taps_rows[:, : 2 * KW, :values].reshape(-1, 2, KW, values), core, 1, False
+    )
+    grad_taps = jnp.transpose(taps_rows, (1, 0, 2)).reshape(KW, width)
 
     def chosen(pair):
         return jnp.where(core == 0, pair[0], pair[1]).reshape(1, micro_count, rows, width)
@@ -1225,14 +1384,14 @@
     return (
         chosen(outputs),
         chosen(back),
-        totals[0][None],
+        gains[0][None],
         grad_query[None],
         grad_key[None],
         grad_value[None],
         grad_gconv[None],
-        totals[2:][None],
+        grad_taps[None],
         grad_out[None],
-        totals[1][None],
+        gains[1][None],
         grad_gate[None],
         grad_up[None],
         grad_down[None],

time: 925 us -> 851 us (0.920)
  Pallas kernels: 636 us -> 605 us
  local copies, waits for them, and re-layouts: 37.2 us -> 22.2 us
  between operations: 16 us -> 2.31 us
  waiting for transfers between devices: 13.3 us -> 0 us
    pallas_call x9, Pallas kernels: 574 us -> 541 us  [communicate(): pl.pallas_call(functools.partial(comm_kernel, plan), out_shape=shapes, in...]
    psum x1 -> x0, waiting for transfers between devices: 13.3 us -> none  [on_device(): totals = lax.psum(jnp.stack(packed), ('section', 'seq', 'head'))]
  transfers between devices with their start and end apart: 1 -> 0, of which waited for: 1 -> 0; matrix products, arithmetic and copies ran while one was open for 6% -> 0% of each run, Pallas kernels for 7% -> 0%
where the time goes in v5:
time: 851 us; the launch traced here: 842 us
  Pallas kernels  605 us (71%)
  other arithmetic  131 us (15%)
  matrix products  75.8 us (9%)
  local copies, waits for them, and re-layouts  22.2 us (3%)
    pallas_call x9, Pallas kernels, communicate(): pl.pallas_call(functools.partial(comm_kernel, plan), out_shape=shapes, in...  541 us
    pallas_call x4, Pallas kernels, attention_call(): pl.pallas_call(functools.partial(kernel, seq_reach()), out_shape=shapes,...  63.3 us
    dot_general x8, matrix products, dot_t(): return jnp.einsum('tc,dc->td', a, b, preferred_element_type=jnp.float32)  38.5 us
    dot_general x8, matrix products, dot_n(): return jnp.dot(a, b, preferred_element_type=jnp.float32)  37.3 us
    reduce_sum x4, other arithmetic, rms_norm(): vector * lax.rsqrt(jnp.mean(vector * vector, axis=-1, keepdims=True) + ep...  21.4 us
    reduce_sum x4, other arithmetic, rms_norm(): jnp.mean(vector * vector, axis=-1, keepdims=True) + epsilon  17.9 us
    convert_element_type x2, other arithmetic, on_device(): grad = (back_middle + back_x).astype(jnp.bfloat16)  17.7 us

profile of v5, /device:TPU:0, one launch (start us, length us, event | category | flops | bytes accessed | tf_op | source)
XLA Modules:
  0.0 841.6 jit_solution(13121708871186341479)
XLA Ops:
  5.4 2.1 stack.150.col
  8.0 2.0 all_gather.10
  10.1 1.5 slice_bitcast_fusion.25
  12.0 1.3 pad_maximum_fusion.3.refs_0_.refs_1_
  13.8 29.5 %comm1.1 = (bf16[4,448,512]{2,1,0:T(8,128)(2,1)}, bf16[4,448,256]{2,1,0:T(8,128)(2,1)S(1)}) custom-call(bf16[2,448,512]{2,1,0:T(8,128)(2,1)} %pad_maximum_fusion.3.refs_0_.refs_1_, bf16[2,448,256]{2,1,0:T(8,128)(2,1)S(1)} %fusion.60.refs_1_.refs_2_), custom_call_target="tpu_custom_call" | custom-call | tf_op jit(solution)/shard_map/comm1/pallas_call | solution.py:655
  43.3 1.9 all-gather
  45.3 2.8 fusion.8
  48.8 3.7 fusion.35.proj
  52.6 13.0 %attention10.2 = (bf16[2,512,256]{2,1,0:T(8,128)(2,1)S(1)}, f32[2,512,256]{2,1,0:T(8,128)S(1)}, f32[2,512,256]{2,1,0:T(8,128)S(1)}, bf16[2,160,256]{2,1,0:T(8,128)(2,1)S(1)}, f32[1,2,16,256]{3,2,1,0:T(8,128)S(1)}) custom-call(f32[2,512,512]{2,1,0:T(8,128)S(1)} %fusion.35.proj, f32[2,512,8]{2,1,0:T(8,128)S(1)} %stack.150.col, ...), custom_call_target="tpu_custom_call" | custom-call | tf_op jit(solution)/shard_map/attention10/pallas_call | solution.py:1080
  65.7 3.0 convolution_convert_fusion.7
  69.3 2.2 maximum_maximum_fusion.refs_1_
  72.0 70.2 %comm2.1 = (bf16[2,512,1792]{2,1,0:T(8,128)(2,1)}, bf16[4,448,1216]{2,1,0:T(8,128)(2,1)}, bf16[4,448,608]{2,1,0:T(8,128)(2,1)}) custom-call(bf16[2,512,1792]{2,1,0:T(8,128)(2,1)} %bitcast.304, bf16[2,448,1216]{2,1,0:T(8,128)(2,1)} %maximum_maximum_fusion.refs_1_, bf16[2,448,608]{2,1,0:T(8,128)(2,1)S(1)} %pad_maximum_fusion.2.refs_2_.refs_3_), custom_call_target="tpu_custom_call" | custom-call | tf_op jit(solution)/shard_map/comm2/pallas_call | solution.py:655
  142.2 3.5 multiply_reduce_fusion.5
  146.3 1.8 all-gather.1
  148.2 1.4 multiply_convert_fusion.3
  149.6 4.9 fusion.80
  154.5 2.4 copy-done.41
  158.5 4.5 convolution_convert_fusion.5
  163.1 62.1 %comm4.1 = (bf16[2,512,1792]{2,1,0:T(8,128)(2,1)}, bf16[4,448,512]{2,1,0:T(8,128)(2,1)}, bf16[4,448,256]{2,1,0:T(8,128)(2,1)S(1)}, bf16[4,448,608]{2,1,0:T(8,128)(2,1)}) custom-call(bf16[2,512,1792]{2,1,0:T(8,128)(2,1)} %bitcast.312, bf16[2,448,512]{2,1,0:T(8,128)(2,1)} %pad_maximum_fusion.3.refs_0_.refs_1_, ...), custom_call_target="tpu_custom_call" | custom-call | tf_op jit(solution)/shard_map/comm4/pallas_call | solution.py:655
  225.2 7.1 fusion.23
  232.3 4.2 fusion.37.proj
  236.5 13.0 %attention10.3 = (bf16[2,512,256]{2,1,0:T(8,128)(2,1)S(1)}, f32[2,512,256]{2,1,0:T(8,128)S(1)}, f32[2,512,256]{2,1,0:T(8,128)S(1)}, bf16[2,160,256]{2,1,0:T(8,128)(2,1)S(1)}, f32[1,2,16,256]{3,2,1,0:T(8,128)S(1)}) custom-call(f32[2,512,512]{2,1,0:T(8,128)S(1)} %fusion.37.proj, f32[2,512,8]{2,1,0:T(8,128)S(1)} %stack.150.col, ...), custom_call_target="tpu_custom_call" | custom-call | tf_op jit(solution)/shard_map/attention10/pallas_call | solution.py:1080
  249.5 3.0 convolution_convert_fusion.6
  252.5 66.3 %comm3.1 = (bf16[2,512,1792]{2,1,0:T(8,128)(2,1)}, bf16[4,448,1216]{2,1,0:T(8,128)(2,1)}) custom-call(bf16[2,512,1792]{2,1,0:T(8,128)(2,1)} %bitcast.305, bf16[2,448,1216]{2,1,0:T(8,128)(2,1)} %maximum_maximum_fusion.refs_1_), custom_call_target="tpu_custom_call" | custom-call | tf_op jit(solution)/shard_map/comm3/pallas_call | solution.py:655
  318.8 4.6 multiply_reduce_fusion.4
  324.1 1.3 multiply_convert_fusion.2
  325.5 7.4 fusion.81
  332.9 3.6 fusion.50
  336.5 2.4 pad_maximum_fusion.refs_2_
  339.0 6.3 fusion.11
  345.3 3.1 multiply_convert_fusion.1.refs_1_
  348.4 8.8 %convolution_convert_fusion.3 = bf16[1024,1792]{1,0:T(8,128)(2,1)} fusion(bf16[1792,1216]{1,0:T(8,128)(2,1)} %bitcast.361, bf16[1024,608]{1,0:T(8,128)(2,1)S(1)} %get-tuple-element.225, bf16[1024,608]{1,0:T(8,128)(2,1)S(1)} %get-tuple-element.224), kind=kOutput, calls=%fused_computation.80 | convolution fusion | flops 4469555200 | bytes 10518528 | tf_op jit(solution)/shard_map/tc,dc->td/dot_general | solution.py:1207
  357.1 59.5 %comm5.1 = (bf16[2,512,1792]{2,1,0:T(8,128)(2,1)}, bf16[1792,1216]{1,0:T(8,128)(2,1)}, bf16[1792,608]{1,0:T(8,128)(2,1)}) custom-call(bf16[2,512,1792]{2,1,0:T(8,128)(2,1)} %bitcast.311, bf16[1024,1792]{1,0:T(8,128)(2,1)} %multiply_convert_fusion.1.refs_1_, bf16[1024,1216]{1,0:T(8,128)(2,1)} %pad_maximum_fusion.refs_2_, bf16[1024,1792]{1,0:T(8,128)(2,1)} %bitcast.302, ...), custom_call_target="tpu_custom_call" | custom-call | tf_op jit(solution)/shard_map/comm5/pallas_call | solution.py:655
  416.7 5.9 multiply_reduce_fusion
  424.1 5.9 fusion.78.refs_4_
  430.1 3.1 fusion.41.bg
  433.5 18.6 %attention11.2 = (bf16[2,512,512]{2,1,0:T(8,128)(2,1)S(1)}, f32[8,256]{1,0:T(8,128)S(1)}) custom-call(f32[2,512,256]{2,1,0:T(8,128)S(1)} %fusion.41.bg, f32[2,512,512]{2,1,0:T(8,128)} %copy-done.2, f32[2,512,256]{2,1,0:T(8,128)S(1)} %get-tuple-element.75.att, f32[2,512,256]{2,1,0:T(8,128)S(1)} %get-tuple-element.76.conv, ...), custom_call_target="tpu_custom_call" | custom-call | tf_op jit(solution)/shard_map/attention11/pallas_call | solution.py:1080
  452.1 4.0 convolution_convert_fusion.2
  456.1 60.4 %comm8.1 = (bf16[2,512,1792]{2,1,0:T(8,128)(2,1)}, bf16[2,4,448,1216]{3,2,1,0:T(8,128)(2,1)}, bf16[1792,512]{1,0:T(8,128)(2,1)}, bf16[1792,256]{1,0:T(8,128)(2,1)S(1)}) custom-call(bf16[2,512,1792]{2,1,0:T(8,128)(2,1)} %bitcast.316, bf16[4,448,1216]{2,1,0:T(8,128)(2,1)} %bitcast.308, bf16[1024,1792]{1,0:T(8,128)(2,1)} %get-tuple-element.218.refs_2_, ...), custom_call_target="tpu_custom_call" | custom-call | tf_op jit(solution)/shard_map/comm8/pallas_call | solution.py:655
  516.5 5.0 fusion.5
  521.9 9.4 %fusion.17.refs_6_ = bf16[1024,1792]{1,0:T(8,128)(2,1)} fusion(bf16[1024,1792]{1,0:T(8,128)(2,1)} %copy-done.33, bf16[2,512,1792]{2,1,0:T(8,128)(2,1)} %get-tuple-element.81, f32[1024]{0:T(1024)S(1)} %multiply_multiply_fusion.3, f32[1792]{0:T(1024)S(1)} %get-tuple-element.210, f32[1024]{0:T(1024)S(1)} %rsqrt.66, f32[1024]{0:T(1024)S(1)} %multiply_multiply_fusion.5, ...), kind=kLoop, calls=%fused_computation.41 | loop fusion | flops 34865152 | bytes 22050816 | tf_op jit(solution)/shard_map/convert_element_type | solution.py:1343
  531.3 8.2 fusion.15
  539.6 7.5 fusion.53
  547.0 2.4 pad_maximum_fusion.1.refs_5_
  549.5 6.7 convolution_convert_fusion.1
  556.2 61.6 %comm6.1 = (bf16[2,512,1792]{2,1,0:T(8,128)(2,1)}, bf16[2,4,448,608]{3,2,1,0:T(8,128)(2,1)}, bf16[2,4,448,512]{3,2,1,0:T(8,128)(2,1)}, bf16[2,4,448,256]{3,2,1,0...) custom-call(bf16[2,512,1792]{2,1,0:T(8,128)(2,1)} %bitcast.309, bf16[4,448,608]{2,1,0:T(8,128)(2,1)} %bitcast.317, ...), custom_call_target="tpu_custom_call" | custom-call | tf_op jit(solution)/shard_map/comm6/pallas_call | solution.py:655
  617.9 5.9 multiply_reduce_fusion.1
  625.3 7.5 fusion.20
  632.8 3.1 fusion.39.bg
  635.9 18.7 %attention11.3 = (bf16[2,512,512]{2,1,0:T(8,128)(2,1)S(1)}, f32[8,256]{1,0:T(8,128)S(1)}) custom-call(f32[2,512,256]{2,1,0:T(8,128)S(1)} %fusion.39.bg, f32[2,512,512]{2,1,0:T(8,128)} %copy-done.1, f32[2,512,256]{2,1,0:T(8,128)S(1)} %get-tuple-element.87.att, f32[2,512,256]{2,1,0:T(8,128)S(1)} %get-tuple-element.88.conv, ...), custom_call_target="tpu_custom_call" | custom-call | tf_op jit(solution)/shard_map/attention11/pallas_call | solution.py:1080
  654.6 4.0 convolution_convert_fusion
  658.6 62.1 %comm7.1 = (bf16[2,512,1792]{2,1,0:T(8,128)(2,1)}, bf16[2,4,448,1216]{3,2,1,0:T(8,128)(2,1)}, bf16[1792,512]{1,0:T(8,128)(2,1)}, bf16[1792,256]{1,0:T(8,128)(2,1)S(1)}) custom-call(bf16[2,512,1792]{2,1,0:T(8,128)(2,1)} %bitcast.310, bf16[4,448,1216]{2,1,0:T(8,128)(2,1)} %bitcast.307, ...), custom_call_target="tpu_custom_call", output_to_operand_aliasing={{1}: (2, {})} | custom-call | tf_op jit(solution)/shard_map/comm7/pallas_call | solution.py:655
  720.7 4.6 fusion.9
  725.5 4.6 convolution_convert_fusion.4
  730.0 69.6 %comm9.1 = (bf16[2,512,1792]{2,1,0:T(8,128)(2,1)}, bf16[2,4,448,608]{3,2,1,0:T(8,128)(2,1)}, bf16[2,4,448,512]{3,2,1,0:T(8,128)(2,1)}, bf16[2,4,448,256]{3,2,1,0...) custom-call(bf16[2,512,1792]{2,1,0:T(8,128)(2,1)} %bitcast.315, ...), custom_call_target="tpu_custom_call", output_to_operand_aliasing={{1}: (4, {}), {2}: (5, {}), {3}: (6, {})} | custom-call | tf_op jit(solution)/shard_map/comm9/pallas_call | solution.py:655
  799.6 3.4 convert_reduce_fusion.1
  803.2 1.8 maximum_bitcast_fusion.2
  805.0 5.7 convert_reduce_fusion
  811.4 1.8 maximum_bitcast_fusion.1
  813.2 1.8 maximum_bitcast_fusion
  815.7 1.2 copy.193
  816.9 2.8 convert_reduce_fusion.2
  824.4 12.1 %fusion.34 = bf16[1,2,512,1792]{3,2,1,0:T(8,128)(2,1)} fusion(bf16[2,512,1792]{2,1,0:T(8,128)(2,1)} %fusion.15, bf16[2,512,1792]{2,1,0:T(8,128)(2,1)} %param.16, bf16[2,512,1792]{2,1,0:T(8,128)(2,1)} %get-tuple-element.99, f32[2,512]{1,0:T(2,128)S(1)} %multiply_multiply_fusion, f32[1792]{0:T(1024)S(1)} %copy-done.48, f32[2,512]{1,0:T(2,128)S(1)} %copy-done.54, ...), kind=kLoop, calls=%fused_computation.87 | loop fusion | flops 36700160 | bytes 22050816 | tf_op jit(solution)/shard_map/jit(_where)/select_n | solution.py:1382
  836.5 3.5 fusion.32
  (247 shorter events, 22.1 us)
Async XLA Ops:
  2.8 5.2 copy-start.60
  3.8 7.8 copy-start.51
  4.6 7.2 copy-start.52
  7.6 5.7 copy-start.46
  10.1 42.4 %copy-start.11 = (f32[8,256]{1,0:T(8,128)}, f32[8,256]{1,0:T(8,128)S(1)}, u32[]{:S(2)}) copy-start(f32[8,256]{1,0:T(8,128)S(1)} %get-tuple-element.265.taps) | copy-start | bytes 24580
  11.6 31.7 %copy-start.61 = (bf16[1,1792]{1,0:T(2,128)(2,1)S(1)}, bf16[1,1792]{1,0:T(2,128)(2,1)}, u32[]{:S(2)}) copy-start(bf16[1,1792]{1,0:T(2,128)(2,1)} %param.18) | copy-start | bytes 10756
  43.3 22.3 %copy-start.8 = (bf16[4,448,256]{2,1,0:T(8,128)(2,1)}, bf16[4,448,256]{2,1,0:T(8,128)(2,1)S(1)}, u32[]{:S(2)}) copy-start(bf16[4,448,256]{2,1,0:T(8,128)(2,1)S(1)} %get-tuple-element.63) | copy-start | bytes 2752516
  43.3 5.5 copy-start.13
  45.3 7.1 copy-start.47
  48.2 4.3 copy-start.57
  48.8 3.7 copy-start.53
  48.8 3.7 copy-start.3
  48.8 3.8 copy-start.10
  52.5 16.2 %copy-start.1 = (f32[2,512,512]{2,1,0:T(8,128)}, f32[2,512,512]{2,1,0:T(8,128)S(1)}, u32[]{:S(2)}) copy-start(f32[2,512,512]{2,1,0:T(8,128)S(1)} %fusion.35.proj) | copy-start | bytes 6291460
  71.9 73.8 %copy-start = (bf16[2,448,608]{2,1,0:T(8,128)(2,1)}, bf16[2,448,608]{2,1,0:T(8,128)(2,1)S(1)}, u32[]{:S(2)}) copy-start(bf16[2,448,608]{2,1,0:T(8,128)(2,1)S(1)} %pad_maximum_fusion.2.refs_2_.refs_3_) | copy-start | bytes 3268612
  72.0 70.2 %copy-start.14 = (bf16[2,512,1792]{2,1,0:T(8,128)(2,1)S(1)}, bf16[2,512,1792]{2,1,0:T(8,128)(2,1)}, u32[]{:S(2)}) copy-start(bf16[2,512,1792]{2,1,0:T(8,128)(2,1)} %param.16) | copy-start | bytes 11010052
  142.2 4.1 copy-start.62
  142.2 6.0 copy-start.23
  142.2 7.3 slice-start
  145.7 3.8 copy-start.49
  157.6 5.4 copy-start.40
  163.1 62.1 %copy-start.15 = (bf16[2,512,1792]{2,1,0:T(8,128)(2,1)S(1)}, bf16[2,512,1792]{2,1,0:T(8,128)(2,1)}, u32[]{:S(2)}) copy-start(bf16[2,512,1792]{2,1,0:T(8,128)(2,1)} %param.16) | copy-start | bytes 11010052
  225.2 7.1 copy-start.68
  236.5 16.1 %copy-start.2 = (f32[2,512,512]{2,1,0:T(8,128)}, f32[2,512,512]{2,1,0:T(8,128)S(1)}, u32[]{:S(2)}) copy-start(f32[2,512,512]{2,1,0:T(8,128)S(1)} %fusion.37.proj) | copy-start | bytes 6291460
  318.8 4.6 copy-start.19
  318.8 5.3 copy-start.26
  325.5 7.4 copy-start.30
  325.5 7.4 copy-start.63
  332.9 6.1 copy-start.24
  345.3 3.1 copy-start.33
  416.7 6.0 copy-start.20
  416.7 6.4 copy-start.31
  416.7 7.4 copy-start.34
  424.1 6.0 copy-start.27
  424.1 6.0 copy-start.35
  433.1 19.0 %copy-start.69 = (bf16[4,448,512]{2,1,0:T(8,128)(2,1)S(1)}, bf16[4,448,512]{2,1,0:T(8,128)(2,1)}, u32[]{:S(2)}) copy-start(bf16[4,448,512]{2,1,0:T(8,128)(2,1)} %get-tuple-element.68) | copy-start | bytes 5505028
  452.1 4.0 copy-start.7
  516.5 5.1 copy-start.21
  516.5 5.3 copy-start.32
  521.8 9.5 %copy-start.28 = (bf16[2,512,1792]{2,1,0:T(8,128)(2,1)S(1)}, bf16[2,512,1792]{2,1,0:T(8,128)(2,1)}, u32[]{:S(2)}) copy-start(bf16[2,512,1792]{2,1,0:T(8,128)(2,1)} %get-tuple-element.221) | copy-start | bytes 11010052
  521.9 9.5 %copy-start.36 = (bf16[2,512,1792]{2,1,0:T(8,128)(2,1)S(1)}, bf16[2,512,1792]{2,1,0:T(8,128)(2,1)}, u32[]{:S(2)}) copy-start(bf16[2,512,1792]{2,1,0:T(8,128)(2,1)} %get-tuple-element.74) | copy-start | bytes 11010052
  531.3 8.2 copy-start.66
  539.6 9.9 %slice-start.2 = ((s8[4587520]{0:T(1024)(128)(4,1)}), s8[4194304]{0:T(1024)(128)(4,1)S(1)}, s32[]{:S(2)}) async-start(s8[4587520]{0:T(1024)(128)(4,1)} %bitcast.357), calls=%async_computation.2 | async-start | bytes 8388608
  539.6 9.9 %slice-start.3 = ((s8[4587520]{0:T(1024)(128)(4,1)}), s8[393216]{0:T(1024)(128)(4,1)S(1)}, s32[]{:S(2)}) async-start(s8[4587520]{0:T(1024)(128)(4,1)} %bitcast.357), calls=%async_computation.3 | async-start | bytes 786432
  556.2 61.6 %copy-start.50 = (f32[2,512]{1,0:T(2,128)S(1)}, f32[2,512]{1,0:T(2,128)}, u32[]{:S(2)}) copy-start(f32[2,512]{1,0:T(2,128)} %copy-done.49) | copy-start | bytes 12292
  617.8 6.0 copy-start.59
  617.9 6.0 copy-start.17
  617.9 6.4 copy-start.25
  617.9 7.4 copy-start.37
  617.9 7.4 copy-start.48
  625.3 7.5 copy-start.56
  625.3 7.5 copy-start.9
  625.3 7.5 copy-start.38
  635.9 18.7 %copy-start.67 = (bf16[4,448,512]{2,1,0:T(8,128)(2,1)S(1)}, bf16[4,448,512]{2,1,0:T(8,128)(2,1)}, u32[]{:S(2)}) copy-start(bf16[4,448,512]{2,1,0:T(8,128)(2,1)} %get-tuple-element.61) | copy-start | bytes 5505028
  654.6 4.0 copy-start.6
  654.6 4.0 copy-start.5
  658.6 62.1 %copy-start.18 = (bf16[2,512,1792]{2,1,0:T(8,128)(2,1)S(1)}, bf16[2,512,1792]{2,1,0:T(8,128)(2,1)}, u32[]{:S(2)}) copy-start(bf16[2,512,1792]{2,1,0:T(8,128)(2,1)} %param.16) | copy-start | bytes 11010052
  658.6 62.1 %copy-start.54 = (f32[2,512]{1,0:T(2,128)S(1)}, f32[2,512]{1,0:T(2,128)}, u32[]{:S(2)}) copy-start(f32[2,512]{1,0:T(2,128)} %copy-done.53) | copy-start | bytes 12292
  720.7 4.7 copy-start.64
  811.4 3.6 copy-start.39
  819.9 4.5 copy-start.58
  824.3 12.1 %copy-start.22 = (bf16[2,512,1792]{2,1,0:T(8,128)(2,1)S(1)}, bf16[2,512,1792]{2,1,0:T(8,128)(2,1)}, u32[]{:S(2)}) copy-start(bf16[2,512,1792]{2,1,0:T(8,128)(2,1)} %get-tuple-element.71) | copy-start | bytes 11010052
  824.4 12.1 %copy-start.29 = (bf16[2,512,1792]{2,1,0:T(8,128)(2,1)S(1)}, bf16[2,512,1792]{2,1,0:T(8,128)(2,1)}, u32[]{:S(2)}) copy-start(bf16[2,512,1792]{2,1,0:T(8,128)(2,1)} %get-tuple-element.221) | copy-start | bytes 11010052
  824.4 12.1 %copy-start.42 = (bf16[2,512,1792]{2,1,0:T(8,128)(2,1)S(1)}, bf16[2,512,1792]{2,1,0:T(8,128)(2,1)}, u32[]{:S(2)}) copy-start(bf16[2,512,1792]{2,1,0:T(8,128)(2,1)} %get-tuple-element.102) | copy-start | bytes 11010052
  (10 other events, 23.5 us)

commit v6 on v5

--- a/solution.py
+++ b/solution.py
@@ -61,16 +61,18 @@
 
 
 PIECES = 4
+FIRST_TILE = 8
+LEAD = 3
 
 
 class LineSum:
-    def __init__(self, p_ref, o_ref, scratch, chunks, lag):
-        self.p_ref, self.o_ref, self.chunks, self.lag = p_ref, o_ref, chunks, lag
-        self.pin, self.low, self.high, self.out = scratch[:4]
-        self.ps, self.pr, self.rs, self.rl, self.rh, self.bs, self.br, self.ts, self.tr = scratch[4:]
+    def __init__(self, lhs, w, o_ref, scratch, chunks, lag):
+        self.lhs, self.w, self.o_ref, self.chunks, self.lag = lhs, w, o_ref, chunks, lag
+        self.p_ref, self.pin, self.low, self.high, self.out = scratch[:5]
+        self.ps, self.pr, self.rs, self.rl, self.rh, self.bs, self.br, self.ts, self.tr = scratch[5:]
         self.z, self.n = lax.axis_index("head"), lax.axis_size("head")
         self.core = lax.axis_index("section")
-        self.half = p_ref.shape[1] // 2
+        self.half = lhs.shape[1] // 2
         self.step = self.half // chunks
         self.depth = max((self.n - 1) // 2, self.n - 1 - (self.n - 1) // 2)
         self.turns = chunks + 2 * self.depth * lag
@@ -79,7 +81,8 @@
     def scratch(rows, width, chunks):
         dma = pltpu.SemaphoreType.DMA
         each = dma((2, chunks))
-        return [pltpu.VMEM((rows, width), jnp.bfloat16)] * 4 + [
+        whole = pltpu.VMEM((2, rows, width), jnp.bfloat16)
+        return [whole] + [pltpu.VMEM((rows, width), jnp.bfloat16)] * 4 + [
             dma((1,)), dma((2, PIECES)), dma((2,)), each, each, dma((2, 2)), each, dma((1,)), dma((1,))
         ]
 
@@ -121,10 +124,21 @@
         at = self.o_ref.at[self.core, r]
         return remote(at, at, self.ts.at[0], self.tr.at[0], section=1 - self.core)
 
-    def start(self):
-        for k in range(PIECES):
-            for d in range(2):
-                self.part(d, k).start()
+    def make(self, i):
+        size = self.half // PIECES
+        places = [
+            (m, pl.ds(pl.multiple_of(d * self.half + i * size, size), size))
+            for m in range(2)
+            for d in range(2)
+        ]
+        left = jnp.concatenate([self.lhs[m, r, :] for m, r in places], axis=0)
+        made = lax.dot_general(
+            left, self.w[...], (((1,), (1,)), ((), ())), preferred_element_type=jnp.float32
+        ).astype(jnp.bfloat16)
+        for at, (m, r) in enumerate(places):
+            self.p_ref[m, r, :] = made[at * size : (at + 1) * size]
+        for d in range(2):
+            self.part(d, i).start()
 
     def gathered(self, d, k):
         r = self.rng(d, k)
@@ -555,7 +569,7 @@
         return taken
 
     p_in, w_in, g_in, _, m_in, s_in = (
-        take(has_sum), take(count_in), take(count_out), take(kept), take(2 * count_made),
+        take(2 * has_sum), take(count_in), take(count_out), take(kept), take(2 * count_made),
         take(small_in),
     )
     p_out, w_out, g_out, m_out, s_out = (
@@ -565,8 +579,7 @@
     jobs = []
     later = []
     if has_sum:
-        line = LineSum(p_in[0], p_out[0], take(13), chunks, lag)
-        line.start()
+        line = LineSum(p_in[0], p_in[1], p_out[0], take(14), chunks, lag)
     if count_in:
         weights = Gather(layer_in, w_in, w_out, take(5))
         jobs.append(weights)
@@ -587,8 +600,12 @@
         tiles = sum(product.tiles for product in made)
 
         def turn(t, carry):
-            line.turn(t)
-            i = t - 2
+            @pl.when((t < LEAD * PIECES) & (t % LEAD == 0))
+            def _():
+                line.make(t // LEAD)
+
+            line.turn(t - LEAD)
+            i = t - LEAD - FIRST_TILE
             for product in made:
 
                 @pl.when((i >= 0) & (i < product.tiles))
@@ -598,14 +615,14 @@
                 i = i - product.tiles
             for when, act in later:
 
-                @pl.when(t == when)
+                @pl.when(t == when + LEAD)
                 def _(act=act):
                     act()
 
             return carry
 
-        last = max([line.turns, tiles + 2] + [when + 1 for when, _ in later])
-        lax.fori_loop(0, last, turn, 0)
+        last = max([line.turns, tiles + FIRST_TILE] + [when + 1 for when, _ in later])
+        lax.fori_loop(0, last + LEAD, turn, 0)
         line.finish()
     else:
         for _, act in later:
@@ -620,12 +637,15 @@
     n = lax.axis_size("seq")
     layer_in, w_in = gather if gather else (0, [])
     layer_out, g_in = scatter if scatter else (0, [])
-    p_in = [] if partial is None else [partial]
+    p_in = [] if partial is None else list(partial)
+    has_sum = 0 if partial is None else 1
+    if has_sum:
+        summed = (partial[0].shape[0], partial[0].shape[1], partial[1].shape[0])
     m_in = [a for pair in products for a in pair]
     vmem, anywhere = pl.BlockSpec(memory_space=pltpu.VMEM), pl.BlockSpec(memory_space=pl.ANY)
     scratch = []
     if p_in:
-        scratch += LineSum.scratch(partial.shape[1], partial.shape[2], chunks)
+        scratch += LineSum.scratch(summed[1], summed[2], chunks)
     if w_in:
         scratch += Gather.scratch(len(w_in), n)
     if g_in:
@@ -641,28 +661,29 @@
             jax.ShapeDtypeStruct((2 * depth, 8, narrow), jnp.float32),
         ]
     shapes = (
-        [jax.ShapeDtypeStruct(p.shape, jnp.bfloat16) for p in p_in]
+        ([jax.ShapeDtypeStruct(summed, jnp.bfloat16)] if has_sum else [])
         + [jax.ShapeDtypeStruct((n,) + w.shape[1:], jnp.bfloat16) for w in w_in]
         + [jax.ShapeDtypeStruct((2,) + g.shape, jnp.bfloat16) for g in g_in]
         + [jax.ShapeDtypeStruct((a.shape[1], b.shape[1]), jnp.bfloat16) for a, b in products]
         + s_shapes
     )
     plan = (
-        len(p_in), layer_in, len(w_in), layer_out, len(g_in), len(into), len(products), len(s_in),
+        has_sum, layer_in, len(w_in), layer_out, len(g_in), len(into), len(products), len(s_in),
         chunks, lag,
     )
     first = len(p_in) + len(w_in)
+    first_out = has_sum + len(w_in)
     outs = pl.pallas_call(
         functools.partial(comm_kernel, plan),
         out_shape=shapes,
         in_specs=[vmem] * first
         + [anywhere] * (len(g_in) + len(into) + len(m_in))
         + [vmem] * len(s_in),
-        out_specs=[vmem] * len(p_in)
+        out_specs=[vmem] * has_sum
         + [anywhere] * (len(w_in) + len(g_in) + len(products))
         + [vmem] * len(s_shapes),
         scratch_shapes=scratch,
-        input_output_aliases={first + len(g_in) + i: first + i for i in range(len(into))},
+        input_output_aliases={first + len(g_in) + i: first_out + i for i in range(len(into))},
         name=f"comm{cid}",
         compiler_params=pltpu.CompilerParams(
             collective_id=cid, has_side_effects=True, vmem_limit_bytes=52 << 20
@@ -670,9 +691,9 @@
     )(*p_in, *w_in, *g_in, *into, *m_in, *s_in)
     return (
         outs[0] if p_in else None,
-        [a.reshape((-1,) + a.shape[2:]) for a in outs[len(p_in) : first]],
-        outs[first : first + len(g_in)],
-        outs[first + len(g_in) :],
+        [a.reshape((-1,) + a.shape[2:]) for a in outs[has_sum : first_out]],
+        outs[first_out : first_out + len(g_in)],
+        outs[first_out + len(g_in) :],
     )
 
 
@@ -1203,8 +1224,8 @@
     return grad.reshape((n, grad.shape[0] // n) + grad.shape[1:])
 
 
-def dot_t(a, b):
-    return jnp.einsum("tc,dc->td", a, b, preferred_element_type=jnp.float32)
+def held(a):
+    return lax.optimization_barrier(a.astype(jnp.bfloat16))
 
 
 def dot_n(a, b):
@@ -1256,7 +1277,7 @@
     hidden_cols = own_down.shape[2]
 
     def as_parts(flat):
-        return flat.astype(jnp.bfloat16).reshape(micro_count, rows, width)
+        return flat.reshape(micro_count, rows, -1)
 
     def spread(summed):
         return summed.astype(jnp.float32).reshape(total, width)
@@ -1271,8 +1292,8 @@
         normed = rms_norm(x, gains_one[layer]).astype(jnp.bfloat16)
         proj = dot_n(normed, w_mix[layer]).reshape(micro_count, rows, 2 * wide)
         gated, *attn = attention_forward(proj, taps_both[layer], marks, tables)
-        gated = gated.reshape(total, wide)
-        partial = as_parts(dot_t(gated, w_o[layer]))
+        gated_flat = gated.reshape(total, wide)
+        partial = (gated, w_o[layer])
         if layer == 0:
             summed, (w_gu[0], w_d[0]), _, _ = communicate(
                 2, partial=partial, gather=(0, [own_ffn, own_down])
@@ -1281,15 +1302,16 @@
             summed, (w_gu[1],), _, _ = communicate(3, partial=partial, gather=(1, [own_ffn]))
         middle = x + spread(summed)
         normed_two = rms_norm(middle, gains_two[layer]).astype(jnp.bfloat16)
-        both = dot_n(normed_two, w_gu[layer])
+        middle = held(middle).astype(jnp.float32)
+        both = held(dot_n(normed_two, w_gu[layer])).astype(jnp.float32)
         hidden = (jax.nn.silu(both[:, :hidden_cols]) * both[:, hidden_cols:]).astype(jnp.bfloat16)
-        partial = as_parts(dot_t(hidden, w_d[layer]))
-        kept[layer] = (x, normed, proj, gated, attn, middle, normed_two, both, hidden)
+        partial = (as_parts(hidden), w_d[layer])
+        kept[layer] = (x, normed, proj, gated_flat, attn, middle, normed_two, both, hidden)
         if layer == 0:
             summed, (w_mix[1], w_o[1], w_d[1]), _, _ = communicate(
                 4, partial=partial, gather=(1, [own_mix, own_out, own_down])
             )
-            outputs.append((middle + spread(summed)).astype(jnp.bfloat16))
+            outputs.append(held(middle + spread(summed)))
             x = outputs[0].astype(jnp.float32)
         else:
             last_partial = partial
@@ -1300,7 +1322,7 @@
     made = []
     into = [None] * 4
     for layer in (1, 0):
-        x, normed, proj, gated, attn, middle, normed_two, both, hidden = kept[layer]
+        x, normed, proj, gated_flat, attn, middle, normed_two, both, hidden = kept[layer]
         grad_wide = grad.astype(jnp.float32)
         back_hidden = dot_n(grad, w_d[layer])
         gate_pre, upward = both[:, :hidden_cols], both[:, hidden_cols:]
@@ -1312,7 +1334,7 @@
             ],
             axis=1,
         )
-        partial = as_parts(dot_t(back_both, w_gu[layer]))
+        partial = (as_parts(back_both), w_gu[layer])
         products = ((normed_two, back_both), (grad, hidden))
         if layer == 1:
             summed, _, _, (grad_gu, grad_d) = communicate(5, partial=partial, products=products)
@@ -1323,19 +1345,20 @@
         _, norm_back_two = jax.vjp(rms_norm, middle, gains_two[layer])
         back_middle, gain_two = norm_back_two(spread(summed))
         back_middle = grad_wide + back_middle
-        back_branch = back_middle.astype(jnp.bfloat16)
+        back_branch = held(back_middle)
+        back_middle = back_branch.astype(jnp.float32)
         back_gated = dot_n(back_branch, w_o[layer])
         back_proj, taps_grad = attention_backward(
             back_gated.reshape(micro_count, rows, wide), proj, attn, taps_both[layer], marks, tables
         )
-        back_proj = back_proj.reshape(total, 2 * wide)
-        partial = as_parts(dot_t(back_proj, w_mix[layer]))
+        back_flat = back_proj.reshape(total, 2 * wide)
+        partial = (back_proj, w_mix[layer])
         summed, _, into[:1], (grad_mix, grad_o) = communicate(
             7 + layer,
             partial=partial,
             scatter=(layer, [by_seq(grad_gu)]),
             into=into[:1] if layer == 0 else (),
-            products=((normed, back_proj), (back_branch, gated)),
+            products=((normed, back_flat), (back_branch, gated_flat)),
         )
         made = [by_seq(grad_d), by_seq(grad_mix), by_seq(grad_o)]
         _, norm_back_one = jax.vjp(rms_norm, x, gains_one[layer])

time: 851 us -> 804 us (0.945)
  matrix products: 75.8 us -> 27.6 us
  other arithmetic: 131 us -> 105 us
  local copies, waits for them, and re-layouts: 22.2 us -> 42.7 us
    dot_general x8 -> x0, matrix products: 38.5 us -> none  [dot_t(): return jnp.einsum('tc,dc->td', a, b, preferred_element_type=jnp.float32)]
    convert_element_type x2 -> x1, other arithmetic: 17.7 us -> 4.23 us  [on_device(): grad = (back_middle + back_x).astype(jnp.bfloat16)]
    dot_general x8, matrix products: 37.3 us -> 27.6 us  [dot_n(): return jnp.dot(a, b, preferred_element_type=jnp.float32)]
    optimization_barrier x0 -> x2, local copies, waits for them, and re-layouts: none -> 8.71 us  [held(): return lax.optimization_barrier(a.astype(jnp.bfloat16))]
    unnamed x157 -> x161, local copies, waits for them, and re-layouts: 9.48 us -> 17.3 us
    reduce_sum x4 -> x6, other arithmetic: 17.9 us -> 13.4 us  [rms_norm(): jnp.mean(vector * vector, axis=-1, keepdims=True) + epsilon]
where the time goes in v6:
time: 804 us; the launch traced here: 796 us
  Pallas kernels  612 us (76%)
  other arithmetic  105 us (13%)
  local copies, waits for them, and re-layouts  42.7 us (5%)
  matrix products  27.6 us (3%)
    pallas_call x9, Pallas kernels, communicate(): pl.pallas_call(functools.partial(comm_kernel, plan), out_shape=shapes, in...  548 us
    pallas_call x4, Pallas kernels, attention_call(): pl.pallas_call(functools.partial(kernel, seq_reach()), out_shape=shapes,...  64.3 us
    dot_general x8, matrix products, dot_n(): return jnp.dot(a, b, preferred_element_type=jnp.float32)  27.6 us
    reduce_sum x4, other arithmetic, rms_norm(): vector * lax.rsqrt(jnp.mean(vector * vector, axis=-1, keepdims=True) + ep...  19.7 us
    unnamed x161, local copies, waits for them, and re-layouts  17.3 us

profile of v6, /device:TPU:0, one launch (start us, length us, event | category | flops | bytes accessed | tf_op | source)
XLA Modules:
  0.0 795.8 jit_solution(7080983131887391737)
XLA Ops:
  2.7 2.8 fusion.29
  6.3 2.0 all-gather
  8.4 1.8 all-gather.1
  10.3 1.8 all_gather.10
  17.4 2.1 stack.150.col
  19.5 1.6 slice_bitcast_fusion.25
  21.1 2.4 pad_maximum_fusion.3.refs_0_.refs_2_
  23.8 1.2 pad_maximum_fusion.2.refs_3_.refs_4_
  25.6 2.2 maximum_maximum_fusion.refs_2_
  27.7 29.5 %comm1.1 = (bf16[4,448,512]{2,1,0:T(8,128)(2,1)}, bf16[4,448,256]{2,1,0:T(8,128)(2,1)S(1)}) custom-call(bf16[2,448,512]{2,1,0:T(8,128)(2,1)} %pad_maximum_fusion.3.refs_0_.refs_2_, bf16[2,448,256]{2,1,0:T(8,128)(2,1)S(1)} %fusion.52.refs_1_.refs_3_), custom_call_target="tpu_custom_call" | custom-call | tf_op jit(solution)/shard_map/comm1/pallas_call | solution.py:676
  57.3 4.0 fusion.35.proj
  61.3 13.1 %attention10.2 = (bf16[2,512,256]{2,1,0:T(8,128)(2,1)S(1)}, f32[2,512,256]{2,1,0:T(8,128)S(1)}, f32[2,512,256]{2,1,0:T(8,128)S(1)}, bf16[2,160,256]{2,1,0:T(8,128)(2,1)S(1)}, f32[1,2,16,256]{3,2,1,0:T(8,128)S(1)}) custom-call(f32[2,512,512]{2,1,0:T(8,128)S(1)} %fusion.35.proj, f32[2,512,8]{2,1,0:T(8,128)S(1)} %stack.150.col, ...), custom_call_target="tpu_custom_call" | custom-call | tf_op jit(solution)/shard_map/attention10/pallas_call | solution.py:1101
  76.4 68.1 %comm2.1 = (bf16[2,512,1792]{2,1,0:T(8,128)(2,1)}, bf16[4,448,1216]{2,1,0:T(8,128)(2,1)}, bf16[4,448,608]{2,1,0:T(8,128)(2,1)}) custom-call(bf16[2,512,256]{2,1,0:T(8,128)(2,1)S(1)} %get-tuple-element.62.refs_0_, bf16[1792,256]{1,0:T(8,128)(2,1)S(1)} %bitcast.258, bf16[2,448,1216]{2,1,0:T(8,128)(2,1)} %maximum_maximum_fusion.refs_2_, ...), custom_call_target="tpu_custom_call" | custom-call | tf_op jit(solution)/shard_map/comm2/pallas_call | solution.py:676
  144.6 3.5 multiply_reduce_fusion.1
  148.2 1.4 multiply_convert_fusion.2
  149.6 6.0 convolution_convert_fusion.1
  155.6 4.3 copy.186
  159.9 2.1 convert_element_type.179
  162.1 2.7 multiply_convert_fusion.5.refs_8_
  164.9 63.8 %comm4.1 = (bf16[2,512,1792]{2,1,0:T(8,128)(2,1)}, bf16[4,448,512]{2,1,0:T(8,128)(2,1)}, bf16[4,448,256]{2,1,0:T(8,128)(2,1)S(1)}, bf16[4,448,608]{2,1,0:T(8,128)(2,1)}) custom-call(bf16[2,512,608]{2,1,0:T(8,128)(2,1)} %bitcast.276, bf16[1792,608]{1,0:T(8,128)(2,1)} %bitcast.291, bf16[2,448,512]{2,1,0:T(8,128)(2,1)} %pad_maximum_fusion.3.refs_0_.refs_2_, ...), custom_call_target="tpu_custom_call" | custom-call | tf_op jit(solution)/shard_map/comm4/pallas_call | solution.py:676
  228.7 6.1 multiply_convert_fusion
  234.8 1.9 fusion.17
  238.5 1.9 copy-done.53
  240.3 2.0 fusion.68.proj
  242.4 13.1 %attention10.3 = (bf16[2,512,256]{2,1,0:T(8,128)(2,1)S(1)}, f32[2,512,256]{2,1,0:T(8,128)S(1)}, f32[2,512,256]{2,1,0:T(8,128)S(1)}, bf16[2,160,256]{2,1,0:T(8,128)(2,1)S(1)}, f32[1,2,16,256]{3,2,1,0:T(8,128)S(1)}) custom-call(f32[2,512,512]{2,1,0:T(8,128)S(1)} %fusion.68.proj, f32[2,512,8]{2,1,0:T(8,128)S(1)} %stack.150.col, ...), custom_call_target="tpu_custom_call" | custom-call | tf_op jit(solution)/shard_map/attention10/pallas_call | solution.py:1101
  258.1 66.3 %comm3.1 = (bf16[2,512,1792]{2,1,0:T(8,128)(2,1)}, bf16[4,448,1216]{2,1,0:T(8,128)(2,1)}) custom-call(bf16[2,512,256]{2,1,0:T(8,128)(2,1)S(1)} %get-tuple-element.69.refs_0_, bf16[1792,256]{1,0:T(8,128)(2,1)S(1)} %bitcast.260, bf16[2,448,1216]{2,1,0:T(8,128)(2,1)} %maximum_maximum_fusion.refs_2_), custom_call_target="tpu_custom_call" | custom-call | tf_op jit(solution)/shard_map/comm3/pallas_call | solution.py:676
  324.4 3.5 multiply_reduce_fusion
  328.0 2.9 multiply_convert_fusion.1
  330.9 1.9 copy-done.34
  333.9 6.1 convolution_convert_fusion
  339.9 4.4 copy.187
  344.3 2.3 convert_element_type.188
  347.9 3.7 fusion.43
  351.5 2.4 pad_maximum_fusion.refs_3_
  354.0 63.0 %comm5.1 = (bf16[2,512,1792]{2,1,0:T(8,128)(2,1)}, bf16[1792,1216]{1,0:T(8,128)(2,1)}, bf16[1792,608]{1,0:T(8,128)(2,1)}) custom-call(bf16[2,512,1216]{2,1,0:T(8,128)(2,1)} %bitcast.269, bf16[1792,1216]{1,0:T(8,128)(2,1)} %bitcast.277, bf16[1024,1792]{1,0:T(8,128)(2,1)} %copy-done.54, bf16[1024,1216]{1,0:T(8,128)(2,1)} %pad_maximum_fusion.refs_3_, ...), custom_call_target="tpu_custom_call" | custom-call | tf_op jit(solution)/shard_map/comm5/pallas_call | solution.py:676
  417.0 5.0 fusion.7
  422.1 3.2 fusion.9.refs_5_
  425.3 1.8 copy-done.45
  428.3 19.1 %attention11.2 = (bf16[2,512,512]{2,1,0:T(8,128)(2,1)S(1)}, f32[8,256]{1,0:T(8,128)S(1)}) custom-call(f32[2,512,256]{2,1,0:T(8,128)S(1)} %fusion.69.bg, f32[2,512,512]{2,1,0:T(8,128)} %copy-done.1, f32[2,512,256]{2,1,0:T(8,128)S(1)} %copy-done.17, f32[2,512,256]{2,1,0:T(8,128)S(1)} %copy-done.19, bf16[2,160,256]{2,1,0:T(8,128)(2,1)S(1)} %get-tuple-element.77.sin, ...), custom_call_target="tpu_custom_call" | custom-call | tf_op jit(solution)/shard_map/attention11/pallas_call | solution.py:1101
  448.5 61.4 %comm8.1 = (bf16[2,512,1792]{2,1,0:T(8,128)(2,1)}, bf16[2,4,448,1216]{3,2,1,0:T(8,128)(2,1)}, bf16[1792,512]{1,0:T(8,128)(2,1)}, bf16[1792,256]{1,0:T(8,128)(2,1)S(1)}) custom-call(bf16[2,512,512]{2,1,0:T(8,128)(2,1)} %copy-done.5, bf16[1792,512]{1,0:T(8,128)(2,1)} %bitcast.300, bf16[4,448,1216]{2,1,0:T(8,128)(2,1)} %bitcast.281, ...), custom_call_target="tpu_custom_call" | custom-call | tf_op jit(solution)/shard_map/comm8/pallas_call | solution.py:676
  509.9 5.0 fusion.5
  515.0 4.2 fusion.11.refs_7_
  519.3 3.7 fusion.46
  523.0 2.4 pad_maximum_fusion.1.refs_6_
  525.4 64.4 %comm6.1 = (bf16[2,512,1792]{2,1,0:T(8,128)(2,1)}, bf16[2,4,448,608]{3,2,1,0:T(8,128)(2,1)}, bf16[2,4,448,512]{3,2,1,0:T(8,128)(2,1)}, bf16[2,4,448,256]{3,2,1,0...) custom-call(bf16[2,512,1216]{2,1,0:T(8,128)(2,1)} %bitcast.270, bf16[1792,1216]{1,0:T(8,128)(2,1)} %bitcast.282, ...), custom_call_target="tpu_custom_call" | custom-call | tf_op jit(solution)/shard_map/comm6/pallas_call | solution.py:676
  589.8 5.0 fusion.6
  594.9 2.9 fusion.13.refs_6_
  597.8 1.8 copy-done.43
  600.8 19.0 %attention11.3 = (bf16[2,512,512]{2,1,0:T(8,128)(2,1)S(1)}, f32[8,256]{1,0:T(8,128)S(1)}) custom-call(f32[2,512,256]{2,1,0:T(8,128)S(1)} %fusion.70.bg, f32[2,512,512]{2,1,0:T(8,128)} %copy-done, f32[2,512,256]{2,1,0:T(8,128)S(1)} %copy-done.13, f32[2,512,256]{2,1,0:T(8,128)S(1)} %copy-done.15, bf16[2,160,256]{2,1,0:T(8,128)(2,1)S(1)} %get-tuple-element.89.sin, ...), custom_call_target="tpu_custom_call" | custom-call | tf_op jit(solution)/shard_map/attention11/pallas_call | solution.py:1101
  620.8 62.7 %comm7.1 = (bf16[2,512,1792]{2,1,0:T(8,128)(2,1)}, bf16[2,4,448,1216]{3,2,1,0:T(8,128)(2,1)}, bf16[1792,512]{1,0:T(8,128)(2,1)}, bf16[1792,256]{1,0:T(8,128)(2,1)S(1)}) custom-call(bf16[2,512,512]{2,1,0:T(8,128)(2,1)} %copy-done.4, bf16[1792,512]{1,0:T(8,128)(2,1)} %bitcast.297, bf16[4,448,1216]{2,1,0:T(8,128)(2,1)} %bitcast.286, ...), custom_call_target="tpu_custom_call", output_to_operand_aliasing={{1}: (3, {})} | custom-call | tf_op jit(solution)/shard_map/comm7/pallas_call | solution.py:676
  683.5 4.6 fusion.30
  688.1 6.0 fusion.38
  694.2 68.8 %comm9.1 = (bf16[2,512,1792]{2,1,0:T(8,128)(2,1)}, bf16[2,4,448,608]{3,2,1,0:T(8,128)(2,1)}, bf16[2,4,448,512]{3,2,1,0:T(8,128)(2,1)}, bf16[2,4,448,256]{3,2,1,0...) custom-call(bf16[2,512,608]{2,1,0:T(8,128)(2,1)} %bitcast.253, ...), custom_call_target="tpu_custom_call", output_to_operand_aliasing={{1}: (5, {}), {2}: (6, {}), {3}: (7, {})} | custom-call | tf_op jit(solution)/shard_map/comm9/pallas_call | solution.py:676
  763.1 5.4 fusion.37
  770.5 1.2 copy.195
  771.7 2.8 convert_reduce_fusion.2
  775.9 1.2 maximum_bitcast_fusion.4
  778.0 1.2 maximum_bitcast_fusion.3
  779.2 3.8 convert_reduce_fusion.1
  783.1 1.8 maximum_bitcast_fusion.2
  784.9 3.6 convert_reduce_fusion
  788.5 3.2 slice_bitcast_fusion.3
  791.7 1.8 maximum_bitcast_fusion.1
  793.5 1.8 maximum_bitcast_fusion
  (247 shorter events, 26.5 us)
Async XLA Ops:
  0.6 7.7 copy-start.68
  0.7 12.6 %copy-start.63 = (bf16[1,448,448]{2,1,0:T(8,128)(2,1)S(1)}, bf16[1,448,448]{2,1,0:T(8,128)(2,1)}, u32[]{:S(2)}) copy-start(bf16[1,448,448]{2,1,0:T(8,128)(2,1)} %param.24) | copy-start | bytes 1204228
  0.7 9.6 %copy-start.66 = (bf16[1,3,1792]{2,1,0:T(4,128)(2,1)S(1)}, bf16[1,3,1792]{2,1,0:T(4,128)(2,1)}, u32[]{:S(2)}) copy-start(bf16[1,3,1792]{2,1,0:T(4,128)(2,1)} %param.23) | copy-start | bytes 32260
  0.7 11.5 %copy-start.65 = (bf16[1,448,64]{1,2,0:T(8,128)(2,1)S(1)}, bf16[1,448,64]{1,2,0:T(8,128)(2,1)}, u32[]{:S(2)}) copy-start(bf16[1,448,64]{1,2,0:T(8,128)(2,1)} %param.20) | copy-start | bytes 172036
  0.7 11.5 %copy-start.64 = (bf16[1,448,64]{1,2,0:T(8,128)(2,1)S(1)}, bf16[1,448,64]{1,2,0:T(8,128)(2,1)}, u32[]{:S(2)}) copy-start(bf16[1,448,64]{1,2,0:T(8,128)(2,1)} %param.19) | copy-start | bytes 172036
  0.7 5.6 copy-start.67
  13.7 14.0 %copy-start.6 = (bf16[2,448,256]{2,1,0:T(8,128)(2,1)}, bf16[2,448,256]{2,1,0:T(8,128)(2,1)S(1)}, u32[]{:S(2)}) copy-start(bf16[2,448,256]{2,1,0:T(8,128)(2,1)S(1)} %fusion.52.refs_1_.refs_3_) | copy-start | bytes 1376260
  19.5 4.0 copy-start.62
  21.1 3.9 copy-start.60
  21.1 3.8 copy-start.61
  25.6 31.7 %copy-start.31 = (bf16[2,512,1792]{2,1,0:T(8,128)(2,1)S(1)}, bf16[2,512,1792]{2,1,0:T(8,128)(2,1)}, u32[]{:S(2)}) copy-start(bf16[2,512,1792]{2,1,0:T(8,128)(2,1)} %param.16) | copy-start | bytes 11010052
  57.2 19.2 %copy-start.20 = (bf16[4,448,256]{2,1,0:T(8,128)(2,1)}, bf16[4,448,256]{2,1,0:T(8,128)(2,1)S(1)}, u32[]{:S(2)}) copy-start(bf16[4,448,256]{2,1,0:T(8,128)(2,1)S(1)} %get-tuple-element.63) | copy-start | bytes 2752516
  57.3 4.0 copy-start.2
  57.3 4.0 copy-start.24
  61.3 83.3 %copy-start = (f32[2,512,512]{2,1,0:T(8,128)}, f32[2,512,512]{2,1,0:T(8,128)S(1)}, u32[]{:S(2)}) copy-start(f32[2,512,512]{2,1,0:T(8,128)S(1)} %fusion.35.proj) | copy-start | bytes 6291460
  76.4 71.7 %copy-start.8 = (bf16[2,512,256]{2,1,0:T(8,128)(2,1)}, bf16[2,512,256]{2,1,0:T(8,128)(2,1)S(1)}, u32[]{:S(2)}) copy-start(bf16[2,512,256]{2,1,0:T(8,128)(2,1)S(1)} %get-tuple-element.62.refs_0_) | copy-start | bytes 1572868
  76.4 71.7 %copy-start.25 = (f32[1,2,16,256]{3,2,1,0:T(8,128)}, f32[1,2,16,256]{3,2,1,0:T(8,128)S(1)}, u32[]{:S(2)}) copy-start(f32[1,2,16,256]{3,2,1,0:T(8,128)S(1)} %get-tuple-element.90.edge) | copy-start | bytes 98308
  144.6 3.6 copy-start.42
  144.6 5.0 slice-start.7
  162.1 2.8 copy-start.47
  162.1 2.8 copy-start.7
  164.9 63.8 %copy-start.32 = (bf16[2,512,1792]{2,1,0:T(8,128)(2,1)S(1)}, bf16[2,512,1792]{2,1,0:T(8,128)(2,1)}, u32[]{:S(2)}) copy-start(bf16[2,512,1792]{2,1,0:T(8,128)(2,1)} %param.16) | copy-start | bytes 11010052
  228.7 29.4 %copy-start.22 = (bf16[4,448,256]{2,1,0:T(8,128)(2,1)}, bf16[4,448,256]{2,1,0:T(8,128)(2,1)S(1)}, u32[]{:S(2)}) copy-start(bf16[4,448,256]{2,1,0:T(8,128)(2,1)S(1)} %get-tuple-element.70) | copy-start | bytes 2752516
  228.7 6.1 copy-start.56
  236.7 91.2 %copy-start.29 = (bf16[1024,1792]{1,0:T(8,128)(2,1)}, bf16[1024,1792]{1,0:T(8,128)(2,1)S(1)}, u32[]{:S(2)}) copy-start(bf16[1024,1792]{1,0:T(8,128)(2,1)S(1)} %get-tuple-element.246) | copy-start | bytes 11010052
  237.6 2.8 copy-start.59
  242.4 85.5 %copy-start.1 = (f32[2,512,512]{2,1,0:T(8,128)}, f32[2,512,512]{2,1,0:T(8,128)S(1)}, u32[]{:S(2)}) copy-start(f32[2,512,512]{2,1,0:T(8,128)S(1)} %fusion.68.proj) | copy-start | bytes 6291460
  258.1 69.8 %copy-start.10 = (bf16[2,512,256]{2,1,0:T(8,128)(2,1)}, bf16[2,512,256]{2,1,0:T(8,128)(2,1)S(1)}, u32[]{:S(2)}) copy-start(bf16[2,512,256]{2,1,0:T(8,128)(2,1)S(1)} %get-tuple-element.69.refs_0_) | copy-start | bytes 1572868
  324.4 3.6 copy-start.50
  327.9 5.9 slice-start.5
  328.0 5.9 slice-start.6
  330.9 3.0 copy-start.54
  344.3 2.8 copy-start.51
  344.3 3.5 copy-start.58
  351.5 65.5 %copy-start.3 = (bf16[1024,608]{1,0:T(8,128)(2,1)}, bf16[1024,608]{1,0:T(8,128)(2,1)S(1)}, u32[]{:S(2)}) copy-start(bf16[1024,608]{1,0:T(8,128)(2,1)S(1)} %get-tuple-element.239.refs_5_) | copy-start | bytes 3735556
  354.0 63.1 %copy-start.35 = (bf16[1024,1792]{1,0:T(8,128)(2,1)S(1)}, bf16[1024,1792]{1,0:T(8,128)(2,1)}, u32[]{:S(2)}) copy-start(bf16[1024,1792]{1,0:T(8,128)(2,1)} %copy-done.34) | copy-start | bytes 11010052
  417.0 5.1 copy-start.49
  417.0 5.1 copy-start.52
  422.1 5.1 copy-start.23
  425.3 3.0 copy-start.17
  425.3 3.0 copy-start.19
  425.3 3.0 copy-start.28
  428.3 20.1 %copy-start.11 = (bf16[2,512,256]{2,1,0:T(8,128)(2,1)S(1)}, bf16[2,512,256]{2,1,0:T(8,128)(2,1)}, u32[]{:S(2)}) copy-start(bf16[2,512,256]{2,1,0:T(8,128)(2,1)} %copy-done.10) | copy-start | bytes 1572868
  448.4 61.4 %copy-start.30 = (bf16[1024,1792]{1,0:T(8,128)(2,1)S(1)}, bf16[1024,1792]{1,0:T(8,128)(2,1)}, u32[]{:S(2)}) copy-start(bf16[1024,1792]{1,0:T(8,128)(2,1)} %copy-done.29) | copy-start | bytes 11010052
  509.9 5.1 copy-start.46
  509.9 9.3 %slice-start.3 = ((s8[5242880]{0:T(1024)(128)(4,1)}), s8[4194304]{0:T(1024)(128)(4,1)S(1)}, s32[]{:S(2)}) async-start(s8[5242880]{0:T(1024)(128)(4,1)} %bitcast.271), calls=%async_computation.3 | async-start | bytes 8388608
  515.0 4.3 slice-start.4
  515.0 4.3 copy-start.57
  519.3 3.7 copy-start.39
  525.4 64.4 %copy-start.38 = (bf16[1024,1792]{1,0:T(8,128)(2,1)S(1)}, bf16[1024,1792]{1,0:T(8,128)(2,1)}, u32[]{:S(2)}) copy-start(bf16[1024,1792]{1,0:T(8,128)(2,1)} %copy-done.37) | copy-start | bytes 11010052
  589.8 5.1 copy-start.40
  589.8 5.1 copy-start.48
  594.9 4.8 copy-start.21
  597.8 3.0 copy-start.13
  597.8 3.0 copy-start.15
  597.8 3.0 copy-start.26
  600.8 19.9 %copy-start.9 = (bf16[2,512,256]{2,1,0:T(8,128)(2,1)S(1)}, bf16[2,512,256]{2,1,0:T(8,128)(2,1)}, u32[]{:S(2)}) copy-start(bf16[2,512,256]{2,1,0:T(8,128)(2,1)} %copy-done.8) | copy-start | bytes 1572868
  620.8 62.7 %copy-start.33 = (bf16[2,512,1792]{2,1,0:T(8,128)(2,1)S(1)}, bf16[2,512,1792]{2,1,0:T(8,128)(2,1)}, u32[]{:S(2)}) copy-start(bf16[2,512,1792]{2,1,0:T(8,128)(2,1)} %param.16) | copy-start | bytes 11010052
  683.5 4.7 copy-start.41
  683.5 4.7 copy-start.44
  694.2 68.8 %copy-start.36 = (bf16[1024,1792]{1,0:T(8,128)(2,1)S(1)}, bf16[1024,1792]{1,0:T(8,128)(2,1)}, u32[]{:S(2)}) copy-start(bf16[1024,1792]{1,0:T(8,128)(2,1)} %copy-done.34) | copy-start | bytes 11010052
  763.1 6.8 copy-start.55
  778.0 6.9 slice-start
  779.2 5.8 slice-start.1
  (14 other events, 19.3 us)

commit v7 on v6

--- a/solution.py
+++ b/solution.py
@@ -1254,8 +1254,8 @@
     total = micro_count * rows
 
     def halves(weight):
-        cols = weight.shape[1] // 2
-        return jnp.stack([weight[:, :cols], weight[:, cols:]])
+        middle = weight.shape[1] // 2
+        return jnp.stack([weight[:, :middle], weight[:, middle:]])
 
     own_mix = jnp.concatenate(
         [halves(w[0]) for w in (w_value, w_query, w_gate_conv, w_key)], axis=2
@@ -1264,8 +1264,13 @@
     keys = w_query.shape[2] // 2
     wide = values + keys
     own_out = jnp.pad(halves(w_out[0].T), ((0, 0), (0, 0), (0, keys)))
-    own_ffn = jnp.concatenate([halves(w_gate[0]), halves(w_up[0])], axis=2)
-    own_down = halves(w_down[0].T)
+    cols = w_gate.shape[2] // 2
+
+    def filled(half):
+        return jnp.pad(half, ((0, 0), (0, 0), (0, -cols % 128)))
+
+    own_ffn = jnp.concatenate([filled(halves(w_gate[0])), filled(halves(w_up[0]))], axis=2)
+    own_down = filled(halves(w_down[0].T))
     gains_one = lax.all_gather(gain_attn[0], "section").astype(jnp.float32)
     gains_two = lax.all_gather(gain_ffn[0], "section").astype(jnp.float32)
     taps_all = lax.all_gather(conv_taps[0], "section").astype(jnp.float32)
@@ -1391,9 +1396,9 @@
     grad_gconv = joined(grad_mix[:, :, wide : wide + values])
     grad_key = joined(grad_mix[:, :, wide + values :])
     grad_out = joined(grad_o[:, :, :values]).T
-    grad_gate = joined(grad_gu[:, :, :hidden_cols])
-    grad_up = joined(grad_gu[:, :, hidden_cols:])
-    grad_down = joined(grad_d).T
+    grad_gate = joined(grad_gu[:, :, :cols])
+    grad_up = joined(grad_gu[:, :, hidden_cols : hidden_cols + cols])
+    grad_down = joined(grad_d[:, :, :cols]).T
 
     gains = lax.dynamic_index_in_dim(gains[:4].reshape(2, 2, width), core, 1, False)
     taps_rows = lax.dynamic_index_in_dim(

time: 804 us -> 787 us (0.979)
  local copies, waits for them, and re-layouts: 42.7 us -> 29.4 us
    optimization_barrier x2 -> x0, local copies, waits for them, and re-layouts: 8.71 us -> none  [held(): return lax.optimization_barrier(a.astype(jnp.bfloat16))]
    unnamed x161 -> x111, local copies, waits for them, and re-layouts: 17.3 us -> 13.3 us
where the time goes in v7:
time: 787 us; the launch traced here: 779 us
  Pallas kernels  610 us (78%)
  other arithmetic  105 us (13%)
  local copies, waits for them, and re-layouts  29.4 us (4%)
  matrix products  26.6 us (3%)
    pallas_call x9, Pallas kernels, communicate(): pl.pallas_call(functools.partial(comm_kernel, plan), out_shape=shapes, in...  546 us
    pallas_call x4, Pallas kernels, attention_call(): pl.pallas_call(functools.partial(kernel, seq_reach()), out_shape=shapes,...  64 us
    dot_general x8, matrix products, dot_n(): return jnp.dot(a, b, preferred_element_type=jnp.float32)  26.6 us
    reduce_sum x4, other arithmetic, rms_norm(): vector * lax.rsqrt(jnp.mean(vector * vector, axis=-1, keepdims=True) + ep...  20.8 us

profile of v7, /device:TPU:0, one launch (start us, length us, event | category | flops | bytes accessed | tf_op | source)
XLA Modules:
  0.0 779.4 jit_solution(6721495102305692344)
XLA Ops:
  2.7 2.8 fusion.29
  6.3 2.0 all-gather
  8.4 1.8 all-gather.1
  10.3 1.8 all_gather.10
  14.7 1.0 copy.150
  17.3 2.1 stack.150.col
  19.5 1.6 slice_bitcast_fusion.25
  21.1 2.2 pad_maximum_fusion.3.refs_0_.refs_2_
  24.2 1.6 pad_maximum_fusion.2.refs_2_
  26.1 1.1 fusion.58.refs_3_.refs_4_
  27.2 29.5 %comm1.1 = (bf16[4,448,512]{2,1,0:T(8,128)(2,1)}, bf16[4,448,256]{2,1,0:T(8,128)(2,1)S(1)}) custom-call(bf16[2,448,512]{2,1,0:T(8,128)(2,1)} %pad_maximum_fusion.3.refs_0_.refs_2_, bf16[2,448,256]{2,1,0:T(8,128)(2,1)S(1)} %fusion.61.refs_1_.refs_3_), custom_call_target="tpu_custom_call" | custom-call | tf_op jit(solution)/shard_map/comm1/pallas_call | solution.py:676
  56.7 4.8 fusion.35.proj
  61.5 13.1 %attention10.2 = (bf16[2,512,256]{2,1,0:T(8,128)(2,1)S(1)}, f32[2,512,256]{2,1,0:T(8,128)S(1)}, f32[2,512,256]{2,1,0:T(8,128)S(1)}, bf16[2,160,256]{2,1,0:T(8,128)(2,1)S(1)}, f32[1,2,16,256]{3,2,1,0:T(8,128)S(1)}) custom-call(f32[2,512,512]{2,1,0:T(8,128)S(1)} %fusion.35.proj, f32[2,512,8]{2,1,0:T(8,128)S(1)} %stack.150.col, ...), custom_call_target="tpu_custom_call" | custom-call | tf_op jit(solution)/shard_map/attention10/pallas_call | solution.py:1101
  74.6 66.7 %comm2.1 = (bf16[2,512,1792]{2,1,0:T(8,128)(2,1)}, bf16[4,448,1280]{2,1,0:T(8,128)(2,1)}, bf16[4,448,640]{2,1,0:T(8,128)(2,1)}) custom-call(bf16[2,512,256]{2,1,0:T(8,128)(2,1)S(1)} %get-tuple-element.62.refs_0_, bf16[1792,256]{1,0:T(8,128)(2,1)S(1)} %bitcast.258, bf16[2,448,1280]{2,1,0:T(8,128)(2,1)} %pad_maximum_fusion.2.refs_2_, ...), custom_call_target="tpu_custom_call" | custom-call | tf_op jit(solution)/shard_map/comm2/pallas_call | solution.py:676
  141.3 4.6 multiply_reduce_fusion.1
  146.6 1.4 multiply_convert_fusion.2
  148.0 5.1 convolution_convert_fusion.1
  153.5 2.3 multiply_convert_fusion.5.refs_8_
  156.3 64.4 %comm4.1 = (bf16[2,512,1792]{2,1,0:T(8,128)(2,1)}, bf16[4,448,512]{2,1,0:T(8,128)(2,1)}, bf16[4,448,256]{2,1,0:T(8,128)(2,1)S(1)}, bf16[4,448,640]{2,1,0:T(8,128)(2,1)}) custom-call(bf16[2,512,640]{2,1,0:T(8,128)(2,1)} %bitcast.276, bf16[1792,640]{1,0:T(8,128)(2,1)} %bitcast.291, bf16[2,448,512]{2,1,0:T(8,128)(2,1)} %pad_maximum_fusion.3.refs_0_.refs_2_, ...), custom_call_target="tpu_custom_call" | custom-call | tf_op jit(solution)/shard_map/comm4/pallas_call | solution.py:676
  220.7 5.9 multiply_convert_fusion
  226.5 1.9 fusion.17
  230.3 1.9 copy-done.28
  232.2 2.0 fusion.77.proj
  234.2 13.4 %attention10.3 = (bf16[2,512,256]{2,1,0:T(8,128)(2,1)S(1)}, f32[2,512,256]{2,1,0:T(8,128)S(1)}, f32[2,512,256]{2,1,0:T(8,128)S(1)}, bf16[2,160,256]{2,1,0:T(8,128)(2,1)S(1)}, f32[1,2,16,256]{3,2,1,0:T(8,128)S(1)}) custom-call(f32[2,512,512]{2,1,0:T(8,128)S(1)} %fusion.77.proj, f32[2,512,8]{2,1,0:T(8,128)S(1)} %stack.150.col, ...), custom_call_target="tpu_custom_call" | custom-call | tf_op jit(solution)/shard_map/attention10/pallas_call | solution.py:1101
  247.6 66.1 %comm3.1 = (bf16[2,512,1792]{2,1,0:T(8,128)(2,1)}, bf16[4,448,1280]{2,1,0:T(8,128)(2,1)}) custom-call(bf16[2,512,256]{2,1,0:T(8,128)(2,1)S(1)} %get-tuple-element.69.refs_0_, bf16[1792,256]{1,0:T(8,128)(2,1)S(1)} %bitcast.260, bf16[2,448,1280]{2,1,0:T(8,128)(2,1)} %pad_maximum_fusion.2.refs_2_), custom_call_target="tpu_custom_call" | custom-call | tf_op jit(solution)/shard_map/comm3/pallas_call | solution.py:676
  313.8 4.5 multiply_reduce_fusion
  319.1 2.6 multiply_convert_fusion.1
  322.5 5.1 convolution_convert_fusion
  328.1 1.6 copy-done.27
  330.4 3.7 fusion.43
  334.2 1.8 pad_maximum_fusion.refs_3_
  336.0 62.9 %comm5.1 = (bf16[2,512,1792]{2,1,0:T(8,128)(2,1)}, bf16[1792,1280]{1,0:T(8,128)(2,1)}, bf16[1792,640]{1,0:T(8,128)(2,1)}) custom-call(bf16[2,512,1280]{2,1,0:T(8,128)(2,1)} %bitcast.269, bf16[1792,1280]{1,0:T(8,128)(2,1)} %bitcast.277, bf16[1024,1792]{1,0:T(8,128)(2,1)} %copy-done.29, bf16[1024,1280]{1,0:T(8,128)(2,1)} %pad_maximum_fusion.refs_3_, ...), custom_call_target="tpu_custom_call" | custom-call | tf_op jit(solution)/shard_map/comm5/pallas_call | solution.py:676
  399.0 5.4 fusion.7
  404.4 4.3 fusion.9.refs_5_
  408.8 1.8 copy-done.22
  410.6 1.1 fusion.78.bg
  411.7 18.6 %attention11.2 = (bf16[2,512,512]{2,1,0:T(8,128)(2,1)S(1)}, f32[8,256]{1,0:T(8,128)S(1)}) custom-call(f32[2,512,256]{2,1,0:T(8,128)S(1)} %fusion.78.bg, f32[2,512,512]{2,1,0:T(8,128)} %copy-done.1, f32[2,512,256]{2,1,0:T(8,128)S(1)} %get-tuple-element.75.att, f32[2,512,256]{2,1,0:T(8,128)S(1)} %get-tuple-element.76.conv, ...), custom_call_target="tpu_custom_call" | custom-call | tf_op jit(solution)/shard_map/attention11/pallas_call | solution.py:1101
  431.3 61.2 %comm8.1 = (bf16[2,512,1792]{2,1,0:T(8,128)(2,1)}, bf16[2,4,448,1280]{3,2,1,0:T(8,128)(2,1)}, bf16[1792,512]{1,0:T(8,128)(2,1)}, bf16[1792,256]{1,0:T(8,128)(2,1)S(1)}) custom-call(bf16[2,512,512]{2,1,0:T(8,128)(2,1)} %copy-done.5, bf16[1792,512]{1,0:T(8,128)(2,1)} %bitcast.300, bf16[4,448,1280]{2,1,0:T(8,128)(2,1)} %bitcast.281, ...), custom_call_target="tpu_custom_call" | custom-call | tf_op jit(solution)/shard_map/comm8/pallas_call | solution.py:676
  492.6 5.4 fusion.5
  498.1 4.3 fusion.11.refs_7_
  502.4 3.6 fusion.46
  506.1 1.7 pad_maximum_fusion.1.refs_6_
  507.8 64.3 %comm6.1 = (bf16[2,512,1792]{2,1,0:T(8,128)(2,1)}, bf16[2,4,448,640]{3,2,1,0:T(8,128)(2,1)}, bf16[2,4,448,512]{3,2,1,0:T(8,128)(2,1)}, bf16[2,4,448,256]{3,2,1,0...) custom-call(bf16[2,512,1280]{2,1,0:T(8,128)(2,1)} %bitcast.270, bf16[1792,1280]{1,0:T(8,128)(2,1)} %bitcast.282, ...), custom_call_target="tpu_custom_call" | custom-call | tf_op jit(solution)/shard_map/comm6/pallas_call | solution.py:676
  572.1 5.4 fusion.6
  577.5 4.1 fusion.13.refs_6_
  581.7 1.8 copy-done.20
  583.5 1.1 fusion.79.bg
  584.6 18.8 %attention11.3 = (bf16[2,512,512]{2,1,0:T(8,128)(2,1)S(1)}, f32[8,256]{1,0:T(8,128)S(1)}) custom-call(f32[2,512,256]{2,1,0:T(8,128)S(1)} %fusion.79.bg, f32[2,512,512]{2,1,0:T(8,128)} %copy-done, f32[2,512,256]{2,1,0:T(8,128)S(1)} %get-tuple-element.87.att, f32[2,512,256]{2,1,0:T(8,128)S(1)} %get-tuple-element.88.conv, ...), custom_call_target="tpu_custom_call" | custom-call | tf_op jit(solution)/shard_map/attention11/pallas_call | solution.py:1101
  603.5 1.0 copy-done.4
  604.4 62.7 %comm7.1 = (bf16[2,512,1792]{2,1,0:T(8,128)(2,1)}, bf16[2,4,448,1280]{3,2,1,0:T(8,128)(2,1)}, bf16[1792,512]{1,0:T(8,128)(2,1)}, bf16[1792,256]{1,0:T(8,128)(2,1)S(1)}) custom-call(bf16[2,512,512]{2,1,0:T(8,128)(2,1)} %copy-done.4, bf16[1792,512]{1,0:T(8,128)(2,1)} %bitcast.297, bf16[4,448,1280]{2,1,0:T(8,128)(2,1)} %bitcast.286, ...), custom_call_target="tpu_custom_call", output_to_operand_aliasing={{1}: (3, {})} | custom-call | tf_op jit(solution)/shard_map/comm7/pallas_call | solution.py:676
  667.1 4.5 fusion.30
  671.7 5.8 fusion.38
  677.6 68.7 %comm9.1 = (bf16[2,512,1792]{2,1,0:T(8,128)(2,1)}, bf16[2,4,448,640]{3,2,1,0:T(8,128)(2,1)}, bf16[2,4,448,512]{3,2,1,0:T(8,128)(2,1)}, bf16[2,4,448,256]{3,2,1,0...) custom-call(bf16[2,512,640]{2,1,0:T(8,128)(2,1)} %bitcast.253, ...), custom_call_target="tpu_custom_call", output_to_operand_aliasing={{1}: (5, {}), {2}: (6, {}), {3}: (7, {})} | custom-call | tf_op jit(solution)/shard_map/comm9/pallas_call | solution.py:676
  746.4 6.4 fusion.37
  754.8 1.2 copy.161
  756.0 2.8 convert_reduce_fusion.2
  760.2 1.2 maximum_bitcast_fusion.4
  762.3 1.2 maximum_bitcast_fusion.3
  763.5 3.7 convert_reduce_fusion.1
  767.4 1.8 maximum_bitcast_fusion.2
  769.2 3.5 convert_reduce_fusion
  772.7 2.6 slice_bitcast_fusion.3
  775.3 1.8 maximum_bitcast_fusion.1
  777.1 1.8 maximum_bitcast_fusion
  (197 shorter events, 19.6 us)
Async XLA Ops:
  0.6 7.7 copy-start.43
  0.7 12.6 %copy-start.38 = (bf16[1,448,448]{2,1,0:T(8,128)(2,1)S(1)}, bf16[1,448,448]{2,1,0:T(8,128)(2,1)}, u32[]{:S(2)}) copy-start(bf16[1,448,448]{2,1,0:T(8,128)(2,1)} %param.24) | copy-start | bytes 1204228
  0.7 9.6 %copy-start.41 = (bf16[1,3,1792]{2,1,0:T(4,128)(2,1)S(1)}, bf16[1,3,1792]{2,1,0:T(4,128)(2,1)}, u32[]{:S(2)}) copy-start(bf16[1,3,1792]{2,1,0:T(4,128)(2,1)} %param.23) | copy-start | bytes 32260
  0.7 11.5 %copy-start.40 = (bf16[1,448,64]{1,2,0:T(8,128)(2,1)S(1)}, bf16[1,448,64]{1,2,0:T(8,128)(2,1)}, u32[]{:S(2)}) copy-start(bf16[1,448,64]{1,2,0:T(8,128)(2,1)} %param.20) | copy-start | bytes 172036
  0.7 11.5 %copy-start.39 = (bf16[1,448,64]{1,2,0:T(8,128)(2,1)S(1)}, bf16[1,448,64]{1,2,0:T(8,128)(2,1)}, u32[]{:S(2)}) copy-start(bf16[1,448,64]{1,2,0:T(8,128)(2,1)} %param.19) | copy-start | bytes 172036
  0.7 5.6 copy-start.42
  19.5 3.9 copy-start.35
  19.5 4.1 copy-start.36
  23.9 1.8 copy-start.37
  56.7 4.8 copy-start.2
  56.7 4.8 copy-start.6
  61.5 79.8 %copy-start = (f32[2,512,512]{2,1,0:T(8,128)}, f32[2,512,512]{2,1,0:T(8,128)S(1)}, u32[]{:S(2)}) copy-start(f32[2,512,512]{2,1,0:T(8,128)S(1)} %fusion.35.proj) | copy-start | bytes 6291460
  141.3 4.6 copy-start.10
  141.3 5.3 copy-start.19
  141.3 6.7 slice-start.7
  146.6 1.4 slice-start.8
  153.5 2.8 copy-start.24
  220.7 5.9 copy-start.31
  226.5 1.9 copy-start.14
  228.5 1.8 copy-start.7
  229.3 2.9 copy-start.34
  230.3 1.9 copy-start.28
  234.2 84.1 %copy-start.1 = (f32[2,512,512]{2,1,0:T(8,128)}, f32[2,512,512]{2,1,0:T(8,128)S(1)}, u32[]{:S(2)}) copy-start(f32[2,512,512]{2,1,0:T(8,128)S(1)} %fusion.77.proj) | copy-start | bytes 6291460
  313.8 4.6 copy-start.8
  313.8 5.3 copy-start.26
  318.3 4.1 slice-start.5
  319.1 3.4 slice-start.6
  321.7 6.0 copy-start.12
  321.7 6.0 copy-start.29
  327.6 2.0 copy-start.27
  327.7 2.8 copy-start.33
  334.2 64.8 %copy-start.3 = (bf16[1024,640]{1,0:T(8,128)(2,1)}, bf16[1024,640]{1,0:T(8,128)(2,1)S(1)}, u32[]{:S(2)}) copy-start(bf16[1024,640]{1,0:T(8,128)(2,1)S(1)} %get-tuple-element.226.refs_5_) | copy-start | bytes 3932164
  398.9 5.5 copy-start.13
  398.9 5.5 copy-start.25
  408.8 1.8 copy-start.22
  430.3 1.0 copy-start.5
  492.6 5.5 copy-start.9
  492.6 5.5 copy-start.23
  492.6 9.8 %slice-start.3 = ((s8[5242880]{0:T(1024)(128)(4,1)}), s8[4194304]{0:T(1024)(128)(4,1)S(1)}, s32[]{:S(2)}) async-start(s8[5242880]{0:T(1024)(128)(4,1)} %bitcast.271), calls=%async_computation.3 | async-start | bytes 8388608
  498.1 4.3 slice-start.4
  498.1 4.3 copy-start.32
  502.4 3.7 copy-start.16
  572.1 5.5 copy-start.15
  572.1 5.5 copy-start.17
  581.6 1.8 copy-start.20
  603.5 1.0 copy-start.4
  604.4 62.7 %copy-start.11 = (bf16[2,512,1792]{2,1,0:T(8,128)(2,1)S(1)}, bf16[2,512,1792]{2,1,0:T(8,128)(2,1)}, u32[]{:S(2)}) copy-start(bf16[2,512,1792]{2,1,0:T(8,128)(2,1)} %param.16) | copy-start | bytes 11010052
  667.1 4.6 copy-start.18
  667.1 4.6 copy-start.21
  746.3 7.8 %copy-start.30 = (bf16[2,4,448,256]{3,2,1,0:T(8,128)(2,1)S(1)}, bf16[2,4,448,256]{3,2,1,0:T(8,128)(2,1)}, u32[]{:S(2)}) copy-start(bf16[2,4,448,256]{3,2,1,0:T(8,128)(2,1)} %get-tuple-element.106) | copy-start | bytes 5505028
  762.3 6.9 slice-start
  763.5 5.7 slice-start.1
  767.2 2.0 slice-start.2

commit v8 on v7

--- a/solution.py
+++ b/solution.py
@@ -1271,9 +1271,9 @@
 
     own_ffn = jnp.concatenate([filled(halves(w_gate[0])), filled(halves(w_up[0]))], axis=2)
     own_down = filled(halves(w_down[0].T))
-    gains_one = lax.all_gather(gain_attn[0], "section").astype(jnp.float32)
-    gains_two = lax.all_gather(gain_ffn[0], "section").astype(jnp.float32)
-    taps_all = lax.all_gather(conv_taps[0], "section").astype(jnp.float32)
+    rows_of_layer = jnp.concatenate([gain_attn, gain_ffn, conv_taps[0]], axis=0)
+    rows_all = lax.all_gather(rows_of_layer, "section").astype(jnp.float32)
+    gains_one, gains_two, taps_all = rows_all[:, 0], rows_all[:, 1], rows_all[:, 2:]
     taps_both = lax.dynamic_slice_in_dim(taps_all, (head_index * 2 + core) * values, values, 2)
     taps_both = jnp.pad(taps_both, ((0, 0), (0, 8 - KW), (0, keys)))
     first, rest = feature_tables(values)

time: 787 us -> 784 us (level)
  no operation moved by 1% of the time
where the time goes in v8:
time: 784 us; the launch traced here: 776 us
  Pallas kernels  610 us (78%)
  other arithmetic  105 us (13%)
  local copies, waits for them, and re-layouts  29.5 us (4%)
  matrix products  26.6 us (3%)
    pallas_call x9, Pallas kernels, communicate(): pl.pallas_call(functools.partial(comm_kernel, plan), out_shape=shapes, in...  546 us
    pallas_call x4, Pallas kernels, attention_call(): pl.pallas_call(functools.partial(kernel, seq_reach()), out_shape=shapes,...  63.8 us
    dot_general x8, matrix products, dot_n(): return jnp.dot(a, b, preferred_element_type=jnp.float32)  26.6 us
    reduce_sum x4, other arithmetic, rms_norm(): vector * lax.rsqrt(jnp.mean(vector * vector, axis=-1, keepdims=True) + ep...  20.8 us

profile of v8, /device:TPU:0, one launch (start us, length us, event | category | flops | bytes accessed | tf_op | source)
XLA Modules:
  0.0 775.8 jit_solution(5127849037949328714)
XLA Ops:
  2.7 2.8 fusion.29
  6.4 2.0 all-gather.1
  11.1 1.0 copy.150
  13.7 2.2 stack.150.col
  15.9 1.6 slice_bitcast_fusion.25
  17.5 2.2 pad_maximum_fusion.3.refs_0_.refs_2_
  20.6 1.6 pad_maximum_fusion.2.refs_2_
  22.4 1.1 fusion.58.refs_3_.refs_4_
  23.6 29.5 %comm1.1 = (bf16[4,448,512]{2,1,0:T(8,128)(2,1)}, bf16[4,448,256]{2,1,0:T(8,128)(2,1)S(1)}) custom-call(bf16[2,448,512]{2,1,0:T(8,128)(2,1)} %pad_maximum_fusion.3.refs_0_.refs_2_, bf16[2,448,256]{2,1,0:T(8,128)(2,1)S(1)} %fusion.61.refs_1_.refs_3_), custom_call_target="tpu_custom_call" | custom-call | tf_op jit(solution)/shard_map/comm1/pallas_call | solution.py:676
  53.1 4.8 fusion.35.proj
  57.9 13.1 %attention10.2 = (bf16[2,512,256]{2,1,0:T(8,128)(2,1)S(1)}, f32[2,512,256]{2,1,0:T(8,128)S(1)}, f32[2,512,256]{2,1,0:T(8,128)S(1)}, bf16[2,160,256]{2,1,0:T(8,128)(2,1)S(1)}, f32[1,2,16,256]{3,2,1,0:T(8,128)S(1)}) custom-call(f32[2,512,512]{2,1,0:T(8,128)S(1)} %fusion.35.proj, f32[2,512,8]{2,1,0:T(8,128)S(1)} %stack.150.col, ...), custom_call_target="tpu_custom_call" | custom-call | tf_op jit(solution)/shard_map/attention10/pallas_call | solution.py:1101
  71.1 66.7 %comm2.1 = (bf16[2,512,1792]{2,1,0:T(8,128)(2,1)}, bf16[4,448,1280]{2,1,0:T(8,128)(2,1)}, bf16[4,448,640]{2,1,0:T(8,128)(2,1)}) custom-call(bf16[2,512,256]{2,1,0:T(8,128)(2,1)S(1)} %get-tuple-element.62.refs_0_, bf16[1792,256]{1,0:T(8,128)(2,1)S(1)} %bitcast.259, bf16[2,448,1280]{2,1,0:T(8,128)(2,1)} %pad_maximum_fusion.2.refs_2_, ...), custom_call_target="tpu_custom_call" | custom-call | tf_op jit(solution)/shard_map/comm2/pallas_call | solution.py:676
  137.8 4.6 multiply_reduce_fusion.1
  143.1 1.4 multiply_convert_fusion.2
  144.5 5.1 convolution_convert_fusion.1
  150.0 2.4 multiply_convert_fusion.5.refs_8_
  152.8 64.3 %comm4.1 = (bf16[2,512,1792]{2,1,0:T(8,128)(2,1)}, bf16[4,448,512]{2,1,0:T(8,128)(2,1)}, bf16[4,448,256]{2,1,0:T(8,128)(2,1)S(1)}, bf16[4,448,640]{2,1,0:T(8,128)(2,1)}) custom-call(bf16[2,512,640]{2,1,0:T(8,128)(2,1)} %bitcast.277, bf16[1792,640]{1,0:T(8,128)(2,1)} %bitcast.292, bf16[2,448,512]{2,1,0:T(8,128)(2,1)} %pad_maximum_fusion.3.refs_0_.refs_2_, ...), custom_call_target="tpu_custom_call" | custom-call | tf_op jit(solution)/shard_map/comm4/pallas_call | solution.py:676
  217.2 5.9 multiply_convert_fusion
  223.0 1.9 fusion.17
  225.8 0.9 fusion.4.refs_3_
  226.7 1.9 copy-done.28
  228.6 2.0 fusion.77.proj
  230.7 13.4 %attention10.3 = (bf16[2,512,256]{2,1,0:T(8,128)(2,1)S(1)}, f32[2,512,256]{2,1,0:T(8,128)S(1)}, f32[2,512,256]{2,1,0:T(8,128)S(1)}, bf16[2,160,256]{2,1,0:T(8,128)(2,1)S(1)}, f32[1,2,16,256]{3,2,1,0:T(8,128)S(1)}) custom-call(f32[2,512,512]{2,1,0:T(8,128)S(1)} %fusion.77.proj, f32[2,512,8]{2,1,0:T(8,128)S(1)} %stack.150.col, ...), custom_call_target="tpu_custom_call" | custom-call | tf_op jit(solution)/shard_map/attention10/pallas_call | solution.py:1101
  244.1 66.2 %comm3.1 = (bf16[2,512,1792]{2,1,0:T(8,128)(2,1)}, bf16[4,448,1280]{2,1,0:T(8,128)(2,1)}) custom-call(bf16[2,512,256]{2,1,0:T(8,128)(2,1)S(1)} %get-tuple-element.69.refs_0_, bf16[1792,256]{1,0:T(8,128)(2,1)S(1)} %bitcast.261, bf16[2,448,1280]{2,1,0:T(8,128)(2,1)} %pad_maximum_fusion.2.refs_2_), custom_call_target="tpu_custom_call" | custom-call | tf_op jit(solution)/shard_map/comm3/pallas_call | solution.py:676
  310.3 4.5 multiply_reduce_fusion
  315.6 2.8 multiply_convert_fusion.1
  319.2 5.1 convolution_convert_fusion
  324.8 1.6 copy-done.27
  327.1 3.8 fusion.43
  331.0 1.8 pad_maximum_fusion.refs_3_
  332.8 62.9 %comm5.1 = (bf16[2,512,1792]{2,1,0:T(8,128)(2,1)}, bf16[1792,1280]{1,0:T(8,128)(2,1)}, bf16[1792,640]{1,0:T(8,128)(2,1)}) custom-call(bf16[2,512,1280]{2,1,0:T(8,128)(2,1)} %bitcast.270, bf16[1792,1280]{1,0:T(8,128)(2,1)} %bitcast.278, bf16[1024,1792]{1,0:T(8,128)(2,1)} %copy-done.29, bf16[1024,1280]{1,0:T(8,128)(2,1)} %pad_maximum_fusion.refs_3_, ...), custom_call_target="tpu_custom_call" | custom-call | tf_op jit(solution)/shard_map/comm5/pallas_call | solution.py:676
  395.7 5.4 fusion.7
  401.2 4.1 fusion.9.refs_5_
  405.3 1.8 copy-done.22
  407.1 1.1 fusion.78.bg
  408.3 18.5 %attention11.2 = (bf16[2,512,512]{2,1,0:T(8,128)(2,1)S(1)}, f32[8,256]{1,0:T(8,128)S(1)}) custom-call(f32[2,512,256]{2,1,0:T(8,128)S(1)} %fusion.78.bg, f32[2,512,512]{2,1,0:T(8,128)} %copy-done.1, f32[2,512,256]{2,1,0:T(8,128)S(1)} %get-tuple-element.75.att, f32[2,512,256]{2,1,0:T(8,128)S(1)} %get-tuple-element.76.conv, ...), custom_call_target="tpu_custom_call" | custom-call | tf_op jit(solution)/shard_map/attention11/pallas_call | solution.py:1101
  426.8 1.0 copy-done.5
  427.8 61.2 %comm8.1 = (bf16[2,512,1792]{2,1,0:T(8,128)(2,1)}, bf16[2,4,448,1280]{3,2,1,0:T(8,128)(2,1)}, bf16[1792,512]{1,0:T(8,128)(2,1)}, bf16[1792,256]{1,0:T(8,128)(2,1)S(1)}) custom-call(bf16[2,512,512]{2,1,0:T(8,128)(2,1)} %copy-done.5, bf16[1792,512]{1,0:T(8,128)(2,1)} %bitcast.301, bf16[4,448,1280]{2,1,0:T(8,128)(2,1)} %bitcast.282, ...), custom_call_target="tpu_custom_call" | custom-call | tf_op jit(solution)/shard_map/comm8/pallas_call | solution.py:676
  489.0 5.4 fusion.5
  494.5 4.2 fusion.11.refs_7_
  498.8 3.5 fusion.46
  502.3 1.7 pad_maximum_fusion.1.refs_6_
  504.1 64.3 %comm6.1 = (bf16[2,512,1792]{2,1,0:T(8,128)(2,1)}, bf16[2,4,448,640]{3,2,1,0:T(8,128)(2,1)}, bf16[2,4,448,512]{3,2,1,0:T(8,128)(2,1)}, bf16[2,4,448,256]{3,2,1,0...) custom-call(bf16[2,512,1280]{2,1,0:T(8,128)(2,1)} %bitcast.271, bf16[1792,1280]{1,0:T(8,128)(2,1)} %bitcast.283, ...), custom_call_target="tpu_custom_call" | custom-call | tf_op jit(solution)/shard_map/comm6/pallas_call | solution.py:676
  568.4 5.4 fusion.6
  573.8 4.0 fusion.13.refs_6_
  577.9 1.8 copy-done.20
  579.7 1.1 fusion.79.bg
  580.8 18.7 %attention11.3 = (bf16[2,512,512]{2,1,0:T(8,128)(2,1)S(1)}, f32[8,256]{1,0:T(8,128)S(1)}) custom-call(f32[2,512,256]{2,1,0:T(8,128)S(1)} %fusion.79.bg, f32[2,512,512]{2,1,0:T(8,128)} %copy-done, f32[2,512,256]{2,1,0:T(8,128)S(1)} %get-tuple-element.87.att, f32[2,512,256]{2,1,0:T(8,128)S(1)} %get-tuple-element.88.conv, ...), custom_call_target="tpu_custom_call" | custom-call | tf_op jit(solution)/shard_map/attention11/pallas_call | solution.py:1101
  599.6 1.0 copy-done.4
  600.5 62.6 %comm7.1 = (bf16[2,512,1792]{2,1,0:T(8,128)(2,1)}, bf16[2,4,448,1280]{3,2,1,0:T(8,128)(2,1)}, bf16[1792,512]{1,0:T(8,128)(2,1)}, bf16[1792,256]{1,0:T(8,128)(2,1)S(1)}) custom-call(bf16[2,512,512]{2,1,0:T(8,128)(2,1)} %copy-done.4, bf16[1792,512]{1,0:T(8,128)(2,1)} %bitcast.298, bf16[4,448,1280]{2,1,0:T(8,128)(2,1)} %bitcast.287, ...), custom_call_target="tpu_custom_call", output_to_operand_aliasing={{1}: (3, {})} | custom-call | tf_op jit(solution)/shard_map/comm7/pallas_call | solution.py:676
  663.2 4.6 fusion.30
  667.8 5.9 fusion.38
  673.8 68.7 %comm9.1 = (bf16[2,512,1792]{2,1,0:T(8,128)(2,1)}, bf16[2,4,448,640]{3,2,1,0:T(8,128)(2,1)}, bf16[2,4,448,512]{3,2,1,0:T(8,128)(2,1)}, bf16[2,4,448,256]{3,2,1,0...) custom-call(bf16[2,512,640]{2,1,0:T(8,128)(2,1)} %bitcast.254, ...), custom_call_target="tpu_custom_call", output_to_operand_aliasing={{1}: (5, {}), {2}: (6, {}), {3}: (7, {})} | custom-call | tf_op jit(solution)/shard_map/comm9/pallas_call | solution.py:676
  742.5 6.6 fusion.37
  751.2 1.2 copy.161
  752.4 2.8 convert_reduce_fusion.2
  756.5 1.2 maximum_bitcast_fusion.4
  758.6 1.2 maximum_bitcast_fusion.3
  759.8 3.8 convert_reduce_fusion.1
  763.8 1.8 maximum_bitcast_fusion.2
  765.6 3.5 convert_reduce_fusion
  769.1 2.6 slice_bitcast_fusion.3
  771.7 1.8 maximum_bitcast_fusion.1
  773.5 1.8 maximum_bitcast_fusion
  (195 shorter events, 17.7 us)
Async XLA Ops:
  0.6 5.7 copy-start.42
  0.7 9.0 %copy-start.38 = (bf16[1,448,448]{2,1,0:T(8,128)(2,1)S(1)}, bf16[1,448,448]{2,1,0:T(8,128)(2,1)}, u32[]{:S(2)}) copy-start(bf16[1,448,448]{2,1,0:T(8,128)(2,1)} %param.24) | copy-start | bytes 1204228
  0.7 5.7 copy-start.41
  0.7 8.0 %copy-start.40 = (bf16[1,448,64]{1,2,0:T(8,128)(2,1)S(1)}, bf16[1,448,64]{1,2,0:T(8,128)(2,1)}, u32[]{:S(2)}) copy-start(bf16[1,448,64]{1,2,0:T(8,128)(2,1)} %param.20) | copy-start | bytes 172036
  0.7 7.9 %copy-start.39 = (bf16[1,448,64]{1,2,0:T(8,128)(2,1)S(1)}, bf16[1,448,64]{1,2,0:T(8,128)(2,1)}, u32[]{:S(2)}) copy-start(bf16[1,448,64]{1,2,0:T(8,128)(2,1)} %param.19) | copy-start | bytes 172036
  0.7 5.6 copy-start.43
  15.9 3.9 copy-start.35
  15.9 4.1 copy-start.36
  20.3 1.8 copy-start.37
  53.1 4.8 copy-start.2
  53.1 4.8 copy-start.6
  57.9 79.9 %copy-start = (f32[2,512,512]{2,1,0:T(8,128)}, f32[2,512,512]{2,1,0:T(8,128)S(1)}, u32[]{:S(2)}) copy-start(f32[2,512,512]{2,1,0:T(8,128)S(1)} %fusion.35.proj) | copy-start | bytes 6291460
  137.8 4.6 copy-start.10
  137.8 5.3 copy-start.19
  137.8 6.7 slice-start.7
  143.1 1.4 slice-start.8
  150.0 2.8 copy-start.24
  217.1 5.9 copy-start.31
  223.0 1.9 copy-start.14
  225.0 1.8 copy-start.7
  225.8 2.9 copy-start.34
  226.7 1.9 copy-start.28
  230.7 84.2 %copy-start.1 = (f32[2,512,512]{2,1,0:T(8,128)}, f32[2,512,512]{2,1,0:T(8,128)S(1)}, u32[]{:S(2)}) copy-start(f32[2,512,512]{2,1,0:T(8,128)S(1)} %fusion.77.proj) | copy-start | bytes 6291460
  310.3 4.6 copy-start.8
  310.3 5.3 copy-start.26
  314.8 4.3 slice-start.5
  315.6 3.6 slice-start.6
  318.4 6.0 copy-start.12
  318.4 6.0 copy-start.29
  324.3 2.0 copy-start.27
  324.4 2.8 copy-start.33
  331.0 64.8 %copy-start.3 = (bf16[1024,640]{1,0:T(8,128)(2,1)}, bf16[1024,640]{1,0:T(8,128)(2,1)S(1)}, u32[]{:S(2)}) copy-start(bf16[1024,640]{1,0:T(8,128)(2,1)S(1)} %get-tuple-element.226.refs_5_) | copy-start | bytes 3932164
  395.7 5.5 copy-start.13
  395.7 5.5 copy-start.25
  405.3 1.8 copy-start.22
  426.8 1.0 copy-start.5
  489.0 5.5 copy-start.9
  489.0 5.5 copy-start.23
  489.0 9.8 %slice-start.3 = ((s8[5242880]{0:T(1024)(128)(4,1)}), s8[4194304]{0:T(1024)(128)(4,1)S(1)}, s32[]{:S(2)}) async-start(s8[5242880]{0:T(1024)(128)(4,1)} %bitcast.272), calls=%async_computation.3 | async-start | bytes 8388608
  494.5 4.3 slice-start.4
  494.5 4.3 copy-start.32
  498.8 3.5 copy-start.16
  568.4 5.5 copy-start.15
  568.4 5.5 copy-start.17
  577.8 1.8 copy-start.20
  599.6 1.0 copy-start.4
  600.5 62.6 %copy-start.11 = (bf16[2,512,1792]{2,1,0:T(8,128)(2,1)S(1)}, bf16[2,512,1792]{2,1,0:T(8,128)(2,1)}, u32[]{:S(2)}) copy-start(bf16[2,512,1792]{2,1,0:T(8,128)(2,1)} %param.16) | copy-start | bytes 11010052
  663.2 4.6 copy-start.18
  663.2 4.6 copy-start.21
  742.5 8.0 %copy-start.30 = (bf16[2,4,448,256]{3,2,1,0:T(8,128)(2,1)S(1)}, bf16[2,4,448,256]{3,2,1,0:T(8,128)(2,1)}, u32[]{:S(2)}) copy-start(bf16[2,4,448,256]{3,2,1,0:T(8,128)(2,1)} %get-tuple-element.106) | copy-start | bytes 5505028
  758.6 7.0 slice-start
  759.8 5.8 slice-start.1
  763.6 2.0 slice-start.2

commit v9 on v8

--- a/solution.py
+++ b/solution.py
@@ -676,7 +676,8 @@
     outs = pl.pallas_call(
         functools.partial(comm_kernel, plan),
         out_shape=shapes,
-        in_specs=[vmem] * first
+        in_specs=[vmem] * len(p_in)
+        + [anywhere if has_sum else vmem] * len(w_in)
         + [anywhere] * (len(g_in) + len(into) + len(m_in))
         + [vmem] * len(s_in),
         out_specs=[vmem] * has_sum

time: 784 us -> 780 us (level)
  no operation moved by 1% of the time
where the time goes in v9:
time: 780 us; the launch traced here: 772 us
  Pallas kernels  606 us (78%)
  other arithmetic  105 us (13%)
  local copies, waits for them, and re-layouts  29.5 us (4%)
  matrix products  26.6 us (3%)
    pallas_call x9, Pallas kernels, communicate(): pl.pallas_call(functools.partial(comm_kernel, plan), out_shape=shapes, in...  542 us
    pallas_call x4, Pallas kernels, attention_call(): pl.pallas_call(functools.partial(kernel, seq_reach()), out_shape=shapes,...  63.8 us
    dot_general x8, matrix products, dot_n(): return jnp.dot(a, b, preferred_element_type=jnp.float32)  26.6 us
    reduce_sum x4, other arithmetic, rms_norm(): vector * lax.rsqrt(jnp.mean(vector * vector, axis=-1, keepdims=True) + ep...  20.8 us

profile of v9, /device:TPU:0, one launch (start us, length us, event | category | flops | bytes accessed | tf_op | source)
XLA Modules:
  0.0 771.7 jit_solution(13932260645997759724)
XLA Ops:
  2.7 2.8 fusion.29
  6.4 2.0 all-gather.1
  11.1 1.0 copy.150
  13.7 2.2 stack.150.col
  15.9 1.6 slice_bitcast_fusion.25
  17.5 2.2 pad_maximum_fusion.3.refs_0_.refs_2_
  20.6 1.6 pad_maximum_fusion.2.refs_2_
  22.4 1.1 fusion.58.refs_3_.refs_4_
  23.6 29.5 %comm1.1 = (bf16[4,448,512]{2,1,0:T(8,128)(2,1)}, bf16[4,448,256]{2,1,0:T(8,128)(2,1)S(1)}) custom-call(bf16[2,448,512]{2,1,0:T(8,128)(2,1)} %pad_maximum_fusion.3.refs_0_.refs_2_, bf16[2,448,256]{2,1,0:T(8,128)(2,1)S(1)} %fusion.61.refs_1_.refs_3_), custom_call_target="tpu_custom_call" | custom-call | tf_op jit(solution)/shard_map/comm1/pallas_call | solution.py:676
  53.1 4.8 fusion.35.proj
  57.9 13.1 %attention10.2 = (bf16[2,512,256]{2,1,0:T(8,128)(2,1)S(1)}, f32[2,512,256]{2,1,0:T(8,128)S(1)}, f32[2,512,256]{2,1,0:T(8,128)S(1)}, bf16[2,160,256]{2,1,0:T(8,128)(2,1)S(1)}, f32[1,2,16,256]{3,2,1,0:T(8,128)S(1)}) custom-call(f32[2,512,512]{2,1,0:T(8,128)S(1)} %fusion.35.proj, f32[2,512,8]{2,1,0:T(8,128)S(1)} %stack.150.col, ...), custom_call_target="tpu_custom_call" | custom-call | tf_op jit(solution)/shard_map/attention10/pallas_call | solution.py:1102
  71.1 65.0 %comm2.1 = (bf16[2,512,1792]{2,1,0:T(8,128)(2,1)}, bf16[4,448,1280]{2,1,0:T(8,128)(2,1)}, bf16[4,448,640]{2,1,0:T(8,128)(2,1)}) custom-call(bf16[2,512,256]{2,1,0:T(8,128)(2,1)S(1)} %get-tuple-element.62.refs_0_, bf16[1792,256]{1,0:T(8,128)(2,1)S(1)} %bitcast.259, bf16[2,448,1280]{2,1,0:T(8,128)(2,1)} %pad_maximum_fusion.2.refs_2_, ...), custom_call_target="tpu_custom_call" | custom-call | tf_op jit(solution)/shard_map/comm2/pallas_call | solution.py:676
  136.1 4.6 multiply_reduce_fusion.1
  141.3 1.4 multiply_convert_fusion.2
  142.7 5.1 convolution_convert_fusion.1
  148.3 2.4 multiply_convert_fusion.5.refs_8_
  151.1 63.8 %comm4.1 = (bf16[2,512,1792]{2,1,0:T(8,128)(2,1)}, bf16[4,448,512]{2,1,0:T(8,128)(2,1)}, bf16[4,448,256]{2,1,0:T(8,128)(2,1)S(1)}, bf16[4,448,640]{2,1,0:T(8,128)(2,1)}) custom-call(bf16[2,512,640]{2,1,0:T(8,128)(2,1)} %bitcast.277, bf16[1792,640]{1,0:T(8,128)(2,1)} %bitcast.292, bf16[2,448,512]{2,1,0:T(8,128)(2,1)} %pad_maximum_fusion.3.refs_0_.refs_2_, ...), custom_call_target="tpu_custom_call" | custom-call | tf_op jit(solution)/shard_map/comm4/pallas_call | solution.py:676
  214.9 5.9 multiply_convert_fusion
  220.7 1.9 fusion.17
  223.5 0.9 fusion.4.refs_3_
  224.4 1.9 copy-done.28
  226.4 2.0 fusion.77.proj
  228.4 13.4 %attention10.3 = (bf16[2,512,256]{2,1,0:T(8,128)(2,1)S(1)}, f32[2,512,256]{2,1,0:T(8,128)S(1)}, f32[2,512,256]{2,1,0:T(8,128)S(1)}, bf16[2,160,256]{2,1,0:T(8,128)(2,1)S(1)}, f32[1,2,16,256]{3,2,1,0:T(8,128)S(1)}) custom-call(f32[2,512,512]{2,1,0:T(8,128)S(1)} %fusion.77.proj, f32[2,512,8]{2,1,0:T(8,128)S(1)} %stack.150.col, ...), custom_call_target="tpu_custom_call" | custom-call | tf_op jit(solution)/shard_map/attention10/pallas_call | solution.py:1102
  241.8 64.3 %comm3.1 = (bf16[2,512,1792]{2,1,0:T(8,128)(2,1)}, bf16[4,448,1280]{2,1,0:T(8,128)(2,1)}) custom-call(bf16[2,512,256]{2,1,0:T(8,128)(2,1)S(1)} %get-tuple-element.69.refs_0_, bf16[1792,256]{1,0:T(8,128)(2,1)S(1)} %bitcast.261, bf16[2,448,1280]{2,1,0:T(8,128)(2,1)} %pad_maximum_fusion.2.refs_2_), custom_call_target="tpu_custom_call" | custom-call | tf_op jit(solution)/shard_map/comm3/pallas_call | solution.py:676
  306.2 4.5 multiply_reduce_fusion
  311.4 2.8 multiply_convert_fusion.1
  315.1 5.1 convolution_convert_fusion
  320.6 1.6 copy-done.27
  323.0 3.8 fusion.43
  326.8 1.8 pad_maximum_fusion.refs_3_
  328.7 62.9 %comm5.1 = (bf16[2,512,1792]{2,1,0:T(8,128)(2,1)}, bf16[1792,1280]{1,0:T(8,128)(2,1)}, bf16[1792,640]{1,0:T(8,128)(2,1)}) custom-call(bf16[2,512,1280]{2,1,0:T(8,128)(2,1)} %bitcast.270, bf16[1792,1280]{1,0:T(8,128)(2,1)} %bitcast.278, bf16[1024,1792]{1,0:T(8,128)(2,1)} %copy-done.29, bf16[1024,1280]{1,0:T(8,128)(2,1)} %pad_maximum_fusion.refs_3_, ...), custom_call_target="tpu_custom_call" | custom-call | tf_op jit(solution)/shard_map/comm5/pallas_call | solution.py:676
  391.6 5.4 fusion.7
  397.1 4.1 fusion.9.refs_5_
  401.2 1.8 copy-done.22
  403.0 1.1 fusion.78.bg
  404.1 18.5 %attention11.2 = (bf16[2,512,512]{2,1,0:T(8,128)(2,1)S(1)}, f32[8,256]{1,0:T(8,128)S(1)}) custom-call(f32[2,512,256]{2,1,0:T(8,128)S(1)} %fusion.78.bg, f32[2,512,512]{2,1,0:T(8,128)} %copy-done.1, f32[2,512,256]{2,1,0:T(8,128)S(1)} %get-tuple-element.75.att, f32[2,512,256]{2,1,0:T(8,128)S(1)} %get-tuple-element.76.conv, ...), custom_call_target="tpu_custom_call" | custom-call | tf_op jit(solution)/shard_map/attention11/pallas_call | solution.py:1102
  422.7 1.0 copy-done.5
  423.6 61.3 %comm8.1 = (bf16[2,512,1792]{2,1,0:T(8,128)(2,1)}, bf16[2,4,448,1280]{3,2,1,0:T(8,128)(2,1)}, bf16[1792,512]{1,0:T(8,128)(2,1)}, bf16[1792,256]{1,0:T(8,128)(2,1)S(1)}) custom-call(bf16[2,512,512]{2,1,0:T(8,128)(2,1)} %copy-done.5, bf16[1792,512]{1,0:T(8,128)(2,1)} %bitcast.301, bf16[4,448,1280]{2,1,0:T(8,128)(2,1)} %bitcast.282, ...), custom_call_target="tpu_custom_call" | custom-call | tf_op jit(solution)/shard_map/comm8/pallas_call | solution.py:676
  484.9 5.4 fusion.5
  490.4 4.2 fusion.11.refs_7_
  494.7 3.5 fusion.46
  498.2 1.7 pad_maximum_fusion.1.refs_6_
  500.0 64.3 %comm6.1 = (bf16[2,512,1792]{2,1,0:T(8,128)(2,1)}, bf16[2,4,448,640]{3,2,1,0:T(8,128)(2,1)}, bf16[2,4,448,512]{3,2,1,0:T(8,128)(2,1)}, bf16[2,4,448,256]{3,2,1,0...) custom-call(bf16[2,512,1280]{2,1,0:T(8,128)(2,1)} %bitcast.271, bf16[1792,1280]{1,0:T(8,128)(2,1)} %bitcast.283, ...), custom_call_target="tpu_custom_call" | custom-call | tf_op jit(solution)/shard_map/comm6/pallas_call | solution.py:676
  564.3 5.4 fusion.6
  569.7 4.0 fusion.13.refs_6_
  573.8 1.8 copy-done.20
  575.6 1.1 fusion.79.bg
  576.7 18.7 %attention11.3 = (bf16[2,512,512]{2,1,0:T(8,128)(2,1)S(1)}, f32[8,256]{1,0:T(8,128)S(1)}) custom-call(f32[2,512,256]{2,1,0:T(8,128)S(1)} %fusion.79.bg, f32[2,512,512]{2,1,0:T(8,128)} %copy-done, f32[2,512,256]{2,1,0:T(8,128)S(1)} %get-tuple-element.87.att, f32[2,512,256]{2,1,0:T(8,128)S(1)} %get-tuple-element.88.conv, ...), custom_call_target="tpu_custom_call" | custom-call | tf_op jit(solution)/shard_map/attention11/pallas_call | solution.py:1102
  595.5 1.0 copy-done.4
  596.4 62.6 %comm7.1 = (bf16[2,512,1792]{2,1,0:T(8,128)(2,1)}, bf16[2,4,448,1280]{3,2,1,0:T(8,128)(2,1)}, bf16[1792,512]{1,0:T(8,128)(2,1)}, bf16[1792,256]{1,0:T(8,128)(2,1)S(1)}) custom-call(bf16[2,512,512]{2,1,0:T(8,128)(2,1)} %copy-done.4, bf16[1792,512]{1,0:T(8,128)(2,1)} %bitcast.298, bf16[4,448,1280]{2,1,0:T(8,128)(2,1)} %bitcast.287, ...), custom_call_target="tpu_custom_call", output_to_operand_aliasing={{1}: (3, {})} | custom-call | tf_op jit(solution)/shard_map/comm7/pallas_call | solution.py:676
  659.1 4.6 fusion.30
  663.7 5.9 fusion.38
  669.7 68.7 %comm9.1 = (bf16[2,512,1792]{2,1,0:T(8,128)(2,1)}, bf16[2,4,448,640]{3,2,1,0:T(8,128)(2,1)}, bf16[2,4,448,512]{3,2,1,0:T(8,128)(2,1)}, bf16[2,4,448,256]{3,2,1,0...) custom-call(bf16[2,512,640]{2,1,0:T(8,128)(2,1)} %bitcast.254, ...), custom_call_target="tpu_custom_call", output_to_operand_aliasing={{1}: (5, {}), {2}: (6, {}), {3}: (7, {})} | custom-call | tf_op jit(solution)/shard_map/comm9/pallas_call | solution.py:676
  738.4 6.6 fusion.37
  747.0 1.2 copy.161
  748.3 2.8 convert_reduce_fusion.2
  752.4 1.2 maximum_bitcast_fusion.4
  754.5 1.2 maximum_bitcast_fusion.3
  755.7 3.8 convert_reduce_fusion.1
  759.7 1.8 maximum_bitcast_fusion.2
  761.5 3.5 convert_reduce_fusion
  765.0 2.6 slice_bitcast_fusion.3
  767.6 1.8 maximum_bitcast_fusion.1
  769.4 1.8 maximum_bitcast_fusion
  (195 shorter events, 17.7 us)
Async XLA Ops:
  0.6 5.7 copy-start.42
  0.7 9.0 %copy-start.38 = (bf16[1,448,448]{2,1,0:T(8,128)(2,1)S(1)}, bf16[1,448,448]{2,1,0:T(8,128)(2,1)}, u32[]{:S(2)}) copy-start(bf16[1,448,448]{2,1,0:T(8,128)(2,1)} %param.24) | copy-start | bytes 1204228
  0.7 5.7 copy-start.41
  0.7 8.0 %copy-start.40 = (bf16[1,448,64]{1,2,0:T(8,128)(2,1)S(1)}, bf16[1,448,64]{1,2,0:T(8,128)(2,1)}, u32[]{:S(2)}) copy-start(bf16[1,448,64]{1,2,0:T(8,128)(2,1)} %param.20) | copy-start | bytes 172036
  0.7 7.9 %copy-start.39 = (bf16[1,448,64]{1,2,0:T(8,128)(2,1)S(1)}, bf16[1,448,64]{1,2,0:T(8,128)(2,1)}, u32[]{:S(2)}) copy-start(bf16[1,448,64]{1,2,0:T(8,128)(2,1)} %param.19) | copy-start | bytes 172036
  0.7 5.6 copy-start.43
  15.9 3.9 copy-start.35
  15.9 4.1 copy-start.36
  20.3 1.8 copy-start.37
  53.1 4.8 copy-start.2
  53.1 4.8 copy-start.6
  57.9 78.1 %copy-start = (f32[2,512,512]{2,1,0:T(8,128)}, f32[2,512,512]{2,1,0:T(8,128)S(1)}, u32[]{:S(2)}) copy-start(f32[2,512,512]{2,1,0:T(8,128)S(1)} %fusion.35.proj) | copy-start | bytes 6291460
  136.0 4.6 copy-start.10
  136.0 5.3 copy-start.19
  136.1 6.7 slice-start.7
  141.3 1.4 slice-start.8
  148.2 2.8 copy-start.24
  214.9 5.9 copy-start.31
  220.7 1.9 copy-start.14
  222.7 1.8 copy-start.7
  223.5 2.9 copy-start.34
  224.4 1.9 copy-start.28
  228.4 82.3 %copy-start.1 = (f32[2,512,512]{2,1,0:T(8,128)}, f32[2,512,512]{2,1,0:T(8,128)S(1)}, u32[]{:S(2)}) copy-start(f32[2,512,512]{2,1,0:T(8,128)S(1)} %fusion.77.proj) | copy-start | bytes 6291460
  306.1 4.6 copy-start.8
  306.1 5.3 copy-start.26
  310.7 4.3 slice-start.5
  311.4 3.6 slice-start.6
  314.2 6.0 copy-start.12
  314.2 6.0 copy-start.29
  320.2 2.0 copy-start.27
  320.2 2.8 copy-start.33
  326.8 64.8 %copy-start.3 = (bf16[1024,640]{1,0:T(8,128)(2,1)}, bf16[1024,640]{1,0:T(8,128)(2,1)S(1)}, u32[]{:S(2)}) copy-start(bf16[1024,640]{1,0:T(8,128)(2,1)S(1)} %get-tuple-element.226.refs_5_) | copy-start | bytes 3932164
  391.6 5.5 copy-start.13
  391.6 5.5 copy-start.25
  401.2 1.8 copy-start.22
  422.7 1.0 copy-start.5
  484.9 5.5 copy-start.9
  484.9 5.5 copy-start.23
  484.9 9.8 %slice-start.3 = ((s8[5242880]{0:T(1024)(128)(4,1)}), s8[4194304]{0:T(1024)(128)(4,1)S(1)}, s32[]{:S(2)}) async-start(s8[5242880]{0:T(1024)(128)(4,1)} %bitcast.272), calls=%async_computation.3 | async-start | bytes 8388608
  490.4 4.3 slice-start.4
  490.4 4.3 copy-start.32
  494.7 3.5 copy-start.16
  564.3 5.5 copy-start.15
  564.3 5.5 copy-start.17
  573.7 1.8 copy-start.20
  595.5 1.0 copy-start.4
  596.4 62.6 %copy-start.11 = (bf16[2,512,1792]{2,1,0:T(8,128)(2,1)S(1)}, bf16[2,512,1792]{2,1,0:T(8,128)(2,1)}, u32[]{:S(2)}) copy-start(bf16[2,512,1792]{2,1,0:T(8,128)(2,1)} %param.16) | copy-start | bytes 11010052
  659.1 4.6 copy-start.18
  659.1 4.6 copy-start.21
  738.4 8.0 %copy-start.30 = (bf16[2,4,448,256]{3,2,1,0:T(8,128)(2,1)S(1)}, bf16[2,4,448,256]{3,2,1,0:T(8,128)(2,1)}, u32[]{:S(2)}) copy-start(bf16[2,4,448,256]{3,2,1,0:T(8,128)(2,1)} %get-tuple-element.106) | copy-start | bytes 5505028
  754.5 7.0 slice-start
  755.7 5.8 slice-start.1
  759.5 2.0 slice-start.2
